TPU v7x, 8 devices: a whole 2x2x1 slice. The times are simulated.
8 devices in a mesh: dp: 2 (over z, y), cp: 4 (over x, core).
Axes of the slice: x: 2, y: 2, z: 1, core: 2. Of those that a mesh axis runs over, the one named last changes fastest.
Arguments:
- hidden: bfloat16 [4096, 2048], P(('dp', 'cp')), parts along dimension 0
- grad_out: bfloat16 [4096, 2048], P(('dp', 'cp')), parts along dimension 0
- w_query: bfloat16 [2048, 16, 128], replicated
- w_key: bfloat16 [2048, 2, 128], replicated
- w_value: bfloat16 [2048, 2, 128], replicated
- w_out: bfloat16 [16, 128, 2048], replicated
Outputs:
- output 1: bfloat16 [4096, 2048], P(('dp', 'cp')), parts along dimension 0
- output 2: bfloat16 [4096, 2048], P(('dp', 'cp')), parts along dimension 0
- output 3: float32 [4096, 16, 128], P('dp'), parts along dimension 0
- output 4: float32 [4096, 2, 128], P('dp'), parts along dimension 0
- output 5: float32 [4096, 2, 128], P('dp'), parts along dimension 0
- output 6: float32 [32, 128, 2048], P('dp'), parts along dimension 0
There are 2 independent parts. A program takes and returns all parts, laid end to end along the dimension named above; an argument that names none is the same for every part.
All inputs are finite; a program needn't handle non-finite values.
Results may differ from a plain program's by a relative error of at most 0.0107973.
Values are sent between devices in bfloat16 or wider.
A program may use at most 1 GiB of HBM per device.

v0:
```python
import jax
import jax.numpy as jnp
from jax import lax
from jax.sharding import PartitionSpec as P


def token_positions(groups, tok_local):
    half_len = tok_local // 2
    row_ids = jnp.arange(groups * tok_local)
    owner_dev = row_ids // tok_local
    within = row_ids % tok_local
    block_idx = jnp.where(within < half_len, owner_dev, 2 * groups - 1 - owner_dev)
    return block_idx * half_len + within % half_len


def solution(mesh):
    groups = mesh.shape["cp"]
    row_spec = P(("dp", "cp"), None)
    rep_spec = P(None, None, None)
    part_spec = P("dp", None, None)

    def device_layer(hidden, grad_out, w_query, w_key, w_value, w_out):
        tok_local, model_width = hidden.shape
        num_heads, head_dim = w_query.shape[1], w_query.shape[2]
        kv_heads = w_key.shape[1]
        group_size = num_heads // kv_heads
        half_len = tok_local // 2
        score_scale = head_dim ** -0.5
        group_rank = lax.axis_index("cp")
        key_pos = token_positions(groups, tok_local)
        local_idx = jnp.arange(tok_local)
        query_pos = jnp.where(local_idx < half_len, group_rank, 2 * groups - 1 - group_rank) * half_len + local_idx % half_len
        visible = query_pos[:, None] >= key_pos[None, :]
        wq_flat = w_query.reshape(model_width, num_heads * head_dim)
        wk_flat = w_key.reshape(model_width, kv_heads * head_dim)
        wv_flat = w_value.reshape(model_width, kv_heads * head_dim)
        wo_flat = w_out.reshape(num_heads * head_dim, model_width)
        query_heads = jnp.dot(hidden, wq_flat, preferred_element_type=jnp.float32).astype(jnp.bfloat16)
        query_heads = query_heads.reshape(tok_local, kv_heads, group_size, head_dim)
        key_local = jnp.dot(hidden, wk_flat, preferred_element_type=jnp.float32).astype(jnp.bfloat16)
        value_local = jnp.dot(hidden, wv_flat, preferred_element_type=jnp.float32).astype(jnp.bfloat16)
        kv_local = jnp.stack([key_local, value_local]).reshape(2, tok_local, kv_heads, head_dim)
        kv_all = lax.all_gather(kv_local, "cp", axis=1, tiled=True)
        key_rows, value_rows = kv_all[0], kv_all[1]
        scores = jnp.einsum("tkgd,skd->kgts", query_heads, key_rows, preferred_element_type=jnp.float32) * score_scale
        masked = jnp.where(visible, scores, -jnp.inf)
        log_norm = jax.nn.logsumexp(masked, axis=-1)
        att_probs = jnp.exp(masked - log_norm[..., None]).astype(jnp.bfloat16)
        attended = jnp.einsum("kgts,skd->tkgd", att_probs, value_rows, preferred_element_type=jnp.float32).astype(jnp.bfloat16)
        att_flat = attended.reshape(tok_local, num_heads * head_dim)
        output = jnp.dot(att_flat, wo_flat, preferred_element_type=jnp.float32).astype(jnp.bfloat16)
        dout_flat = jnp.einsum("tm,em->te", grad_out, wo_flat, preferred_element_type=jnp.float32).astype(jnp.bfloat16)
        dout_heads = dout_flat.reshape(tok_local, kv_heads, group_size, head_dim)
        delta_rows = jnp.einsum("tkgd,tkgd->kgt", dout_heads, attended, preferred_element_type=jnp.float32)
        d_probs = jnp.einsum("tkgd,skd->kgts", dout_heads, value_rows, preferred_element_type=jnp.float32)
        d_scores = (att_probs.astype(jnp.float32) * (d_probs - delta_rows[..., None])).astype(jnp.bfloat16)
        query_grad = jnp.einsum("kgts,skd->tkgd", d_scores, key_rows, preferred_element_type=jnp.float32) * score_scale
        query_grad = query_grad.astype(jnp.bfloat16).reshape(tok_local, num_heads * head_dim)
        key_part = jnp.einsum("kgts,tkgd->skd", d_scores, query_heads, preferred_element_type=jnp.float32) * score_scale
        value_part = jnp.einsum("kgts,tkgd->skd", att_probs, dout_heads, preferred_element_type=jnp.float32)
        kv_grad = lax.psum_scatter(jnp.stack([key_part, value_part]), "cp", scatter_dimension=1, tiled=True)
        key_grad = kv_grad[0].astype(jnp.bfloat16).reshape(tok_local, kv_heads * head_dim)
        value_grad = kv_grad[1].astype(jnp.bfloat16).reshape(tok_local, kv_heads * head_dim)
        grad_hidden = (
            jnp.einsum("te,me->tm", query_grad, wq_flat, preferred_element_type=jnp.float32)
            + jnp.einsum("te,me->tm", key_grad, wk_flat, preferred_element_type=jnp.float32)
            + jnp.einsum("te,me->tm", value_grad, wv_flat, preferred_element_type=jnp.float32)
        ).astype(jnp.bfloat16)
        weight_parts = (
            jnp.einsum("tm,te->me", hidden, query_grad, preferred_element_type=jnp.float32),
            jnp.einsum("tm,te->me", hidden, key_grad, preferred_element_type=jnp.float32),
            jnp.einsum("tm,te->me", hidden, value_grad, preferred_element_type=jnp.float32),
            jnp.einsum("te,tm->em", att_flat, grad_out, preferred_element_type=jnp.float32),
        )
        grad_w_query, grad_w_key, grad_w_value, grad_w_out = lax.psum(weight_parts, "cp")
        return (
            output,
            grad_hidden,
            grad_w_query.reshape(model_width, num_heads, head_dim),
            grad_w_key.reshape(model_width, kv_heads, head_dim),
            grad_w_value.reshape(model_width, kv_heads, head_dim),
            grad_w_out.reshape(num_heads, head_dim, model_width),
        )

    return jax.shard_map(
        device_layer,
        mesh=mesh,
        in_specs=(row_spec, row_spec, rep_spec, rep_spec, rep_spec, rep_spec),
        out_specs=(row_spec, row_spec, part_spec, part_spec, part_spec, part_spec),
        check_vma=False,
    )
```

profile of v0, /device:TPU:0, one launch (start us, length us, event | category | flops | bytes accessed | tf_op | source)
XLA Modules:
  0.0 1024.8 jit_solution(16465895642984908970)
XLA Ops:
  7.2 0.0 copy-start
  7.2 0.0 copy-start.6
  7.2 0.0 all-gather.2.cloned.1.call-start
  7.2 1.5 copy-done
  8.8 2.7 convolution_convert_fusion.4
  11.4 1.1 copy.12
  12.6 0.0 copy-done.6
  12.6 1.5 convolution_convert_fusion.3
  14.0 1.1 copy.13
  15.2 0.8 pad_maximum_fusion.1
  16.0 0.0 all-gather.2.cloned.1.call-update
  16.0 0.0 reduce-scatter.2.cloned.1.call-start
  16.1 8.2 fusion.19
  24.3 0.0 copy-start.9
  24.3 2.0 copy.58
  26.2 0.0 copy-done.9
  26.2 8.1 fusion.18
  34.4 0.6 copy.59
  35.0 0.0 copy-start.1
  35.0 1.3 copy-done.1
  36.3 2.3 bitcast_convert_fusion
  38.7 5.2 copy.40
  43.9 0.8 broadcast_compare_fusion
  44.7 0.0 all-gather.2.cloned.1.call-done
  44.7 26.8 %fusion.2 = (f32[2,8,512]{2,1,0:T(8,128)S(1)}, f32[2,2048,512,8]{2,1,3,0:T(8,128)}) fusion(pred[512,2048]{0,1:T(8,128)(4,1)S(1)} %broadcast_compare_fusion, bf16[512,2,8,128]{3,2,1,0:T(8,128)(2,1)} %bitcast.151, bf16[2,2048,2,128]{3,1,2,0:T(8,128)(2,1)} %all-gather.2.cloned.1.call-done), kind=kOutput, calls=%fused_computation.6 | convolution fusion | flops 4345290752 | bytes 71335936 | tf_op jit(solution)/shard_map/tkgd,skd->kgts/dot_general | solution.py:45
  71.5 21.5 %exponential_reduce_fusion = f32[2,8,512]{2,1,0:T(8,128)S(1)} fusion(f32[2,2048,512,8]{2,1,3,0:T(8,128)} %get-tuple-element.13, f32[2,8,512]{2,1,0:T(8,128)S(1)} %is-finite_select_fusion, pred[512,2048]{0,1:T(8,128)(4,1)S(1)} %broadcast_compare_fusion), kind=kLoop, calls=%fused_computation.5 | loop fusion | flops 67100672 | bytes 68222976 | tf_op jit(solution)/shard_map/reduce_sum | solution.py:47
  93.1 33.7 %exponential_convert_fusion = bf16[2,8,512,2048]{2,3,1,0:T(8,128)(2,1)} fusion(f32[2,2048,512,8]{2,1,3,0:T(8,128)} %get-tuple-element.13, f32[2,8,512]{2,1,0:T(8,128)S(1)} %log_add_fusion, pred[512,2048]{0,1:T(8,128)(4,1)S(1)} %broadcast_compare_fusion), kind=kLoop, calls=%fused_computation.4 | loop fusion | flops 67108864 | bytes 101744640 | tf_op jit(solution)/shard_map/convert_element_type | solution.py:48
  126.8 48.2 %copy.46 = bf16[2,8,512,2048]{3,1,0,2:T(8,128)(2,1)} copy(bf16[2,8,512,2048]{2,3,1,0:T(8,128)(2,1)} %exponential_convert_fusion) | data formatting | bytes 67108864 | tf_op jit(solution)/shard_map/convert_element_type | solution.py:48
  175.0 18.0 %multiply_reduce_fusion = (f32[2,8,512]{2,1,0:T(8,128)S(1)}, bf16[2,128,8,512]{3,1,2,0:T(8,128)(2,1)}) fusion(f32[2,8,512,128]{2,3,1,0:T(8,128)} %copy.40, bf16[2,8,512,2048]{2,3,1,0:T(8,128)(2,1)} %exponential_convert_fusion, bf16[2,2048,2,128]{3,1,2,0:T(8,128)(2,1)} %all-gather.2.cloned.1.call-done), kind=kOutput, calls=%fused_computation.17 | convolution fusion | flops 4299153408 | bytes 40927232 | tf_op jit(solution)/shard_map/kgts,skd->tkgd/dot_general | solution.py:49
  193.0 24.2 %fusion.1 = bf16[2,8,512,2048]{2,3,1,0:T(8,128)(2,1)} fusion(bf16[2,8,512,2048]{2,3,1,0:T(8,128)(2,1)} %exponential_convert_fusion, f32[2,8,512]{2,1,0:T(8,128)S(1)} %get-tuple-element.14, bf16[512,2,8,128]{3,2,1,0:T(8,128)(2,1)} %bitcast.145, bf16[2,2048,2,128]{3,1,2,0:T(8,128)(2,1)} %all-gather.2.cloned.1.call-done), kind=kOutput, calls=%fused_computation.2 | convolution fusion | flops 4362076160 | bytes 70287360 | tf_op jit(solution)/shard_map/tkgd,skd->kgts/dot_general | solution.py:55
  217.2 48.2 %copy.44 = bf16[2,8,512,2048]{3,1,0,2:T(8,128)(2,1)} copy(bf16[2,8,512,2048]{2,3,1,0:T(8,128)(2,1)} %fusion.1) | data formatting | bytes 67108864 | tf_op jit(solution)/shard_map/convert_element_type | solution.py:56
  265.4 14.9 %fusion.14 = f32[1,2048,2,128]{1,3,2,0:T(8,128)} fusion(bf16[512,2,8,128]{3,2,1,0:T(8,128)(2,1)} %bitcast.152, bf16[2,8,512,2048]{3,1,0,2:T(8,128)(2,1)} %copy.44), kind=kOutput, calls=%fused_computation.25 | convolution fusion | flops 4295491584 | bytes 37748736 | tf_op jit(solution)/shard_map/kgts,tkgd->skd/dot_general | solution.py:59
  280.4 13.0 %convolution_bitcast_fusion = f32[1,2048,2,128]{1,3,2,0:T(8,128)S(1)} fusion(bf16[512,2,8,128]{3,2,1,0:T(8,128)(2,1)S(1)} %bitcast.146, bf16[2,8,512,2048]{3,1,0,2:T(8,128)(2,1)} %copy.46), kind=kOutput, calls=%fused_computation.22 | convolution fusion | flops 4294967296 | bytes 37748736 | tf_op jit(solution)/shard_map/kgts,tkgd->skd/dot_general | solution.py:60
  293.3 3.9 pad_maximum_fusion
  297.3 0.0 reduce-scatter.2.cloned.1.call-update
  297.3 0.0 all-reduce.3.cloned.1.call-start
  297.3 16.8 %multiply_convert_fusion = bf16[2,128,8,512]{3,1,2,0:T(8,128)(2,1)} fusion(bf16[2,8,512,2048]{2,3,1,0:T(8,128)(2,1)} %fusion.1, bf16[2,2048,2,128]{3,1,2,0:T(8,128)(2,1)} %all-gather.2.cloned.1.call-done), kind=kOutput, calls=%fused_computation.18 | convolution fusion | flops 4297064448 | bytes 36700160 | tf_op jit(solution)/shard_map/kgts,skd->tkgd/dot_general | solution.py:57
  314.2 10.3 %fusion.47 = f32[2048,2048]{1,0:T(8,128)} fusion(bf16[512,2048]{0,1:T(8,128)(2,1)} %bitcast.159, bf16[512,2048]{1,0:T(8,128)(2,1)S(1)} %copy-done), kind=kOutput, calls=%fused_computation.79 | convolution fusion | flops 4294967296 | bytes 20971520 | tf_op jit(solution)/shard_map/tm,te->me/dot_general | solution.py:70
  324.5 17.6 %copy.28 = f32[2048,16,128]{2,1,0:T(8,128)} copy(f32[2048,16,128]{0,2,1:T(8,128)} %bitcast.150) | data formatting | bytes 33554432 | tf_op jit(solution)/shard_map/reshape | solution.py:79
  342.2 12.9 %fusion.50 = f32[2048,2048]{1,0:T(8,128)} fusion(bf16[512,2048]{0,1:T(8,128)(2,1)} %bitcast.157, bf16[512,2048]{1,0:T(8,128)(2,1)} %param.7), kind=kOutput, calls=%fused_computation.82 | convolution fusion | flops 4294967296 | bytes 20971520 | tf_op jit(solution)/shard_map/te,tm->em/dot_general | solution.py:73
  355.1 1.3 fusion.46
  356.3 2.0 fusion.48
  358.4 4.1 copy.29
  362.5 2.0 fusion.49
  364.5 4.2 copy.30
  368.7 0.0 all-reduce.3.cloned.1.call-update
  368.7 0.0 copy-start.3
  368.7 7.9 fusion.3
  376.7 0.0 copy-done.3
  376.7 0.0 copy-start.8
  376.7 9.4 convolution_convert_fusion.1
  386.1 0.0 copy-done.8
  386.1 0.8 fusion.27
  386.9 0.5 copy-done.7
  387.3 2.3 fusion.9
  389.6 602.8 %all-reduce.3.cloned.1.call-done = (f32[2048,16,128]{2,1,0:T(8,128)}, f32[2048,2,128]{2,1,0:T(2,128)}, f32[2048,2,128]{2,1,0:T(2,128)}, f32[16,128,2048]{2,1,0:T(8,128)}) async-done(((f32[2048,16,128]{2,1,0:T(8,128)}, f32[2048,2,128]{2,1,0:T(2,128)}, f32[2048,2,128]{2,1,0:T(2,128)}, f32[16,128,2048]{2,1,0:T(8,128)}), (f32[2048,16,128]{2,1,0:T(8,128)}, f32[2048,2,128]{2,1,0:T(2,128)}, ...) | async-done | bytes 37748752 | tf_op jit(solution)/shard_map/psum | solution.py:75
  992.4 12.7 %copy.94 = f32[2048,16,128]{2,1,0:T(8,128)} copy(f32[2048,16,128]{2,1,0:T(8,128)} %get-tuple-element.18) | data formatting | bytes 33554432
  1005.0 0.0 copy-done.5
  1005.0 1.3 copy.95
  1006.4 1.9 copy-done.4
  1008.3 1.3 copy.96
  1009.6 0.8 slice-done.2
  1010.4 1.2 slice-done.3
  1011.6 6.2 copy.97
  (17 shorter events, 0.1 us)
Async XLA Ops:
  7.2 1.6 copy-start
  7.2 5.4 copy-start.6
  7.2 37.5 %all-gather.2.cloned.1.call-start = ((), (), s32[]{:S(2)}) async-start(), calls=%async_computation.1 | async-start | bytes 2621440 | tf_op jit(solution)/shard_map/all_gather | solution.py:43
  16.0 339.0 %reduce-scatter.2.cloned.1.call-start = ((), (), s32[]{:S(2)}) async-start(), calls=%async_computation.2 | async-start | bytes 5242880 | tf_op jit(solution)/shard_map/reduce_scatter | solution.py:61
  24.3 2.0 copy-start.9
  35.0 1.3 copy-start.1
  265.4 14.9 %copy-start.2 = (bf16[64,8,16,128]{3,2,1,0:T(8,128)(2,1)S(1)}, bf16[64,8,16,128]{3,2,1,0:T(8,128)(2,1)}, u32[]{:S(2)}) copy-start(bf16[64,8,16,128]{3,2,1,0:T(8,128)(2,1)} %copy-done.1) | copy-start | bytes 6291460
  297.3 695.1 %all-reduce.3.cloned.1.call-start = ((), (), s32[]{:S(2)}) async-start(), calls=%async_computation.3 | async-start | bytes 75497472 | tf_op jit(solution)/shard_map/psum | solution.py:75
  368.7 7.9 copy-start.3
  376.7 9.4 copy-start.8
  386.1 1.2 copy-start.7
  992.4 17.2 %slice-start = ((s8[16777216]{0:T(1024)(128)(4,1)}), s8[4194304]{0:T(1024)(128)(4,1)S(1)}, s32[]{:S(2)}) async-start(s8[16777216]{0:T(1024)(128)(4,1)} %bitcast.148), calls=%async_computation.4 | async-start | bytes 8388608
  992.4 12.7 %copy-start.5 = (f32[2048,2,128]{2,1,0:T(2,128)S(1)}, f32[2048,2,128]{2,1,0:T(2,128)}, u32[]{:S(2)}) copy-start(f32[2048,2,128]{2,1,0:T(2,128)} %get-tuple-element.19) | copy-start | bytes 6291460
  992.4 17.2 %slice-start.1 = ((s8[16777216]{0:T(1024)(128)(4,1)}), s8[4194304]{0:T(1024)(128)(4,1)S(1)}, s32[]{:S(2)}) async-start(s8[16777216]{0:T(1024)(128)(4,1)} %bitcast.148), calls=%async_computation.5 | async-start | bytes 8388608
  992.4 18.1 %slice-start.2 = ((s8[16777216]{0:T(1024)(128)(4,1)}), s8[4194304]{0:T(1024)(128)(4,1)S(1)}, s32[]{:S(2)}) async-start(s8[16777216]{0:T(1024)(128)(4,1)} %bitcast.148), calls=%async_computation.6 | async-start | bytes 8388608
  992.4 19.3 %slice-start.3 = ((s8[16777216]{0:T(1024)(128)(4,1)}), s8[4194304]{0:T(1024)(128)(4,1)S(1)}, s32[]{:S(2)}) async-start(s8[16777216]{0:T(1024)(128)(4,1)} %bitcast.148), calls=%async_computation.7 | async-start | bytes 8388608
  1005.0 3.2 copy-start.4
Sparse Core Ops, SparseCore 0:
  16.2 22.3 all-gather.1
  297.4 41.1 reduce-scatter.1
  368.8 623.4 all-reduce.2
where the time goes:
time: 1040 us; the launch traced here: 1020 us
  waiting for transfers between devices  603 us (58%)
  matrix products  182 us (18%)
  local copies, waits for them, and re-layouts  162 us (16%)
  other arithmetic  63.2 us (6%)
  between operations  14.4 us (1%)
    psum x1, waiting for transfers between devices, device_layer(): lax.psum(weight_parts, 'cp')  603 us
    convert_element_type x1, local copies, waits for them, and re-layouts, device_layer(): att_probs = jnp.exp(masked - log_norm[..., None]).astype(jnp.bfloat16)  48.2 us
    convert_element_type x1, local copies, waits for them, and re-layouts, device_layer(): (att_probs.astype(jnp.float32) * (d_probs - delta_rows[..., None])).astyp...  48.2 us
    unnamed x35, local copies, waits for them, and re-layouts  36.6 us
    convert_element_type x1, other arithmetic, device_layer(): att_probs = jnp.exp(masked - log_norm[..., None]).astype(jnp.bfloat16)  33.7 us
    dot_general x1, matrix products, device_layer(): jnp.einsum('tkgd,skd->kgts', query_heads, key_rows, preferred_element_typ...  26.8 us
    dot_general x1, matrix products, device_layer(): jnp.einsum('tkgd,skd->kgts', dout_heads, value_rows, preferred_element_ty...  24.2 us
    reduce_sum x1, other arithmetic, device_layer(): log_norm = jax.nn.logsumexp(masked, axis=-1)  21.5 us
  transfers between devices with their start and end apart: 3, of which 1 were waited for; matrix products, arithmetic and copies ran while one was open for 10% of the time, Pallas kernels for 0%

commit v1 on v0

v1 whole, which is shorter than its diff:
```python
import functools
import math

import jax
import jax.numpy as jnp
from jax import lax
from jax.experimental import pallas as pl
from jax.experimental.pallas import tpu as pltpu
from jax.sharding import PartitionSpec as P

BLK = 256
LOW = -3.0e38
F32 = jnp.float32
BF16 = jnp.bfloat16


def dot(a, b):
    return jnp.dot(a, b, preferred_element_type=F32)


def dot_nt(a, b):
    return lax.dot_general(a, b, (((1,), (1,)), ((), ())), preferred_element_type=F32)


def dot_tn(a, b):
    return lax.dot_general(a, b, (((0,), (0,)), ((), ())), preferred_element_type=F32)


def params(n=1, mib=60):
    return pltpu.CompilerParams(
        dimension_semantics=("arbitrary",) * n, vmem_limit_bytes=mib * 1024 * 1024
    )


def cost(flops, nbytes):
    return pl.CostEstimate(flops=int(flops), bytes_accessed=int(nbytes), transcendentals=0)


def proj_kernel(trans, num_w, sc, a_hbm, b_hbm, *refs):
    w_refs, out_ref, xs, sems = refs[:num_w], refs[num_w], refs[num_w + 1], refs[num_w + 2]
    i = pl.program_id(0)
    first = pltpu.make_async_copy(a_hbm, xs.at[0], sems.at[0])
    second = pltpu.make_async_copy(b_hbm, xs.at[1], sems.at[1])

    @pl.when(i == 0)
    def _():
        first.start()
        second.start()
        first.wait()

    @pl.when(i == 1)
    def _():
        second.wait()

    col = 0
    for w in w_refs:
        width = w.shape[0] if trans else w.shape[1]
        res = (dot_nt if trans else dot)(xs[i], w[...])
        out_ref[:, col : col + width] = res.astype(BF16)
        col += width


def project(core, a, b, weights, width, trans):
    rows, depth = a.shape
    if trans:
        specs = [pl.BlockSpec((width, depth), lambda i, s: (s[0], 0)) for _ in weights]
    else:
        specs = [pl.BlockSpec((depth, width), lambda i, s: (0, s[0])) for _ in weights]
    total = width * len(weights)
    return pl.pallas_call(
        functools.partial(proj_kernel, trans, len(weights)),
        out_shape=jax.ShapeDtypeStruct((2 * rows, total), BF16),
        grid_spec=pltpu.PrefetchScalarGridSpec(
            num_scalar_prefetch=1,
            grid=(2,),
            in_specs=[pl.BlockSpec(memory_space=pl.ANY)] * 2 + specs,
            out_specs=pl.BlockSpec((rows, total), lambda i, s: (i, 0)),
            scratch_shapes=[pltpu.VMEM((2, rows, depth), BF16), pltpu.SemaphoreType.DMA((2,))],
        ),
        compiler_params=params(),
        cost_estimate=cost(4 * rows * depth * total, 2 * (2 * rows * depth + depth * total + 2 * rows * total)),
    )(core, a, b, *weights)


def attn_kernel(heads, scale, final, sc, q_ref, do_ref, kv_a, kv_b, *refs):
    if final:
        init_ref, o_ref, dq_ref, dkv_ref = refs[:4]
        scratch = refs[4:]
    else:
        o_ref, dq_ref, dkv_ref = refs[:3]
        scratch = refs[3:]
    ks, vs, kt, vt, dk, dv, qt, dot_t, qst, dost, s_ref, p_ref, ds_ref, ot, dqt = scratch
    step = pl.program_id(0)
    wide = heads * BLK
    hd = 128
    c2 = scale * math.log2(math.e)

    @pl.when(step == 0)
    def _():
        for i in range(8):
            src = kv_a if i < 4 else kv_b
            rows = slice((i % 4) * BLK, (i % 4 + 1) * BLK)
            at = pl.ds(pl.multiple_of(sc[i] * BLK, BLK), BLK)
            kk, vv = src[rows, :hd], src[rows, hd:]
            ks[at, :] = kk
            vs[at, :] = vv
            kt[:, at] = kk.T
            vt[:, at] = vv.T
            if final:
                init_rows = slice(i * BLK, (i + 1) * BLK)
                dk[at, :] = init_ref[init_rows, :hd]
                dv[at, :] = init_ref[init_rows, hd:]
            else:
                dk[at, :] = jnp.zeros((BLK, hd), F32)
                dv[at, :] = jnp.zeros((BLK, hd), F32)

    for h in range(heads):
        cols = slice(h * hd, (h + 1) * hd)
        span = slice(h * BLK, (h + 1) * BLK)
        qh, dh = q_ref[:, cols], do_ref[:, cols]
        qst[span, :] = qh
        dost[span, :] = dh
        qt[:, span] = qh.T
        dot_t[:, span] = dh.T

    b = sc[8 + step]

    def softmax_block(j, stats, masked):
        m8, l8 = stats
        at = pl.ds(pl.multiple_of(j * BLK, BLK), BLK)
        t = dot(ks[at, :], qt[...]) * c2
        if masked:
            key = lax.broadcasted_iota(jnp.int32, (BLK, wide), 0)
            query = lax.broadcasted_iota(jnp.int32, (BLK, wide), 1) % BLK
            t = jnp.where(key <= query, t, LOW)
        s_ref[at, :] = t
        t3 = t.reshape(BLK // 8, 8, wide)
        new = jnp.maximum(m8, jnp.max(t3, axis=0))
        e = jnp.exp2(t3 - new[None])
        return new, l8 * jnp.exp2(m8 - new) + jnp.sum(e, axis=0)

    stats = (jnp.full((8, wide), LOW, F32), jnp.zeros((8, wide), F32))
    stats = lax.fori_loop(0, b, lambda j, st: softmax_block(j, st, False), stats)
    m8, l8 = softmax_block(b, stats, True)
    top = jnp.max(m8, axis=0, keepdims=True)
    lse = top + jnp.log2(jnp.sum(l8 * jnp.exp2(m8 - top), axis=0, keepdims=True))

    ot[...] = jnp.zeros_like(ot)

    def value_block(j, _):
        at = pl.ds(pl.multiple_of(j * BLK, BLK), BLK)
        p = jnp.exp2(s_ref[at, :] - lse).astype(BF16)
        p_ref[at, :] = p
        ot[...] += dot(vt[:, at], p)
        return 0

    lax.fori_loop(0, b + 1, value_block, 0)

    o_round = ot[...].astype(BF16)
    delta = jnp.sum(o_round.astype(F32) * dot_t[...].astype(F32), axis=0, keepdims=True)
    for h in range(heads):
        o_ref[:, h * hd : (h + 1) * hd] = o_round[:, h * BLK : (h + 1) * BLK].T
    dqt[...] = jnp.zeros_like(dqt)

    def grad_block(j, _):
        at = pl.ds(pl.multiple_of(j * BLK, BLK), BLK)
        dp = dot(vs[at, :], dot_t[...])
        dv[at, :] += dot(p_ref[at, :], dost[...])
        ds = (p_ref[at, :].astype(F32) * (dp - delta)).astype(BF16)
        ds_ref[...] = ds
        dqt[...] += dot(kt[:, at], ds_ref[...])
        dk[at, :] += dot(ds_ref[...], qst[...])
        return 0

    lax.fori_loop(0, b + 1, grad_block, 0)

    for h in range(heads):
        dq_ref[:, h * hd : (h + 1) * hd] = (dqt[:, h * BLK : (h + 1) * BLK] * scale).astype(BF16).T

    @pl.when(step == pl.num_programs(0) - 1)
    def _():
        for i in range(8):
            at = pl.ds(pl.multiple_of(sc[i] * BLK, BLK), BLK)
            if final:
                out = pl.ds(pl.multiple_of((i // 4 * 4 + sc[12 + i % 4]) * BLK, BLK), BLK)
                dkv_ref[out, :hd] = (dk[at, :] * scale).astype(BF16)
                dkv_ref[out, hd:] = dv[at, :].astype(BF16)
            else:
                out = slice(i * BLK, (i + 1) * BLK)
                dkv_ref[out, :hd] = dk[at, :]
                dkv_ref[out, hd:] = dv[at, :]


def attention(sc, q, do, kv_a, kv_b, init, scale):
    final = init is not None
    rows, width = q.shape
    heads = width // 128
    wide = heads * BLK
    seq = 2 * rows
    row_spec = pl.BlockSpec((BLK, width), lambda i, s: (i, 0))
    out_spec = pl.BlockSpec((BLK, width), lambda i, s: (s[12 + i], 0))
    full = lambda shape: pl.BlockSpec(shape, lambda i, s: (0, 0))
    ins = [q, do, kv_a, kv_b] + ([init] if final else [])
    in_specs = [row_spec, row_spec, full(kv_a.shape), full(kv_b.shape)]
    if final:
        in_specs.append(full(init.shape))
    return pl.pallas_call(
        functools.partial(attn_kernel, heads, scale, final),
        out_shape=(
            jax.ShapeDtypeStruct((rows, width), BF16),
            jax.ShapeDtypeStruct((rows, width), BF16),
            jax.ShapeDtypeStruct((seq, 256), BF16 if final else F32),
        ),
        grid_spec=pltpu.PrefetchScalarGridSpec(
            num_scalar_prefetch=1,
            grid=(rows // BLK,),
            in_specs=in_specs,
            out_specs=(out_spec, out_spec, full((seq, 256))),
            scratch_shapes=[
                pltpu.VMEM((seq, 128), BF16),
                pltpu.VMEM((seq, 128), BF16),
                pltpu.VMEM((128, seq), BF16),
                pltpu.VMEM((128, seq), BF16),
                pltpu.VMEM((seq, 128), F32),
                pltpu.VMEM((seq, 128), F32),
                pltpu.VMEM((128, wide), BF16),
                pltpu.VMEM((128, wide), BF16),
                pltpu.VMEM((wide, 128), BF16),
                pltpu.VMEM((wide, 128), BF16),
                pltpu.VMEM((seq, wide), F32),
                pltpu.VMEM((seq, wide), BF16),
                pltpu.VMEM((BLK, wide), BF16),
                pltpu.VMEM((128, wide), F32),
                pltpu.VMEM((128, wide), F32),
            ],
        ),
        compiler_params=params(),
        cost_estimate=cost(24e9, 20e6),
    )(sc, *ins)


def y_kernel(sc, o_mine, o_other, w_mine, w_other, out_ref):
    out_ref[...] = (dot(o_mine[...], w_mine[...]) + dot(o_other[...], w_other[...])).astype(BF16)


def out_rows(core, o_mine, o_other, wo):
    rows, half, model, tile = 512, o_mine.shape[1], wo.shape[1], 512
    return pl.pallas_call(
        y_kernel,
        out_shape=jax.ShapeDtypeStruct((rows, model), BF16),
        grid_spec=pltpu.PrefetchScalarGridSpec(
            num_scalar_prefetch=1,
            grid=(model // tile,),
            in_specs=[
                pl.BlockSpec((rows, half), lambda i, s: (s[0], 0)),
                pl.BlockSpec((rows, half), lambda i, s: (s[0], 0)),
                pl.BlockSpec((half, tile), lambda i, s: (s[0], i)),
                pl.BlockSpec((half, tile), lambda i, s: (1 - s[0], i)),
            ],
            out_specs=pl.BlockSpec((rows, tile), lambda i, s: (0, i)),
        ),
        compiler_params=params(),
        cost_estimate=cost(4 * rows * half * model, 12e6),
    )(core, o_mine, o_other, wo, wo)


def dx_kernel(sc, q_mine, q_other, kv_mine, kv_other, wq_mine, wq_other, wk_mine, wk_other, wv_mine, wv_other, out_ref):
    hd = 128
    acc = dot_nt(q_mine[...], wq_mine[...]) + dot_nt(q_other[...], wq_other[...])
    acc += dot_nt(kv_mine[:, :hd], wk_mine[...]) + dot_nt(kv_other[:, :hd], wk_other[...])
    acc += dot_nt(kv_mine[:, hd:], wv_mine[...]) + dot_nt(kv_other[:, hd:], wv_other[...])
    out_ref[...] = acc.astype(BF16)


def grad_rows(core, dq_mine, dq_other, dkv_mine, dkv_other, wq, wk, wv):
    rows, half, model, tile = 512, dq_mine.shape[1], wq.shape[0], 512
    mine = lambda i, s: (s[0], 0)
    return pl.pallas_call(
        dx_kernel,
        out_shape=jax.ShapeDtypeStruct((rows, model), BF16),
        grid_spec=pltpu.PrefetchScalarGridSpec(
            num_scalar_prefetch=1,
            grid=(model // tile,),
            in_specs=[
                pl.BlockSpec((rows, half), mine),
                pl.BlockSpec((rows, half), mine),
                pl.BlockSpec((rows, 256), mine),
                pl.BlockSpec((rows, 256), mine),
                pl.BlockSpec((tile, half), lambda i, s: (i, s[0])),
                pl.BlockSpec((tile, half), lambda i, s: (i, 1 - s[0])),
                pl.BlockSpec((tile, 128), lambda i, s: (i, s[0])),
                pl.BlockSpec((tile, 128), lambda i, s: (i, 1 - s[0])),
                pl.BlockSpec((tile, 128), lambda i, s: (i, s[0])),
                pl.BlockSpec((tile, 128), lambda i, s: (i, 1 - s[0])),
            ],
            out_specs=pl.BlockSpec((rows, tile), lambda i, s: (0, i)),
        ),
        compiler_params=params(),
        cost_estimate=cost(4 * rows * half * model * 1.25, 14e6),
    )(core, dq_mine, dq_other, dkv_mine, dkv_other, wq, wq, wk, wk, wv, wv)


def dwq_kernel(aliased, sc, x0, x1, x2, x3, q0, q1, q2, q3, k0, k1, k2, k3, *refs):
    out_ref, kv_ref = refs[-2:]
    xs = [x[...].T for x in (x0, x1, x2, x3)]
    acc = sum(dot(x, q[...]) for x, q in zip(xs, (q0, q1, q2, q3)))
    for h in range(8):
        out_ref[:, h, :] = acc[:, h * 128 : (h + 1) * 128]
    kv_ref[...] = sum(dot(x, k[...]) for x, k in zip(xs, (k0, k1, k2, k3)))


def grad_wq(sc, xs, dq_chip, dq_rem, dkv, flip, into):
    model, half, rows, tile = xs[0].shape[1], dq_chip.shape[1], 512, 256
    x_spec = pl.BlockSpec((rows, tile), lambda i, s: (0, i))
    at = lambda f, base=0: lambda i, s: (base + (1 - s[0] if f else s[0]), 0)
    specs = [x_spec] * 4
    specs += [pl.BlockSpec((rows, half), at(f)) for f in (0, 1, 0, 1)]
    specs += [pl.BlockSpec((rows, 256), at(f, base)) for f, base in ((0, 0), (1, 0), (0, 2), (1, 2))]
    ins = list(xs) + [dq_chip, dq_chip, dq_rem, dq_rem, dkv, dkv, dkv, dkv]
    alias = {}
    if into is not None:
        specs.append(pl.BlockSpec(memory_space=pl.ANY))
        ins.append(into)
        alias = {len(ins): 0}
    col = (lambda i, s: (i, 1 - s[0], 0)) if flip else (lambda i, s: (i, s[0], 0))
    return pl.pallas_call(
        functools.partial(dwq_kernel, into is not None),
        out_shape=(
            jax.ShapeDtypeStruct((model, 16, 128), F32),
            jax.ShapeDtypeStruct((model, 256), F32),
        ),
        grid_spec=pltpu.PrefetchScalarGridSpec(
            num_scalar_prefetch=1,
            grid=(model // tile,),
            in_specs=specs,
            out_specs=(
                pl.BlockSpec((tile, 8, 128), col),
                pl.BlockSpec((tile, 256), lambda i, s: (i, 0)),
            ),
        ),
        input_output_aliases=alias,
        compiler_params=params(),
        cost_estimate=cost(2 * 2048 * model * (half + 256), 22e6),
    )(sc, *ins)


def dwo_kernel(aliased, sc, o0, o1, o2, o3, y0, y1, y2, y3, *refs):
    out_ref = refs[-1]
    out_ref[...] = sum(dot(o[...].T, y[...]) for o, y in zip((o0, o1, o2, o3), (y0, y1, y2, y3)))


def grad_wo(sc, ys, o_chip, o_rem, flip, into):
    model, half, rows, tile = ys[0].shape[1], o_chip.shape[1], 512, 256
    at = lambda f: lambda i, s: ((1 - s[0] if f else s[0]), i)
    specs = [pl.BlockSpec((rows, tile), at(f)) for f in (0, 1, 0, 1)]
    specs += [pl.BlockSpec((rows, model), lambda i, s: (0, 0))] * 4
    ins = [o_chip, o_chip, o_rem, o_rem] + list(ys)
    alias = {}
    if into is not None:
        specs.append(pl.BlockSpec(memory_space=pl.ANY))
        ins.append(into)
        alias = {len(ins): 0}
    steps = half // tile
    base = (lambda i, s: ((1 - s[0]) * steps + i, 0)) if flip else (lambda i, s: (s[0] * steps + i, 0))
    return pl.pallas_call(
        functools.partial(dwo_kernel, into is not None),
        out_shape=jax.ShapeDtypeStruct((2 * half, model), F32),
        grid_spec=pltpu.PrefetchScalarGridSpec(
            num_scalar_prefetch=1,
            grid=(steps,),
            in_specs=specs,
            out_specs=pl.BlockSpec((tile, model), base),
        ),
        input_output_aliases=alias,
        compiler_params=params(),
        cost_estimate=cost(2 * 2048 * model * half, 22e6),
    )(sc, *ins)


def solution(mesh):
    row_spec = P(("dp", "cp"), None)
    rep_spec = P(None, None, None)
    part_spec = P("dp", None, None)
    core_swap = [(0, 1), (1, 0), (2, 3), (3, 2)]
    chip_swap = [(0, 2), (2, 0), (1, 3), (3, 1)]

    def device_layer(x, dy, w_query, w_key, w_value, w_out):
        rows, model = x.shape
        num_heads, hd = w_query.shape[1:]
        kv_heads = w_key.shape[1]
        scale = hd ** -0.5
        rank = lax.axis_index("cp").astype(jnp.int32)
        core = (rank & 1).reshape(1)
        devs = [rank, rank ^ 1, rank ^ 2, rank ^ 3]
        kv_pos = [p for e in devs for p in (e, 7 - e)]
        slots = [p for e in devs[:2] for p in ((e & 1) * 2, (e & 1) * 2 + 1)]
        sc_chip = jnp.stack(kv_pos + kv_pos[:4] + slots)
        sc_rem = jnp.stack(kv_pos + kv_pos[4:] + slots)

        to_core = lambda v: lax.ppermute(v, "cp", core_swap)
        to_chip = lambda v: lax.ppermute(v, "cp", chip_swap)

        x_p = to_core(x)
        dy_p = to_core(dy)
        wk = w_key.reshape(model, kv_heads * hd)
        wv = w_value.reshape(model, kv_heads * hd)
        wq = w_query.reshape(model, num_heads * hd)
        wo = w_out.reshape(num_heads * hd, model)

        kv = project(core, x, x_p, (wk, wv), hd, False)
        kv_r = to_chip(kv)
        x_send, kv2 = lax.optimization_barrier((x, kv))
        x_r = to_chip(x_send)
        dy_send, _ = lax.optimization_barrier((dy, kv))
        dy_r = to_chip(dy_send)
        x_rp = to_core(x_r)
        dy_rp = to_core(dy_r)

        q = project(core, x, x_p, (wq,), 1024, False)
        do = project(core, dy, dy_p, (wo,), 1024, True)
        o_c, dq_c, dkv_part = attention(sc_chip, q, do, kv2, kv_r, None, scale)
        o_co = to_core(o_c)
        y = out_rows(core, o_c, o_co, wo)

        q_rem = project(core, x_r, x_rp, (wq,), 1024, False)
        do_rem = project(core, dy_r, dy_rp, (wo,), 1024, True)
        o_r, dq_r, dkv = attention(sc_rem, q_rem, do_rem, kv2, kv_r, dkv_part, scale)
        dq_co = to_core(dq_c)
        dkv_o = to_core(dkv)
        dq_ro = to_core(dq_r)
        o_ro = to_core(o_r)

        xs = (x, x_p, x_r, x_rp)
        ys = (dy, dy_p, dy_r, dy_rp)
        gwo = grad_wo(core, ys, o_c, o_r, False, None)
        gwq, gkv = grad_wq(core, xs, dq_c, dq_r, dkv, False, None)
        dx = grad_rows(core, dq_c, dq_co, dkv, dkv_o, wq, wk, wv)
        gwo = grad_wo(core, ys, o_co, o_ro, True, gwo)
        gwq, gkv_o = grad_wq(core, xs, dq_co, dq_ro, dkv_o, True, gwq)
        low = core[0] == 0
        first, second = jnp.where(low, gkv, gkv_o), jnp.where(low, gkv_o, gkv)
        gwk = jnp.stack([first[:, :hd], second[:, :hd]], axis=1)
        gwv = jnp.stack([first[:, hd:], second[:, hd:]], axis=1)
        return y, dx, gwq, gwk, gwv, gwo.reshape(num_heads, hd, model)

    return jax.shard_map(
        device_layer,
        mesh=mesh,
        in_specs=(row_spec, row_spec, rep_spec, rep_spec, rep_spec, rep_spec),
        out_specs=(row_spec, row_spec, part_spec, part_spec, part_spec, part_spec),
        check_vma=False,
    )
```

time: 1040 us -> 316 us (0.30); the launches traced: 1020 us -> 312 us
  waiting for transfers between devices: 603 us -> 27.6 us
  Pallas kernels: 0 us -> 234 us
  matrix products: 182 us -> 0 us
  local copies, waits for them, and re-layouts: 162 us -> 38.5 us
  other arithmetic: 63.2 us -> 2.77 us
  between operations: 14.4 us -> 1.24 us
    psum x1 -> x0, waiting for transfers between devices: 603 us -> none  [device_layer(): lax.psum(weight_parts, 'cp')]
    pallas_call x0 -> x13, Pallas kernels: none -> 234 us  [the longest x2 102 us: attention(): pl.pallas_call(functools.partial(attn_kernel, heads, scale, final), out_s...]
    dot_general x18 -> x0, matrix products: 182 us -> none  [the longest x1 26.8 us: device_layer(): jnp.einsum('tkgd,skd->kgts', query_heads, key_rows, preferred_element_typ...]
    convert_element_type x2 -> x0, local copies, waits for them, and re-layouts: 96.4 us -> none  [the longest x1 48.2 us: device_layer(): att_probs = jnp.exp(masked - log_norm[..., None]).astype(jnp.bfloat16)]
    convert_element_type x1 -> x0, other arithmetic: 33.7 us -> none  [device_layer(): att_probs = jnp.exp(masked - log_norm[..., None]).astype(jnp.bfloat16)]
    ppermute x0 -> x12, waiting for transfers between devices: none -> 27.6 us  [the longest x3 27.6 us: device_layer(): to_chip = lambda v: lax.ppermute(v, 'cp', chip_swap)]
    reshape x3 -> x1, local copies, waits for them, and re-layouts: 25.9 us -> 2.86 us  [device_layer(): wv = w_value.reshape(model, kv_heads * hd)]
    reduce_sum x1 -> x0, other arithmetic: 21.5 us -> none  [device_layer(): log_norm = jax.nn.logsumexp(masked, axis=-1)]
  transfers between devices with their start and end apart: 3 -> 12, of which waited for: 1 -> 1; matrix products, arithmetic and copies ran while one was open for 10% -> 11% of each run, Pallas kernels for 0% -> 70%
where the time goes in v1:
time: 316 us; the launch traced here: 312 us
  Pallas kernels  234 us (74%)
  local copies, waits for them, and re-layouts  38.5 us (12%)
  waiting for transfers between devices  27.6 us (9%)
  starting transfers between devices  7.51 us (2%)
    pallas_call x2, Pallas kernels, attention(): pl.pallas_call(functools.partial(attn_kernel, heads, scale, final), out_s...  102 us
    pallas_call x5, Pallas kernels, project(): pl.pallas_call(functools.partial(proj_kernel, trans, len(weights)), out_s...  44.4 us
    pallas_call x2, Pallas kernels, grad_wq(): pl.pallas_call(functools.partial(dwq_kernel, into is not None), out_shape...  38.3 us
    unnamed x15, local copies, waits for them, and re-layouts  33.9 us
    pallas_call x2, Pallas kernels, grad_wo(): pl.pallas_call(functools.partial(dwo_kernel, into is not None), out_shape...  29.6 us
    ppermute x3, waiting for transfers between devices, device_layer(): to_chip = lambda v: lax.ppermute(v, 'cp', chip_swap)  27.6 us
    pallas_call x1, Pallas kernels, grad_rows(): pl.pallas_call(dx_kernel, out_shape=jax.ShapeDtypeStruct((rows, model), B...  11.4 us
    pallas_call x1, Pallas kernels, out_rows(): pl.pallas_call(y_kernel, out_shape=jax.ShapeDtypeStruct((rows, model), BF...  8.63 us
  transfers between devices with their start and end apart: 12, of which 1 were waited for; matrix products, arithmetic and copies ran while one was open for 11% of the time, Pallas kernels for 70%

profile of v1, /device:TPU:0, one launch (start us, length us, event | category | flops | bytes accessed | tf_op | source)
XLA Modules:
  0.0 311.7 jit_solution(2370785071430219655)
XLA Ops:
  0.6 0.9 collective-permute-start
  1.5 0.0 collective-permute-start.1
  1.5 0.0 copy-start.4
  1.6 11.0 %copy.22 = bf16[256,8,16,128]{3,1,2,0:T(8,128)(2,1)} copy(bf16[256,8,16,128]{3,2,1,0:T(8,128)(2,1)} %bitcast.42) | data formatting | bytes 16777216
  12.6 0.7 stack.92.sc
  13.3 0.0 copy-done.4
  13.3 2.9 copy_bitcast_fusion.1
  16.1 0.0 collective-permute-done.b_hbm.x1
  16.1 6.2 %shard_map.111.kv_a = bf16[1024,256]{1,0:T(8,128)(2,1)} custom-call(s32[1]{0:T(128)} %bitcast.sc, bf16[512,2048]{1,0:T(8,128)(2,1)} %x0.3, bf16[512,2048]{1,0:T(8,128)(2,1)} %collective-permute-done.b_hbm.x1, bf16[2048,256]{1,0:T(8,128)(2,1)} %get-tuple-element.45.refs_0_.wk_mine.wk_other, bf16[2048,256]{1,0:T(8,128)(2,1)} %get-tuple-element.44.refs_1_.wv_mine.wv_other), custom_call_target="tpu_custom_call" | custom-call | flops 1073741824 | bytes 5767168 | tf_op jit(solution)/shard_map/pallas_call | solution.py:70
  22.3 3.0 collective-permute-start.2
  25.3 0.0 collective-permute-start.5
  25.3 2.0 collective-permute-start.7
  27.3 9.4 %shard_map.109.q_ref = bf16[1024,1024]{1,0:T(8,128)(2,1)} custom-call(s32[1]{0:T(128)} %bitcast.sc, bf16[512,2048]{1,0:T(8,128)(2,1)} %x0.3, bf16[512,2048]{1,0:T(8,128)(2,1)} %collective-permute-done.b_hbm.x1, bf16[2048,2048]{1,0:T(8,128)(2,1)} %bitcast.33), custom_call_target="tpu_custom_call" | custom-call | flops 4294967296 | bytes 10485760 | tf_op jit(solution)/shard_map/pallas_call | solution.py:70
  36.8 0.0 collective-permute-done.1.b_hbm.y1
  36.8 0.0 copy-start.1
  36.8 1.3 copy-done.1
  38.1 9.5 %shard_map.110.do_ref = bf16[1024,1024]{1,0:T(8,128)(2,1)} custom-call(s32[1]{0:T(128)} %bitcast.sc, bf16[512,2048]{1,0:T(8,128)(2,1)} %y0.3, bf16[512,2048]{1,0:T(8,128)(2,1)} %copy-done.1, bf16[2048,2048]{1,0:T(8,128)(2,1)} %bitcast.38), custom_call_target="tpu_custom_call" | custom-call | flops 4294967296 | bytes 10485760 | tf_op jit(solution)/shard_map/pallas_call | solution.py:70
  47.7 0.0 collective-permute-done.2.kv_b
  47.7 0.0 copy-start.5
  47.7 0.8 copy-done.5
  48.5 50.8 %shard_map.112 = (bf16[1024,1024]{1,0:T(8,128)(2,1)}, bf16[1024,1024]{1,0:T(8,128)(2,1)}, f32[2048,256]{1,0:T(8,128)}) custom-call(s32[16]{0:T(128)} %stack.92.sc, bf16[1024,1024]{1,0:T(8,128)(2,1)} %shard_map.109.q_ref, bf16[1024,1024]{1,0:T(8,128)(2,1)} %shard_map.110.do_ref, bf16[1024,256]{1,0:T(8,128)(2,1)} %shard_map.111.kv_a, bf16[1024,256]{1,0:T(8,128)(2,1)} %copy-done.5), custom_call_target="tpu_custom_call" | custom-call | flops 24000000000 | bytes 20000000 | tf_op jit(solution)/shard_map/pallas_call | solution.py:207
  99.2 0.0 collective-permute-start.3
  99.2 0.0 collective-permute-done.5.a_hbm.x2
  99.3 0.5 collective-permute-start.6
  99.8 27.6 %collective-permute-done.7.a_hbm.y2 = bf16[512,2048]{1,0:T(8,128)(2,1)} collective-permute-done((bf16[512,2048]{1,0:T(8,128)(2,1)}, bf16[512,2048]{1,0:T(8,128)(2,1)}, u32[]{:S(2)}, u32[]{:S(2)}) %collective-permute-start.7) | collective-permute-done | bytes 2097184 | tf_op jit(solution)/shard_map/ppermute | solution.py:401
  127.3 0.0 collective-permute-start.8
  127.3 0.7 stack.93.sc
  128.0 0.5 collective-permute-start.4
  128.5 0.0 collective-permute-done.3.o_other.o0.o1
  128.5 0.0 copy-start
  128.5 1.4 copy-done
  129.9 8.6 %shard_map.113 = bf16[512,2048]{1,0:T(8,128)(2,1)} custom-call(s32[1]{0:T(128)} %bitcast.sc, bf16[1024,1024]{1,0:T(8,128)(2,1)} %get-tuple-element.20.o_mine.o0.o1, bf16[1024,1024]{1,0:T(8,128)(2,1)} %copy-done, bf16[2048,2048]{1,0:T(8,128)(2,1)} %bitcast.39, bf16[2048,2048]{1,0:T(8,128)(2,1)} %bitcast.40), custom_call_target="tpu_custom_call" | custom-call | flops 4294967296 | bytes 12000000 | tf_op jit(solution)/shard_map/pallas_call | solution.py:248
  138.5 0.0 collective-permute-done.6.b_hbm.x3
  138.5 9.5 %shard_map.114.q_ref = bf16[1024,1024]{1,0:T(8,128)(2,1)} custom-call(s32[1]{0:T(128)} %bitcast.sc, bf16[512,2048]{1,0:T(8,128)(2,1)} %collective-permute-done.5.a_hbm.x2, bf16[512,2048]{1,0:T(8,128)(2,1)} %collective-permute-done.6.b_hbm.x3, bf16[2048,2048]{1,0:T(8,128)(2,1)} %bitcast.34), custom_call_target="tpu_custom_call" | custom-call | flops 4294967296 | bytes 10485760 | tf_op jit(solution)/shard_map/pallas_call | solution.py:70
  148.0 0.0 collective-permute-done.8.b_hbm.y3
  148.0 9.8 %shard_map.115.do_ref = bf16[1024,1024]{1,0:T(8,128)(2,1)} custom-call(s32[1]{0:T(128)} %bitcast.sc, bf16[512,2048]{1,0:T(8,128)(2,1)} %collective-permute-done.7.a_hbm.y2, bf16[512,2048]{1,0:T(8,128)(2,1)} %collective-permute-done.8.b_hbm.y3, bf16[2048,2048]{1,0:T(8,128)(2,1)} %bitcast.41), custom_call_target="tpu_custom_call" | custom-call | flops 4294967296 | bytes 10485760 | tf_op jit(solution)/shard_map/pallas_call | solution.py:70
  157.8 51.1 %shard_map.116 = (bf16[1024,1024]{1,0:T(8,128)(2,1)}, bf16[1024,1024]{1,0:T(8,128)(2,1)}, bf16[2048,256]{1,0:T(8,128)(2,1)}) custom-call(s32[16]{0:T(128)} %stack.93.sc, bf16[1024,1024]{1,0:T(8,128)(2,1)} %shard_map.114.q_ref, bf16[1024,1024]{1,0:T(8,128)(2,1)} %shard_map.115.do_ref, bf16[1024,256]{1,0:T(8,128)(2,1)} %shard_map.111.kv_a, ...), custom_call_target="tpu_custom_call" | custom-call | flops 24000000000 | bytes 20000000 | tf_op jit(solution)/shard_map/pallas_call | solution.py:207
  208.9 0.1 collective-permute-start.9
  209.0 0.4 collective-permute-start.10
  209.4 0.1 collective-permute-start.11
  209.5 14.8 %shard_map.120.refs_0_ = f32[2048,2048]{1,0:T(8,128)} custom-call(s32[1]{0:T(128)} %bitcast.sc, bf16[1024,1024]{1,0:T(8,128)(2,1)} %get-tuple-element.20.o_mine.o0.o1, bf16[1024,1024]{1,0:T(8,128)(2,1)} %get-tuple-element.20.o_mine.o0.o1, bf16[1024,1024]{1,0:T(8,128)(2,1)} %get-tuple-element.31.o2.o3, bf16[1024,1024]{1,0:T(8,128)(2,1)} %get-tuple-element.31.o2.o3, ...), custom_call_target="tpu_custom_call" | custom-call | flops 8589934592 | bytes 22000000 | tf_op jit(solution)/shard_map/pallas_call | solution.py:365
  224.3 19.0 %shard_map.118 = (f32[2048,16,128]{2,1,0:T(8,128)}, f32[2048,256]{1,0:T(8,128)}) custom-call(s32[1]{0:T(128)} %bitcast.sc, bf16[512,2048]{1,0:T(8,128)(2,1)} %x0.3, bf16[512,2048]{1,0:T(8,128)(2,1)} %collective-permute-done.b_hbm.x1, bf16[512,2048]{1,0:T(8,128)(2,1)} %collective-permute-done.5.a_hbm.x2, bf16[512,2048]{1,0:T(8,128)(2,1)} %collective-permute-done.6.b_hbm.x3, ...), custom_call_target="tpu_custom_call" | custom-call | flops 10737418240 | bytes 22000000 | tf_op jit(solution)/shard_map/pallas_call | solution.py:326
  243.3 0.0 collective-permute-done.4.q_other.q0.q1
  243.3 0.0 collective-permute-done.9.kv_other.k0.k1.k2.k3
  243.3 0.0 copy-start.3
  243.4 1.0 copy-done.3
  244.3 11.4 %shard_map.117 = bf16[512,2048]{1,0:T(8,128)(2,1)} custom-call(s32[1]{0:T(128)} %bitcast.sc, bf16[1024,1024]{1,0:T(8,128)(2,1)} %get-tuple-element.21.q_mine.q0.q1, bf16[1024,1024]{1,0:T(8,128)(2,1)} %collective-permute-done.4.q_other.q0.q1, bf16[2048,256]{1,0:T(8,128)(2,1)} %get-tuple-element.25.kv_mine.k0.k1.k2.k3, bf16[2048,256]{1,0:T(8,128)(2,1)} %copy-done.3, ...), custom_call_target="tpu_custom_call" | custom-call | flops 5368709120 | bytes 14000000 | tf_op jit(solution)/shard_map/pallas_call | solution.py:278
  255.7 0.0 collective-permute-done.10.q2.q3
  255.7 19.3 %shard_map.119 = (f32[2048,16,128]{2,1,0:T(8,128)}, f32[2048,256]{1,0:T(8,128)}) custom-call(s32[1]{0:T(128)} %bitcast.sc, bf16[512,2048]{1,0:T(8,128)(2,1)} %x0.3, bf16[512,2048]{1,0:T(8,128)(2,1)} %collective-permute-done.b_hbm.x1, bf16[512,2048]{1,0:T(8,128)(2,1)} %collective-permute-done.5.a_hbm.x2, ...), custom_call_target="tpu_custom_call", output_to_operand_aliasing={{0}: (13, {})} | custom-call | flops 10737418240 | bytes 22000000 | tf_op jit(solution)/shard_map/pallas_call | solution.py:326
  275.0 2.5 broadcast_select_fusion.1
  277.5 0.1 slice_bitcast_fusion
  277.6 0.1 slice_bitcast_fusion.1
  277.8 0.1 pad_maximum_fusion
  277.9 8.6 %copy.14 = f32[2048,2,128]{2,1,0:T(2,128)} copy(f32[2048,2,128]{2,0,1:T(8,128)S(1)} %pad_maximum_fusion) | data formatting | bytes 4194304
  286.5 0.1 pad_maximum_fusion.1
  286.6 8.6 %copy.15 = f32[2048,2,128]{2,1,0:T(2,128)} copy(f32[2048,2,128]{2,0,1:T(8,128)S(1)} %pad_maximum_fusion.1) | data formatting | bytes 4194304
  295.1 0.0 collective-permute-done.11.o2.o3
  295.2 0.0 copy-start.2
  295.2 1.3 copy-done.2
  296.5 14.8 %shard_map.121 = f32[2048,2048]{1,0:T(8,128)} custom-call(s32[1]{0:T(128)} %bitcast.sc, bf16[1024,1024]{1,0:T(8,128)(2,1)} %copy-done, bf16[1024,1024]{1,0:T(8,128)(2,1)} %copy-done, bf16[1024,1024]{1,0:T(8,128)(2,1)} %copy-done.2, bf16[1024,1024]{1,0:T(8,128)(2,1)} %copy-done.2, bf16[512,2048]{1,0:T(8,128)(2,1)} %y0.3, ...), custom_call_target="tpu_custom_call", output_to_operand_aliasing={{}: (9, {})} | custom-call | flops 8589934592 | bytes 22000000 | tf_op jit(solution)/shard_map/pallas_call | solution.py:365
Async XLA Ops:
  0.6 15.5 %collective-permute-start = (bf16[512,2048]{1,0:T(8,128)(2,1)}, bf16[512,2048]{1,0:T(8,128)(2,1)}, u32[]{:S(2)}, u32[]{:S(2)}) collective-permute-start(bf16[512,2048]{1,0:T(8,128)(2,1)} %x0.3), channel_id=1, source_target_pairs={{0,1},{1,0},{2,3},{3,2},{4,5},{5,4},{6,7},{7,6}} | collective-permute-start | bytes 6291464 | tf_op jit(solution)/shard_map/ppermute | solution.py:400
  1.5 35.3 %collective-permute-start.1 = (bf16[512,2048]{1,0:T(8,128)(2,1)}, bf16[512,2048]{1,0:T(8,128)(2,1)S(1)}, u32[]{:S(2)}, u32[]{:S(2)}) collective-permute-start(bf16[512,2048]{1,0:T(8,128)(2,1)} %y0.3), channel_id=1, source_target_pairs={{0,1},{1,0},{2,3},{3,2},{4,5},{5,4},{6,7},{7,6}} | collective-permute-start | bytes 6291464 | tf_op jit(solution)/shard_map/ppermute | solution.py:400
  1.5 11.7 %copy-start.4 = (bf16[2048,2,128]{2,1,0:T(2,128)(2,1)S(1)}, bf16[2048,2,128]{2,1,0:T(2,128)(2,1)}, u32[]{:S(2)}) copy-start(bf16[2048,2,128]{2,1,0:T(2,128)(2,1)} %param.10) | copy-start | bytes 3145732
  22.3 25.3 %collective-permute-start.2 = (bf16[1024,256]{1,0:T(8,128)(2,1)}, bf16[1024,256]{1,0:T(8,128)(2,1)S(1)}, u32[]{:S(2)}, u32[]{:S(2)}) collective-permute-start(bf16[1024,256]{1,0:T(8,128)(2,1)} %shard_map.111.kv_a), channel_id=1, source_target_pairs={{0,2},{2,0},{1,3},{3,1},{4,6},{6,4},{5,7},{7,5}} | collective-permute-start | bytes 1572872 | tf_op jit(solution)/shard_map/ppermute | solution.py:401
  25.3 73.9 %collective-permute-start.5 = (bf16[512,2048]{1,0:T(8,128)(2,1)}, bf16[512,2048]{1,0:T(8,128)(2,1)}, u32[]{:S(2)}, u32[]{:S(2)}) collective-permute-start(bf16[512,2048]{1,0:T(8,128)(2,1)} %x0.3), channel_id=1, source_target_pairs={{0,2},{2,0},{1,3},{3,1},{4,6},{6,4},{5,7},{7,5}} | collective-permute-start | bytes 6291464 | tf_op jit(solution)/shard_map/ppermute | solution.py:401
  25.3 102.0 %collective-permute-start.7 = (bf16[512,2048]{1,0:T(8,128)(2,1)}, bf16[512,2048]{1,0:T(8,128)(2,1)}, u32[]{:S(2)}, u32[]{:S(2)}) collective-permute-start(bf16[512,2048]{1,0:T(8,128)(2,1)} %y0.3), channel_id=1, source_target_pairs={{0,2},{2,0},{1,3},{3,1},{4,6},{6,4},{5,7},{7,5}} | collective-permute-start | bytes 6291464 | tf_op jit(solution)/shard_map/ppermute | solution.py:401
  36.8 1.3 copy-start.1
  47.7 0.8 copy-start.5
  99.2 29.3 %collective-permute-start.3 = (bf16[1024,1024]{1,0:T(8,128)(2,1)}, bf16[1024,1024]{1,0:T(8,128)(2,1)S(1)}, u32[]{:S(2)}, u32[]{:S(2)}) collective-permute-start(bf16[1024,1024]{1,0:T(8,128)(2,1)} %get-tuple-element.20.o_mine.o0.o1), channel_id=1, source_target_pairs={{0,1},{1,0},{2,3},{3,2},{4,5},{5,4},{6,7},{7,6}} | collective-permute-start | bytes 6291464 | tf_op jit(solution)/shard_map/ppermute | solution.py:400
  99.3 39.3 %collective-permute-start.6 = (bf16[512,2048]{1,0:T(8,128)(2,1)}, bf16[512,2048]{1,0:T(8,128)(2,1)}, u32[]{:S(2)}, u32[]{:S(2)}) collective-permute-start(bf16[512,2048]{1,0:T(8,128)(2,1)} %collective-permute-done.5.a_hbm.x2), channel_id=1, source_target_pairs={{0,1},{1,0},{2,3},{3,2},{4,5},{5,4},{6,7},{7,6}} | collective-permute-start | bytes 6291464 | tf_op jit(solution)/shard_map/ppermute | solution.py:400
  127.3 20.7 %collective-permute-start.8 = (bf16[512,2048]{1,0:T(8,128)(2,1)}, bf16[512,2048]{1,0:T(8,128)(2,1)}, u32[]{:S(2)}, u32[]{:S(2)}) collective-permute-start(bf16[512,2048]{1,0:T(8,128)(2,1)} %collective-permute-done.7.a_hbm.y2), channel_id=1, source_target_pairs={{0,1},{1,0},{2,3},{3,2},{4,5},{5,4},{6,7},{7,6}} | collective-permute-start | bytes 6291464 | tf_op jit(solution)/shard_map/ppermute | solution.py:400
  128.0 115.3 %collective-permute-start.4 = (bf16[1024,1024]{1,0:T(8,128)(2,1)}, bf16[1024,1024]{1,0:T(8,128)(2,1)}, u32[]{:S(2)}, u32[]{:S(2)}) collective-permute-start(bf16[1024,1024]{1,0:T(8,128)(2,1)} %get-tuple-element.21.q_mine.q0.q1), channel_id=1, source_target_pairs={{0,1},{1,0},{2,3},{3,2},{4,5},{5,4},{6,7},{7,6}} | collective-permute-start | bytes 6291464 | tf_op jit(solution)/shard_map/ppermute | solution.py:400
  128.5 1.4 copy-start
  208.9 34.4 %collective-permute-start.9 = (bf16[2048,256]{1,0:T(8,128)(2,1)}, bf16[2048,256]{1,0:T(8,128)(2,1)S(1)}, u32[]{:S(2)}, u32[]{:S(2)}) collective-permute-start(bf16[2048,256]{1,0:T(8,128)(2,1)} %get-tuple-element.25.kv_mine.k0.k1.k2.k3), channel_id=1, source_target_pairs={{0,1},{1,0},{2,3},{3,2},{4,5},{5,4},{6,7},{7,6}} | collective-permute-start | bytes 3145736 | tf_op jit(solution)/shard_map/ppermute | solution.py:400
  209.0 46.7 %collective-permute-start.10 = (bf16[1024,1024]{1,0:T(8,128)(2,1)}, bf16[1024,1024]{1,0:T(8,128)(2,1)}, u32[]{:S(2)}, u32[]{:S(2)}) collective-permute-start(bf16[1024,1024]{1,0:T(8,128)(2,1)} %get-tuple-element.26.q2.q3), channel_id=1, source_target_pairs={{0,1},{1,0},{2,3},{3,2},{4,5},{5,4},{6,7},{7,6}} | collective-permute-start | bytes 6291464 | tf_op jit(solution)/shard_map/ppermute | solution.py:400
  209.4 85.7 %collective-permute-start.11 = (bf16[1024,1024]{1,0:T(8,128)(2,1)}, bf16[1024,1024]{1,0:T(8,128)(2,1)S(1)}, u32[]{:S(2)}, u32[]{:S(2)}) collective-permute-start(bf16[1024,1024]{1,0:T(8,128)(2,1)} %get-tuple-element.31.o2.o3), channel_id=1, source_target_pairs={{0,1},{1,0},{2,3},{3,2},{4,5},{5,4},{6,7},{7,6}} | collective-permute-start | bytes 6291464 | tf_op jit(solution)/shard_map/ppermute | solution.py:400
  243.3 1.0 copy-start.3
  295.2 1.3 copy-start.2

commit v2 on v1

v2 whole, which is shorter than its diff:
```python
import functools
import math

import jax
import jax.numpy as jnp
from jax import lax
from jax.experimental import pallas as pl
from jax.experimental.pallas import tpu as pltpu
from jax.sharding import PartitionSpec as P

BLK = 256
LOW = -3.0e38
F32 = jnp.float32
BF16 = jnp.bfloat16


def dot(a, b):
    return jnp.dot(a, b, preferred_element_type=F32)


def dot_nt(a, b):
    return lax.dot_general(a, b, (((1,), (1,)), ((), ())), preferred_element_type=F32)


def dot_tn(a, b):
    return lax.dot_general(a, b, (((0,), (0,)), ((), ())), preferred_element_type=F32)


def params(n=1, mib=60):
    return pltpu.CompilerParams(
        dimension_semantics=("arbitrary",) * n, vmem_limit_bytes=mib * 1024 * 1024
    )


def cost(flops, nbytes):
    return pl.CostEstimate(flops=int(flops), bytes_accessed=int(nbytes), transcendentals=0)


def heads_kernel(w_ref, out_ref, wide):
    rows, num, hd = w_ref.shape
    wide[...] = w_ref[...].astype(F32).reshape(rows * num, hd)
    for h in range(num):
        out_ref[:, h * hd : (h + 1) * hd] = wide[pl.ds(h, rows, stride=num), :].astype(BF16)


def flat_heads(w):
    model, num, hd = w.shape
    tile = 256
    return pl.pallas_call(
        heads_kernel,
        out_shape=jax.ShapeDtypeStruct((model, num * hd), BF16),
        grid=(model // tile,),
        in_specs=[pl.BlockSpec((tile, num, hd), lambda i: (i, 0, 0))],
        out_specs=pl.BlockSpec((tile, num * hd), lambda i: (i, 0)),
        scratch_shapes=[pltpu.VMEM((tile * num, hd), F32)],
        compiler_params=params(),
        cost_estimate=cost(4e9, 4 * model * num * hd),
    )(w)


def proj_kernel(trans, rows, sc, *refs):
    num = len(rows)
    xs_hbm, (w_ref, out_ref, xs, sems) = refs[:num], refs[num:]
    copies, base = [], 0
    for n, (x, r) in enumerate(zip(xs_hbm, rows)):
        copies.append(pltpu.make_async_copy(x, xs.at[base : base + r, :], sems.at[n]))
        base += r

    @pl.when(pl.program_id(0) == 0)
    def _():
        for cp in copies:
            cp.start()
        for cp in copies:
            cp.wait()

    out_ref[...] = (dot_nt if trans else dot)(xs[...], w_ref[...]).astype(BF16)


def project(core, pieces, w, width, trans):
    rows, depth, tile = [p.shape[0] for p in pieces], pieces[0].shape[1], 256
    total, steps = sum(rows), width // tile
    if trans:
        spec = pl.BlockSpec((tile, depth), lambda i, s: (s[0] * steps + i, 0))
    else:
        spec = pl.BlockSpec((depth, tile), lambda i, s: (0, s[0] * steps + i))
    return pl.pallas_call(
        functools.partial(proj_kernel, trans, rows),
        out_shape=jax.ShapeDtypeStruct((total, width), BF16),
        grid_spec=pltpu.PrefetchScalarGridSpec(
            num_scalar_prefetch=1,
            grid=(steps,),
            in_specs=[pl.BlockSpec(memory_space=pl.ANY)] * len(pieces) + [spec],
            out_specs=pl.BlockSpec((total, tile), lambda i, s: (0, i)),
            scratch_shapes=[pltpu.VMEM((total, depth), BF16), pltpu.SemaphoreType.DMA((len(pieces),))],
        ),
        compiler_params=params(),
        cost_estimate=cost(2 * total * depth * width, 2 * (total * depth + depth * width + total * width)),
    )(core, *pieces, w)


def kv_kernel(x_ref, wk_ref, wv_ref, out_ref):
    out_ref[:, :256] = dot(x_ref[...], wk_ref[...]).astype(BF16)
    out_ref[:, 256:] = dot(x_ref[...], wv_ref[...]).astype(BF16)


def project_kv(x, wk, wv):
    rows, depth = x.shape
    tile = 256
    return pl.pallas_call(
        kv_kernel,
        out_shape=jax.ShapeDtypeStruct((rows, 512), BF16),
        grid=(rows // tile,),
        in_specs=[
            pl.BlockSpec((tile, depth), lambda i: (i, 0)),
            pl.BlockSpec((depth, 256), lambda i: (0, 0)),
            pl.BlockSpec((depth, 256), lambda i: (0, 0)),
        ],
        out_specs=pl.BlockSpec((tile, 512), lambda i: (i, 0)),
        compiler_params=params(),
        cost_estimate=cost(2 * rows * depth * 512, 5e6),
    )(x, wk, wv)


def attn_kernel(heads, scale, first, final, sc, q_ref, do_ref, *refs):
    kv_refs, refs = refs[:8], refs[8:]
    if first:
        o_ref, dq_ref, dkv_ref = refs[:3]
        scratch = refs[3:]
    else:
        init_ref, o_ref, dq_ref, dkv_ref = refs[:4]
        scratch = refs[4:]
    ks, vs, kt, vt, dk, dv, qt, dot_t, qst, dost, s_ref, p_ref, ds_ref, ot, dqt, m_ref, l_ref = scratch
    step = pl.program_id(0)
    wide = heads * BLK
    hd = 128
    c2 = scale * math.log2(math.e)

    @pl.when(step == 0)
    def _():
        for i in range(8):
            rows = slice((i % 2) * BLK, (i % 2 + 1) * BLK)
            at = pl.ds(pl.multiple_of(sc[i] * BLK, BLK), BLK)
            kk, vv = kv_refs[i // 2][rows, :], kv_refs[4 + i // 2][rows, :]
            ks[at, :] = kk
            vs[at, :] = vv
            kt[:, at] = kk.T
            vt[:, at] = vv.T
            if not first:
                init_rows = slice(i * BLK, (i + 1) * BLK)
                dk[at, :] = init_ref[init_rows, :hd]
                dv[at, :] = init_ref[init_rows, hd:]
            else:
                dk[at, :] = jnp.zeros((BLK, hd), F32)
                dv[at, :] = jnp.zeros((BLK, hd), F32)

    for h in range(heads):
        cols = slice(h * hd, (h + 1) * hd)
        span = slice(h * BLK, (h + 1) * BLK)
        qh, dh = q_ref[:, cols], do_ref[:, cols]
        qst[span, :] = qh
        dost[span, :] = dh
        qt[:, span] = qh.T
        dot_t[:, span] = dh.T

    b = sc[8 + step]

    def softmax_block(j, masked):
        at = pl.ds(pl.multiple_of(j * BLK, BLK), BLK)
        for h in range(heads):
            span = slice(h * BLK, (h + 1) * BLK)
            t = dot(ks[at, :], qt[:, span]) * c2
            if masked:
                key = lax.broadcasted_iota(jnp.int32, (BLK, BLK), 0)
                query = lax.broadcasted_iota(jnp.int32, (BLK, BLK), 1)
                t = jnp.where(key <= query, t, LOW)
            s_ref[at, span] = t
            m8 = m_ref[:, span]
            new = jnp.maximum(m8, jnp.max(t.reshape(BLK // 8, 8, BLK), axis=0))
            e = jnp.exp2(s_ref[at, span].reshape(BLK // 8, 8, BLK) - new[None])
            l_ref[:, span] = l_ref[:, span] * jnp.exp2(m8 - new) + jnp.sum(e, axis=0)
            m_ref[:, span] = new

    m_ref[...] = jnp.full((8, wide), LOW, F32)
    l_ref[...] = jnp.zeros((8, wide), F32)

    def open_block(j, _):
        softmax_block(j, False)
        return 0

    lax.fori_loop(0, b, open_block, 0)
    softmax_block(b, True)
    m8 = m_ref[...]
    top = jnp.max(m8, axis=0, keepdims=True)
    lse = top + jnp.log2(jnp.sum(l_ref[...] * jnp.exp2(m8 - top), axis=0, keepdims=True))

    ot[...] = jnp.zeros_like(ot)

    def value_block(j, _):
        at = pl.ds(pl.multiple_of(j * BLK, BLK), BLK)
        for h in range(heads):
            span = slice(h * BLK, (h + 1) * BLK)
            p = jnp.exp2(s_ref[at, span] - lse[:, span]).astype(BF16)
            p_ref[at, span] = p
            ot[:, span] += dot(vt[:, at], p)
        return 0

    lax.fori_loop(0, b + 1, value_block, 0)

    o_round = ot[...].astype(BF16)
    delta = jnp.sum(o_round.astype(F32) * dot_t[...].astype(F32), axis=0, keepdims=True)
    for h in range(heads):
        o_ref[:, h * hd : (h + 1) * hd] = o_round[:, h * BLK : (h + 1) * BLK].T
    dqt[...] = jnp.zeros_like(dqt)

    def grad_block(j, _):
        at = pl.ds(pl.multiple_of(j * BLK, BLK), BLK)
        dp = dot(vs[at, :], dot_t[...])
        dv[at, :] += dot(p_ref[at, :], dost[...])
        ds = (p_ref[at, :].astype(F32) * (dp - delta)).astype(BF16)
        ds_ref[...] = ds
        dqt[...] += dot(kt[:, at], ds_ref[...])
        dk[at, :] += dot(ds_ref[...], qst[...])
        return 0

    lax.fori_loop(0, b + 1, grad_block, 0)

    for h in range(heads):
        dq_ref[:, h * hd : (h + 1) * hd] = (dqt[:, h * BLK : (h + 1) * BLK] * scale).astype(BF16).T

    @pl.when(step == pl.num_programs(0) - 1)
    def _():
        for i in range(8):
            at = pl.ds(pl.multiple_of(sc[i] * BLK, BLK), BLK)
            if final:
                out = pl.ds(pl.multiple_of(sc[16 + i] * BLK, BLK), BLK)
                dkv_ref[out, :hd] = (dk[at, :] * scale).astype(BF16)
                dkv_ref[out, hd:] = dv[at, :].astype(BF16)
            else:
                out = slice(i * BLK, (i + 1) * BLK)
                dkv_ref[out, :hd] = dk[at, :]
                dkv_ref[out, hd:] = dv[at, :]


def attention(sc, q, do, kv_pieces, init, final, scale):
    first = init is None
    rows, width = q.shape
    heads = width // 128
    wide = heads * BLK
    seq = 2048
    row_spec = pl.BlockSpec((BLK, width), lambda i, s: (i, 0))
    out_spec = pl.BlockSpec((BLK, width), lambda i, s: (s[12 + i], 0))
    full = lambda shape: pl.BlockSpec(shape, lambda i, s: (0, 0))
    ins = [q, do] + list(kv_pieces) * 2 + ([] if first else [init])
    in_specs = [row_spec, row_spec]
    in_specs += [pl.BlockSpec((512, 128), lambda i, s: (0, s[24]))] * 4
    in_specs += [pl.BlockSpec((512, 128), lambda i, s: (0, 2 + s[24]))] * 4
    if not first:
        in_specs.append(full(init.shape))
    return pl.pallas_call(
        functools.partial(attn_kernel, heads, scale, first, final),
        out_shape=(
            jax.ShapeDtypeStruct((rows, width), BF16),
            jax.ShapeDtypeStruct((rows, width), BF16),
            jax.ShapeDtypeStruct((seq, 256), BF16 if final else F32),
        ),
        grid_spec=pltpu.PrefetchScalarGridSpec(
            num_scalar_prefetch=1,
            grid=(rows // BLK,),
            in_specs=in_specs,
            out_specs=(out_spec, out_spec, full((seq, 256))),
            scratch_shapes=[
                pltpu.VMEM((seq, 128), BF16),
                pltpu.VMEM((seq, 128), BF16),
                pltpu.VMEM((128, seq), BF16),
                pltpu.VMEM((128, seq), BF16),
                pltpu.VMEM((seq, 128), F32),
                pltpu.VMEM((seq, 128), F32),
                pltpu.VMEM((128, wide), BF16),
                pltpu.VMEM((128, wide), BF16),
                pltpu.VMEM((wide, 128), BF16),
                pltpu.VMEM((wide, 128), BF16),
                pltpu.VMEM((seq, wide), F32),
                pltpu.VMEM((seq, wide), BF16),
                pltpu.VMEM((BLK, wide), BF16),
                pltpu.VMEM((128, wide), F32),
                pltpu.VMEM((128, wide), F32),
                pltpu.VMEM((8, wide), F32),
                pltpu.VMEM((8, wide), F32),
            ],
        ),
        compiler_params=params(),
        cost_estimate=cost(6e9 * (rows // BLK), 20e6),
    )(sc, *ins)


def y_kernel(sc, o_mine, o_other, w_mine, w_other, out_ref):
    out_ref[...] = (dot(o_mine[...], w_mine[...]) + dot(o_other[...], w_other[...])).astype(BF16)


def out_rows(core, o_mine, o_other, wo):
    rows, half, model, tile = 512, o_mine.shape[1], wo.shape[1], 256
    return pl.pallas_call(
        y_kernel,
        out_shape=jax.ShapeDtypeStruct((rows, model), BF16),
        grid_spec=pltpu.PrefetchScalarGridSpec(
            num_scalar_prefetch=1,
            grid=(model // tile,),
            in_specs=[
                pl.BlockSpec((rows, half), lambda i, s: (s[0], 0)),
                pl.BlockSpec((rows, half), lambda i, s: (s[0], 0)),
                pl.BlockSpec((half, tile), lambda i, s: (s[0], i)),
                pl.BlockSpec((half, tile), lambda i, s: (1 - s[0], i)),
            ],
            out_specs=pl.BlockSpec((rows, tile), lambda i, s: (0, i)),
        ),
        compiler_params=params(),
        cost_estimate=cost(4 * rows * half * model, 12e6),
    )(core, o_mine, o_other, wo, wo)


def dx_kernel(sc, q_mine, q_other, kv_mine, kv_other, wq_mine, wq_other, wk_mine, wk_other, wv_mine, wv_other, out_ref):
    hd = 128
    acc = dot_nt(q_mine[...], wq_mine[...]) + dot_nt(q_other[...], wq_other[...])
    acc += dot_nt(kv_mine[:, :hd], wk_mine[...]) + dot_nt(kv_other[:, :hd], wk_other[...])
    acc += dot_nt(kv_mine[:, hd:], wv_mine[...]) + dot_nt(kv_other[:, hd:], wv_other[...])
    out_ref[...] = acc.astype(BF16)


def grad_rows(core, dq_mine, dq_other, dkv_mine, dkv_other, wq, wk, wv):
    rows, half, model, tile = 512, dq_mine.shape[1], wq.shape[0], 256
    mine = lambda i, s: (s[0], 0)
    return pl.pallas_call(
        dx_kernel,
        out_shape=jax.ShapeDtypeStruct((rows, model), BF16),
        grid_spec=pltpu.PrefetchScalarGridSpec(
            num_scalar_prefetch=1,
            grid=(model // tile,),
            in_specs=[
                pl.BlockSpec((rows, half), mine),
                pl.BlockSpec((rows, half), mine),
                pl.BlockSpec((rows, 256), mine),
                pl.BlockSpec((rows, 256), mine),
                pl.BlockSpec((tile, half), lambda i, s: (i, s[0])),
                pl.BlockSpec((tile, half), lambda i, s: (i, 1 - s[0])),
                pl.BlockSpec((tile, 128), lambda i, s: (i, s[0])),
                pl.BlockSpec((tile, 128), lambda i, s: (i, 1 - s[0])),
                pl.BlockSpec((tile, 128), lambda i, s: (i, s[0])),
                pl.BlockSpec((tile, 128), lambda i, s: (i, 1 - s[0])),
            ],
            out_specs=pl.BlockSpec((rows, tile), lambda i, s: (0, i)),
        ),
        compiler_params=params(),
        cost_estimate=cost(4 * rows * half * model * 1.25, 14e6),
    )(core, dq_mine, dq_other, dkv_mine, dkv_other, wq, wq, wk, wk, wv, wv)


def piece_specs(width, s_col):
    flips = (0, 1, 0, 1, 0, 1)
    return [
        pl.BlockSpec((512 if n < 2 else 256, width), lambda g, i, s, f=f: (1 - s[0] if f else s[0], s_col(g, i)))
        for n, f in enumerate(flips)
    ]


def dwq_kernel(sc, *refs):
    xs_in, mine, other, kvm, kvo = refs[:6], refs[6:12], refs[12:18], refs[18:24], refs[24:30]
    out_ref, gk_ref, gv_ref = refs[30:33]
    g = pl.program_id(0)
    tile = out_ref.shape[0]

    def store(rhs):
        acc = sum(dot(x[...].T, q[...]) for x, q in zip(xs_in, rhs))
        flat = out_ref.reshape(tile * 8, 128)
        for h in range(8):
            flat[pl.ds(h, tile, stride=8), :] = acc[:, h * 128 : (h + 1) * 128]

    @pl.when(g == 0)
    def _():
        store(mine)

    @pl.when(g == 1)
    def _():
        store(other)
        core = sc[0]
        k_flat, v_flat = gk_ref.reshape(tile * 2, 128), gv_ref.reshape(tile * 2, 128)
        for src, head in ((kvm, core), (kvo, 1 - core)):
            acc = sum(dot(x[...].T, k[...]) for x, k in zip(xs_in, src))
            k_flat[pl.ds(head, tile, stride=2), :] = acc[:, :128]
            v_flat[pl.ds(head, tile, stride=2), :] = acc[:, 128:]


def grad_wq(core, xs, mine, other, kvm, kvo):
    model, half, tile = xs[0].shape[1], mine[0].shape[1], 256
    x_specs = [pl.BlockSpec((x.shape[0], tile), lambda g, i, s: (0, i)) for x in xs]
    q_specs = piece_specs(half, lambda g, i: 0)
    kv_at = ((0, 512, 0), (1, 512, 0), (0, 256, 4), (1, 256, 4), (0, 256, 6), (1, 256, 6))
    kv_specs = [
        pl.BlockSpec((r, 256), lambda g, i, s, f=f, base=base: (base + (1 - s[0] if f else s[0]), 0))
        for f, r, base in kv_at
    ]
    ex = lambda t: [t[0], t[0], t[1], t[1], t[2], t[2]]
    small = pl.BlockSpec((tile, 2, 128), lambda g, i, s: (i * g, 0, 0))
    return pl.pallas_call(
        dwq_kernel,
        out_shape=(
            jax.ShapeDtypeStruct((model, 16, 128), F32),
            jax.ShapeDtypeStruct((model, 2, 128), F32),
            jax.ShapeDtypeStruct((model, 2, 128), F32),
        ),
        grid_spec=pltpu.PrefetchScalarGridSpec(
            num_scalar_prefetch=1,
            grid=(2, model // tile),
            in_specs=x_specs + q_specs + q_specs + kv_specs + kv_specs,
            out_specs=(
                pl.BlockSpec((tile, 8, 128), lambda g, i, s: (i, (s[0] + g) % 2, 0)),
                small,
                small,
            ),
        ),
        compiler_params=params(2),
        cost_estimate=cost(2 * 2048 * model * (2 * half + 512), 40e6),
    )(core, *xs, *ex(mine), *ex(other), *([kvm] * 6), *([kvo] * 6))


def dwo_kernel(sc, *refs):
    mine, other, ys, out_ref = refs[:6], refs[6:12], refs[12:18], refs[18]
    g = pl.program_id(0)

    def store(lhs):
        out_ref[...] = sum(dot(o[...].T, y[...]) for o, y in zip(lhs, ys))

    @pl.when(g == 0)
    def _():
        store(mine)

    @pl.when(g == 1)
    def _():
        store(other)


def grad_wo(core, ys, mine, other):
    model, half, tile = ys[0].shape[1], mine[0].shape[1], 256
    steps = half // tile
    specs = piece_specs(tile, lambda g, i: jnp.where(g == 0, i, steps - 1))
    specs += piece_specs(tile, lambda g, i: jnp.where(g == 0, 0, i))
    specs += [pl.BlockSpec(y.shape, lambda g, i, s: (0, 0)) for y in ys]
    ex = lambda t: [t[0], t[0], t[1], t[1], t[2], t[2]]
    return pl.pallas_call(
        dwo_kernel,
        out_shape=jax.ShapeDtypeStruct((2 * half, model), F32),
        grid_spec=pltpu.PrefetchScalarGridSpec(
            num_scalar_prefetch=1,
            grid=(2, steps),
            in_specs=specs,
            out_specs=pl.BlockSpec((tile, model), lambda g, i, s: ((s[0] + g) % 2 * steps + i, 0)),
        ),
        compiler_params=params(2),
        cost_estimate=cost(4 * 2048 * model * half, 40e6),
    )(core, *ex(mine), *ex(other), *ys)


def solution(mesh):
    row_spec = P(("dp", "cp"), None)
    rep_spec = P(None, None, None)
    part_spec = P("dp", None, None)
    core_swap = [(0, 1), (1, 0), (2, 3), (3, 2)]
    chip_swap = [(0, 2), (2, 0), (1, 3), (3, 1)]

    def device_layer(x, dy, w_query, w_key, w_value, w_out):
        rows, model = x.shape
        num_heads, hd = w_query.shape[1:]
        kv_heads = w_key.shape[1]
        scale = hd ** -0.5
        rank = lax.axis_index("cp").astype(jnp.int32)
        c = rank & 1
        core = c.reshape(1)
        devs = [rank, rank ^ 1, rank ^ 2, rank ^ 3]
        kv_pos = [p for e in devs for p in (e, 7 - e)]
        own_slots = [p for e in devs[:2] for p in ((e & 1) * 2, (e & 1) * 2 + 1)]
        far_slots = []
        for e in devs[2:]:
            far_slots += [jnp.where((e & 1) == 1, 4, 6) + (e & 1), jnp.where((e & 1) == 0, 4, 6) + (e & 1)]
        pos_a = [jnp.where((e & 1) == 0, 7 - e, e) for e in devs[2:]]
        pos_b = [jnp.where((e & 1) == 0, e, 7 - e) for e in devs[2:]]
        far = [c, 1 - c]
        tail = own_slots + far_slots + [c]
        sc_chip = jnp.stack(kv_pos + kv_pos[:4] + own_slots + tail)
        sc_a = jnp.stack(kv_pos + pos_a * 2 + far * 2 + tail)
        sc_b = jnp.stack(kv_pos + pos_b * 2 + far * 2 + tail)

        to_core = lambda v: lax.ppermute(v, "cp", core_swap)
        to_chip = lambda v: lax.ppermute(v, "cp", chip_swap)

        wk = w_key.reshape(model, kv_heads * hd)
        wv = w_value.reshape(model, kv_heads * hd)
        wo = w_out.reshape(num_heads * hd, model)
        x_p = to_core(x)
        dy_p = to_core(dy)

        kv = project_kv(x, wk, wv)
        kv_r = to_chip(kv)
        kv_p = to_core(kv)
        x_s, dy_s, w_s, _ = lax.optimization_barrier((x, dy, w_query, kv))
        cut = lambda v, at: lax.dynamic_slice(v, (at * BLK, 0), (BLK, model))
        x_a = to_chip(cut(x_s, 1 - c))
        dy_a = to_chip(cut(dy_s, 1 - c))
        x_b = to_chip(cut(x_s, c))
        dy_b = to_chip(cut(dy_s, c))
        kv_rp = to_core(kv_r)
        wq = flat_heads(w_s)
        pieces = (kv, kv_p, kv_r, kv_rp)
        q = project(core, (x, x_p), wq, 1024, False)
        do = project(core, (dy, dy_p), wo, 1024, True)
        o_c, dq_c, part = attention(sc_chip, q, do, pieces, None, False, scale)
        x_a, dy_a, o_c, dq_c = lax.optimization_barrier((x_a, dy_a, o_c, dq_c))
        x_pa, dy_pa, o_co, dq_co = to_core(x_a), to_core(dy_a), to_core(o_c), to_core(dq_c)

        q = project(core, (x_a, x_pa), wq, 1024, False)
        do = project(core, (dy_a, dy_pa), wo, 1024, True)
        o_a, dq_a, part = attention(sc_a, q, do, pieces, part, False, scale)
        x_b, dy_b, o_a, dq_a = lax.optimization_barrier((x_b, dy_b, o_a, dq_a))
        x_pb, dy_pb, o_ao, dq_ao = to_core(x_b), to_core(dy_b), to_core(o_a), to_core(dq_a)

        q = project(core, (x_b, x_pb), wq, 1024, False)
        do = project(core, (dy_b, dy_pb), wo, 1024, True)
        o_b, dq_b, dkv = attention(sc_b, q, do, pieces, part, True, scale)
        o_co, dkv = lax.optimization_barrier((o_co, dkv))
        dkv_o, o_bo, dq_bo = to_core(dkv), to_core(o_b), to_core(dq_b)
        y = out_rows(core, o_c, o_co, wo)

        xs = (x, x_p, x_a, x_pa, x_b, x_pb)
        ys = (dy, dy_p, dy_a, dy_pa, dy_b, dy_pb)
        gwo = grad_wo(core, ys, (o_c, o_a, o_b), (o_co, o_ao, o_bo))
        dx = grad_rows(core, dq_c, dq_co, dkv, dkv_o, wq, wk, wv)
        gwq, gwk, gwv = grad_wq(core, xs, (dq_c, dq_a, dq_b), (dq_co, dq_ao, dq_bo), dkv, dkv_o)
        return y, dx, gwq, gwk, gwv, gwo.reshape(num_heads, hd, model)

    return jax.shard_map(
        device_layer,
        mesh=mesh,
        in_specs=(row_spec, row_spec, rep_spec, rep_spec, rep_spec, rep_spec),
        out_specs=(row_spec, row_spec, part_spec, part_spec, part_spec, part_spec),
        check_vma=False,
    )
```

time: 316 us -> 285 us (0.902)
  waiting for transfers between devices: 27.6 us -> 0.98 us
  local copies, waits for them, and re-layouts: 38.5 us -> 13.3 us
  Pallas kernels: 234 us -> 257 us
    unnamed x15 -> x20, local copies, waits for them, and re-layouts: 33.9 us -> 3.84 us
    ppermute x3 -> x5, waiting for transfers between devices: 27.6 us -> 0.01 us  [device_layer(): to_chip = lambda v: lax.ppermute(v, 'cp', chip_swap)]
    pallas_call x11 -> x13, Pallas kernels: 214 us -> 235 us  [the longest x3 107 us: attention(): pl.pallas_call(functools.partial(attn_kernel, heads, scale, first, final)...]
    dynamic_slice x0 -> x2, local copies, waits for them, and re-layouts: none -> 4.31 us  [device_layer(): cut = lambda v, at: lax.dynamic_slice(v, (at * BLK, 0), (BLK, model))]
    ppermute x3 -> x5, starting transfers between devices: 5 us -> 6.57 us  [device_layer(): to_chip = lambda v: lax.ppermute(v, 'cp', chip_swap)]
  transfers between devices with their start and end apart: 12 -> 20, of which waited for: 1 -> 1; matrix products, arithmetic and copies ran while one was open for 11% -> 3% of each run, Pallas kernels for 70% -> 82%
where the time goes in v2:
time: 285 us; the launch traced here: 283 us
  Pallas kernels  257 us (90%)
  local copies, waits for them, and re-layouts  13.3 us (5%)
  starting transfers between devices  10.6 us (4%)
    pallas_call x3, Pallas kernels, attention(): pl.pallas_call(functools.partial(attn_kernel, heads, scale, first, final)...  107 us
    pallas_call x6, Pallas kernels, project(): pl.pallas_call(functools.partial(proj_kernel, trans, rows), out_shape=jax...  48 us
    pallas_call x1, Pallas kernels, grad_wq(): pl.pallas_call(dwq_kernel, out_shape=(jax.ShapeDtypeStruct((model, 16, 12...  36.4 us
    pallas_call x1, Pallas kernels, grad_wo(): pl.pallas_call(dwo_kernel, out_shape=jax.ShapeDtypeStruct((2 * half, mode...  26.1 us
    pallas_call x1, Pallas kernels, flat_heads(): pl.pallas_call(heads_kernel, out_shape=jax.ShapeDtypeStruct((model, num *...  12.5 us
    pallas_call x1, Pallas kernels, grad_rows(): pl.pallas_call(dx_kernel, out_shape=jax.ShapeDtypeStruct((rows, model), B...  12.4 us
    pallas_call x1, Pallas kernels, out_rows(): pl.pallas_call(y_kernel, out_shape=jax.ShapeDtypeStruct((rows, model), BF...  10.4 us
    ppermute x5, starting transfers between devices, device_layer(): to_chip = lambda v: lax.ppermute(v, 'cp', chip_swap)  6.57 us
  transfers between devices with their start and end apart: 20, of which 1 were waited for; matrix products, arithmetic and copies ran while one was open for 3% of the time, Pallas kernels for 82%

profile of v2, /device:TPU:0, one launch (start us, length us, event | category | flops | bytes accessed | tf_op | source)
XLA Modules:
  0.0 283.3 jit_solution(17762144737408552610)
XLA Ops:
  0.6 0.9 collective-permute-start.2
  1.5 0.0 collective-permute-start.3
  1.5 3.2 %copy_bitcast_fusion = (bf16[2048,256]{1,0:T(8,128)(2,1)}, bf16[2048,256]{1,0:T(8,128)(2,1)}) fusion(bf16[256,8,2,128]{3,2,1,0:T(2,128)(2,1)} %bitcast.35, bf16[256,8,2,128]{3,2,1,0:T(2,128)(2,1)} %bitcast.36), kind=kLoop, calls=%fused_computation | loop fusion | bytes 4194304 | tf_op jit(solution)/shard_map/reshape | solution.py:495
  4.7 4.1 %shard_map.109.refs_0_.refs_4_ = bf16[512,512]{1,0:T(8,128)(2,1)} custom-call(bf16[512,2048]{1,0:T(8,128)(2,1)} %refs_0_.5, bf16[2048,256]{1,0:T(8,128)(2,1)} %get-tuple-element.61.wk_ref.wk_mine.wk_other, bf16[2048,256]{1,0:T(8,128)(2,1)} %get-tuple-element.60.wv_ref.wv_mine.wv_other), custom_call_target="tpu_custom_call" | custom-call | flops 1073741824 | bytes 5000000 | tf_op jit(solution)/shard_map/pallas_call | solution.py:109
  8.9 0.5 collective-permute-start.4
  9.4 2.5 collective-permute-start.5
  11.9 1.2 constant_dynamic-slice_fusion.1
  13.0 0.0 collective-permute-start
  13.1 0.7 stack.64.sc
  13.7 3.1 %constant_dynamic-slice_fusion = (bf16[256,2048]{1,0:T(8,128)(2,1)}, bf16[256,2048]{1,0:T(8,128)(2,1)}) fusion(bf16[512,2048]{1,0:T(8,128)(2,1)} %refs_12_.1, s32[]{:T(128)S(6)} %select_n.41, s32[]{:T(128)S(6)} %select_n.34), kind=kLoop, calls=%fused_computation.2 | loop fusion | bytes 4194312 | tf_op jit(solution)/shard_map/dynamic_slice | solution.py:504
  16.9 12.5 %shard_map.110.refs_2_.wq_mine.wq_other = bf16[2048,2048]{1,0:T(8,128)(2,1)} custom-call(bf16[2048,16,128]{2,1,0:T(8,128)(2,1)} %w_ref), custom_call_target="tpu_custom_call" | custom-call | flops 4000000000 | bytes 16777216 | tf_op jit(solution)/shard_map/pallas_call | solution.py:49
  29.4 0.0 collective-permute-done.5.refs_2_.refs_6_
  29.4 2.0 collective-permute-start.1
  31.4 0.0 collective-permute-done.2.refs_1_
  31.4 0.0 collective-permute-start.6
  31.4 9.6 %shard_map.111.q_ref = bf16[1024,1024]{1,0:T(8,128)(2,1)} custom-call(s32[1]{0:T(128)} %bitcast.sc, bf16[512,2048]{1,0:T(8,128)(2,1)} %refs_0_.5, bf16[512,2048]{1,0:T(8,128)(2,1)} %collective-permute-done.2.refs_1_, bf16[2048,2048]{1,0:T(8,128)(2,1)} %shard_map.110.refs_2_.wq_mine.wq_other), custom_call_target="tpu_custom_call" | custom-call | flops 4294967296 | bytes 10485760 | tf_op jit(solution)/shard_map/pallas_call | solution.py:86
  41.0 0.0 collective-permute-done.3.refs_1_.refs_13_
  41.0 9.7 %shard_map.112.do_ref = bf16[1024,1024]{1,0:T(8,128)(2,1)} custom-call(s32[1]{0:T(128)} %bitcast.sc, bf16[512,2048]{1,0:T(8,128)(2,1)} %refs_12_.1, bf16[512,2048]{1,0:T(8,128)(2,1)} %collective-permute-done.3.refs_1_.refs_13_, bf16[2048,2048]{1,0:T(8,128)(2,1)} %bitcast.30), custom_call_target="tpu_custom_call" | custom-call | flops 4294967296 | bytes 10485760 | tf_op jit(solution)/shard_map/pallas_call | solution.py:86
  50.7 0.0 collective-permute-done.4.refs_1_.refs_5_
  50.7 0.0 collective-permute-done.6.refs_3_.refs_7_
  50.7 0.8 copy-done.9
  51.5 50.6 %shard_map.113 = (bf16[1024,1024]{1,0:T(8,128)(2,1)}, bf16[1024,1024]{1,0:T(8,128)(2,1)}, f32[2048,256]{1,0:T(8,128)}) custom-call(s32[25]{0:T(128)} %stack.64.sc, bf16[1024,1024]{1,0:T(8,128)(2,1)} %shard_map.111.q_ref, bf16[1024,1024]{1,0:T(8,128)(2,1)} %shard_map.112.do_ref, bf16[512,512]{1,0:T(8,128)(2,1)} %shard_map.109.refs_0_.refs_4_, ...), custom_call_target="tpu_custom_call" | custom-call | flops 24000000000 | bytes 20000000 | tf_op jit(solution)/shard_map/pallas_call | solution.py:259
  102.1 0.0 collective-permute-done.refs_0_.refs_2_
  102.1 0.0 collective-permute-done.1.refs_0_.refs_14_
  102.2 0.4 collective-permute-start.10
  102.6 0.1 collective-permute-start.11
  102.7 0.0 collective-permute-start.8
  102.7 2.0 collective-permute-start.9
  104.7 0.7 stack.71.sc
  105.4 0.0 collective-permute-done.10.refs_1_.refs_3_
  105.4 7.1 %shard_map.114.q_ref = bf16[512,1024]{1,0:T(8,128)(2,1)} custom-call(s32[1]{0:T(128)} %bitcast.sc, bf16[256,2048]{1,0:T(8,128)(2,1)} %copy-done.2, bf16[256,2048]{1,0:T(8,128)(2,1)} %collective-permute-done.10.refs_1_.refs_3_, bf16[2048,2048]{1,0:T(8,128)(2,1)} %shard_map.110.refs_2_.wq_mine.wq_other), custom_call_target="tpu_custom_call" | custom-call | flops 2147483648 | bytes 7340032 | tf_op jit(solution)/shard_map/pallas_call | solution.py:86
  112.6 0.0 collective-permute-done.11.refs_1_.refs_15_
  112.6 1.0 copy-done.4
  113.6 7.3 %shard_map.115.do_ref = bf16[512,1024]{1,0:T(8,128)(2,1)} custom-call(s32[1]{0:T(128)} %bitcast.sc, bf16[256,2048]{1,0:T(8,128)(2,1)} %copy-done.3, bf16[256,2048]{1,0:T(8,128)(2,1)} %copy-done.4, bf16[2048,2048]{1,0:T(8,128)(2,1)} %bitcast.31), custom_call_target="tpu_custom_call" | custom-call | flops 2147483648 | bytes 7340032 | tf_op jit(solution)/shard_map/pallas_call | solution.py:86
  120.8 30.9 %shard_map.116 = (bf16[512,1024]{1,0:T(8,128)(2,1)}, bf16[512,1024]{1,0:T(8,128)(2,1)}, f32[2048,256]{1,0:T(8,128)}) custom-call(s32[25]{0:T(128)} %stack.71.sc, bf16[512,1024]{1,0:T(8,128)(2,1)} %shard_map.114.q_ref, bf16[512,1024]{1,0:T(8,128)(2,1)} %shard_map.115.do_ref, bf16[512,512]{1,0:T(8,128)(2,1)} %shard_map.109.refs_0_.refs_4_, ...), custom_call_target="tpu_custom_call" | custom-call | flops 12000000000 | bytes 20000000 | tf_op jit(solution)/shard_map/pallas_call | solution.py:259
  151.8 0.0 collective-permute-done.8.refs_0_.refs_4_
  151.8 0.0 collective-permute-done.9.refs_0_.refs_16_
  151.8 0.0 collective-permute-start.12
  151.8 0.5 collective-permute-start.13
  152.3 0.0 collective-permute-start.7
  152.3 0.6 stack.68.sc
  153.0 0.5 collective-permute-start.14
  153.4 0.0 collective-permute-start.16
  153.5 0.9 collective-permute-done.12.refs_1_.refs_5_
  154.4 7.1 %shard_map.117.q_ref = bf16[512,1024]{1,0:T(8,128)(2,1)} custom-call(s32[1]{0:T(128)} %bitcast.sc, bf16[256,2048]{1,0:T(8,128)(2,1)} %collective-permute-done.8.refs_0_.refs_4_, bf16[256,2048]{1,0:T(8,128)(2,1)} %collective-permute-done.12.refs_1_.refs_5_, bf16[2048,2048]{1,0:T(8,128)(2,1)} %shard_map.110.refs_2_.wq_mine.wq_other), custom_call_target="tpu_custom_call" | custom-call | flops 2147483648 | bytes 7340032 | tf_op jit(solution)/shard_map/pallas_call | solution.py:86
  161.6 0.0 collective-permute-done.13.refs_1_.refs_17_
  161.6 1.1 copy-done.5
  162.6 7.2 %shard_map.118.do_ref = bf16[512,1024]{1,0:T(8,128)(2,1)} custom-call(s32[1]{0:T(128)} %bitcast.sc, bf16[256,2048]{1,0:T(8,128)(2,1)} %collective-permute-done.9.refs_0_.refs_16_, bf16[256,2048]{1,0:T(8,128)(2,1)} %copy-done.5, bf16[2048,2048]{1,0:T(8,128)(2,1)} %bitcast.32), custom_call_target="tpu_custom_call" | custom-call | flops 2147483648 | bytes 7340032 | tf_op jit(solution)/shard_map/pallas_call | solution.py:86
  169.9 25.8 %shard_map.119 = (bf16[512,1024]{1,0:T(8,128)(2,1)}, bf16[512,1024]{1,0:T(8,128)(2,1)}, bf16[2048,256]{1,0:T(8,128)(2,1)}) custom-call(s32[25]{0:T(128)} %stack.68.sc, bf16[512,1024]{1,0:T(8,128)(2,1)} %shard_map.117.q_ref, bf16[512,1024]{1,0:T(8,128)(2,1)} %shard_map.118.do_ref, bf16[512,512]{1,0:T(8,128)(2,1)} %shard_map.109.refs_0_.refs_4_, ...), custom_call_target="tpu_custom_call" | custom-call | flops 12000000000 | bytes 20000000 | tf_op jit(solution)/shard_map/pallas_call | solution.py:259
  195.7 0.0 collective-permute-done.7.o_other.refs_6_.refs_7_
  195.7 0.2 collective-permute-start.15
  195.9 0.3 collective-permute-start.17
  196.2 0.2 collective-permute-start.18
  196.4 10.4 %shard_map.120 = bf16[512,2048]{1,0:T(8,128)(2,1)} custom-call(s32[1]{0:T(128)} %bitcast.sc, bf16[1024,1024]{1,0:T(8,128)(2,1)} %get-tuple-element.36.o_mine.refs_0_.refs_1_, bf16[1024,1024]{1,0:T(8,128)(2,1)} %collective-permute-done.7.o_other.refs_6_.refs_7_, bf16[2048,2048]{1,0:T(8,128)(2,1)} %bitcast.33, bf16[2048,2048]{1,0:T(8,128)(2,1)} %bitcast.34), custom_call_target="tpu_custom_call" | custom-call | flops 4294967296 | bytes 12000000 | tf_op jit(solution)/shard_map/pallas_call | solution.py:302
  206.8 0.0 collective-permute-done.14.q_other.refs_12_.refs_13_
  206.8 0.4 collective-permute-start.19
  207.2 0.0 collective-permute-done.16.refs_14_.refs_15_
  207.2 0.0 collective-permute-done.15.kv_other.refs_24_.refs_25_.refs_26_.refs_27_.refs_28_.refs_29_
  207.2 0.0 collective-permute-done.17.refs_16_.refs_17_
  207.2 1.0 copy-done.6
  208.2 36.4 %shard_map.122 = (f32[2048,16,128]{2,1,0:T(8,128)}, f32[2048,2,128]{2,1,0:T(2,128)}, f32[2048,2,128]{2,1,0:T(2,128)}) custom-call(s32[1]{0:T(128)} %bitcast.sc, bf16[512,2048]{1,0:T(8,128)(2,1)} %refs_0_.5, bf16[512,2048]{1,0:T(8,128)(2,1)} %collective-permute-done.2.refs_1_, bf16[256,2048]{1,0:T(8,128)(2,1)} %copy-done.2, ...), custom_call_target="tpu_custom_call" | custom-call | flops 21474836480 | bytes 40000000 | tf_op jit(solution)/shard_map/pallas_call | solution.py:403
  244.6 12.4 %shard_map.121 = bf16[512,2048]{1,0:T(8,128)(2,1)} custom-call(s32[1]{0:T(128)} %bitcast.sc, bf16[1024,1024]{1,0:T(8,128)(2,1)} %get-tuple-element.47.q_mine.refs_6_.refs_7_, bf16[1024,1024]{1,0:T(8,128)(2,1)} %collective-permute-done.14.q_other.refs_12_.refs_13_, ...), custom_call_target="tpu_custom_call" | custom-call | flops 5368709120 | bytes 14000000 | tf_op jit(solution)/shard_map/pallas_call | solution.py:332
  256.9 0.0 collective-permute-done.19.refs_10_.refs_11_
  256.9 26.1 %shard_map.123 = f32[2048,2048]{1,0:T(8,128)} custom-call(s32[1]{0:T(128)} %bitcast.sc, bf16[1024,1024]{1,0:T(8,128)(2,1)} %get-tuple-element.36.o_mine.refs_0_.refs_1_, bf16[1024,1024]{1,0:T(8,128)(2,1)} %get-tuple-element.36.o_mine.refs_0_.refs_1_, bf16[512,1024]{1,0:T(8,128)(2,1)} %get-tuple-element.54.refs_2_.refs_3_, ...), custom_call_target="tpu_custom_call" | custom-call | flops 17179869184 | bytes 40000000 | tf_op jit(solution)/shard_map/pallas_call | solution.py:448
  (17 shorter events, 0.0 us)
Async XLA Ops:
  0.6 30.8 %collective-permute-start.2 = (bf16[512,2048]{1,0:T(8,128)(2,1)}, bf16[512,2048]{1,0:T(8,128)(2,1)}, u32[]{:S(2)}, u32[]{:S(2)}) collective-permute-start(bf16[512,2048]{1,0:T(8,128)(2,1)} %refs_0_.5), channel_id=1, source_target_pairs={{0,1},{1,0},{2,3},{3,2},{4,5},{5,4},{6,7},{7,6}} | collective-permute-start | bytes 6291464 | tf_op jit(solution)/shard_map/ppermute | solution.py:491
  1.5 39.5 %collective-permute-start.3 = (bf16[512,2048]{1,0:T(8,128)(2,1)}, bf16[512,2048]{1,0:T(8,128)(2,1)}, u32[]{:S(2)}, u32[]{:S(2)}) collective-permute-start(bf16[512,2048]{1,0:T(8,128)(2,1)} %refs_12_.1), channel_id=1, source_target_pairs={{0,1},{1,0},{2,3},{3,2},{4,5},{5,4},{6,7},{7,6}} | collective-permute-start | bytes 6291464 | tf_op jit(solution)/shard_map/ppermute | solution.py:491
  4.7 7.1 %copy-start = (bf16[512,2048]{1,0:T(8,128)(2,1)S(1)}, bf16[512,2048]{1,0:T(8,128)(2,1)}, u32[]{:S(2)}) copy-start(bf16[512,2048]{1,0:T(8,128)(2,1)} %refs_0_.5) | copy-start | bytes 6291460
  8.9 41.8 %collective-permute-start.4 = (bf16[512,512]{1,0:T(8,128)(2,1)}, bf16[512,512]{1,0:T(8,128)(2,1)}, u32[]{:S(2)}, u32[]{:S(2)}) collective-permute-start(bf16[512,512]{1,0:T(8,128)(2,1)} %shard_map.109.refs_0_.refs_4_), channel_id=1, source_target_pairs={{0,1},{1,0},{2,3},{3,2},{4,5},{5,4},{6,7},{7,6}} | collective-permute-start | bytes 1572872 | tf_op jit(solution)/shard_map/ppermute | solution.py:491
  9.4 20.0 %collective-permute-start.5 = (bf16[512,512]{1,0:T(8,128)(2,1)}, bf16[512,512]{1,0:T(8,128)(2,1)}, u32[]{:S(2)}, u32[]{:S(2)}) collective-permute-start(bf16[512,512]{1,0:T(8,128)(2,1)} %shard_map.109.refs_0_.refs_4_), channel_id=1, source_target_pairs={{0,2},{2,0},{1,3},{3,1},{4,6},{6,4},{5,7},{7,5}} | collective-permute-start | bytes 1572872 | tf_op jit(solution)/shard_map/ppermute | solution.py:492
  13.0 89.1 %collective-permute-start = (bf16[256,2048]{1,0:T(8,128)(2,1)S(1)}, bf16[256,2048]{1,0:T(8,128)(2,1)S(1)}, u32[]{:S(2)}, u32[]{:S(2)}) collective-permute-start(bf16[256,2048]{1,0:T(8,128)(2,1)S(1)} %get-tuple-element.59), channel_id=1, source_target_pairs={{0,2},{2,0},{1,3},{3,1},{4,6},{6,4},{5,7},{7,5}} | collective-permute-start | bytes 3145736 | tf_op jit(solution)/shard_map/ppermute | solution.py:492
  29.4 72.7 %collective-permute-start.1 = (bf16[256,2048]{1,0:T(8,128)(2,1)}, bf16[256,2048]{1,0:T(8,128)(2,1)S(1)}, u32[]{:S(2)}, u32[]{:S(2)}) collective-permute-start(bf16[256,2048]{1,0:T(8,128)(2,1)} %get-tuple-element.57), channel_id=1, source_target_pairs={{0,2},{2,0},{1,3},{3,1},{4,6},{6,4},{5,7},{7,5}} | collective-permute-start | bytes 3145736 | tf_op jit(solution)/shard_map/ppermute | solution.py:492
  31.4 19.3 %collective-permute-start.6 = (bf16[512,512]{1,0:T(8,128)(2,1)}, bf16[512,512]{1,0:T(8,128)(2,1)S(1)}, u32[]{:S(2)}, u32[]{:S(2)}) collective-permute-start(bf16[512,512]{1,0:T(8,128)(2,1)} %collective-permute-done.5.refs_2_.refs_6_), channel_id=1, source_target_pairs={{0,1},{1,0},{2,3},{3,2},{4,5},{5,4},{6,7},{7,6}} | collective-permute-start | bytes 1572872 | tf_op jit(solution)/shard_map/ppermute | solution.py:491
  50.7 0.8 copy-start.9
  102.1 3.3 %copy-start.2 = (bf16[256,2048]{1,0:T(8,128)(2,1)}, bf16[256,2048]{1,0:T(8,128)(2,1)S(1)}, u32[]{:S(2)}) copy-start(bf16[256,2048]{1,0:T(8,128)(2,1)S(1)} %collective-permute-done.refs_0_.refs_2_) | copy-start | bytes 3145732
  102.1 10.4 %copy-start.3 = (bf16[256,2048]{1,0:T(8,128)(2,1)}, bf16[256,2048]{1,0:T(8,128)(2,1)S(1)}, u32[]{:S(2)}) copy-start(bf16[256,2048]{1,0:T(8,128)(2,1)S(1)} %collective-permute-done.1.refs_0_.refs_14_) | copy-start | bytes 3145732
  102.2 3.3 %collective-permute-start.10 = (bf16[256,2048]{1,0:T(8,128)(2,1)S(1)}, bf16[256,2048]{1,0:T(8,128)(2,1)}, u32[]{:S(2)}, u32[]{:S(2)}) collective-permute-start(bf16[256,2048]{1,0:T(8,128)(2,1)S(1)} %collective-permute-done.refs_0_.refs_2_), channel_id=1, source_target_pairs={{0,1},{1,0},{2,3},{3,2},{4,5},{5,4},{6,7},{7,6}} | collective-permute-start | bytes 3145736 | tf_op jit(solution)/shard_map/ppermute | solution.py:491
  102.6 10.0 %collective-permute-start.11 = (bf16[256,2048]{1,0:T(8,128)(2,1)S(1)}, bf16[256,2048]{1,0:T(8,128)(2,1)S(1)}, u32[]{:S(2)}, u32[]{:S(2)}) collective-permute-start(bf16[256,2048]{1,0:T(8,128)(2,1)S(1)} %collective-permute-done.1.refs_0_.refs_14_), channel_id=1, source_target_pairs={{0,1},{1,0},{2,3},{3,2},{4,5},{5,4},{6,7},{7,6}} | collective-permute-start | bytes 3145736 | tf_op jit(solution)/shard_map/ppermute | solution.py:491
  102.7 49.1 %collective-permute-start.8 = (bf16[256,2048]{1,0:T(8,128)(2,1)}, bf16[256,2048]{1,0:T(8,128)(2,1)}, u32[]{:S(2)}, u32[]{:S(2)}) collective-permute-start(bf16[256,2048]{1,0:T(8,128)(2,1)} %get-tuple-element.58), channel_id=1, source_target_pairs={{0,2},{2,0},{1,3},{3,1},{4,6},{6,4},{5,7},{7,5}} | collective-permute-start | bytes 3145736 | tf_op jit(solution)/shard_map/ppermute | solution.py:492
  102.7 49.0 %collective-permute-start.9 = (bf16[256,2048]{1,0:T(8,128)(2,1)}, bf16[256,2048]{1,0:T(8,128)(2,1)}, u32[]{:S(2)}, u32[]{:S(2)}) collective-permute-start(bf16[256,2048]{1,0:T(8,128)(2,1)} %get-tuple-element.56), channel_id=1, source_target_pairs={{0,2},{2,0},{1,3},{3,1},{4,6},{6,4},{5,7},{7,5}} | collective-permute-start | bytes 3145736 | tf_op jit(solution)/shard_map/ppermute | solution.py:492
  112.6 1.0 copy-start.4
  120.8 31.5 %copy-start.1 = (bf16[1024,1024]{1,0:T(8,128)(2,1)S(1)}, bf16[1024,1024]{1,0:T(8,128)(2,1)}, u32[]{:S(2)}) copy-start(bf16[1024,1024]{1,0:T(8,128)(2,1)} %get-tuple-element.36.o_mine.refs_0_.refs_1_) | copy-start | bytes 6291460
  151.8 2.6 collective-permute-start.12
  151.8 9.7 %collective-permute-start.13 = (bf16[256,2048]{1,0:T(8,128)(2,1)}, bf16[256,2048]{1,0:T(8,128)(2,1)S(1)}, u32[]{:S(2)}, u32[]{:S(2)}) collective-permute-start(bf16[256,2048]{1,0:T(8,128)(2,1)} %collective-permute-done.9.refs_0_.refs_16_), channel_id=1, source_target_pairs={{0,1},{1,0},{2,3},{3,2},{4,5},{5,4},{6,7},{7,6}} | collective-permute-start | bytes 3145736 | tf_op jit(solution)/shard_map/ppermute | solution.py:491
  152.3 43.4 %collective-permute-start.7 = (bf16[1024,1024]{1,0:T(8,128)(2,1)S(1)}, bf16[1024,1024]{1,0:T(8,128)(2,1)}, u32[]{:S(2)}, u32[]{:S(2)}) collective-permute-start(bf16[1024,1024]{1,0:T(8,128)(2,1)S(1)} %copy-done.1), channel_id=1, source_target_pairs={{0,1},{1,0},{2,3},{3,2},{4,5},{5,4},{6,7},{7,6}} | collective-permute-start | bytes 6291464 | tf_op jit(solution)/shard_map/ppermute | solution.py:491
  153.0 53.8 %collective-permute-start.14 = (bf16[1024,1024]{1,0:T(8,128)(2,1)}, bf16[1024,1024]{1,0:T(8,128)(2,1)}, u32[]{:S(2)}, u32[]{:S(2)}) collective-permute-start(bf16[1024,1024]{1,0:T(8,128)(2,1)} %get-tuple-element.47.q_mine.refs_6_.refs_7_), channel_id=1, source_target_pairs={{0,1},{1,0},{2,3},{3,2},{4,5},{5,4},{6,7},{7,6}} | collective-permute-start | bytes 6291464 | tf_op jit(solution)/shard_map/ppermute | solution.py:491
  153.4 53.7 %collective-permute-start.16 = (bf16[512,1024]{1,0:T(8,128)(2,1)}, bf16[512,1024]{1,0:T(8,128)(2,1)}, u32[]{:S(2)}, u32[]{:S(2)}) collective-permute-start(bf16[512,1024]{1,0:T(8,128)(2,1)} %get-tuple-element.49.refs_8_.refs_9_), channel_id=1, source_target_pairs={{0,1},{1,0},{2,3},{3,2},{4,5},{5,4},{6,7},{7,6}} | collective-permute-start | bytes 3145736 | tf_op jit(solution)/shard_map/ppermute | solution.py:491
  161.6 1.1 copy-start.5
  169.9 26.3 %copy-start.7 = (bf16[512,1024]{1,0:T(8,128)(2,1)S(1)}, bf16[512,1024]{1,0:T(8,128)(2,1)}, u32[]{:S(2)}) copy-start(bf16[512,1024]{1,0:T(8,128)(2,1)} %get-tuple-element.54.refs_2_.refs_3_) | copy-start | bytes 3145732
  195.7 11.5 %collective-permute-start.15 = (bf16[2048,256]{1,0:T(8,128)(2,1)}, bf16[2048,256]{1,0:T(8,128)(2,1)S(1)}, u32[]{:S(2)}, u32[]{:S(2)}) collective-permute-start(bf16[2048,256]{1,0:T(8,128)(2,1)} %get-tuple-element.48.kv_mine.refs_18_.refs_19_.refs_20_.refs_21_.refs_22_.refs_23_), channel_id=1, source_target_pairs={{0,1},{1,0},{2,3},{3,2},{4,5},{5,4},{6,7},{7,6}} | collective-permute-start | bytes 3145736 | tf_op jit(solution)/shard_map/ppermute | solution.py:491
  195.9 10.9 %copy-start.8 = (bf16[512,1024]{1,0:T(8,128)(2,1)S(1)}, bf16[512,1024]{1,0:T(8,128)(2,1)}, u32[]{:S(2)}) copy-start(bf16[512,1024]{1,0:T(8,128)(2,1)} %get-tuple-element.55.refs_4_.refs_5_) | copy-start | bytes 3145732
  195.9 11.3 %collective-permute-start.17 = (bf16[512,1024]{1,0:T(8,128)(2,1)}, bf16[512,1024]{1,0:T(8,128)(2,1)}, u32[]{:S(2)}, u32[]{:S(2)}) collective-permute-start(bf16[512,1024]{1,0:T(8,128)(2,1)} %get-tuple-element.50.refs_10_.refs_11_), channel_id=1, source_target_pairs={{0,1},{1,0},{2,3},{3,2},{4,5},{5,4},{6,7},{7,6}} | collective-permute-start | bytes 3145736 | tf_op jit(solution)/shard_map/ppermute | solution.py:491
  196.2 60.7 %collective-permute-start.18 = (bf16[512,1024]{1,0:T(8,128)(2,1)S(1)}, bf16[512,1024]{1,0:T(8,128)(2,1)}, u32[]{:S(2)}, u32[]{:S(2)}) collective-permute-start(bf16[512,1024]{1,0:T(8,128)(2,1)S(1)} %copy-done.7), channel_id=1, source_target_pairs={{0,1},{1,0},{2,3},{3,2},{4,5},{5,4},{6,7},{7,6}} | collective-permute-start | bytes 3145736 | tf_op jit(solution)/shard_map/ppermute | solution.py:491
  206.8 50.1 %collective-permute-start.19 = (bf16[512,1024]{1,0:T(8,128)(2,1)S(1)}, bf16[512,1024]{1,0:T(8,128)(2,1)}, u32[]{:S(2)}, u32[]{:S(2)}) collective-permute-start(bf16[512,1024]{1,0:T(8,128)(2,1)S(1)} %copy-done.8), channel_id=1, source_target_pairs={{0,1},{1,0},{2,3},{3,2},{4,5},{5,4},{6,7},{7,6}} | collective-permute-start | bytes 3145736 | tf_op jit(solution)/shard_map/ppermute | solution.py:491
  207.2 1.0 copy-start.6

commit v3 on v2

v3 whole, which is shorter than its diff:
```python
import functools
import math

import jax
import jax.numpy as jnp
from jax import lax
from jax.experimental import pallas as pl
from jax.experimental.pallas import tpu as pltpu
from jax.sharding import PartitionSpec as P

BLK = 256
LOW = -3.0e38
F32 = jnp.float32
BF16 = jnp.bfloat16


def dot(a, b):
    return jnp.dot(a, b, preferred_element_type=F32)


def dot_nt(a, b):
    return lax.dot_general(a, b, (((1,), (1,)), ((), ())), preferred_element_type=F32)


def params(n=1, mib=60):
    return pltpu.CompilerParams(
        dimension_semantics=("arbitrary",) * n, vmem_limit_bytes=mib * 1024 * 1024
    )


def cost(flops, nbytes):
    return pl.CostEstimate(flops=int(flops), bytes_accessed=int(nbytes), transcendentals=0)


def heads_kernel(w_ref, perm_ref, out_ref):
    rows, num, hd = w_ref.shape
    flat = w_ref.reshape(rows * num, hd)
    group = num * 16
    for g in range(0, rows // 16, 2):
        pair = [flat[(g + n) * group : (g + n + 1) * group, :] for n in range(2)]
        res = dot(perm_ref[...], jnp.concatenate(pair, axis=1)).astype(BF16)
        for n in range(2):
            for h in range(num):
                out_ref[(g + n) * 16 : (g + n + 1) * 16, h * hd : (h + 1) * hd] = res[
                    h * 16 : (h + 1) * 16, n * hd : (n + 1) * hd
                ]


def flat_heads(w):
    model, num, hd = w.shape
    tile = 256
    row = jnp.arange(num * 16)
    perm = ((row % 16 * num + row // 16)[:, None] == row[None, :]).astype(BF16)
    return pl.pallas_call(
        heads_kernel,
        out_shape=jax.ShapeDtypeStruct((model, num * hd), BF16),
        grid=(model // tile,),
        in_specs=[
            pl.BlockSpec((tile, num, hd), lambda i: (i, 0, 0)),
            pl.BlockSpec((num * 16, num * 16), lambda i: (0, 0)),
        ],
        out_specs=pl.BlockSpec((tile, num * hd), lambda i: (i, 0)),
        compiler_params=params(),
        cost_estimate=cost(4e9, 4 * model * num * hd),
    )(w, perm)


def kv_kernel(sc, x_ref, dy_ref, wk_ref, wv_ref, out_ref, xa, xb, dya, dyb):
    out_ref[:, :256] = dot(x_ref[...], wk_ref[...]).astype(BF16)
    out_ref[:, 256:] = dot(x_ref[...], wv_ref[...]).astype(BF16)

    @pl.when(pl.program_id(0) == 1 - sc[0])
    def _():
        xa[...] = x_ref[...]
        dya[...] = dy_ref[...]

    @pl.when(pl.program_id(0) == sc[0])
    def _():
        xb[...] = x_ref[...]
        dyb[...] = dy_ref[...]


def project_kv(core, x, dy, wk, wv):
    rows, depth = x.shape
    row = pl.BlockSpec((BLK, depth), lambda i, s: (i, 0))
    fixed = lambda shape: pl.BlockSpec(shape, lambda i, s: (0, 0))
    half = jax.ShapeDtypeStruct((BLK, depth), BF16)
    return pl.pallas_call(
        kv_kernel,
        out_shape=(jax.ShapeDtypeStruct((rows, 512), BF16), half, half, half, half),
        grid_spec=pltpu.PrefetchScalarGridSpec(
            num_scalar_prefetch=1,
            grid=(rows // BLK,),
            in_specs=[row, row, fixed((depth, 256)), fixed((depth, 256))],
            out_specs=(pl.BlockSpec((BLK, 512), lambda i, s: (i, 0)),) + (fixed((BLK, depth)),) * 4,
        ),
        compiler_params=params(),
        cost_estimate=cost(2 * rows * depth * 512, 8e6),
    )(core, x, dy, wk, wv)


def attn_kernel(heads, scale, first, final, sc, wq_hbm, wo_hbm, *refs):
    x_hbm, dy_hbm, kv_refs, refs = refs[:2], refs[2:4], refs[4:12], refs[12:]
    if first:
        o_ref, dq_ref, dkv_ref = refs[:3]
        scratch = refs[3:]
    else:
        init_ref, o_ref, dq_ref, dkv_ref = refs[:4]
        scratch = refs[4:]
    ks, vs, kt, vt, dk, dv, qt, dot_t, qst, dost, s_ref, p_ref, ds_ref, ot, dqt, m_ref, l_ref, wq, wo, xs, dys, w_sem, x_sem, dy_sem = scratch
    step = pl.program_id(0)
    wide = heads * BLK
    hd = 128
    c2 = scale * math.log2(math.e)

    steps = 2 * x_hbm[0].shape[0] // BLK
    core = pl.multiple_of(sc[24] * heads * hd, heads * hd)
    load_wq = pltpu.make_async_copy(wq_hbm.at[:, pl.ds(core, heads * hd)], wq, w_sem.at[0])
    load_wo = pltpu.make_async_copy(wo_hbm.at[pl.ds(core, heads * hd), :], wo, w_sem.at[1])

    def load_rows(n):
        piece, row = divmod(n, steps // 2)
        src = pl.ds(row * BLK, BLK)
        return (
            pltpu.make_async_copy(x_hbm[piece].at[src, :], xs.at[n % 2], x_sem.at[n % 2]),
            pltpu.make_async_copy(dy_hbm[piece].at[src, :], dys.at[n % 2], dy_sem.at[n % 2]),
        )

    @pl.when(step == 0)
    def _():
        load_x, load_dy = load_rows(0)
        load_x.start()
        load_wq.start()
        load_dy.start()
        load_wo.start()

    for n in range(1, steps):

        @pl.when(step == n - 1)
        def _():
            for cp in load_rows(n):
                cp.start()

    @pl.when(step == 0)
    def _():
        for i in range(8):
            rows = slice((i % 2) * BLK, (i % 2 + 1) * BLK)
            at = pl.ds(pl.multiple_of(sc[i] * BLK, BLK), BLK)
            kk, vv = kv_refs[i // 2][rows, :], kv_refs[4 + i // 2][rows, :]
            ks[at, :] = kk
            vs[at, :] = vv
            kt[:, at] = kk.T
            vt[:, at] = vv.T
            if not first:
                init_rows = slice(i * BLK, (i + 1) * BLK)
                dk[at, :] = init_ref[init_rows, :hd]
                dv[at, :] = init_ref[init_rows, hd:]
            else:
                dk[at, :] = jnp.zeros((BLK, hd), F32)
                dv[at, :] = jnp.zeros((BLK, hd), F32)

    @pl.when(step == 0)
    def _():
        load_wq.wait()

    slot = step % 2
    pltpu.make_async_copy(x_hbm[0].at[0:BLK, :], xs.at[slot], x_sem.at[slot]).wait()
    q = dot(xs[slot], wq[...]).astype(BF16)
    for h in range(heads):
        qh = q[:, h * hd : (h + 1) * hd]
        qst[h * BLK : (h + 1) * BLK, :] = qh
        qt[:, h * BLK : (h + 1) * BLK] = qh.T

    @pl.when(step == 0)
    def _():
        load_wo.wait()

    pltpu.make_async_copy(dy_hbm[0].at[0:BLK, :], dys.at[slot], dy_sem.at[slot]).wait()
    do = dot_nt(dys[slot], wo[...]).astype(BF16)
    for h in range(heads):
        dh = do[:, h * hd : (h + 1) * hd]
        dost[h * BLK : (h + 1) * BLK, :] = dh
        dot_t[:, h * BLK : (h + 1) * BLK] = dh.T

    b = sc[8 + step]

    def softmax_block(j, masked):
        at = pl.ds(pl.multiple_of(j * BLK, BLK), BLK)
        for h in range(heads):
            span = slice(h * BLK, (h + 1) * BLK)
            t = dot(ks[at, :], qt[:, span]) * c2
            if masked:
                key = lax.broadcasted_iota(jnp.int32, (BLK, BLK), 0)
                query = lax.broadcasted_iota(jnp.int32, (BLK, BLK), 1)
                t = jnp.where(key <= query, t, LOW)
            s_ref[at, span] = t
            m8 = m_ref[:, span]
            new = jnp.maximum(m8, jnp.max(t.reshape(BLK // 8, 8, BLK), axis=0))
            e = jnp.exp2(s_ref[at, span].reshape(BLK // 8, 8, BLK) - new[None])
            l_ref[:, span] = l_ref[:, span] * jnp.exp2(m8 - new) + jnp.sum(e, axis=0)
            m_ref[:, span] = new

    m_ref[...] = jnp.full((8, wide), LOW, F32)
    l_ref[...] = jnp.zeros((8, wide), F32)

    def open_block(j, _):
        softmax_block(j, False)
        return 0

    lax.fori_loop(0, b, open_block, 0)
    softmax_block(b, True)
    m8 = m_ref[...]
    top = jnp.max(m8, axis=0, keepdims=True)
    lse = top + jnp.log2(jnp.sum(l_ref[...] * jnp.exp2(m8 - top), axis=0, keepdims=True))

    ot[...] = jnp.zeros_like(ot)

    def value_block(j, _):
        at = pl.ds(pl.multiple_of(j * BLK, BLK), BLK)
        for h in range(heads):
            span = slice(h * BLK, (h + 1) * BLK)
            p = jnp.exp2(s_ref[at, span] - lse[:, span]).astype(BF16)
            p_ref[at, span] = p
            ot[:, span] += dot(vt[:, at], p)
        return 0

    lax.fori_loop(0, b + 1, value_block, 0)

    o_round = ot[...].astype(BF16)
    delta = jnp.sum(o_round.astype(F32) * dot_t[...].astype(F32), axis=0, keepdims=True)
    for h in range(heads):
        o_ref[h * hd : (h + 1) * hd, :] = o_round[:, h * BLK : (h + 1) * BLK]
    dqt[...] = jnp.zeros_like(dqt)

    def grad_block(j, _):
        at = pl.ds(pl.multiple_of(j * BLK, BLK), BLK)
        dp = dot(vs[at, :], dot_t[...])
        dv[at, :] += dot(p_ref[at, :], dost[...])
        ds = (p_ref[at, :].astype(F32) * (dp - delta)).astype(BF16)
        ds_ref[...] = ds
        dqt[...] += dot(kt[:, at], ds_ref[...])
        dk[at, :] += dot(ds_ref[...], qst[...])
        return 0

    lax.fori_loop(0, b + 1, grad_block, 0)

    for h in range(heads):
        dq_ref[:, h * hd : (h + 1) * hd] = (dqt[:, h * BLK : (h + 1) * BLK] * scale).astype(BF16).T

    @pl.when(step == pl.num_programs(0) - 1)
    def _():
        for i in range(8):
            at = pl.ds(pl.multiple_of(sc[i] * BLK, BLK), BLK)
            if final:
                out = pl.ds(pl.multiple_of(sc[16 + i] * BLK, BLK), BLK)
                dkv_ref[out, :hd] = (dk[at, :] * scale).astype(BF16)
                dkv_ref[out, hd:] = dv[at, :].astype(BF16)
            else:
                out = slice(i * BLK, (i + 1) * BLK)
                dkv_ref[out, :hd] = dk[at, :]
                dkv_ref[out, hd:] = dv[at, :]


def attention(sc, wq, wo, x_pieces, dy_pieces, kv_pieces, init, final, scale):
    first = init is None
    rows, width, model = 2 * x_pieces[0].shape[0], wq.shape[1] // 2, wq.shape[0]
    hd = 128
    heads = width // hd
    wide = heads * BLK
    seq = 2048
    o_spec = pl.BlockSpec((width, BLK), lambda i, s: (0, s[12 + i]))
    out_spec = pl.BlockSpec((BLK, width), lambda i, s: (s[12 + i], 0))
    full = lambda shape: pl.BlockSpec(shape, lambda i, s: (0, 0), pipeline_mode=pl.Buffered(1))
    ins = [wq, wo, *x_pieces, *dy_pieces] + list(kv_pieces) * 2 + ([] if first else [init])
    in_specs = [pl.BlockSpec(memory_space=pl.ANY)] * 6
    in_specs += [pl.BlockSpec((2 * BLK, hd), lambda i, s: (0, s[24]))] * 4
    in_specs += [pl.BlockSpec((2 * BLK, hd), lambda i, s: (0, 2 + s[24]))] * 4
    if not first:
        in_specs.append(full(init.shape))
    return pl.pallas_call(
        functools.partial(attn_kernel, heads, scale, first, final),
        out_shape=(
            jax.ShapeDtypeStruct((width, rows), BF16),
            jax.ShapeDtypeStruct((rows, width), BF16),
            jax.ShapeDtypeStruct((seq, 256), BF16 if final else F32),
        ),
        grid_spec=pltpu.PrefetchScalarGridSpec(
            num_scalar_prefetch=1,
            grid=(rows // BLK,),
            in_specs=in_specs,
            out_specs=(o_spec, out_spec, full((seq, 256))),
            scratch_shapes=[
                *[pltpu.VMEM((seq, hd), BF16) for _ in "kv"],
                *[pltpu.VMEM((hd, seq), BF16) for _ in "kv"],
                *[pltpu.VMEM((seq, hd), F32) for _ in "kv"],
                *[pltpu.VMEM((hd, wide), BF16) for _ in "qd"],
                *[pltpu.VMEM((wide, hd), BF16) for _ in "qd"],
                pltpu.VMEM((seq, wide), F32),
                pltpu.VMEM((seq, wide), BF16),
                pltpu.VMEM((BLK, wide), BF16),
                *[pltpu.VMEM((hd, wide), F32) for _ in "od"],
                *[pltpu.VMEM((8, wide), F32) for _ in "ml"],
                pltpu.VMEM((model, width), BF16),
                pltpu.VMEM((width, model), BF16),
                *[pltpu.VMEM((2, BLK, model), BF16) for _ in "xd"],
                *[pltpu.SemaphoreType.DMA((2,)) for _ in "wxd"],
            ],
        ),
        compiler_params=params(1, 63),
        cost_estimate=cost(8e9 * (rows // BLK), 20e6),
    )(sc, *ins)


def y_kernel(sc, o_mine, o_other, w_mine, w_other, out_ref, os):
    half = o_mine.shape[0]

    @pl.when(pl.program_id(0) == 0)
    def _():
        os[:, :half] = o_mine[...].T
        os[:, half:] = o_other[...].T

    out_ref[...] = (dot(os[:, :half], w_mine[...]) + dot(os[:, half:], w_other[...])).astype(BF16)


def out_rows(core, o_mine, o_other, wo):
    rows, half, model, tile = 512, o_mine.shape[0], wo.shape[1], 512
    return pl.pallas_call(
        y_kernel,
        out_shape=jax.ShapeDtypeStruct((rows, model), BF16),
        grid_spec=pltpu.PrefetchScalarGridSpec(
            num_scalar_prefetch=1,
            grid=(model // tile,),
            in_specs=[
                pl.BlockSpec((half, rows), lambda i, s: (0, s[0])),
                pl.BlockSpec((half, rows), lambda i, s: (0, s[0])),
                pl.BlockSpec((half, tile), lambda i, s: (s[0], i)),
                pl.BlockSpec((half, tile), lambda i, s: (1 - s[0], i)),
            ],
            out_specs=pl.BlockSpec((rows, tile), lambda i, s: (0, i)),
            scratch_shapes=[pltpu.VMEM((rows, 2 * half), BF16)],
        ),
        compiler_params=params(),
        cost_estimate=cost(4 * rows * half * model, 12e6),
    )(core, o_mine, o_other, wo, wo)


def dx_kernel(sc, q_mine, q_other, kv_mine, kv_other, wq_mine, wq_other, wk_mine, wk_other, wv_mine, wv_other, out_ref):
    kv = jnp.concatenate([kv_mine[...], kv_other[...]], axis=1)
    w = jnp.concatenate([wk_mine[...], wv_mine[...], wk_other[...], wv_other[...]], axis=1)
    acc = dot_nt(q_mine[...], wq_mine[...]) + dot_nt(q_other[...], wq_other[...])
    out_ref[...] = (acc + dot_nt(kv, w)).astype(BF16)


def grad_rows(core, dq_mine, dq_other, dkv_mine, dkv_other, wq, wk, wv):
    rows, half, model, tile = 512, dq_mine.shape[1], wq.shape[0], 512
    hd = 128
    mine = lambda i, s: (s[0], 0)
    near, far = lambda i, s: (i, s[0]), lambda i, s: (i, 1 - s[0])
    return pl.pallas_call(
        dx_kernel,
        out_shape=jax.ShapeDtypeStruct((rows, model), BF16),
        grid_spec=pltpu.PrefetchScalarGridSpec(
            num_scalar_prefetch=1,
            grid=(model // tile,),
            in_specs=[
                *[pl.BlockSpec((rows, n), mine) for n in (half, half, 2 * hd, 2 * hd)],
                *[pl.BlockSpec((tile, n), at) for n in (half, hd, hd) for at in (near, far)],
            ],
            out_specs=pl.BlockSpec((rows, tile), lambda i, s: (0, i)),
        ),
        compiler_params=params(),
        cost_estimate=cost(4 * rows * half * model * 1.25, 14e6),
    )(core, dq_mine, dq_other, dkv_mine, dkv_other, wq, wq, wk, wk, wv, wv)


PIECES = ((0, 512), (1, 512), (0, 256), (1, 256), (0, 256), (1, 256))
STARTS = (0, 512, 1024, 1280, 1536, 1792)


def dwq_kernel(sc, *refs):
    xs_in, mine, other, kvm, kvo = refs[:6], refs[6:12], refs[12:18], refs[18:24], refs[24:30]
    out_ref, gk_ref, gv_ref, xt = refs[30:34]
    g, i = pl.program_id(0), pl.program_id(1)
    tile = out_ref.shape[0]

    def part(rhs):
        return sum(dot(xt[i, :, s : s + n], r[...]) for s, (_, n), r in zip(STARTS, PIECES, rhs))

    def store(rhs):
        acc = part(rhs)
        flat = out_ref.reshape(tile * 8, 128)
        for h in range(8):
            flat[pl.ds(h, tile, stride=8), :] = acc[:, h * 128 : (h + 1) * 128]

    @pl.when(g == 0)
    def _():
        for s, (_, n), x in zip(STARTS, PIECES, xs_in):
            xt[i, :, s : s + n] = x[...].T
        store(mine)

    @pl.when(g == 1)
    def _():
        store(other)
        core = sc[0]
        k_flat, v_flat = gk_ref.reshape(tile * 2, 128), gv_ref.reshape(tile * 2, 128)
        for src, head in ((kvm, core), (kvo, 1 - core)):
            acc = part(src)
            k_flat[pl.ds(head, tile, stride=2), :] = acc[:, :128]
            v_flat[pl.ds(head, tile, stride=2), :] = acc[:, 128:]


def grad_wq(core, xs, mine, other, kvm, kvo):
    model, half, tile = xs[0].shape[1], mine[0].shape[1], 256
    tiles = model // tile
    x_specs = [pl.BlockSpec((n, tile), lambda g, i, s: (0, jnp.where(g == 0, i, tiles - 1))) for _, n in PIECES]
    q_specs = [pl.BlockSpec((n, half), lambda g, i, s, f=f: (1 - s[0] if f else s[0], 0)) for f, n in PIECES]
    kv_specs = [
        pl.BlockSpec((n, 256), lambda g, i, s, f=f, at=at: (at + (1 - s[0] if f else s[0]), 0))
        for (f, n), at in zip(PIECES, (0, 0, 4, 4, 6, 6))
    ]
    ex = lambda t: [t[0], t[0], t[1], t[1], t[2], t[2]]
    small = pl.BlockSpec((tile, 2, 128), lambda g, i, s: (i * g, 0, 0))
    return pl.pallas_call(
        dwq_kernel,
        out_shape=(
            jax.ShapeDtypeStruct((model, 16, 128), F32),
            jax.ShapeDtypeStruct((model, 2, 128), F32),
            jax.ShapeDtypeStruct((model, 2, 128), F32),
        ),
        grid_spec=pltpu.PrefetchScalarGridSpec(
            num_scalar_prefetch=1,
            grid=(2, tiles),
            in_specs=x_specs + q_specs + q_specs + kv_specs + kv_specs,
            out_specs=(
                pl.BlockSpec((tile, 8, 128), lambda g, i, s: (i, (s[0] + g) % 2, 0)),
                small,
                small,
            ),
            scratch_shapes=[pltpu.VMEM((tiles, tile, 2048), BF16)],
        ),
        compiler_params=params(2),
        cost_estimate=cost(2 * 2048 * model * (2 * half + 512), 40e6),
    )(core, *xs, *ex(mine), *ex(other), *([kvm] * 6), *([kvo] * 6))


def dwo_kernel(sc, *refs):
    mine, other, ys, out_ref = refs[:6], refs[6:12], refs[12:18], refs[18]

    def store(lhs):
        out_ref[...] = sum(dot(o[...], y[...]) for o, y in zip(lhs, ys))

    @pl.when(pl.program_id(1) == 0)
    def _():
        store(mine)

    @pl.when(pl.program_id(1) == 1)
    def _():
        store(other)


def grad_wo(core, ys, mine, other):
    model, half, tile, wide = ys[0].shape[1], mine[0].shape[0], 512, 1024
    steps = half // tile
    specs = []
    for rest in (0, 1):
        specs += [
            pl.BlockSpec(
                (tile, n),
                lambda j, g, i, s, f=f, rest=rest: (
                    jnp.where(g == rest, i, 0 if rest else steps - 1),
                    1 - s[0] if f else s[0],
                ),
            )
            for f, n in PIECES
        ]
    specs += [pl.BlockSpec((n, wide), lambda j, g, i, s: (0, j)) for _, n in PIECES]
    ex = lambda t: [t[0], t[0], t[1], t[1], t[2], t[2]]
    return pl.pallas_call(
        dwo_kernel,
        out_shape=jax.ShapeDtypeStruct((2 * half, model), F32),
        grid_spec=pltpu.PrefetchScalarGridSpec(
            num_scalar_prefetch=1,
            grid=(model // wide, 2, steps),
            in_specs=specs,
            out_specs=pl.BlockSpec((tile, wide), lambda j, g, i, s: ((s[0] + g) % 2 * steps + i, j)),
        ),
        compiler_params=params(3),
        cost_estimate=cost(4 * 2048 * model * half, 40e6),
    )(core, *ex(mine), *ex(other), *ys)


def solution(mesh):
    row_spec = P(("dp", "cp"), None)
    rep_spec = P(None, None, None)
    part_spec = P("dp", None, None)
    core_swap = [(0, 1), (1, 0), (2, 3), (3, 2)]
    chip_swap = [(0, 2), (2, 0), (1, 3), (3, 1)]

    def device_layer(x, dy, w_query, w_key, w_value, w_out):
        rows, model = x.shape
        num_heads, hd = w_query.shape[1:]
        kv_heads = w_key.shape[1]
        scale = hd ** -0.5
        rank = lax.axis_index("cp").astype(jnp.int32)
        c = rank & 1
        core = c.reshape(1)
        devs = [rank, rank ^ 1, rank ^ 2, rank ^ 3]
        kv_pos = [p for e in devs for p in (e, 7 - e)]
        own_slots = [p for e in devs[:2] for p in ((e & 1) * 2, (e & 1) * 2 + 1)]
        far_slots = []
        for e in devs[2:]:
            far_slots += [jnp.where((e & 1) == 1, 4, 6) + (e & 1), jnp.where((e & 1) == 0, 4, 6) + (e & 1)]
        pos_a = [jnp.where((e & 1) == 0, 7 - e, e) for e in devs[2:]]
        pos_b = [jnp.where((e & 1) == 0, e, 7 - e) for e in devs[2:]]
        far = [c, 1 - c]
        tail = own_slots + far_slots + [c]
        sc_chip = jnp.stack(kv_pos + kv_pos[:4] + own_slots + tail)
        sc_a = jnp.stack(kv_pos + pos_a * 2 + far * 2 + tail)
        sc_b = jnp.stack(kv_pos + pos_b * 2 + far * 2 + tail)

        to_core = lambda v: lax.ppermute(v, "cp", core_swap)
        to_chip = lambda v: lax.ppermute(v, "cp", chip_swap)

        wk = w_key.reshape(model, kv_heads * hd)
        wv = w_value.reshape(model, kv_heads * hd)
        wo = w_out.reshape(num_heads * hd, model)
        x_p = to_core(x)
        dy_p = to_core(dy)

        kv, x_a, x_b, dy_a, dy_b = project_kv(core, x, dy, wk, wv)
        kv_r, kv_p = to_chip(kv), to_core(kv)
        w_s, _ = lax.optimization_barrier((w_query, kv))
        x_a, dy_a, x_b, dy_b = to_chip(x_a), to_chip(dy_a), to_chip(x_b), to_chip(dy_b)
        wq = flat_heads(w_s)
        kv_rp = to_core(kv_r)
        pieces = (kv, kv_p, kv_r, kv_rp)

        o_c, dq_c, part = attention(sc_chip, wq, wo, (x, x_p), (dy, dy_p), pieces, None, False, scale)
        x_a, dy_a, o_c, dq_c = lax.optimization_barrier((x_a, dy_a, o_c, dq_c))
        x_pa, dy_pa, o_co, dq_co = to_core(x_a), to_core(dy_a), to_core(o_c), to_core(dq_c)

        o_a, dq_a, part = attention(sc_a, wq, wo, (x_a, x_pa), (dy_a, dy_pa), pieces, part, False, scale)
        x_b, dy_b, o_a, dq_a = lax.optimization_barrier((x_b, dy_b, o_a, dq_a))
        x_pb, dy_pb, o_ao, dq_ao = to_core(x_b), to_core(dy_b), to_core(o_a), to_core(dq_a)

        o_b, dq_b, dkv = attention(sc_b, wq, wo, (x_b, x_pb), (dy_b, dy_pb), pieces, part, True, scale)
        o_co, dkv = lax.optimization_barrier((o_co, dkv))
        dkv_o, o_bo, dq_bo = to_core(dkv), to_core(o_b), to_core(dq_b)
        y = out_rows(core, o_c, o_co, wo)

        xs = (x, x_p, x_a, x_pa, x_b, x_pb)
        ys = (dy, dy_p, dy_a, dy_pa, dy_b, dy_pb)
        gwo = grad_wo(core, ys, (o_c, o_a, o_b), (o_co, o_ao, o_bo))
        dx = grad_rows(core, dq_c, dq_co, dkv, dkv_o, wq, wk, wv)
        gwq, gwk, gwv = grad_wq(core, xs, (dq_c, dq_a, dq_b), (dq_co, dq_ao, dq_bo), dkv, dkv_o)
        return y, dx, gwq, gwk, gwv, gwo.reshape(num_heads, hd, model)

    return jax.shard_map(
        device_layer,
        mesh=mesh,
        in_specs=(row_spec, row_spec, rep_spec, rep_spec, rep_spec, rep_spec),
        out_specs=(row_spec, row_spec, part_spec, part_spec, part_spec, part_spec),
        check_vma=False,
    )
```

time: 285 us -> 276 us (0.968)
  Pallas kernels: 257 us -> 233 us
  waiting for transfers between devices: 0.98 us -> 21.5 us
  local copies, waits for them, and re-layouts: 13.3 us -> 7.85 us
    pallas_call x7 -> x1, Pallas kernels: 52.2 us -> 6 us  [project_kv(): pl.pallas_call(kv_kernel, out_shape=(jax.ShapeDtypeStruct((rows, 512), BF...]
    pallas_call x3, Pallas kernels: 107 us -> 133 us  [attention(): pl.pallas_call(functools.partial(attn_kernel, heads, scale, first, final)...]
    ppermute x5, waiting for transfers between devices: 0.01 us -> 18.1 us  [device_layer(): to_chip = lambda v: lax.ppermute(v, 'cp', chip_swap)]
    dynamic_slice x2 -> x0, local copies, waits for them, and re-layouts: 4.31 us -> none  [device_layer(): cut = lambda v, at: lax.dynamic_slice(v, (at * BLK, 0), (BLK, model))]
  transfers between devices with their start and end apart: 20 -> 20, of which waited for: 1 -> 5; matrix products, arithmetic and copies ran while one was open for 3% -> 2% of each run, Pallas kernels for 82% -> 75%
where the time goes in v3:
time: 276 us; the launch traced here: 275 us
  Pallas kernels  233 us (84%)
  waiting for transfers between devices  21.5 us (8%)
  starting transfers between devices  10.6 us (4%)
  local copies, waits for them, and re-layouts  7.85 us (3%)
    pallas_call x3, Pallas kernels, attention(): pl.pallas_call(functools.partial(attn_kernel, heads, scale, first, final)...  133 us
    pallas_call x1, Pallas kernels, grad_wq(): pl.pallas_call(dwq_kernel, out_shape=(jax.ShapeDtypeStruct((model, 16, 12...  35.9 us
    pallas_call x1, Pallas kernels, grad_wo(): pl.pallas_call(dwo_kernel, out_shape=jax.ShapeDtypeStruct((2 * half, mode...  27.7 us
    ppermute x5, waiting for transfers between devices, device_layer(): to_chip = lambda v: lax.ppermute(v, 'cp', chip_swap)  18.1 us
    pallas_call x1, Pallas kernels, flat_heads(): pl.pallas_call(heads_kernel, out_shape=jax.ShapeDtypeStruct((model, num *...  10.4 us
    pallas_call x1, Pallas kernels, grad_rows(): pl.pallas_call(dx_kernel, out_shape=jax.ShapeDtypeStruct((rows, model), B...  10.3 us
    pallas_call x1, Pallas kernels, out_rows(): pl.pallas_call(y_kernel, out_shape=jax.ShapeDtypeStruct((rows, model), BF...  9.31 us
    ppermute x5, starting transfers between devices, device_layer(): to_chip = lambda v: lax.ppermute(v, 'cp', chip_swap)  7.09 us
  transfers between devices with their start and end apart: 20, of which 5 were waited for; matrix products, arithmetic and copies ran while one was open for 2% of the time, Pallas kernels for 75%

profile of v3, /device:TPU:0, one launch (start us, length us, event | category | flops | bytes accessed | tf_op | source)
XLA Modules:
  0.0 275.0 jit_solution(9407532317467078800)
XLA Ops:
  0.6 0.9 collective-permute-start.2
  1.5 0.0 collective-permute-start.3
  1.5 3.2 %copy_bitcast_fusion = (bf16[2048,256]{1,0:T(8,128)(2,1)}, bf16[2048,256]{1,0:T(8,128)(2,1)}) fusion(bf16[256,8,2,128]{3,2,1,0:T(2,128)(2,1)} %bitcast.35, bf16[256,8,2,128]{3,2,1,0:T(2,128)(2,1)} %bitcast.36), kind=kLoop, calls=%fused_computation | loop fusion | bytes 4194304 | tf_op jit(solution)/shard_map/reshape | solution.py:525
  4.7 6.0 %shard_map.109 = (bf16[512,512]{1,0:T(8,128)(2,1)}, bf16[256,2048]{1,0:T(8,128)(2,1)}, bf16[256,2048]{1,0:T(8,128)(2,1)}, bf16[256,2048]{1,0:T(8,128)(2,1)}, bf16[256,2048]{1,0:T(8,128)(2,1)}) custom-call(s32[1]{0:T(128)} %bitcast.sc, bf16[512,2048]{1,0:T(8,128)(2,1)} %refs_0_.3, bf16[512,2048]{1,0:T(8,128)(2,1)} %refs_12_.1, ...), custom_call_target="tpu_custom_call" | custom-call | flops 1073741824 | bytes 8000000 | tf_op jit(solution)/shard_map/pallas_call | solution.py:88
  10.7 3.0 %collective-permute-start.5 = (bf16[512,512]{1,0:T(8,128)(2,1)}, bf16[512,512]{1,0:T(8,128)(2,1)S(1)}, u32[]{:S(2)}, u32[]{:S(2)}) collective-permute-start(bf16[512,512]{1,0:T(8,128)(2,1)} %get-tuple-element.36.refs_4_.refs_8_), channel_id=1, source_target_pairs={{0,2},{2,0},{1,3},{3,1},{4,6},{6,4},{5,7},{7,5}} | collective-permute-start | bytes 1572872 | tf_op jit(solution)/shard_map/ppermute | solution.py:522
  13.7 0.0 collective-permute-start.4
  13.7 0.1 collective-permute-start
  13.8 0.7 stack.64.sc
  14.4 12.0 %collective-permute-done.5.refs_6_.refs_10_ = bf16[512,512]{1,0:T(8,128)(2,1)S(1)} collective-permute-done((bf16[512,512]{1,0:T(8,128)(2,1)}, bf16[512,512]{1,0:T(8,128)(2,1)S(1)}, u32[]{:S(2)}, u32[]{:S(2)}) %collective-permute-start.5) | collective-permute-done | bytes 524320 | tf_op jit(solution)/shard_map/ppermute | solution.py:522
  26.5 0.0 collective-permute-start.6
  26.5 0.8 fusion.perm_ref
  27.3 10.4 %shard_map.110.wq_hbm.wq_mine.wq_other = bf16[2048,2048]{1,0:T(8,128)(2,1)} custom-call(bf16[2048,16,128]{2,1,0:T(8,128)(2,1)} %w_ref, bf16[256,256]{1,0:T(8,128)(2,1)} %fusion.perm_ref), custom_call_target="tpu_custom_call" | custom-call | flops 4000000000 | bytes 16777216 | tf_op jit(solution)/shard_map/pallas_call | solution.py:54
  37.7 0.0 copy-done.3
  37.7 0.0 collective-permute-done.4.refs_5_.refs_9_
  37.7 0.0 copy-start.4
  37.7 2.0 collective-permute-start.1
  39.8 0.0 collective-permute-done.6.refs_7_.refs_11_
  39.8 0.0 copy-done.4
  39.8 0.0 copy-start.5
  39.8 0.0 collective-permute-done.2.refs_1_
  39.8 0.8 copy-done.5
  40.6 0.0 collective-permute-done.3.refs_3_.refs_13_
  40.6 62.5 %shard_map.111 = (bf16[1024,1024]{1,0:T(8,128)(2,1)}, bf16[1024,1024]{1,0:T(8,128)(2,1)}, f32[2048,256]{1,0:T(8,128)}) custom-call(s32[25]{0:T(128)} %stack.64.sc, bf16[2048,2048]{1,0:T(8,128)(2,1)} %shard_map.110.wq_hbm.wq_mine.wq_other, bf16[2048,2048]{1,0:T(8,128)(2,1)} %bitcast.30, bf16[512,2048]{1,0:T(8,128)(2,1)} %refs_0_.3, ...), custom_call_target="tpu_custom_call" | custom-call | flops 32000000000 | bytes 20000000 | tf_op jit(solution)/shard_map/pallas_call | solution.py:280
  103.1 0.0 collective-permute-done.refs_0_.refs_2_
  103.1 0.0 collective-permute-done.1.refs_2_.refs_14_
  103.1 0.1 collective-permute-start.10
  103.2 0.4 collective-permute-start.11
  103.6 0.8 collective-permute-start.8
  104.4 1.2 collective-permute-start.9
  105.7 0.7 stack.71.sc
  106.3 0.0 collective-permute-done.10.refs_1_.refs_3_
  106.3 0.9 collective-permute-done.11.refs_3_.refs_15_
  107.2 37.9 %shard_map.112 = (bf16[1024,512]{1,0:T(8,128)(2,1)}, bf16[512,1024]{1,0:T(8,128)(2,1)}, f32[2048,256]{1,0:T(8,128)}) custom-call(s32[25]{0:T(128)} %stack.71.sc, bf16[2048,2048]{1,0:T(8,128)(2,1)} %shard_map.110.wq_hbm.wq_mine.wq_other, bf16[2048,2048]{1,0:T(8,128)(2,1)} %bitcast.31, bf16[256,2048]{1,0:T(8,128)(2,1)} %collective-permute-done.refs_0_.refs_2_, ...), custom_call_target="tpu_custom_call" | custom-call | flops 16000000000 | bytes 20000000 | tf_op jit(solution)/shard_map/pallas_call | solution.py:280
  145.2 0.0 collective-permute-done.8.refs_0_.refs_4_
  145.2 6.1 %collective-permute-done.9.refs_2_.refs_16_ = bf16[256,2048]{1,0:T(8,128)(2,1)} collective-permute-done((bf16[256,2048]{1,0:T(8,128)(2,1)}, bf16[256,2048]{1,0:T(8,128)(2,1)}, u32[]{:S(2)}, u32[]{:S(2)}) %collective-permute-start.9) | collective-permute-done | bytes 1048608 | tf_op jit(solution)/shard_map/ppermute | solution.py:522
  151.3 0.0 collective-permute-start.12
  151.3 0.5 collective-permute-start.13
  151.8 0.0 collective-permute-start.7
  151.8 0.6 stack.68.sc
  152.4 0.5 collective-permute-start.14
  152.9 0.0 collective-permute-start.16
  152.9 1.0 collective-permute-done.12.refs_1_.refs_5_
  153.9 1.5 collective-permute-done.13.refs_3_.refs_17_
  155.4 33.0 %shard_map.113 = (bf16[1024,512]{1,0:T(8,128)(2,1)}, bf16[512,1024]{1,0:T(8,128)(2,1)}, bf16[2048,256]{1,0:T(8,128)(2,1)}) custom-call(s32[25]{0:T(128)} %stack.68.sc, bf16[2048,2048]{1,0:T(8,128)(2,1)} %shard_map.110.wq_hbm.wq_mine.wq_other, bf16[2048,2048]{1,0:T(8,128)(2,1)} %bitcast.32, bf16[256,2048]{1,0:T(8,128)(2,1)} %collective-permute-done.8.refs_0_.refs_4_, ...), custom_call_target="tpu_custom_call" | custom-call | flops 16000000000 | bytes 20000000 | tf_op jit(solution)/shard_map/pallas_call | solution.py:280
  188.4 0.0 collective-permute-done.7.o_other.refs_6_.refs_7_
  188.4 0.2 collective-permute-start.15
  188.7 0.3 collective-permute-start.17
  189.0 0.2 collective-permute-start.18
  189.2 9.3 %shard_map.114 = bf16[512,2048]{1,0:T(8,128)(2,1)} custom-call(s32[1]{0:T(128)} %bitcast.sc, bf16[1024,1024]{1,0:T(8,128)(2,1)} %get-tuple-element.40.o_mine.refs_0_.refs_1_, bf16[1024,1024]{1,0:T(8,128)(2,1)} %collective-permute-done.7.o_other.refs_6_.refs_7_, bf16[2048,2048]{1,0:T(8,128)(2,1)} %bitcast.33, bf16[2048,2048]{1,0:T(8,128)(2,1)} %bitcast.34), custom_call_target="tpu_custom_call" | custom-call | flops 4294967296 | bytes 12000000 | tf_op jit(solution)/shard_map/pallas_call | solution.py:327
  198.5 0.0 collective-permute-done.14.q_other.refs_12_.refs_13_
  198.5 0.0 copy-done.1
  198.5 0.3 collective-permute-start.19
  198.8 0.0 collective-permute-done.16.refs_14_.refs_15_
  198.8 0.0 collective-permute-done.15.kv_other.refs_24_.refs_25_.refs_26_.refs_27_.refs_28_.refs_29_
  198.8 0.0 copy-start
  198.8 0.0 collective-permute-done.17.refs_16_.refs_17_
  198.8 1.0 copy-done
  199.8 35.9 %shard_map.116 = (f32[2048,16,128]{2,1,0:T(8,128)}, f32[2048,2,128]{2,1,0:T(2,128)}, f32[2048,2,128]{2,1,0:T(2,128)}) custom-call(s32[1]{0:T(128)} %bitcast.sc, bf16[512,2048]{1,0:T(8,128)(2,1)} %refs_0_.3, bf16[512,2048]{1,0:T(8,128)(2,1)} %collective-permute-done.2.refs_1_, bf16[256,2048]{1,0:T(8,128)(2,1)} %collective-permute-done.refs_0_.refs_2_, ...), custom_call_target="tpu_custom_call" | custom-call | flops 21474836480 | bytes 40000000 | tf_op jit(solution)/shard_map/pallas_call | solution.py:423
  235.7 10.3 %shard_map.115 = bf16[512,2048]{1,0:T(8,128)(2,1)} custom-call(s32[1]{0:T(128)} %bitcast.sc, bf16[1024,1024]{1,0:T(8,128)(2,1)} %get-tuple-element.53.q_mine.refs_6_.refs_7_, bf16[1024,1024]{1,0:T(8,128)(2,1)} %collective-permute-done.14.q_other.refs_12_.refs_13_, ...), custom_call_target="tpu_custom_call" | custom-call | flops 5368709120 | bytes 14000000 | tf_op jit(solution)/shard_map/pallas_call | solution.py:359
  246.0 0.0 collective-permute-done.18.refs_8_.refs_9_
  246.0 0.0 copy-start.2
  246.0 0.0 collective-permute-done.19.refs_10_.refs_11_
  246.1 1.0 copy-done.2
  247.0 27.7 %shard_map.117 = f32[2048,2048]{1,0:T(8,128)} custom-call(s32[1]{0:T(128)} %bitcast.sc, bf16[1024,1024]{1,0:T(8,128)(2,1)} %get-tuple-element.40.o_mine.refs_0_.refs_1_, bf16[1024,1024]{1,0:T(8,128)(2,1)} %get-tuple-element.40.o_mine.refs_0_.refs_1_, bf16[1024,512]{1,0:T(8,128)(2,1)} %get-tuple-element.60.refs_2_.refs_3_, ...), custom_call_target="tpu_custom_call" | custom-call | flops 17179869184 | bytes 40000000 | tf_op jit(solution)/shard_map/pallas_call | solution.py:478
  (3 shorter events, 0.0 us)
Async XLA Ops:
  0.6 39.2 %collective-permute-start.2 = (bf16[512,2048]{1,0:T(8,128)(2,1)}, bf16[512,2048]{1,0:T(8,128)(2,1)}, u32[]{:S(2)}, u32[]{:S(2)}) collective-permute-start(bf16[512,2048]{1,0:T(8,128)(2,1)} %refs_0_.3), channel_id=1, source_target_pairs={{0,1},{1,0},{2,3},{3,2},{4,5},{5,4},{6,7},{7,6}} | collective-permute-start | bytes 6291464 | tf_op jit(solution)/shard_map/ppermute | solution.py:521
  1.5 39.1 %collective-permute-start.3 = (bf16[512,2048]{1,0:T(8,128)(2,1)}, bf16[512,2048]{1,0:T(8,128)(2,1)}, u32[]{:S(2)}, u32[]{:S(2)}) collective-permute-start(bf16[512,2048]{1,0:T(8,128)(2,1)} %refs_12_.1), channel_id=1, source_target_pairs={{0,1},{1,0},{2,3},{3,2},{4,5},{5,4},{6,7},{7,6}} | collective-permute-start | bytes 6291464 | tf_op jit(solution)/shard_map/ppermute | solution.py:521
  10.7 15.7 %collective-permute-start.5 = (bf16[512,512]{1,0:T(8,128)(2,1)}, bf16[512,512]{1,0:T(8,128)(2,1)S(1)}, u32[]{:S(2)}, u32[]{:S(2)}) collective-permute-start(bf16[512,512]{1,0:T(8,128)(2,1)} %get-tuple-element.36.refs_4_.refs_8_), channel_id=1, source_target_pairs={{0,2},{2,0},{1,3},{3,1},{4,6},{6,4},{5,7},{7,5}} | collective-permute-start | bytes 1572872 | tf_op jit(solution)/shard_map/ppermute | solution.py:522
  13.7 24.0 %collective-permute-start.4 = (bf16[512,512]{1,0:T(8,128)(2,1)}, bf16[512,512]{1,0:T(8,128)(2,1)S(1)}, u32[]{:S(2)}, u32[]{:S(2)}) collective-permute-start(bf16[512,512]{1,0:T(8,128)(2,1)} %get-tuple-element.36.refs_4_.refs_8_), channel_id=1, source_target_pairs={{0,1},{1,0},{2,3},{3,2},{4,5},{5,4},{6,7},{7,6}} | collective-permute-start | bytes 1572872 | tf_op jit(solution)/shard_map/ppermute | solution.py:521
  13.7 89.4 %collective-permute-start = (bf16[256,2048]{1,0:T(8,128)(2,1)}, bf16[256,2048]{1,0:T(8,128)(2,1)}, u32[]{:S(2)}, u32[]{:S(2)}) collective-permute-start(bf16[256,2048]{1,0:T(8,128)(2,1)} %get-tuple-element.34), channel_id=1, source_target_pairs={{0,2},{2,0},{1,3},{3,1},{4,6},{6,4},{5,7},{7,5}} | collective-permute-start | bytes 3145736 | tf_op jit(solution)/shard_map/ppermute | solution.py:522
  26.5 11.3 %copy-start.3 = (bf16[512,512]{1,0:T(8,128)(2,1)}, bf16[512,512]{1,0:T(8,128)(2,1)S(1)}, u32[]{:S(2)}) copy-start(bf16[512,512]{1,0:T(8,128)(2,1)S(1)} %collective-permute-done.5.refs_6_.refs_10_) | copy-start | bytes 1572868
  26.5 13.3 %collective-permute-start.6 = (bf16[512,512]{1,0:T(8,128)(2,1)S(1)}, bf16[512,512]{1,0:T(8,128)(2,1)S(1)}, u32[]{:S(2)}, u32[]{:S(2)}) collective-permute-start(bf16[512,512]{1,0:T(8,128)(2,1)S(1)} %collective-permute-done.5.refs_6_.refs_10_), channel_id=1, source_target_pairs={{0,1},{1,0},{2,3},{3,2},{4,5},{5,4},{6,7},{7,6}} | collective-permute-start | bytes 1572872 | tf_op jit(solution)/shard_map/ppermute | solution.py:521
  37.7 2.1 copy-start.4
  37.7 65.4 %collective-permute-start.1 = (bf16[256,2048]{1,0:T(8,128)(2,1)}, bf16[256,2048]{1,0:T(8,128)(2,1)}, u32[]{:S(2)}, u32[]{:S(2)}) collective-permute-start(bf16[256,2048]{1,0:T(8,128)(2,1)} %get-tuple-element.35), channel_id=1, source_target_pairs={{0,2},{2,0},{1,3},{3,1},{4,6},{6,4},{5,7},{7,5}} | collective-permute-start | bytes 3145736 | tf_op jit(solution)/shard_map/ppermute | solution.py:522
  39.8 0.8 copy-start.5
  103.1 3.2 %collective-permute-start.10 = (bf16[256,2048]{1,0:T(8,128)(2,1)}, bf16[256,2048]{1,0:T(8,128)(2,1)}, u32[]{:S(2)}, u32[]{:S(2)}) collective-permute-start(bf16[256,2048]{1,0:T(8,128)(2,1)} %collective-permute-done.refs_0_.refs_2_), channel_id=1, source_target_pairs={{0,1},{1,0},{2,3},{3,2},{4,5},{5,4},{6,7},{7,6}} | collective-permute-start | bytes 3145736 | tf_op jit(solution)/shard_map/ppermute | solution.py:521
  103.2 4.0 %collective-permute-start.11 = (bf16[256,2048]{1,0:T(8,128)(2,1)}, bf16[256,2048]{1,0:T(8,128)(2,1)}, u32[]{:S(2)}, u32[]{:S(2)}) collective-permute-start(bf16[256,2048]{1,0:T(8,128)(2,1)} %collective-permute-done.1.refs_2_.refs_14_), channel_id=1, source_target_pairs={{0,1},{1,0},{2,3},{3,2},{4,5},{5,4},{6,7},{7,6}} | collective-permute-start | bytes 3145736 | tf_op jit(solution)/shard_map/ppermute | solution.py:521
  103.6 41.6 %collective-permute-start.8 = (bf16[256,2048]{1,0:T(8,128)(2,1)}, bf16[256,2048]{1,0:T(8,128)(2,1)}, u32[]{:S(2)}, u32[]{:S(2)}) collective-permute-start(bf16[256,2048]{1,0:T(8,128)(2,1)} %get-tuple-element.41), channel_id=1, source_target_pairs={{0,2},{2,0},{1,3},{3,1},{4,6},{6,4},{5,7},{7,5}} | collective-permute-start | bytes 3145736 | tf_op jit(solution)/shard_map/ppermute | solution.py:522
  104.4 46.8 %collective-permute-start.9 = (bf16[256,2048]{1,0:T(8,128)(2,1)}, bf16[256,2048]{1,0:T(8,128)(2,1)}, u32[]{:S(2)}, u32[]{:S(2)}) collective-permute-start(bf16[256,2048]{1,0:T(8,128)(2,1)} %get-tuple-element.42), channel_id=1, source_target_pairs={{0,2},{2,0},{1,3},{3,1},{4,6},{6,4},{5,7},{7,5}} | collective-permute-start | bytes 3145736 | tf_op jit(solution)/shard_map/ppermute | solution.py:522
  151.3 2.6 collective-permute-start.12
  151.3 4.1 %collective-permute-start.13 = (bf16[256,2048]{1,0:T(8,128)(2,1)}, bf16[256,2048]{1,0:T(8,128)(2,1)}, u32[]{:S(2)}, u32[]{:S(2)}) collective-permute-start(bf16[256,2048]{1,0:T(8,128)(2,1)} %collective-permute-done.9.refs_2_.refs_16_), channel_id=1, source_target_pairs={{0,1},{1,0},{2,3},{3,2},{4,5},{5,4},{6,7},{7,6}} | collective-permute-start | bytes 3145736 | tf_op jit(solution)/shard_map/ppermute | solution.py:521
  151.8 36.6 %collective-permute-start.7 = (bf16[1024,1024]{1,0:T(8,128)(2,1)}, bf16[1024,1024]{1,0:T(8,128)(2,1)}, u32[]{:S(2)}, u32[]{:S(2)}) collective-permute-start(bf16[1024,1024]{1,0:T(8,128)(2,1)} %get-tuple-element.40.o_mine.refs_0_.refs_1_), channel_id=1, source_target_pairs={{0,1},{1,0},{2,3},{3,2},{4,5},{5,4},{6,7},{7,6}} | collective-permute-start | bytes 6291464 | tf_op jit(solution)/shard_map/ppermute | solution.py:521
  152.4 46.1 %collective-permute-start.14 = (bf16[1024,1024]{1,0:T(8,128)(2,1)}, bf16[1024,1024]{1,0:T(8,128)(2,1)}, u32[]{:S(2)}, u32[]{:S(2)}) collective-permute-start(bf16[1024,1024]{1,0:T(8,128)(2,1)} %get-tuple-element.53.q_mine.refs_6_.refs_7_), channel_id=1, source_target_pairs={{0,1},{1,0},{2,3},{3,2},{4,5},{5,4},{6,7},{7,6}} | collective-permute-start | bytes 6291464 | tf_op jit(solution)/shard_map/ppermute | solution.py:521
  152.9 45.9 %collective-permute-start.16 = (bf16[512,1024]{1,0:T(8,128)(2,1)}, bf16[512,1024]{1,0:T(8,128)(2,1)}, u32[]{:S(2)}, u32[]{:S(2)}) collective-permute-start(bf16[512,1024]{1,0:T(8,128)(2,1)} %get-tuple-element.55.refs_8_.refs_9_), channel_id=1, source_target_pairs={{0,1},{1,0},{2,3},{3,2},{4,5},{5,4},{6,7},{7,6}} | collective-permute-start | bytes 3145736 | tf_op jit(solution)/shard_map/ppermute | solution.py:521
  188.4 10.4 %collective-permute-start.15 = (bf16[2048,256]{1,0:T(8,128)(2,1)}, bf16[2048,256]{1,0:T(8,128)(2,1)S(1)}, u32[]{:S(2)}, u32[]{:S(2)}) collective-permute-start(bf16[2048,256]{1,0:T(8,128)(2,1)} %get-tuple-element.54.kv_mine.refs_18_.refs_19_.refs_20_.refs_21_.refs_22_.refs_23_), channel_id=1, source_target_pairs={{0,1},{1,0},{2,3},{3,2},{4,5},{5,4},{6,7},{7,6}} | collective-permute-start | bytes 3145736 | tf_op jit(solution)/shard_map/ppermute | solution.py:521
  188.7 9.8 %copy-start.1 = (bf16[1024,512]{1,0:T(8,128)(2,1)S(1)}, bf16[1024,512]{1,0:T(8,128)(2,1)}, u32[]{:S(2)}) copy-start(bf16[1024,512]{1,0:T(8,128)(2,1)} %get-tuple-element.61.refs_4_.refs_5_) | copy-start | bytes 3145732
  188.7 10.2 %collective-permute-start.17 = (bf16[512,1024]{1,0:T(8,128)(2,1)}, bf16[512,1024]{1,0:T(8,128)(2,1)}, u32[]{:S(2)}, u32[]{:S(2)}) collective-permute-start(bf16[512,1024]{1,0:T(8,128)(2,1)} %get-tuple-element.56.refs_10_.refs_11_), channel_id=1, source_target_pairs={{0,1},{1,0},{2,3},{3,2},{4,5},{5,4},{6,7},{7,6}} | collective-permute-start | bytes 3145736 | tf_op jit(solution)/shard_map/ppermute | solution.py:521
  189.0 57.1 %collective-permute-start.18 = (bf16[1024,512]{1,0:T(8,128)(2,1)}, bf16[1024,512]{1,0:T(8,128)(2,1)S(1)}, u32[]{:S(2)}, u32[]{:S(2)}) collective-permute-start(bf16[1024,512]{1,0:T(8,128)(2,1)} %get-tuple-element.60.refs_2_.refs_3_), channel_id=1, source_target_pairs={{0,1},{1,0},{2,3},{3,2},{4,5},{5,4},{6,7},{7,6}} | collective-permute-start | bytes 3145736 | tf_op jit(solution)/shard_map/ppermute | solution.py:521
  198.5 47.6 %collective-permute-start.19 = (bf16[1024,512]{1,0:T(8,128)(2,1)S(1)}, bf16[1024,512]{1,0:T(8,128)(2,1)}, u32[]{:S(2)}, u32[]{:S(2)}) collective-permute-start(bf16[1024,512]{1,0:T(8,128)(2,1)S(1)} %copy-done.1), channel_id=1, source_target_pairs={{0,1},{1,0},{2,3},{3,2},{4,5},{5,4},{6,7},{7,6}} | collective-permute-start | bytes 3145736 | tf_op jit(solution)/shard_map/ppermute | solution.py:521
  198.8 1.0 copy-start
  246.0 1.0 copy-start.2

commit v4 on v3

--- a/solution.py
+++ b/solution.py
@@ -8,7 +8,12 @@
 from jax.experimental.pallas import tpu as pltpu
 from jax.sharding import PartitionSpec as P
 
+
 BLK = 256
+HD = 128
+DUO = 512
+HALF = 1024
+SEQ = 2048
 LOW = -3.0e38
 F32 = jnp.float32
 BF16 = jnp.bfloat16
@@ -24,7 +29,7 @@
 
 def params(n=1, mib=60):
     return pltpu.CompilerParams(
-        dimension_semantics=("arbitrary",) * n, vmem_limit_bytes=mib * 1024 * 1024
+        dimension_semantics=("arbitrary",) * n, vmem_limit_bytes=mib * HALF * HALF
     )
 
 
@@ -32,42 +37,76 @@
     return pl.CostEstimate(flops=int(flops), bytes_accessed=int(nbytes), transcendentals=0)
 
 
-def heads_kernel(w_ref, perm_ref, out_ref):
-    rows, num, hd = w_ref.shape
-    flat = w_ref.reshape(rows * num, hd)
-    group = num * 16
-    for g in range(0, rows // 16, 2):
-        pair = [flat[(g + n) * group : (g + n + 1) * group, :] for n in range(2)]
-        res = dot(perm_ref[...], jnp.concatenate(pair, axis=1)).astype(BF16)
-        for n in range(2):
-            for h in range(num):
-                out_ref[(g + n) * 16 : (g + n + 1) * 16, h * hd : (h + 1) * hd] = res[
-                    h * 16 : (h + 1) * 16, n * hd : (n + 1) * hd
-                ]
+def heads_kernel(perm_ref, w_hbm, out_hbm, w_in, w_out, in_sem, out_sem):
+    chunks, rows, num, hd = w_in.shape
+    group = perm_ref.shape[0]
+    loads = [
+        pltpu.make_async_copy(w_hbm.at[c * rows : (c + 1) * rows], w_in.at[c], in_sem.at[c]) for c in range(chunks)
+    ]
+    stores = [
+        pltpu.make_async_copy(w_out.at[c], out_hbm.at[c * rows : (c + 1) * rows, :], out_sem.at[c]) for c in range(chunks)
+    ]
+    for cp in loads:
+        cp.start()
+
+    def chunk(c, _):
+        pltpu.make_async_copy(w_hbm.at[:rows], w_in.at[c], in_sem.at[c]).wait()
+        flat = w_in.at[c].reshape(rows * num, hd)
+        for g in range(0, rows // 16, 2):
+            pair = [flat[(g + n) * group : (g + n + 1) * group, :] for n in range(2)]
+            res = dot(perm_ref[...], jnp.concatenate(pair, axis=1)).astype(BF16)
+            for n in range(2):
+                for h in range(num):
+                    w_out[c, (g + n) * 16 : (g + n + 1) * 16, h * hd : (h + 1) * hd] = res[
+                        h * 16 : (h + 1) * 16, n * hd : (n + 1) * hd
+                    ]
+        at = pl.ds(pl.multiple_of(c * rows, rows), rows)
+        pltpu.make_async_copy(w_out.at[c], out_hbm.at[at, :], out_sem.at[c]).start()
+        return 0
+
+    lax.fori_loop(0, chunks, chunk, 0)
+    for cp in stores:
+        cp.wait()
+
+
+def gather_heads(num, rows):
+    row = jnp.arange(num * rows)
+    return ((row % rows * num + row // rows)[:, None] == row[None, :]).astype(BF16)
 
 
 def flat_heads(w):
     model, num, hd = w.shape
-    tile = 256
-    row = jnp.arange(num * 16)
-    perm = ((row % 16 * num + row // 16)[:, None] == row[None, :]).astype(BF16)
+    chunks = 8
+    rows = model // chunks
     return pl.pallas_call(
         heads_kernel,
         out_shape=jax.ShapeDtypeStruct((model, num * hd), BF16),
-        grid=(model // tile,),
-        in_specs=[
-            pl.BlockSpec((tile, num, hd), lambda i: (i, 0, 0)),
-            pl.BlockSpec((num * 16, num * 16), lambda i: (0, 0)),
+        in_specs=[pl.BlockSpec(memory_space=pltpu.VMEM), pl.BlockSpec(memory_space=pl.ANY)],
+        out_specs=pl.BlockSpec(memory_space=pl.ANY),
+        scratch_shapes=[
+            pltpu.VMEM((chunks, rows, num, hd), BF16),
+            pltpu.VMEM((chunks, rows, num * hd), BF16),
+            pltpu.SemaphoreType.DMA((chunks,)),
+            pltpu.SemaphoreType.DMA((chunks,)),
         ],
-        out_specs=pl.BlockSpec((tile, num * hd), lambda i: (i, 0)),
-        compiler_params=params(),
+        compiler_params=pltpu.CompilerParams(vmem_limit_bytes=params(1).vmem_limit_bytes),
         cost_estimate=cost(4e9, 4 * model * num * hd),
-    )(w, perm)
-
-
-def kv_kernel(sc, x_ref, dy_ref, wk_ref, wv_ref, out_ref, xa, xb, dya, dyb):
-    out_ref[:, :256] = dot(x_ref[...], wk_ref[...]).astype(BF16)
-    out_ref[:, 256:] = dot(x_ref[...], wv_ref[...]).astype(BF16)
+    )(gather_heads(num, 16), w)
+
+
+def kv_kernel(sc, x_ref, dy_ref, wk_ref, wv_ref, perm_ref, out_ref, w_ref, xa, xb, dya, dyb):
+    @pl.when(pl.program_id(0) == 0)
+    def _():
+        for g in range(w_ref.shape[0] // HD):
+            rows = slice(g * BLK, (g + 1) * BLK)
+            pair = jnp.concatenate([wk_ref[rows, :], wv_ref[rows, :]], axis=1)
+            res = dot(perm_ref[...], pair).astype(BF16)
+            for h in range(2):
+                for v in range(2):
+                    col = (v * 2 + h) * HD
+                    w_ref[g * HD : (g + 1) * HD, col : col + HD] = res[h * HD : (h + 1) * HD, v * HD : (v + 1) * HD]
+
+    out_ref[...] = dot(x_ref[...], w_ref[...]).astype(BF16)
 
     @pl.when(pl.program_id(0) == 1 - sc[0])
     def _():
@@ -87,16 +126,16 @@
     half = jax.ShapeDtypeStruct((BLK, depth), BF16)
     return pl.pallas_call(
         kv_kernel,
-        out_shape=(jax.ShapeDtypeStruct((rows, 512), BF16), half, half, half, half),
+        out_shape=(jax.ShapeDtypeStruct((rows, DUO), BF16), jax.ShapeDtypeStruct((depth, DUO), BF16), half, half, half, half),
         grid_spec=pltpu.PrefetchScalarGridSpec(
             num_scalar_prefetch=1,
             grid=(rows // BLK,),
-            in_specs=[row, row, fixed((depth, 256)), fixed((depth, 256))],
-            out_specs=(pl.BlockSpec((BLK, 512), lambda i, s: (i, 0)),) + (fixed((BLK, depth)),) * 4,
+            in_specs=[row, row, fixed(wk.shape), fixed(wv.shape), fixed((BLK, BLK))],
+            out_specs=(pl.BlockSpec((BLK, DUO), lambda i, s: (i, 0)), fixed((depth, DUO))) + (fixed((BLK, depth)),) * 4,
         ),
         compiler_params=params(),
-        cost_estimate=cost(2 * rows * depth * 512, 8e6),
-    )(core, x, dy, wk, wv)
+        cost_estimate=cost(2 * rows * depth * DUO, 8e6),
+    )(core, x, dy, wk, wv, gather_heads(2, HD))
 
 
 def attn_kernel(heads, scale, first, final, sc, wq_hbm, wo_hbm, *refs):
@@ -110,13 +149,18 @@
     ks, vs, kt, vt, dk, dv, qt, dot_t, qst, dost, s_ref, p_ref, ds_ref, ot, dqt, m_ref, l_ref, wq, wo, xs, dys, w_sem, x_sem, dy_sem = scratch
     step = pl.program_id(0)
     wide = heads * BLK
-    hd = 128
+    hd = HD
     c2 = scale * math.log2(math.e)
 
     steps = 2 * x_hbm[0].shape[0] // BLK
     core = pl.multiple_of(sc[24] * heads * hd, heads * hd)
-    load_wq = pltpu.make_async_copy(wq_hbm.at[:, pl.ds(core, heads * hd)], wq, w_sem.at[0])
-    load_wo = pltpu.make_async_copy(wo_hbm.at[pl.ds(core, heads * hd), :], wo, w_sem.at[1])
+    load_wq, load_wo = [], []
+    for n in range(4):
+        span = slice(n * DUO, (n + 1) * DUO)
+        load_wq.append(pltpu.make_async_copy(wq_hbm.at[span, pl.ds(core, heads * hd)], wq.at[span, :], w_sem.at[0]))
+        rows = heads * hd // 4
+        dst = wo.at[n * rows : (n + 1) * rows, :]
+        load_wo.append(pltpu.make_async_copy(wo_hbm.at[pl.ds(core + n * rows, rows), :], dst, w_sem.at[1]))
 
     def load_rows(n):
         piece, row = divmod(n, steps // 2)
@@ -130,9 +174,11 @@
     def _():
         load_x, load_dy = load_rows(0)
         load_x.start()
-        load_wq.start()
+        for cp in load_wq:
+            cp.start()
         load_dy.start()
-        load_wo.start()
+        for cp in load_wo:
+            cp.start()
 
     for n in range(1, steps):
 
@@ -161,7 +207,8 @@
 
     @pl.when(step == 0)
     def _():
-        load_wq.wait()
+        for cp in load_wq:
+            cp.wait()
 
     slot = step % 2
     pltpu.make_async_copy(x_hbm[0].at[0:BLK, :], xs.at[slot], x_sem.at[slot]).wait()
@@ -173,7 +220,8 @@
 
     @pl.when(step == 0)
     def _():
-        load_wo.wait()
+        for cp in load_wo:
+            cp.wait()
 
     pltpu.make_async_copy(dy_hbm[0].at[0:BLK, :], dys.at[slot], dy_sem.at[slot]).wait()
     do = dot_nt(dys[slot], wo[...]).astype(BF16)
@@ -264,10 +312,10 @@
 def attention(sc, wq, wo, x_pieces, dy_pieces, kv_pieces, init, final, scale):
     first = init is None
     rows, width, model = 2 * x_pieces[0].shape[0], wq.shape[1] // 2, wq.shape[0]
-    hd = 128
+    hd = HD
     heads = width // hd
     wide = heads * BLK
-    seq = 2048
+    seq = SEQ
     o_spec = pl.BlockSpec((width, BLK), lambda i, s: (0, s[12 + i]))
     out_spec = pl.BlockSpec((BLK, width), lambda i, s: (s[12 + i], 0))
     full = lambda shape: pl.BlockSpec(shape, lambda i, s: (0, 0), pipeline_mode=pl.Buffered(1))
@@ -282,13 +330,13 @@
         out_shape=(
             jax.ShapeDtypeStruct((width, rows), BF16),
             jax.ShapeDtypeStruct((rows, width), BF16),
-            jax.ShapeDtypeStruct((seq, 256), BF16 if final else F32),
+            jax.ShapeDtypeStruct((seq, BLK), BF16 if final else F32),
         ),
         grid_spec=pltpu.PrefetchScalarGridSpec(
             num_scalar_prefetch=1,
             grid=(rows // BLK,),
             in_specs=in_specs,
-            out_specs=(o_spec, out_spec, full((seq, 256))),
+            out_specs=(o_spec, out_spec, full((seq, BLK))),
             scratch_shapes=[
                 *[pltpu.VMEM((seq, hd), BF16) for _ in "kv"],
                 *[pltpu.VMEM((hd, seq), BF16) for _ in "kv"],
@@ -323,7 +371,7 @@
 
 
 def out_rows(core, o_mine, o_other, wo):
-    rows, half, model, tile = 512, o_mine.shape[0], wo.shape[1], 512
+    rows, half, model, tile = DUO, o_mine.shape[0], wo.shape[1], DUO
     return pl.pallas_call(
         y_kernel,
         out_shape=jax.ShapeDtypeStruct((rows, model), BF16),
@@ -344,16 +392,21 @@
     )(core, o_mine, o_other, wo, wo)
 
 
-def dx_kernel(sc, q_mine, q_other, kv_mine, kv_other, wq_mine, wq_other, wk_mine, wk_other, wv_mine, wv_other, out_ref):
-    kv = jnp.concatenate([kv_mine[...], kv_other[...]], axis=1)
-    w = jnp.concatenate([wk_mine[...], wv_mine[...], wk_other[...], wv_other[...]], axis=1)
+def dx_kernel(sc, q_mine, q_other, kv_mine, kv_other, wq_mine, wq_other, wkv, out_ref, kv):
+    hd = HD
+
+    @pl.when(pl.program_id(0) == 0)
+    def _():
+        for n, src in ((sc[0], kv_mine), (1 - sc[0], kv_other)):
+            kv[:, pl.ds(pl.multiple_of(n * hd, hd), hd)] = src[:, :hd]
+            kv[:, pl.ds(pl.multiple_of((2 + n) * hd, hd), hd)] = src[:, hd:]
+
     acc = dot_nt(q_mine[...], wq_mine[...]) + dot_nt(q_other[...], wq_other[...])
-    out_ref[...] = (acc + dot_nt(kv, w)).astype(BF16)
-
-
-def grad_rows(core, dq_mine, dq_other, dkv_mine, dkv_other, wq, wk, wv):
-    rows, half, model, tile = 512, dq_mine.shape[1], wq.shape[0], 512
-    hd = 128
+    out_ref[...] = (acc + dot_nt(kv[...], wkv[...])).astype(BF16)
+
+
+def grad_rows(core, dq_mine, dq_other, dkv_mine, dkv_other, wq, wkv):
+    rows, half, model, tile = DUO, dq_mine.shape[1], wq.shape[0], DUO
     mine = lambda i, s: (s[0], 0)
     near, far = lambda i, s: (i, s[0]), lambda i, s: (i, 1 - s[0])
     return pl.pallas_call(
@@ -363,130 +416,166 @@
             num_scalar_prefetch=1,
             grid=(model // tile,),
             in_specs=[
-                *[pl.BlockSpec((rows, n), mine) for n in (half, half, 2 * hd, 2 * hd)],
-                *[pl.BlockSpec((tile, n), at) for n in (half, hd, hd) for at in (near, far)],
+                *[pl.BlockSpec((rows, n), mine) for n in (half, half, BLK, BLK)],
+                *[pl.BlockSpec((tile, half), at) for at in (near, far)],
+                pl.BlockSpec((tile, DUO), lambda i, s: (i, 0)),
             ],
             out_specs=pl.BlockSpec((rows, tile), lambda i, s: (0, i)),
+            scratch_shapes=[pltpu.VMEM((rows, DUO), BF16)],
         ),
         compiler_params=params(),
         cost_estimate=cost(4 * rows * half * model * 1.25, 14e6),
-    )(core, dq_mine, dq_other, dkv_mine, dkv_other, wq, wq, wk, wk, wv, wv)
-
-
-PIECES = ((0, 512), (1, 512), (0, 256), (1, 256), (0, 256), (1, 256))
-STARTS = (0, 512, 1024, 1280, 1536, 1792)
+    )(core, dq_mine, dq_other, dkv_mine, dkv_other, wq, wq, wkv)
+
+
+PIECES = ((0, DUO), (1, DUO), (0, BLK), (1, BLK), (0, BLK), (1, BLK))
+STARTS = (0, DUO, HALF, 1280, 1536, 1792)
+
+
+def piece_copies(core, arrays, dst, sem, along):
+    copies = []
+    for n, ((flip, size), start) in enumerate(zip(PIECES, STARTS)):
+        at = pl.ds(pl.multiple_of((1 - core if flip else core) * size, size), size)
+        src = arrays[n // 2]
+        if along:
+            copies.append(pltpu.make_async_copy(src.at[:, at], dst.at[:, start : start + size], sem))
+        else:
+            copies.append(pltpu.make_async_copy(src.at[at, :], dst.at[start : start + size, :], sem))
+    return copies
 
 
 def dwq_kernel(sc, *refs):
-    xs_in, mine, other, kvm, kvo = refs[:6], refs[6:12], refs[12:18], refs[18:24], refs[24:30]
-    out_ref, gk_ref, gv_ref, xt = refs[30:34]
+    xs_in, mine, other, kv_in = refs[:6], refs[6:9], refs[9:12], refs[12:14]
+    out_ref, gk_ref, gv_ref, xt, dq, kv, sems = refs[14:]
     g, i = pl.program_id(0), pl.program_id(1)
-    tile = out_ref.shape[0]
-
-    def part(rhs):
-        return sum(dot(xt[i, :, s : s + n], r[...]) for s, (_, n), r in zip(STARTS, PIECES, rhs))
-
-    def store(rhs):
-        acc = part(rhs)
-        flat = out_ref.reshape(tile * 8, 128)
-        for h in range(8):
-            flat[pl.ds(h, tile, stride=8), :] = acc[:, h * 128 : (h + 1) * 128]
+    tile, core, hd = out_ref.shape[0], sc[0], HD
+    first = piece_copies(core, mine, dq.at[0], sems.at[0], False)
+    later = piece_copies(core, other, dq.at[1], sems.at[1], False)
+    for n, src in enumerate(kv_in):
+        parts = [src.at[at : at + size, :] for at, size in ((0, HALF), (HALF, DUO), (1536, DUO))]
+        later += piece_copies(core, parts, kv.at[:, n * BLK : (n + 1) * BLK], sems.at[1], False)
+
+    @pl.when((g == 0) & (i == 0))
+    def _():
+        for cp in first:
+            cp.start()
+
+    @pl.when((g == 0) & (i == 1))
+    def _():
+        for cp in later:
+            cp.start()
 
     @pl.when(g == 0)
     def _():
         for s, (_, n), x in zip(STARTS, PIECES, xs_in):
             xt[i, :, s : s + n] = x[...].T
-        store(mine)
+
+    @pl.when((g == 0) & (i == 0))
+    def _():
+        for cp in first:
+            cp.wait()
+
+    @pl.when((g == 1) & (i == 0))
+    def _():
+        for cp in later:
+            cp.wait()
+
+    acc = dot(xt[i], dq[g])
+    flat = out_ref.reshape(tile * 8, hd)
+    for h in range(8):
+        flat[pl.ds(h, tile, stride=8), :] = acc[:, h * hd : (h + 1) * hd]
 
     @pl.when(g == 1)
     def _():
-        store(other)
-        core = sc[0]
-        k_flat, v_flat = gk_ref.reshape(tile * 2, 128), gv_ref.reshape(tile * 2, 128)
-        for src, head in ((kvm, core), (kvo, 1 - core)):
-            acc = part(src)
-            k_flat[pl.ds(head, tile, stride=2), :] = acc[:, :128]
-            v_flat[pl.ds(head, tile, stride=2), :] = acc[:, 128:]
+        k_flat, v_flat = gk_ref.reshape(tile * 2, hd), gv_ref.reshape(tile * 2, hd)
+        both = dot(xt[i], kv[...])
+        for n, head in enumerate((core, 1 - core)):
+            k_flat[pl.ds(head, tile, stride=2), :] = both[:, 2 * n * hd : (2 * n + 1) * hd]
+            v_flat[pl.ds(head, tile, stride=2), :] = both[:, (2 * n + 1) * hd : (2 * n + 2) * hd]
 
 
 def grad_wq(core, xs, mine, other, kvm, kvo):
-    model, half, tile = xs[0].shape[1], mine[0].shape[1], 256
+    model, half, tile = xs[0].shape[1], mine[0].shape[1], BLK
     tiles = model // tile
     x_specs = [pl.BlockSpec((n, tile), lambda g, i, s: (0, jnp.where(g == 0, i, tiles - 1))) for _, n in PIECES]
-    q_specs = [pl.BlockSpec((n, half), lambda g, i, s, f=f: (1 - s[0] if f else s[0], 0)) for f, n in PIECES]
-    kv_specs = [
-        pl.BlockSpec((n, 256), lambda g, i, s, f=f, at=at: (at + (1 - s[0] if f else s[0]), 0))
-        for (f, n), at in zip(PIECES, (0, 0, 4, 4, 6, 6))
-    ]
-    ex = lambda t: [t[0], t[0], t[1], t[1], t[2], t[2]]
-    small = pl.BlockSpec((tile, 2, 128), lambda g, i, s: (i * g, 0, 0))
+    small = pl.BlockSpec((tile, 2, HD), lambda g, i, s: (i * g, 0, 0))
     return pl.pallas_call(
         dwq_kernel,
         out_shape=(
-            jax.ShapeDtypeStruct((model, 16, 128), F32),
-            jax.ShapeDtypeStruct((model, 2, 128), F32),
-            jax.ShapeDtypeStruct((model, 2, 128), F32),
+            jax.ShapeDtypeStruct((model, 16, HD), F32),
+            jax.ShapeDtypeStruct((model, 2, HD), F32),
+            jax.ShapeDtypeStruct((model, 2, HD), F32),
         ),
         grid_spec=pltpu.PrefetchScalarGridSpec(
             num_scalar_prefetch=1,
             grid=(2, tiles),
-            in_specs=x_specs + q_specs + q_specs + kv_specs + kv_specs,
+            in_specs=x_specs + [pl.BlockSpec(memory_space=pl.ANY)] * 8,
             out_specs=(
-                pl.BlockSpec((tile, 8, 128), lambda g, i, s: (i, (s[0] + g) % 2, 0)),
+                pl.BlockSpec((tile, 8, HD), lambda g, i, s: (i, (s[0] + g) % 2, 0)),
                 small,
                 small,
             ),
-            scratch_shapes=[pltpu.VMEM((tiles, tile, 2048), BF16)],
+            scratch_shapes=[
+                pltpu.VMEM((tiles, tile, SEQ), BF16),
+                pltpu.VMEM((2, SEQ, half), BF16),
+                pltpu.VMEM((SEQ, DUO), BF16),
+                pltpu.SemaphoreType.DMA((2,)),
+            ],
         ),
         compiler_params=params(2),
-        cost_estimate=cost(2 * 2048 * model * (2 * half + 512), 40e6),
-    )(core, *xs, *ex(mine), *ex(other), *([kvm] * 6), *([kvo] * 6))
+        cost_estimate=cost(2 * SEQ * model * (2 * half + DUO), 40e6),
+    )(core, *xs, *mine, *other, kvm, kvo)
 
 
 def dwo_kernel(sc, *refs):
-    mine, other, ys, out_ref = refs[:6], refs[6:12], refs[12:18], refs[18]
-
-    def store(lhs):
-        out_ref[...] = sum(dot(o[...], y[...]) for o, y in zip(lhs, ys))
-
-    @pl.when(pl.program_id(1) == 0)
-    def _():
-        store(mine)
-
-    @pl.when(pl.program_id(1) == 1)
-    def _():
-        store(other)
+    mine, other, ys, (out_ref, o_all, y_all, sems) = refs[:3], refs[3:6], refs[6:12], refs[12:]
+    j, g, i = pl.program_id(0), pl.program_id(1), pl.program_id(2)
+    tile, wide = out_ref.shape
+    o_first = piece_copies(sc[0], mine, o_all.at[0], sems.at[0], True)
+    o_later = piece_copies(sc[0], other, o_all.at[1], sems.at[1], True)
+    y_copies = [
+        [
+            pltpu.make_async_copy(y.at[:, n * wide : (n + 1) * wide], y_all.at[n, s : s + r, :], sems.at[2 + n])
+            for y, s, (_, r) in zip(ys, STARTS, PIECES)
+        ]
+        for n in range(2)
+    ]
+
+    def when(jj, gg, ii, copies, start):
+        @pl.when((j == jj) & (g == gg) & (i == ii))
+        def _():
+            for cp in copies:
+                cp.start() if start else cp.wait()
+
+    when(0, 0, 0, y_copies[0] + o_first, True)
+    when(0, 0, 1, o_later, True)
+    when(0, 1, 0, y_copies[1], True)
+    when(0, 0, 0, y_copies[0] + o_first, False)
+    when(0, 1, 0, o_later, False)
+    when(1, 0, 0, y_copies[1], False)
+    out_ref[...] = dot(o_all[g, pl.ds(pl.multiple_of(i * tile, tile), tile), :], y_all[j])
 
 
 def grad_wo(core, ys, mine, other):
-    model, half, tile, wide = ys[0].shape[1], mine[0].shape[0], 512, 1024
+    model, half, tile, wide = ys[0].shape[1], mine[0].shape[0], DUO, HALF
     steps = half // tile
-    specs = []
-    for rest in (0, 1):
-        specs += [
-            pl.BlockSpec(
-                (tile, n),
-                lambda j, g, i, s, f=f, rest=rest: (
-                    jnp.where(g == rest, i, 0 if rest else steps - 1),
-                    1 - s[0] if f else s[0],
-                ),
-            )
-            for f, n in PIECES
-        ]
-    specs += [pl.BlockSpec((n, wide), lambda j, g, i, s: (0, j)) for _, n in PIECES]
-    ex = lambda t: [t[0], t[0], t[1], t[1], t[2], t[2]]
     return pl.pallas_call(
         dwo_kernel,
         out_shape=jax.ShapeDtypeStruct((2 * half, model), F32),
         grid_spec=pltpu.PrefetchScalarGridSpec(
             num_scalar_prefetch=1,
-            grid=(model // wide, 2, steps),
-            in_specs=specs,
+            grid=(2, 2, steps),
+            in_specs=[pl.BlockSpec(memory_space=pl.ANY)] * 12,
             out_specs=pl.BlockSpec((tile, wide), lambda j, g, i, s: ((s[0] + g) % 2 * steps + i, j)),
+            scratch_shapes=[
+                pltpu.VMEM((2, half, SEQ), BF16),
+                pltpu.VMEM((2, SEQ, wide), BF16),
+                pltpu.SemaphoreType.DMA((4,)),
+            ],
         ),
         compiler_params=params(3),
-        cost_estimate=cost(4 * 2048 * model * half, 40e6),
-    )(core, *ex(mine), *ex(other), *ys)
+        cost_estimate=cost(4 * SEQ * model * half, 40e6),
+    )(core, *mine, *other, *ys)
 
 
 def solution(mesh):
@@ -497,7 +586,7 @@
     chip_swap = [(0, 2), (2, 0), (1, 3), (3, 1)]
 
     def device_layer(x, dy, w_query, w_key, w_value, w_out):
-        rows, model = x.shape
+        _, model = x.shape
         num_heads, hd = w_query.shape[1:]
         kv_heads = w_key.shape[1]
         scale = hd ** -0.5
@@ -521,21 +610,24 @@
         to_core = lambda v: lax.ppermute(v, "cp", core_swap)
         to_chip = lambda v: lax.ppermute(v, "cp", chip_swap)
 
-        wk = w_key.reshape(model, kv_heads * hd)
-        wv = w_value.reshape(model, kv_heads * hd)
+        wk = w_key.reshape(model * kv_heads, hd)
+        wv = w_value.reshape(model * kv_heads, hd)
         wo = w_out.reshape(num_heads * hd, model)
         x_p = to_core(x)
         dy_p = to_core(dy)
 
-        kv, x_a, x_b, dy_a, dy_b = project_kv(core, x, dy, wk, wv)
-        kv_r, kv_p = to_chip(kv), to_core(kv)
+        kv, wkv, x_a, x_b, dy_a, dy_b = project_kv(core, x, dy, wk, wv)
+        far_kv, kv_p = to_chip(kv), to_core(kv)
         w_s, _ = lax.optimization_barrier((w_query, kv))
-        x_a, dy_a, x_b, dy_b = to_chip(x_a), to_chip(dy_a), to_chip(x_b), to_chip(dy_b)
+        x_a, dy_a = to_chip(x_a), to_chip(dy_a)
+        x_b, dy_b = to_chip(x_b), to_chip(dy_b)
         wq = flat_heads(w_s)
+        kv_r, wq = lax.optimization_barrier((far_kv, wq))
         kv_rp = to_core(kv_r)
         pieces = (kv, kv_p, kv_r, kv_rp)
 
-        o_c, dq_c, part = attention(sc_chip, wq, wo, (x, x_p), (dy, dy_p), pieces, None, False, scale)
+        o_c, dq_c, part = attention(
+            sc_chip, wq, wo, (x, x_p), (dy, dy_p), pieces, None, False, scale)
         x_a, dy_a, o_c, dq_c = lax.optimization_barrier((x_a, dy_a, o_c, dq_c))
         x_pa, dy_pa, o_co, dq_co = to_core(x_a), to_core(dy_a), to_core(o_c), to_core(dq_c)
 
@@ -551,7 +643,7 @@
         xs = (x, x_p, x_a, x_pa, x_b, x_pb)
         ys = (dy, dy_p, dy_a, dy_pa, dy_b, dy_pb)
         gwo = grad_wo(core, ys, (o_c, o_a, o_b), (o_co, o_ao, o_bo))
-        dx = grad_rows(core, dq_c, dq_co, dkv, dkv_o, wq, wk, wv)
+        dx = grad_rows(core, dq_c, dq_co, dkv, dkv_o, wq, wkv)
         gwq, gwk, gwv = grad_wq(core, xs, (dq_c, dq_a, dq_b), (dq_co, dq_ao, dq_bo), dkv, dkv_o)
         return y, dx, gwq, gwk, gwv, gwo.reshape(num_heads, hd, model)
 

time: 276 us -> 261 us (0.946)
  waiting for transfers between devices: 21.5 us -> 13.9 us
  Pallas kernels: 233 us -> 229 us
    ppermute x5, waiting for transfers between devices: 18.1 us -> 9.65 us  [device_layer(): to_chip = lambda v: lax.ppermute(v, 'cp', chip_swap)]
    pallas_call x1, Pallas kernels: 27.7 us -> 24.3 us  [grad_wo(): pl.pallas_call(dwo_kernel, out_shape=jax.ShapeDtypeStruct((2 * half, mode...]
    reshape x1 -> x0, local copies, waits for them, and re-layouts: 3.18 us -> none  [device_layer(): wv = w_value.reshape(model, kv_heads * hd)]
  transfers between devices with their start and end apart: 20 -> 20, of which waited for: 5 -> 5; matrix products, arithmetic and copies ran while one was open for 2% -> 1% of each run, Pallas kernels for 75% -> 78%
where the time goes in v4:
time: 261 us
  Pallas kernels  229 us (88%)
  waiting for transfers between devices  13.9 us (5%)
  starting transfers between devices  10.5 us (4%)
  local copies, waits for them, and re-layouts  5.21 us (2%)
    pallas_call x3, Pallas kernels, attention(): pl.pallas_call(functools.partial(attn_kernel, heads, scale, first, final)...  134 us
    pallas_call x1, Pallas kernels, grad_wq(): pl.pallas_call(dwq_kernel, out_shape=(jax.ShapeDtypeStruct((model, 16, HD...  36.1 us
    pallas_call x1, Pallas kernels, grad_wo(): pl.pallas_call(dwo_kernel, out_shape=jax.ShapeDtypeStruct((2 * half, mode...  24.3 us
    pallas_call x1, Pallas kernels, grad_rows(): pl.pallas_call(dx_kernel, out_shape=jax.ShapeDtypeStruct((rows, model), B...  10.4 us
    ppermute x5, waiting for transfers between devices, device_layer(): to_chip = lambda v: lax.ppermute(v, 'cp', chip_swap)  9.65 us
    pallas_call x1, Pallas kernels, out_rows(): pl.pallas_call(y_kernel, out_shape=jax.ShapeDtypeStruct((rows, model), BF...  9.28 us
    pallas_call x1, Pallas kernels, flat_heads(): pl.pallas_call(heads_kernel, out_shape=jax.ShapeDtypeStruct((model, num *...  7.78 us
    pallas_call x1, Pallas kernels, project_kv(): pl.pallas_call(kv_kernel, out_shape=(jax.ShapeDtypeStruct((rows, DUO), BF...  7.37 us
  transfers between devices with their start and end apart: 20, of which 5 were waited for; matrix products, arithmetic and copies ran while one was open for 1% of the time, Pallas kernels for 78%

profile of v4, /device:TPU:0, one launch (start us, length us, event | category | flops | bytes accessed | tf_op | source)
XLA Modules:
  0.0 261.0 jit_solution(9300523210290262349)
XLA Ops:
  0.6 0.9 collective-permute-start.3
  1.5 0.0 collective-permute-start.4
  1.5 0.8 fusion.perm_ref
  2.3 7.4 %shard_map.109 = (bf16[512,512]{1,0:T(8,128)(2,1)}, bf16[2048,512]{1,0:T(8,128)(2,1)}, bf16[256,2048]{1,0:T(8,128)(2,1)}, bf16[256,2048]{1,0:T(8,128)(2,1)}, bf1...) custom-call(s32[1]{0:T(128)} %bitcast.sc, bf16[512,2048]{1,0:T(8,128)(2,1)} %refs_0_.3, bf16[512,2048]{1,0:T(8,128)(2,1)} %refs_6_.1, ...), custom_call_target="tpu_custom_call" | custom-call | flops 1073741824 | bytes 8000000 | tf_op jit(solution)/shard_map/pallas_call | solution.py:127
  9.7 2.9 %collective-permute-start.2 = (bf16[512,512]{1,0:T(8,128)(2,1)}, bf16[512,512]{1,0:T(8,128)(2,1)S(1)}, u32[]{:S(2)}, u32[]{:S(2)}) collective-permute-start(bf16[512,512]{1,0:T(8,128)(2,1)} %get-tuple-element.39.refs_4_.refs_8_), channel_id=1, source_target_pairs={{0,2},{2,0},{1,3},{3,1},{4,6},{6,4},{5,7},{7,5}} | collective-permute-start | bytes 1572872 | tf_op jit(solution)/shard_map/ppermute | solution.py:611
  12.6 0.0 collective-permute-start.5
  12.6 0.8 fusion.1.perm_ref
  13.4 7.8 %shard_map.110.wq_hbm.wq_mine.wq_other = bf16[2048,2048]{1,0:T(8,128)(2,1)} custom-call(bf16[256,256]{1,0:T(8,128)(2,1)} %fusion.1.perm_ref, bf16[2048,16,128]{2,1,0:T(8,128)(2,1)} %w_hbm), custom_call_target="tpu_custom_call" | custom-call | flops 4000000000 | bytes 16777216 | tf_op jit(solution)/shard_map/pallas_call | solution.py:81
  21.2 3.8 %collective-permute-done.2.refs_6_.refs_10_ = bf16[512,512]{1,0:T(8,128)(2,1)S(1)} collective-permute-done((bf16[512,512]{1,0:T(8,128)(2,1)}, bf16[512,512]{1,0:T(8,128)(2,1)S(1)}, u32[]{:S(2)}, u32[]{:S(2)}) %collective-permute-start.2) | collective-permute-done | bytes 524320 | tf_op jit(solution)/shard_map/ppermute | solution.py:611
  24.9 0.0 copy-start.3
  24.9 0.0 collective-permute-start.6
  25.0 1.7 collective-permute-start
  26.7 0.6 stack.64.sc
  27.3 0.0 collective-permute-done.5.refs_5_.refs_9_
  27.3 0.0 copy-start.4
  27.3 0.3 collective-permute-start.1
  27.6 0.0 collective-permute-done.6.refs_7_.refs_11_
  27.6 0.6 copy-done.4
  28.2 0.0 copy-start.5
  28.2 0.0 collective-permute-done.3.refs_1_
  28.2 0.8 copy-done.5
  29.0 0.0 collective-permute-done.4.refs_3_.refs_7_
  29.0 0.0 copy-done.3
  29.0 62.3 %shard_map.111 = (bf16[1024,1024]{1,0:T(8,128)(2,1)}, bf16[1024,1024]{1,0:T(8,128)(2,1)}, f32[2048,256]{1,0:T(8,128)}) custom-call(s32[25]{0:T(128)} %stack.64.sc, bf16[2048,2048]{1,0:T(8,128)(2,1)} %shard_map.110.wq_hbm.wq_mine.wq_other, bf16[2048,2048]{1,0:T(8,128)(2,1)} %bitcast.26, bf16[512,2048]{1,0:T(8,128)(2,1)} %refs_0_.3, ...), custom_call_target="tpu_custom_call" | custom-call | flops 32000000000 | bytes 20000000 | tf_op jit(solution)/shard_map/pallas_call | solution.py:328
  91.2 0.0 collective-permute-done.refs_0_.refs_2_
  91.2 0.0 collective-permute-done.1.refs_2_.refs_8_
  91.2 0.2 collective-permute-start.10
  91.5 0.3 collective-permute-start.11
  91.8 1.2 collective-permute-start.8
  92.9 0.9 collective-permute-start.9
  93.8 0.6 stack.71.sc
  94.4 0.0 collective-permute-done.10.refs_1_.refs_3_
  94.4 1.4 collective-permute-done.11.refs_3_.refs_9_
  95.8 38.2 %shard_map.112 = (bf16[1024,512]{1,0:T(8,128)(2,1)}, bf16[512,1024]{1,0:T(8,128)(2,1)}, f32[2048,256]{1,0:T(8,128)}) custom-call(s32[25]{0:T(128)} %stack.71.sc, bf16[2048,2048]{1,0:T(8,128)(2,1)} %shard_map.110.wq_hbm.wq_mine.wq_other, bf16[2048,2048]{1,0:T(8,128)(2,1)} %bitcast.27, bf16[256,2048]{1,0:T(8,128)(2,1)} %collective-permute-done.refs_0_.refs_2_, ...), custom_call_target="tpu_custom_call" | custom-call | flops 16000000000 | bytes 20000000 | tf_op jit(solution)/shard_map/pallas_call | solution.py:328
  133.9 0.0 collective-permute-done.8.refs_0_.refs_4_
  134.0 5.9 %collective-permute-done.9.refs_2_.refs_10_ = bf16[256,2048]{1,0:T(8,128)(2,1)} collective-permute-done((bf16[256,2048]{1,0:T(8,128)(2,1)}, bf16[256,2048]{1,0:T(8,128)(2,1)}, u32[]{:S(2)}, u32[]{:S(2)}) %collective-permute-start.9) | collective-permute-done | bytes 1048608 | tf_op jit(solution)/shard_map/ppermute | solution.py:611
  139.8 0.0 collective-permute-start.12
  139.8 0.5 collective-permute-start.13
  140.3 0.0 collective-permute-start.7
  140.3 0.6 stack.68.sc
  140.9 0.5 collective-permute-start.14
  141.5 0.0 collective-permute-start.16
  141.5 1.4 collective-permute-done.12.refs_1_.refs_5_
  142.8 1.5 collective-permute-done.13.refs_3_.refs_11_
  144.3 33.3 %shard_map.113 = (bf16[1024,512]{1,0:T(8,128)(2,1)}, bf16[512,1024]{1,0:T(8,128)(2,1)}, bf16[2048,256]{1,0:T(8,128)(2,1)}) custom-call(s32[25]{0:T(128)} %stack.68.sc, bf16[2048,2048]{1,0:T(8,128)(2,1)} %shard_map.110.wq_hbm.wq_mine.wq_other, bf16[2048,2048]{1,0:T(8,128)(2,1)} %bitcast.28, bf16[256,2048]{1,0:T(8,128)(2,1)} %collective-permute-done.8.refs_0_.refs_4_, ...), custom_call_target="tpu_custom_call" | custom-call | flops 16000000000 | bytes 20000000 | tf_op jit(solution)/shard_map/pallas_call | solution.py:328
  177.6 0.0 collective-permute-done.7.o_other.refs_3_
  177.6 0.2 collective-permute-start.15
  177.7 0.0 copy-start.1
  177.8 0.4 collective-permute-start.17
  178.1 0.1 collective-permute-start.18
  178.3 9.3 %shard_map.114 = bf16[512,2048]{1,0:T(8,128)(2,1)} custom-call(s32[1]{0:T(128)} %bitcast.sc, bf16[1024,1024]{1,0:T(8,128)(2,1)} %get-tuple-element.45.o_mine.refs_0_, bf16[1024,1024]{1,0:T(8,128)(2,1)} %collective-permute-done.7.o_other.refs_3_, bf16[2048,2048]{1,0:T(8,128)(2,1)} %bitcast.29, bf16[2048,2048]{1,0:T(8,128)(2,1)} %bitcast.30), custom_call_target="tpu_custom_call" | custom-call | flops 4294967296 | bytes 12000000 | tf_op jit(solution)/shard_map/pallas_call | solution.py:375
  187.5 0.0 collective-permute-done.14.q_other.refs_9_
  187.5 0.0 copy-done.1
  187.6 0.4 collective-permute-start.19
  188.0 0.0 collective-permute-done.16.refs_10_
  188.0 0.0 collective-permute-done.15.kv_other.refs_13_
  188.0 0.0 collective-permute-done.17.refs_11_
  188.0 1.0 copy-done
  189.0 36.1 %shard_map.116 = (f32[2048,16,128]{2,1,0:T(8,128)}, f32[2048,2,128]{2,1,0:T(2,128)}, f32[2048,2,128]{2,1,0:T(2,128)}) custom-call(s32[1]{0:T(128)} %bitcast.sc, bf16[512,2048]{1,0:T(8,128)(2,1)} %refs_0_.3, bf16[512,2048]{1,0:T(8,128)(2,1)} %collective-permute-done.3.refs_1_, bf16[256,2048]{1,0:T(8,128)(2,1)} %collective-permute-done.refs_0_.refs_2_, ...), custom_call_target="tpu_custom_call" | custom-call | flops 21474836480 | bytes 40000000 | tf_op jit(solution)/shard_map/pallas_call | solution.py:502
  225.1 10.4 %shard_map.115 = bf16[512,2048]{1,0:T(8,128)(2,1)} custom-call(s32[1]{0:T(128)} %bitcast.sc, bf16[1024,1024]{1,0:T(8,128)(2,1)} %get-tuple-element.58.q_mine.refs_6_, bf16[1024,1024]{1,0:T(8,128)(2,1)} %collective-permute-done.14.q_other.refs_9_, bf16[2048,256]{1,0:T(8,128)(2,1)} %get-tuple-element.59.kv_mine.refs_12_, bf16[2048,256]{1,0:T(8,128)(2,1)} %copy-done, ...), custom_call_target="tpu_custom_call" | custom-call | flops 5368709120 | bytes 14000000 | tf_op jit(solution)/shard_map/pallas_call | solution.py:412
  235.5 0.0 collective-permute-done.18.refs_4_
  235.5 0.0 collective-permute-done.19.refs_5_
  235.5 1.0 copy-done.2
  236.5 24.3 %shard_map.117 = f32[2048,2048]{1,0:T(8,128)} custom-call(s32[1]{0:T(128)} %bitcast.sc, bf16[1024,1024]{1,0:T(8,128)(2,1)} %get-tuple-element.45.o_mine.refs_0_, bf16[1024,512]{1,0:T(8,128)(2,1)} %get-tuple-element.66.refs_1_, bf16[1024,512]{1,0:T(8,128)(2,1)} %get-tuple-element.67.refs_2_, bf16[1024,1024]{1,0:T(8,128)(2,1)} %collective-permute-done.7.o_other.refs_3_, ...), custom_call_target="tpu_custom_call" | custom-call | flops 17179869184 | bytes 40000000 | tf_op jit(solution)/shard_map/pallas_call | solution.py:562
  (4 shorter events, 0.0 us)
Async XLA Ops:
  0.6 27.5 %collective-permute-start.3 = (bf16[512,2048]{1,0:T(8,128)(2,1)}, bf16[512,2048]{1,0:T(8,128)(2,1)}, u32[]{:S(2)}, u32[]{:S(2)}) collective-permute-start(bf16[512,2048]{1,0:T(8,128)(2,1)} %refs_0_.3), channel_id=1, source_target_pairs={{0,1},{1,0},{2,3},{3,2},{4,5},{5,4},{6,7},{7,6}} | collective-permute-start | bytes 6291464 | tf_op jit(solution)/shard_map/ppermute | solution.py:610
  1.5 27.5 %collective-permute-start.4 = (bf16[512,2048]{1,0:T(8,128)(2,1)}, bf16[512,2048]{1,0:T(8,128)(2,1)}, u32[]{:S(2)}, u32[]{:S(2)}) collective-permute-start(bf16[512,2048]{1,0:T(8,128)(2,1)} %refs_6_.1), channel_id=1, source_target_pairs={{0,1},{1,0},{2,3},{3,2},{4,5},{5,4},{6,7},{7,6}} | collective-permute-start | bytes 6291464 | tf_op jit(solution)/shard_map/ppermute | solution.py:610
  9.7 15.3 %collective-permute-start.2 = (bf16[512,512]{1,0:T(8,128)(2,1)}, bf16[512,512]{1,0:T(8,128)(2,1)S(1)}, u32[]{:S(2)}, u32[]{:S(2)}) collective-permute-start(bf16[512,512]{1,0:T(8,128)(2,1)} %get-tuple-element.39.refs_4_.refs_8_), channel_id=1, source_target_pairs={{0,2},{2,0},{1,3},{3,1},{4,6},{6,4},{5,7},{7,5}} | collective-permute-start | bytes 1572872 | tf_op jit(solution)/shard_map/ppermute | solution.py:611
  12.6 14.7 %collective-permute-start.5 = (bf16[512,512]{1,0:T(8,128)(2,1)}, bf16[512,512]{1,0:T(8,128)(2,1)S(1)}, u32[]{:S(2)}, u32[]{:S(2)}) collective-permute-start(bf16[512,512]{1,0:T(8,128)(2,1)} %get-tuple-element.39.refs_4_.refs_8_), channel_id=1, source_target_pairs={{0,1},{1,0},{2,3},{3,2},{4,5},{5,4},{6,7},{7,6}} | collective-permute-start | bytes 1572872 | tf_op jit(solution)/shard_map/ppermute | solution.py:610
  24.9 4.0 %copy-start.3 = (bf16[512,512]{1,0:T(8,128)(2,1)}, bf16[512,512]{1,0:T(8,128)(2,1)S(1)}, u32[]{:S(2)}) copy-start(bf16[512,512]{1,0:T(8,128)(2,1)S(1)} %collective-permute-done.2.refs_6_.refs_10_) | copy-start | bytes 1572868
  24.9 2.6 %collective-permute-start.6 = (bf16[512,512]{1,0:T(8,128)(2,1)S(1)}, bf16[512,512]{1,0:T(8,128)(2,1)S(1)}, u32[]{:S(2)}, u32[]{:S(2)}) collective-permute-start(bf16[512,512]{1,0:T(8,128)(2,1)S(1)} %collective-permute-done.2.refs_6_.refs_10_), channel_id=1, source_target_pairs={{0,1},{1,0},{2,3},{3,2},{4,5},{5,4},{6,7},{7,6}} | collective-permute-start | bytes 1572872 | tf_op jit(solution)/shard_map/ppermute | solution.py:610
  25.0 66.3 %collective-permute-start = (bf16[256,2048]{1,0:T(8,128)(2,1)}, bf16[256,2048]{1,0:T(8,128)(2,1)}, u32[]{:S(2)}, u32[]{:S(2)}) collective-permute-start(bf16[256,2048]{1,0:T(8,128)(2,1)} %get-tuple-element.37), channel_id=1, source_target_pairs={{0,2},{2,0},{1,3},{3,1},{4,6},{6,4},{5,7},{7,5}} | collective-permute-start | bytes 3145736 | tf_op jit(solution)/shard_map/ppermute | solution.py:611
  27.3 0.9 copy-start.4
  27.3 63.9 %collective-permute-start.1 = (bf16[256,2048]{1,0:T(8,128)(2,1)}, bf16[256,2048]{1,0:T(8,128)(2,1)}, u32[]{:S(2)}, u32[]{:S(2)}) collective-permute-start(bf16[256,2048]{1,0:T(8,128)(2,1)} %get-tuple-element.38), channel_id=1, source_target_pairs={{0,2},{2,0},{1,3},{3,1},{4,6},{6,4},{5,7},{7,5}} | collective-permute-start | bytes 3145736 | tf_op jit(solution)/shard_map/ppermute | solution.py:611
  28.2 0.8 copy-start.5
  91.2 3.2 %collective-permute-start.10 = (bf16[256,2048]{1,0:T(8,128)(2,1)}, bf16[256,2048]{1,0:T(8,128)(2,1)}, u32[]{:S(2)}, u32[]{:S(2)}) collective-permute-start(bf16[256,2048]{1,0:T(8,128)(2,1)} %collective-permute-done.refs_0_.refs_2_), channel_id=1, source_target_pairs={{0,1},{1,0},{2,3},{3,2},{4,5},{5,4},{6,7},{7,6}} | collective-permute-start | bytes 3145736 | tf_op jit(solution)/shard_map/ppermute | solution.py:610
  91.5 4.3 %collective-permute-start.11 = (bf16[256,2048]{1,0:T(8,128)(2,1)}, bf16[256,2048]{1,0:T(8,128)(2,1)}, u32[]{:S(2)}, u32[]{:S(2)}) collective-permute-start(bf16[256,2048]{1,0:T(8,128)(2,1)} %collective-permute-done.1.refs_2_.refs_8_), channel_id=1, source_target_pairs={{0,1},{1,0},{2,3},{3,2},{4,5},{5,4},{6,7},{7,6}} | collective-permute-start | bytes 3145736 | tf_op jit(solution)/shard_map/ppermute | solution.py:610
  91.8 42.2 %collective-permute-start.8 = (bf16[256,2048]{1,0:T(8,128)(2,1)}, bf16[256,2048]{1,0:T(8,128)(2,1)}, u32[]{:S(2)}, u32[]{:S(2)}) collective-permute-start(bf16[256,2048]{1,0:T(8,128)(2,1)} %get-tuple-element.46), channel_id=1, source_target_pairs={{0,2},{2,0},{1,3},{3,1},{4,6},{6,4},{5,7},{7,5}} | collective-permute-start | bytes 3145736 | tf_op jit(solution)/shard_map/ppermute | solution.py:611
  92.9 46.9 %collective-permute-start.9 = (bf16[256,2048]{1,0:T(8,128)(2,1)}, bf16[256,2048]{1,0:T(8,128)(2,1)}, u32[]{:S(2)}, u32[]{:S(2)}) collective-permute-start(bf16[256,2048]{1,0:T(8,128)(2,1)} %get-tuple-element.47), channel_id=1, source_target_pairs={{0,2},{2,0},{1,3},{3,1},{4,6},{6,4},{5,7},{7,5}} | collective-permute-start | bytes 3145736 | tf_op jit(solution)/shard_map/ppermute | solution.py:611
  139.8 3.0 %collective-permute-start.12 = (bf16[256,2048]{1,0:T(8,128)(2,1)}, bf16[256,2048]{1,0:T(8,128)(2,1)}, u32[]{:S(2)}, u32[]{:S(2)}) collective-permute-start(bf16[256,2048]{1,0:T(8,128)(2,1)} %collective-permute-done.8.refs_0_.refs_4_), channel_id=1, source_target_pairs={{0,1},{1,0},{2,3},{3,2},{4,5},{5,4},{6,7},{7,6}} | collective-permute-start | bytes 3145736 | tf_op jit(solution)/shard_map/ppermute | solution.py:610
  139.8 4.5 %collective-permute-start.13 = (bf16[256,2048]{1,0:T(8,128)(2,1)}, bf16[256,2048]{1,0:T(8,128)(2,1)}, u32[]{:S(2)}, u32[]{:S(2)}) collective-permute-start(bf16[256,2048]{1,0:T(8,128)(2,1)} %collective-permute-done.9.refs_2_.refs_10_), channel_id=1, source_target_pairs={{0,1},{1,0},{2,3},{3,2},{4,5},{5,4},{6,7},{7,6}} | collective-permute-start | bytes 3145736 | tf_op jit(solution)/shard_map/ppermute | solution.py:610
  140.3 37.3 %collective-permute-start.7 = (bf16[1024,1024]{1,0:T(8,128)(2,1)}, bf16[1024,1024]{1,0:T(8,128)(2,1)}, u32[]{:S(2)}, u32[]{:S(2)}) collective-permute-start(bf16[1024,1024]{1,0:T(8,128)(2,1)} %get-tuple-element.45.o_mine.refs_0_), channel_id=1, source_target_pairs={{0,1},{1,0},{2,3},{3,2},{4,5},{5,4},{6,7},{7,6}} | collective-permute-start | bytes 6291464 | tf_op jit(solution)/shard_map/ppermute | solution.py:610
  140.9 46.6 %collective-permute-start.14 = (bf16[1024,1024]{1,0:T(8,128)(2,1)}, bf16[1024,1024]{1,0:T(8,128)(2,1)}, u32[]{:S(2)}, u32[]{:S(2)}) collective-permute-start(bf16[1024,1024]{1,0:T(8,128)(2,1)} %get-tuple-element.58.q_mine.refs_6_), channel_id=1, source_target_pairs={{0,1},{1,0},{2,3},{3,2},{4,5},{5,4},{6,7},{7,6}} | collective-permute-start | bytes 6291464 | tf_op jit(solution)/shard_map/ppermute | solution.py:610
  141.5 46.5 %collective-permute-start.16 = (bf16[512,1024]{1,0:T(8,128)(2,1)}, bf16[512,1024]{1,0:T(8,128)(2,1)}, u32[]{:S(2)}, u32[]{:S(2)}) collective-permute-start(bf16[512,1024]{1,0:T(8,128)(2,1)} %get-tuple-element.61.refs_7_), channel_id=1, source_target_pairs={{0,1},{1,0},{2,3},{3,2},{4,5},{5,4},{6,7},{7,6}} | collective-permute-start | bytes 3145736 | tf_op jit(solution)/shard_map/ppermute | solution.py:610
  177.6 10.4 %collective-permute-start.15 = (bf16[2048,256]{1,0:T(8,128)(2,1)}, bf16[2048,256]{1,0:T(8,128)(2,1)S(1)}, u32[]{:S(2)}, u32[]{:S(2)}) collective-permute-start(bf16[2048,256]{1,0:T(8,128)(2,1)} %get-tuple-element.59.kv_mine.refs_12_), channel_id=1, source_target_pairs={{0,1},{1,0},{2,3},{3,2},{4,5},{5,4},{6,7},{7,6}} | collective-permute-start | bytes 3145736 | tf_op jit(solution)/shard_map/ppermute | solution.py:610
  177.7 9.8 %copy-start.1 = (bf16[1024,512]{1,0:T(8,128)(2,1)S(1)}, bf16[1024,512]{1,0:T(8,128)(2,1)}, u32[]{:S(2)}) copy-start(bf16[1024,512]{1,0:T(8,128)(2,1)} %get-tuple-element.67.refs_2_) | copy-start | bytes 3145732
  177.8 10.2 %collective-permute-start.17 = (bf16[512,1024]{1,0:T(8,128)(2,1)}, bf16[512,1024]{1,0:T(8,128)(2,1)}, u32[]{:S(2)}, u32[]{:S(2)}) collective-permute-start(bf16[512,1024]{1,0:T(8,128)(2,1)} %get-tuple-element.62.refs_8_), channel_id=1, source_target_pairs={{0,1},{1,0},{2,3},{3,2},{4,5},{5,4},{6,7},{7,6}} | collective-permute-start | bytes 3145736 | tf_op jit(solution)/shard_map/ppermute | solution.py:610
  178.1 57.3 %collective-permute-start.18 = (bf16[1024,512]{1,0:T(8,128)(2,1)}, bf16[1024,512]{1,0:T(8,128)(2,1)S(1)}, u32[]{:S(2)}, u32[]{:S(2)}) collective-permute-start(bf16[1024,512]{1,0:T(8,128)(2,1)} %get-tuple-element.66.refs_1_), channel_id=1, source_target_pairs={{0,1},{1,0},{2,3},{3,2},{4,5},{5,4},{6,7},{7,6}} | collective-permute-start | bytes 3145736 | tf_op jit(solution)/shard_map/ppermute | solution.py:610
  187.6 47.9 %collective-permute-start.19 = (bf16[1024,512]{1,0:T(8,128)(2,1)S(1)}, bf16[1024,512]{1,0:T(8,128)(2,1)}, u32[]{:S(2)}, u32[]{:S(2)}) collective-permute-start(bf16[1024,512]{1,0:T(8,128)(2,1)S(1)} %copy-done.1), channel_id=1, source_target_pairs={{0,1},{1,0},{2,3},{3,2},{4,5},{5,4},{6,7},{7,6}} | collective-permute-start | bytes 3145736 | tf_op jit(solution)/shard_map/ppermute | solution.py:610
  188.0 1.0 copy-start
  235.5 1.0 copy-start.2

commit v5 on v4

--- a/solution.py
+++ b/solution.py
@@ -14,6 +14,7 @@
 DUO = 512
 HALF = 1024
 SEQ = 2048
+TILE_WQ = 512
 LOW = -3.0e38
 F32 = jnp.float32
 BF16 = jnp.bfloat16
@@ -94,7 +95,7 @@
     )(gather_heads(num, 16), w)
 
 
-def kv_kernel(sc, x_ref, dy_ref, wk_ref, wv_ref, perm_ref, out_ref, w_ref, xa, xb, dya, dyb):
+def kv_kernel(sc, x_ref, dy_ref, wk_ref, wv_ref, perm_ref, out_ref, w_ref, rows_a, rows_b):
     @pl.when(pl.program_id(0) == 0)
     def _():
         for g in range(w_ref.shape[0] // HD):
@@ -110,49 +111,47 @@
 
     @pl.when(pl.program_id(0) == 1 - sc[0])
     def _():
-        xa[...] = x_ref[...]
-        dya[...] = dy_ref[...]
+        rows_a[:BLK, :] = x_ref[...]
+        rows_a[BLK:, :] = dy_ref[...]
 
     @pl.when(pl.program_id(0) == sc[0])
     def _():
-        xb[...] = x_ref[...]
-        dyb[...] = dy_ref[...]
+        rows_b[:BLK, :] = x_ref[...]
+        rows_b[BLK:, :] = dy_ref[...]
 
 
 def project_kv(core, x, dy, wk, wv):
     rows, depth = x.shape
     row = pl.BlockSpec((BLK, depth), lambda i, s: (i, 0))
     fixed = lambda shape: pl.BlockSpec(shape, lambda i, s: (0, 0))
-    half = jax.ShapeDtypeStruct((BLK, depth), BF16)
+    chunk = jax.ShapeDtypeStruct((rows, depth), BF16)
     return pl.pallas_call(
         kv_kernel,
-        out_shape=(jax.ShapeDtypeStruct((rows, DUO), BF16), jax.ShapeDtypeStruct((depth, DUO), BF16), half, half, half, half),
+        out_shape=(jax.ShapeDtypeStruct((rows, DUO), BF16), jax.ShapeDtypeStruct((depth, DUO), BF16), chunk, chunk),
         grid_spec=pltpu.PrefetchScalarGridSpec(
             num_scalar_prefetch=1,
             grid=(rows // BLK,),
             in_specs=[row, row, fixed(wk.shape), fixed(wv.shape), fixed((BLK, BLK))],
-            out_specs=(pl.BlockSpec((BLK, DUO), lambda i, s: (i, 0)), fixed((depth, DUO))) + (fixed((BLK, depth)),) * 4,
+            out_specs=(pl.BlockSpec((BLK, DUO), lambda i, s: (i, 0)), fixed((depth, DUO))) + (fixed((rows, depth)),) * 2,
         ),
         compiler_params=params(),
         cost_estimate=cost(2 * rows * depth * DUO, 8e6),
     )(core, x, dy, wk, wv, gather_heads(2, HD))
 
 
-def attn_kernel(heads, scale, first, final, sc, wq_hbm, wo_hbm, *refs):
+def attn_kernel(heads, scale, first, final, steps, base, sc, wq_hbm, wo_hbm, *refs):
     x_hbm, dy_hbm, kv_refs, refs = refs[:2], refs[2:4], refs[4:12], refs[12:]
     if first:
-        o_ref, dq_ref, dkv_ref = refs[:3]
-        scratch = refs[3:]
+        o_ref, dq_ref, dkv_ref, xt_ref = refs[:4]
+        scratch = refs[4:]
     else:
-        init_ref, o_ref, dq_ref, dkv_ref = refs[:4]
-        scratch = refs[4:]
-    ks, vs, kt, vt, dk, dv, qt, dot_t, qst, dost, s_ref, p_ref, ds_ref, ot, dqt, m_ref, l_ref, wq, wo, xs, dys, w_sem, x_sem, dy_sem = scratch
+        init_ref, o_ref, dq_ref, dkv_ref, xt_ref = refs[:5]
+        scratch = refs[5:]
+    ks, vs, kt, vt, dk, dv, qt, dot_t, qst, dost, s_ref, p_ref, ds_ref, ot, dqt, m_ref, l_ref, ref, wq, wo, xs, dys, w_sem, x_sem, dy_sem = scratch
     step = pl.program_id(0)
-    wide = heads * BLK
     hd = HD
     c2 = scale * math.log2(math.e)
 
-    steps = 2 * x_hbm[0].shape[0] // BLK
     core = pl.multiple_of(sc[24] * heads * hd, heads * hd)
     load_wq, load_wo = [], []
     for n in range(4):
@@ -167,7 +166,7 @@
         src = pl.ds(row * BLK, BLK)
         return (
             pltpu.make_async_copy(x_hbm[piece].at[src, :], xs.at[n % 2], x_sem.at[n % 2]),
-            pltpu.make_async_copy(dy_hbm[piece].at[src, :], dys.at[n % 2], dy_sem.at[n % 2]),
+            pltpu.make_async_copy(dy_hbm[piece].at[pl.ds(base + row * BLK, BLK), :], dys.at[n % 2], dy_sem.at[n % 2]),
         )
 
     @pl.when(step == 0)
@@ -213,6 +212,7 @@
     slot = step % 2
     pltpu.make_async_copy(x_hbm[0].at[0:BLK, :], xs.at[slot], x_sem.at[slot]).wait()
     q = dot(xs[slot], wq[...]).astype(BF16)
+    xt_ref[...] = xs[slot].T
     for h in range(heads):
         qh = q[:, h * hd : (h + 1) * hd]
         qst[h * BLK : (h + 1) * BLK, :] = qh
@@ -232,34 +232,50 @@
 
     b = sc[8 + step]
 
-    def softmax_block(j, masked):
+    def scores(j, h):
         at = pl.ds(pl.multiple_of(j * BLK, BLK), BLK)
+        return at, slice(h * BLK, (h + 1) * BLK), dot(ks[at, :], qt[:, h * BLK : (h + 1) * BLK]) * c2
+
+    def rows_of(t):
+        return t.reshape(BLK // 8, 8, BLK)
+
+    key = lax.broadcasted_iota(jnp.int32, (BLK, BLK), 0)
+    query = lax.broadcasted_iota(jnp.int32, (BLK, BLK), 1)
+    for h in range(heads):
+        at, span, t = scores(b, h)
+        t = jnp.where(key <= query, t, LOW)
+        s_ref[at, span] = t
+        m8 = jnp.max(rows_of(t), axis=0)
+        base = jnp.max(m8, axis=0, keepdims=True)
+        ref[:, span] = base
+        m_ref[:, span] = m8
+        l_ref[:, span] = jnp.sum(jnp.exp2(rows_of(t - base)), axis=0)
+
+    def open_block(j, _):
         for h in range(heads):
-            span = slice(h * BLK, (h + 1) * BLK)
-            t = dot(ks[at, :], qt[:, span]) * c2
-            if masked:
-                key = lax.broadcasted_iota(jnp.int32, (BLK, BLK), 0)
-                query = lax.broadcasted_iota(jnp.int32, (BLK, BLK), 1)
-                t = jnp.where(key <= query, t, LOW)
+            at, span, t = scores(j, h)
             s_ref[at, span] = t
-            m8 = m_ref[:, span]
-            new = jnp.maximum(m8, jnp.max(t.reshape(BLK // 8, 8, BLK), axis=0))
-            e = jnp.exp2(s_ref[at, span].reshape(BLK // 8, 8, BLK) - new[None])
-            l_ref[:, span] = l_ref[:, span] * jnp.exp2(m8 - new) + jnp.sum(e, axis=0)
-            m_ref[:, span] = new
-
-    m_ref[...] = jnp.full((8, wide), LOW, F32)
-    l_ref[...] = jnp.zeros((8, wide), F32)
-
-    def open_block(j, _):
-        softmax_block(j, False)
+            m_ref[:, span] = jnp.maximum(m_ref[:, span], jnp.max(rows_of(t), axis=0))
+            l_ref[:, span] += jnp.sum(jnp.exp2(rows_of(t - ref[:, span])), axis=0)
         return 0
 
     lax.fori_loop(0, b, open_block, 0)
-    softmax_block(b, True)
-    m8 = m_ref[...]
-    top = jnp.max(m8, axis=0, keepdims=True)
-    lse = top + jnp.log2(jnp.sum(l_ref[...] * jnp.exp2(m8 - top), axis=0, keepdims=True))
+
+    @pl.when(jnp.max(m_ref[...] - ref[...]) > 60.0)
+    def _():
+        ref[...] = jnp.max(m_ref[...], axis=0, keepdims=True)
+        l_ref[...] = jnp.zeros_like(l_ref)
+
+        def again(j, _):
+            at = pl.ds(pl.multiple_of(j * BLK, BLK), BLK)
+            for h in range(heads):
+                span = slice(h * BLK, (h + 1) * BLK)
+                l_ref[:, span] += jnp.sum(jnp.exp2(rows_of(s_ref[at, span] - ref[:, span])), axis=0)
+            return 0
+
+        lax.fori_loop(0, b + 1, again, 0)
+
+    lse = ref[...] + jnp.log2(jnp.sum(l_ref[...], axis=0, keepdims=True))
 
     ot[...] = jnp.zeros_like(ot)
 
@@ -309,9 +325,9 @@
                 dkv_ref[out, hd:] = dv[at, :]
 
 
-def attention(sc, wq, wo, x_pieces, dy_pieces, kv_pieces, init, final, scale):
+def attention(sc, wq, wo, x_pieces, dy_pieces, base, kv_pieces, init, final, scale):
     first = init is None
-    rows, width, model = 2 * x_pieces[0].shape[0], wq.shape[1] // 2, wq.shape[0]
+    rows, width, model = 2 * (x_pieces[0].shape[0] - base), wq.shape[1] // 2, wq.shape[0]
     hd = HD
     heads = width // hd
     wide = heads * BLK
@@ -326,17 +342,18 @@
     if not first:
         in_specs.append(full(init.shape))
     return pl.pallas_call(
-        functools.partial(attn_kernel, heads, scale, first, final),
+        functools.partial(attn_kernel, heads, scale, first, final, rows // BLK, base),
         out_shape=(
             jax.ShapeDtypeStruct((width, rows), BF16),
             jax.ShapeDtypeStruct((rows, width), BF16),
             jax.ShapeDtypeStruct((seq, BLK), BF16 if final else F32),
+            jax.ShapeDtypeStruct((model, rows), BF16),
         ),
         grid_spec=pltpu.PrefetchScalarGridSpec(
             num_scalar_prefetch=1,
             grid=(rows // BLK,),
             in_specs=in_specs,
-            out_specs=(o_spec, out_spec, full((seq, BLK))),
+            out_specs=(o_spec, out_spec, full((seq, BLK)), pl.BlockSpec((model, BLK), lambda i, s: (0, s[12 + i]))),
             scratch_shapes=[
                 *[pltpu.VMEM((seq, hd), BF16) for _ in "kv"],
                 *[pltpu.VMEM((hd, seq), BF16) for _ in "kv"],
@@ -348,6 +365,7 @@
                 pltpu.VMEM((BLK, wide), BF16),
                 *[pltpu.VMEM((hd, wide), F32) for _ in "od"],
                 *[pltpu.VMEM((8, wide), F32) for _ in "ml"],
+                pltpu.VMEM((1, wide), F32),
                 pltpu.VMEM((model, width), BF16),
                 pltpu.VMEM((width, model), BF16),
                 *[pltpu.VMEM((2, BLK, model), BF16) for _ in "xd"],
@@ -445,42 +463,29 @@
 
 
 def dwq_kernel(sc, *refs):
-    xs_in, mine, other, kv_in = refs[:6], refs[6:9], refs[9:12], refs[12:14]
-    out_ref, gk_ref, gv_ref, xt, dq, kv, sems = refs[14:]
+    xts, mine, other, kv_in = refs[:3], refs[3:6], refs[6:9], refs[9:11]
+    out_ref, gk_ref, gv_ref, dq, kv, sems = refs[11:]
     g, i = pl.program_id(0), pl.program_id(1)
     tile, core, hd = out_ref.shape[0], sc[0], HD
-    first = piece_copies(core, mine, dq.at[0], sems.at[0], False)
-    later = piece_copies(core, other, dq.at[1], sems.at[1], False)
-    for n, src in enumerate(kv_in):
-        parts = [src.at[at : at + size, :] for at, size in ((0, HALF), (HALF, DUO), (1536, DUO))]
-        later += piece_copies(core, parts, kv.at[:, n * BLK : (n + 1) * BLK], sems.at[1], False)
-
-    @pl.when((g == 0) & (i == 0))
-    def _():
-        for cp in first:
-            cp.start()
-
-    @pl.when((g == 0) & (i == 1))
-    def _():
-        for cp in later:
-            cp.start()
-
-    @pl.when(g == 0)
-    def _():
-        for s, (_, n), x in zip(STARTS, PIECES, xs_in):
-            xt[i, :, s : s + n] = x[...].T
-
-    @pl.when((g == 0) & (i == 0))
-    def _():
-        for cp in first:
-            cp.wait()
-
-    @pl.when((g == 1) & (i == 0))
-    def _():
-        for cp in later:
-            cp.wait()
-
-    acc = dot(xt[i], dq[g])
+    spans = [slice(0, HALF), slice(HALF, HALF + DUO), slice(HALF + DUO, SEQ)]
+    first = [pltpu.make_async_copy(a, dq.at[0, at, :], sems.at[0]) for a, at in zip(mine, spans)]
+    later = [pltpu.make_async_copy(a, dq.at[1, at, :], sems.at[1]) for a, at in zip(other, spans)]
+    later += [
+        pltpu.make_async_copy(a, kv.at[:, n * BLK : (n + 1) * BLK], sems.at[1]) for n, a in enumerate(kv_in)
+    ]
+
+    def when(gg, ii, copies, start):
+        @pl.when((g == gg) & (i == ii))
+        def _():
+            for cp in copies:
+                cp.start() if start else cp.wait()
+
+    when(0, 0, first, True)
+    when(0, 1, later, True)
+    when(0, 0, first, False)
+    when(1, 0, later, False)
+
+    acc = sum(dot(x[...], dq[g, at, :]) for x, at in zip(xts, spans))
     flat = out_ref.reshape(tile * 8, hd)
     for h in range(8):
         flat[pl.ds(h, tile, stride=8), :] = acc[:, h * hd : (h + 1) * hd]
@@ -488,16 +493,15 @@
     @pl.when(g == 1)
     def _():
         k_flat, v_flat = gk_ref.reshape(tile * 2, hd), gv_ref.reshape(tile * 2, hd)
-        both = dot(xt[i], kv[...])
+        both = sum(dot(x[...], kv[at, :]) for x, at in zip(xts, spans))
         for n, head in enumerate((core, 1 - core)):
             k_flat[pl.ds(head, tile, stride=2), :] = both[:, 2 * n * hd : (2 * n + 1) * hd]
             v_flat[pl.ds(head, tile, stride=2), :] = both[:, (2 * n + 1) * hd : (2 * n + 2) * hd]
 
 
-def grad_wq(core, xs, mine, other, kvm, kvo):
-    model, half, tile = xs[0].shape[1], mine[0].shape[1], BLK
+def grad_wq(core, xts, mine, other, kvm, kvo):
+    model, half, tile = xts[0].shape[0], mine[0].shape[1], TILE_WQ
     tiles = model // tile
-    x_specs = [pl.BlockSpec((n, tile), lambda g, i, s: (0, jnp.where(g == 0, i, tiles - 1))) for _, n in PIECES]
     small = pl.BlockSpec((tile, 2, HD), lambda g, i, s: (i * g, 0, 0))
     return pl.pallas_call(
         dwq_kernel,
@@ -509,14 +513,14 @@
         grid_spec=pltpu.PrefetchScalarGridSpec(
             num_scalar_prefetch=1,
             grid=(2, tiles),
-            in_specs=x_specs + [pl.BlockSpec(memory_space=pl.ANY)] * 8,
+            in_specs=[pl.BlockSpec((tile, x.shape[1]), lambda g, i, s: (i, 0)) for x in xts]
+            + [pl.BlockSpec(memory_space=pl.ANY)] * 8,
             out_specs=(
                 pl.BlockSpec((tile, 8, HD), lambda g, i, s: (i, (s[0] + g) % 2, 0)),
                 small,
                 small,
             ),
             scratch_shapes=[
-                pltpu.VMEM((tiles, tile, SEQ), BF16),
                 pltpu.VMEM((2, SEQ, half), BF16),
                 pltpu.VMEM((SEQ, DUO), BF16),
                 pltpu.SemaphoreType.DMA((2,)),
@@ -524,7 +528,7 @@
         ),
         compiler_params=params(2),
         cost_estimate=cost(2 * SEQ * model * (2 * half + DUO), 40e6),
-    )(core, *xs, *mine, *other, kvm, kvo)
+    )(core, *xts, *mine, *other, kvm, kvo)
 
 
 def dwo_kernel(sc, *refs):
@@ -535,7 +539,9 @@
     o_later = piece_copies(sc[0], other, o_all.at[1], sems.at[1], True)
     y_copies = [
         [
-            pltpu.make_async_copy(y.at[:, n * wide : (n + 1) * wide], y_all.at[n, s : s + r, :], sems.at[2 + n])
+            pltpu.make_async_copy(
+                y.at[y.shape[0] - r if r == BLK else 0 :, n * wide : (n + 1) * wide], y_all.at[n, s : s + r, :], sems.at[2 + n]
+            )
             for y, s, (_, r) in zip(ys, STARTS, PIECES)
         ]
         for n in range(2)
@@ -616,35 +622,33 @@
         x_p = to_core(x)
         dy_p = to_core(dy)
 
-        kv, wkv, x_a, x_b, dy_a, dy_b = project_kv(core, x, dy, wk, wv)
+        kv, wkv, r_a, r_b = project_kv(core, x, dy, wk, wv)
         far_kv, kv_p = to_chip(kv), to_core(kv)
         w_s, _ = lax.optimization_barrier((w_query, kv))
-        x_a, dy_a = to_chip(x_a), to_chip(dy_a)
-        x_b, dy_b = to_chip(x_b), to_chip(dy_b)
+        r_a, r_b = to_chip(r_a), to_chip(r_b)
         wq = flat_heads(w_s)
         kv_r, wq = lax.optimization_barrier((far_kv, wq))
         kv_rp = to_core(kv_r)
         pieces = (kv, kv_p, kv_r, kv_rp)
 
-        o_c, dq_c, part = attention(
-            sc_chip, wq, wo, (x, x_p), (dy, dy_p), pieces, None, False, scale)
-        x_a, dy_a, o_c, dq_c = lax.optimization_barrier((x_a, dy_a, o_c, dq_c))
-        x_pa, dy_pa, o_co, dq_co = to_core(x_a), to_core(dy_a), to_core(o_c), to_core(dq_c)
-
-        o_a, dq_a, part = attention(sc_a, wq, wo, (x_a, x_pa), (dy_a, dy_pa), pieces, part, False, scale)
-        x_b, dy_b, o_a, dq_a = lax.optimization_barrier((x_b, dy_b, o_a, dq_a))
-        x_pb, dy_pb, o_ao, dq_ao = to_core(x_b), to_core(dy_b), to_core(o_a), to_core(dq_a)
-
-        o_b, dq_b, dkv = attention(sc_b, wq, wo, (x_b, x_pb), (dy_b, dy_pb), pieces, part, True, scale)
+        o_c, dq_c, part, xt_c = attention(
+            sc_chip, wq, wo, (x, x_p), (dy, dy_p), 0, pieces, None, False, scale)
+        r_a, o_c, dq_c = lax.optimization_barrier((r_a, o_c, dq_c))
+        r_pa, o_co, dq_co = to_core(r_a), to_core(o_c), to_core(dq_c)
+
+        o_a, dq_a, part, xt_a = attention(sc_a, wq, wo, (r_a, r_pa), (r_a, r_pa), BLK, pieces, part, False, scale)
+        r_b, o_a, dq_a = lax.optimization_barrier((r_b, o_a, dq_a))
+        r_pb, o_ao, dq_ao = to_core(r_b), to_core(o_a), to_core(dq_a)
+
+        o_b, dq_b, dkv, xt_b = attention(sc_b, wq, wo, (r_b, r_pb), (r_b, r_pb), BLK, pieces, part, True, scale)
         o_co, dkv = lax.optimization_barrier((o_co, dkv))
         dkv_o, o_bo, dq_bo = to_core(dkv), to_core(o_b), to_core(dq_b)
         y = out_rows(core, o_c, o_co, wo)
 
-        xs = (x, x_p, x_a, x_pa, x_b, x_pb)
-        ys = (dy, dy_p, dy_a, dy_pa, dy_b, dy_pb)
+        ys = (dy, dy_p, r_a, r_pa, r_b, r_pb)
         gwo = grad_wo(core, ys, (o_c, o_a, o_b), (o_co, o_ao, o_bo))
         dx = grad_rows(core, dq_c, dq_co, dkv, dkv_o, wq, wkv)
-        gwq, gwk, gwv = grad_wq(core, xs, (dq_c, dq_a, dq_b), (dq_co, dq_ao, dq_bo), dkv, dkv_o)
+        gwq, gwk, gwv = grad_wq(core, (xt_c, xt_a, xt_b), (dq_c, dq_a, dq_b), (dq_co, dq_ao, dq_bo), dkv, dkv_o)
         return y, dx, gwq, gwk, gwv, gwo.reshape(num_heads, hd, model)
 
     return jax.shard_map(

time: 261 us -> 252 us (0.966)
  Pallas kernels: 229 us -> 219 us
  waiting for transfers between devices: 13.9 us -> 17 us
    pallas_call x1, Pallas kernels: 36.1 us -> 30.9 us  [grad_wq(): pl.pallas_call(dwq_kernel, out_shape=(jax.ShapeDtypeStruct((model, 16, HD...]
    pallas_call x3, Pallas kernels: 134 us -> 129 us  [attention(): pl.pallas_call(functools.partial(attn_kernel, heads, scale, first, final,...]
    ppermute x15 -> x13, waiting for transfers between devices: 4.25 us -> 5.99 us  [device_layer(): to_core = lambda v: lax.ppermute(v, 'cp', core_swap)]
    ppermute x5 -> x3, starting transfers between devices: 7 us -> 5.27 us  [device_layer(): to_chip = lambda v: lax.ppermute(v, 'cp', chip_swap)]
    ppermute x5 -> x3, waiting for transfers between devices: 9.65 us -> 11 us  [device_layer(): to_chip = lambda v: lax.ppermute(v, 'cp', chip_swap)]
  transfers between devices with their start and end apart: 20 -> 16, of which waited for: 5 -> 4; matrix products, arithmetic and copies ran while one was open for 1% -> 1% of each run, Pallas kernels for 78% -> 75%
where the time goes in v5:
time: 252 us
  Pallas kernels  219 us (87%)
  waiting for transfers between devices  17 us (7%)
  starting transfers between devices  8.55 us (3%)
  local copies, waits for them, and re-layouts  4.59 us (2%)
    pallas_call x3, Pallas kernels, attention(): pl.pallas_call(functools.partial(attn_kernel, heads, scale, first, final,...  129 us
    pallas_call x1, Pallas kernels, grad_wq(): pl.pallas_call(dwq_kernel, out_shape=(jax.ShapeDtypeStruct((model, 16, HD...  30.9 us
    pallas_call x1, Pallas kernels, grad_wo(): pl.pallas_call(dwo_kernel, out_shape=jax.ShapeDtypeStruct((2 * half, mode...  24.3 us
    ppermute x3, waiting for transfers between devices, device_layer(): to_chip = lambda v: lax.ppermute(v, 'cp', chip_swap)  11 us
    pallas_call x1, Pallas kernels, grad_rows(): pl.pallas_call(dx_kernel, out_shape=jax.ShapeDtypeStruct((rows, model), B...  10.3 us
    pallas_call x1, Pallas kernels, out_rows(): pl.pallas_call(y_kernel, out_shape=jax.ShapeDtypeStruct((rows, model), BF...  9.3 us
    pallas_call x1, Pallas kernels, flat_heads(): pl.pallas_call(heads_kernel, out_shape=jax.ShapeDtypeStruct((model, num *...  7.78 us
    pallas_call x1, Pallas kernels, project_kv(): pl.pallas_call(kv_kernel, out_shape=(jax.ShapeDtypeStruct((rows, DUO), BF...  7.4 us
  transfers between devices with their start and end apart: 16, of which 4 were waited for; matrix products, arithmetic and copies ran while one was open for 1% of the time, Pallas kernels for 75%

profile of v5, /device:TPU:0, one launch (start us, length us, event | category | flops | bytes accessed | tf_op | source)
XLA Modules:
  0.0 252.0 jit_solution(16762782937429047722)
XLA Ops:
  0.6 0.9 collective-permute-start.2
  1.5 0.0 collective-permute-start.3
  1.5 0.8 fusion.perm_ref
  2.3 7.4 %shard_map.109 = (bf16[512,512]{1,0:T(8,128)(2,1)}, bf16[2048,512]{1,0:T(8,128)(2,1)}, bf16[512,2048]{1,0:T(8,128)(2,1)}, bf16[512,2048]{1,0:T(8,128)(2,1)}) custom-call(s32[1]{0:T(128)} %bitcast.sc, bf16[512,2048]{1,0:T(8,128)(2,1)} %refs_0_.1, bf16[512,2048]{1,0:T(8,128)(2,1)} %refs_6_.1, bf16[4096,128]{1,0:T(8,128)(2,1)} %bitcast.31, ...), custom_call_target="tpu_custom_call" | custom-call | flops 1073741824 | bytes 8000000 | tf_op jit(solution)/shard_map/pallas_call | solution.py:128
  9.7 0.5 collective-permute-start.4
  10.2 2.5 collective-permute-start.1
  12.7 0.8 fusion.1.perm_ref
  13.4 7.8 %shard_map.110.wq_hbm.wq_mine.wq_other = bf16[2048,2048]{1,0:T(8,128)(2,1)} custom-call(bf16[256,256]{1,0:T(8,128)(2,1)} %fusion.1.perm_ref, bf16[2048,16,128]{2,1,0:T(8,128)(2,1)} %w_hbm), custom_call_target="tpu_custom_call" | custom-call | flops 4000000000 | bytes 16777216 | tf_op jit(solution)/shard_map/pallas_call | solution.py:82
  21.2 4.2 %collective-permute-done.1.refs_6_.refs_10_ = bf16[512,512]{1,0:T(8,128)(2,1)S(1)} collective-permute-done((bf16[512,512]{1,0:T(8,128)(2,1)}, bf16[512,512]{1,0:T(8,128)(2,1)S(1)}, u32[]{:S(2)}, u32[]{:S(2)}) %collective-permute-start.1) | collective-permute-done | bytes 524320 | tf_op jit(solution)/shard_map/ppermute | solution.py:617
  25.4 0.0 copy-start.3
  25.4 0.0 collective-permute-start.5
  25.4 1.7 collective-permute-start
  27.2 0.6 stack.64.sc
  27.8 0.0 collective-permute-done.4.refs_5_.refs_9_
  27.8 0.0 copy-done.3
  27.8 0.0 copy-start.2
  27.8 0.0 collective-permute-done.5.refs_7_.refs_11_
  27.9 0.0 copy-start.4
  27.9 0.8 copy-done.4
  28.7 0.0 collective-permute-done.2.refs_1_
  28.7 0.0 collective-permute-done.3.refs_3_.refs_7_
  28.7 0.1 copy-done.2
  28.8 59.9 %shard_map.111 = (bf16[1024,1024]{1,0:T(8,128)(2,1)}, bf16[1024,1024]{1,0:T(8,128)(2,1)}, f32[2048,256]{1,0:T(8,128)}, bf16[2048,1024]{1,0:T(8,128)(2,1)}) custom-call(s32[25]{0:T(128)} %stack.64.sc, bf16[2048,2048]{1,0:T(8,128)(2,1)} %shard_map.110.wq_hbm.wq_mine.wq_other, bf16[2048,2048]{1,0:T(8,128)(2,1)} %bitcast.26, bf16[512,2048]{1,0:T(8,128)(2,1)} %refs_0_.1, ...), custom_call_target="tpu_custom_call" | custom-call | flops 32000000000 | bytes 20000000 | tf_op jit(solution)/shard_map/pallas_call | solution.py:344
  88.7 0.0 collective-permute-done.refs_0_.refs_2_.refs_8_
  88.7 0.3 collective-permute-start.8
  89.0 1.0 collective-permute-start.7
  90.0 0.6 stack.71.sc
  90.6 2.6 %collective-permute-done.8.refs_1_.refs_3_.refs_9_ = bf16[512,2048]{1,0:T(8,128)(2,1)} collective-permute-done((bf16[512,2048]{1,0:T(8,128)(2,1)}, bf16[512,2048]{1,0:T(8,128)(2,1)}, u32[]{:S(2)}, u32[]{:S(2)}) %collective-permute-start.8) | collective-permute-done | bytes 2097184 | tf_op jit(solution)/shard_map/ppermute | solution.py:616
  93.2 37.0 %shard_map.112 = (bf16[1024,512]{1,0:T(8,128)(2,1)}, bf16[512,1024]{1,0:T(8,128)(2,1)}, f32[2048,256]{1,0:T(8,128)}, bf16[2048,512]{1,0:T(8,128)(2,1)}) custom-call(s32[25]{0:T(128)} %stack.71.sc, bf16[2048,2048]{1,0:T(8,128)(2,1)} %shard_map.110.wq_hbm.wq_mine.wq_other, bf16[2048,2048]{1,0:T(8,128)(2,1)} %bitcast.27, ...), custom_call_target="tpu_custom_call" | custom-call | flops 16000000000 | bytes 20000000 | tf_op jit(solution)/shard_map/pallas_call | solution.py:344
  130.3 6.8 %collective-permute-done.7.refs_0_.refs_2_.refs_10_ = bf16[512,2048]{1,0:T(8,128)(2,1)} collective-permute-done((bf16[512,2048]{1,0:T(8,128)(2,1)}, bf16[512,2048]{1,0:T(8,128)(2,1)}, u32[]{:S(2)}, u32[]{:S(2)}) %collective-permute-start.7) | collective-permute-done | bytes 2097184 | tf_op jit(solution)/shard_map/ppermute | solution.py:617
  137.1 0.0 collective-permute-start.9
  137.1 0.6 stack.68.sc
  137.7 0.5 collective-permute-start.6
  138.2 0.0 collective-permute-start.14
  138.2 3.4 %collective-permute-done.9.refs_1_.refs_3_.refs_11_ = bf16[512,2048]{1,0:T(8,128)(2,1)} collective-permute-done((bf16[512,2048]{1,0:T(8,128)(2,1)}, bf16[512,2048]{1,0:T(8,128)(2,1)}, u32[]{:S(2)}, u32[]{:S(2)}) %collective-permute-start.9) | collective-permute-done | bytes 2097184 | tf_op jit(solution)/shard_map/ppermute | solution.py:616
  141.6 32.5 %shard_map.113 = (bf16[1024,512]{1,0:T(8,128)(2,1)}, bf16[512,1024]{1,0:T(8,128)(2,1)}, bf16[2048,256]{1,0:T(8,128)(2,1)}, bf16[2048,512]{1,0:T(8,128)(2,1)}) custom-call(s32[25]{0:T(128)} %stack.68.sc, bf16[2048,2048]{1,0:T(8,128)(2,1)} %shard_map.110.wq_hbm.wq_mine.wq_other, bf16[2048,2048]{1,0:T(8,128)(2,1)} %bitcast.28, ...), custom_call_target="tpu_custom_call" | custom-call | flops 16000000000 | bytes 20000000 | tf_op jit(solution)/shard_map/pallas_call | solution.py:344
  174.1 0.1 collective-permute-start.15
  174.2 0.4 collective-permute-start.10
  174.6 0.1 collective-permute-start.12
  174.7 0.0 collective-permute-done.6.o_other.refs_3_
  174.7 0.4 collective-permute-start.11
  175.1 9.3 %shard_map.114 = bf16[512,2048]{1,0:T(8,128)(2,1)} custom-call(s32[1]{0:T(128)} %bitcast.sc, bf16[1024,1024]{1,0:T(8,128)(2,1)} %get-tuple-element.43.o_mine.refs_0_, bf16[1024,1024]{1,0:T(8,128)(2,1)} %collective-permute-done.6.o_other.refs_3_, bf16[2048,2048]{1,0:T(8,128)(2,1)} %bitcast.29, bf16[2048,2048]{1,0:T(8,128)(2,1)} %bitcast.30), custom_call_target="tpu_custom_call" | custom-call | flops 4294967296 | bytes 12000000 | tf_op jit(solution)/shard_map/pallas_call | solution.py:393
  184.4 0.0 collective-permute-done.14.refs_4_
  184.4 0.1 collective-permute-start.13
  184.5 0.0 collective-permute-done.15.refs_5_
  184.5 24.3 %shard_map.117 = f32[2048,2048]{1,0:T(8,128)} custom-call(s32[1]{0:T(128)} %bitcast.sc, bf16[1024,1024]{1,0:T(8,128)(2,1)} %get-tuple-element.43.o_mine.refs_0_, bf16[1024,512]{1,0:T(8,128)(2,1)} %get-tuple-element.64.refs_1_, bf16[1024,512]{1,0:T(8,128)(2,1)} %get-tuple-element.65.refs_2_, bf16[1024,1024]{1,0:T(8,128)(2,1)} %collective-permute-done.6.o_other.refs_3_, ...), custom_call_target="tpu_custom_call" | custom-call | flops 17179869184 | bytes 40000000 | tf_op jit(solution)/shard_map/pallas_call | solution.py:568
  208.8 0.0 collective-permute-done.10.q_other.refs_6_
  208.8 0.0 copy-start
  208.8 0.0 collective-permute-done.11.kv_other.refs_10_
  208.8 0.0 copy-start.1
  208.8 1.3 copy-done
  210.2 0.4 copy-done.1
  210.6 10.3 %shard_map.115 = bf16[512,2048]{1,0:T(8,128)(2,1)} custom-call(s32[1]{0:T(128)} %bitcast.sc, bf16[1024,1024]{1,0:T(8,128)(2,1)} %get-tuple-element.53.q_mine.refs_3_, bf16[1024,1024]{1,0:T(8,128)(2,1)} %copy-done, bf16[2048,256]{1,0:T(8,128)(2,1)} %get-tuple-element.54.kv_mine.refs_9_, bf16[2048,256]{1,0:T(8,128)(2,1)} %copy-done.1, ...), custom_call_target="tpu_custom_call" | custom-call | flops 5368709120 | bytes 14000000 | tf_op jit(solution)/shard_map/pallas_call | solution.py:430
  220.9 0.0 collective-permute-done.12.refs_7_
  220.9 0.0 collective-permute-done.13.refs_8_
  220.9 30.9 %shard_map.116 = (f32[2048,16,128]{2,1,0:T(8,128)}, f32[2048,2,128]{2,1,0:T(2,128)}, f32[2048,2,128]{2,1,0:T(2,128)}) custom-call(s32[1]{0:T(128)} %bitcast.sc, bf16[2048,1024]{1,0:T(8,128)(2,1)} %get-tuple-element.56.refs_0_, bf16[2048,512]{1,0:T(8,128)(2,1)} %get-tuple-element.57.refs_1_, bf16[2048,512]{1,0:T(8,128)(2,1)} %get-tuple-element.58.refs_2_, ...), custom_call_target="tpu_custom_call" | custom-call | flops 21474836480 | bytes 40000000 | tf_op jit(solution)/shard_map/pallas_call | solution.py:506
  (2 shorter events, 0.0 us)
Async XLA Ops:
  0.6 28.1 %collective-permute-start.2 = (bf16[512,2048]{1,0:T(8,128)(2,1)}, bf16[512,2048]{1,0:T(8,128)(2,1)}, u32[]{:S(2)}, u32[]{:S(2)}) collective-permute-start(bf16[512,2048]{1,0:T(8,128)(2,1)} %refs_0_.1), channel_id=1, source_target_pairs={{0,1},{1,0},{2,3},{3,2},{4,5},{5,4},{6,7},{7,6}} | collective-permute-start | bytes 6291464 | tf_op jit(solution)/shard_map/ppermute | solution.py:616
  1.5 27.2 %collective-permute-start.3 = (bf16[512,2048]{1,0:T(8,128)(2,1)}, bf16[512,2048]{1,0:T(8,128)(2,1)}, u32[]{:S(2)}, u32[]{:S(2)}) collective-permute-start(bf16[512,2048]{1,0:T(8,128)(2,1)} %refs_6_.1), channel_id=1, source_target_pairs={{0,1},{1,0},{2,3},{3,2},{4,5},{5,4},{6,7},{7,6}} | collective-permute-start | bytes 6291464 | tf_op jit(solution)/shard_map/ppermute | solution.py:616
  9.7 18.2 %collective-permute-start.4 = (bf16[512,512]{1,0:T(8,128)(2,1)}, bf16[512,512]{1,0:T(8,128)(2,1)S(1)}, u32[]{:S(2)}, u32[]{:S(2)}) collective-permute-start(bf16[512,512]{1,0:T(8,128)(2,1)} %get-tuple-element.37.refs_4_.refs_8_), channel_id=1, source_target_pairs={{0,1},{1,0},{2,3},{3,2},{4,5},{5,4},{6,7},{7,6}} | collective-permute-start | bytes 1572872 | tf_op jit(solution)/shard_map/ppermute | solution.py:616
  10.2 15.3 %collective-permute-start.1 = (bf16[512,512]{1,0:T(8,128)(2,1)}, bf16[512,512]{1,0:T(8,128)(2,1)S(1)}, u32[]{:S(2)}, u32[]{:S(2)}) collective-permute-start(bf16[512,512]{1,0:T(8,128)(2,1)} %get-tuple-element.37.refs_4_.refs_8_), channel_id=1, source_target_pairs={{0,2},{2,0},{1,3},{3,1},{4,6},{6,4},{5,7},{7,5}} | collective-permute-start | bytes 1572872 | tf_op jit(solution)/shard_map/ppermute | solution.py:617
  25.4 2.4 copy-start.3
  25.4 2.4 collective-permute-start.5
  25.4 63.3 %collective-permute-start = (bf16[512,2048]{1,0:T(8,128)(2,1)}, bf16[512,2048]{1,0:T(8,128)(2,1)}, u32[]{:S(2)}, u32[]{:S(2)}) collective-permute-start(bf16[512,2048]{1,0:T(8,128)(2,1)} %get-tuple-element.36), channel_id=1, source_target_pairs={{0,2},{2,0},{1,3},{3,1},{4,6},{6,4},{5,7},{7,5}} | collective-permute-start | bytes 6291464 | tf_op jit(solution)/shard_map/ppermute | solution.py:617
  27.8 1.0 copy-start.2
  27.9 0.8 copy-start.4
  88.7 4.5 %collective-permute-start.8 = (bf16[512,2048]{1,0:T(8,128)(2,1)}, bf16[512,2048]{1,0:T(8,128)(2,1)}, u32[]{:S(2)}, u32[]{:S(2)}) collective-permute-start(bf16[512,2048]{1,0:T(8,128)(2,1)} %collective-permute-done.refs_0_.refs_2_.refs_8_), channel_id=1, source_target_pairs={{0,1},{1,0},{2,3},{3,2},{4,5},{5,4},{6,7},{7,6}} | collective-permute-start | bytes 6291464 | tf_op jit(solution)/shard_map/ppermute | solution.py:616
  89.0 48.1 %collective-permute-start.7 = (bf16[512,2048]{1,0:T(8,128)(2,1)}, bf16[512,2048]{1,0:T(8,128)(2,1)}, u32[]{:S(2)}, u32[]{:S(2)}) collective-permute-start(bf16[512,2048]{1,0:T(8,128)(2,1)} %get-tuple-element.44), channel_id=1, source_target_pairs={{0,2},{2,0},{1,3},{3,1},{4,6},{6,4},{5,7},{7,5}} | collective-permute-start | bytes 6291464 | tf_op jit(solution)/shard_map/ppermute | solution.py:617
  137.1 4.5 %collective-permute-start.9 = (bf16[512,2048]{1,0:T(8,128)(2,1)}, bf16[512,2048]{1,0:T(8,128)(2,1)}, u32[]{:S(2)}, u32[]{:S(2)}) collective-permute-start(bf16[512,2048]{1,0:T(8,128)(2,1)} %collective-permute-done.7.refs_0_.refs_2_.refs_10_), channel_id=1, source_target_pairs={{0,1},{1,0},{2,3},{3,2},{4,5},{5,4},{6,7},{7,6}} | collective-permute-start | bytes 6291464 | tf_op jit(solution)/shard_map/ppermute | solution.py:616
  137.7 37.0 %collective-permute-start.6 = (bf16[1024,1024]{1,0:T(8,128)(2,1)}, bf16[1024,1024]{1,0:T(8,128)(2,1)}, u32[]{:S(2)}, u32[]{:S(2)}) collective-permute-start(bf16[1024,1024]{1,0:T(8,128)(2,1)} %get-tuple-element.43.o_mine.refs_0_), channel_id=1, source_target_pairs={{0,1},{1,0},{2,3},{3,2},{4,5},{5,4},{6,7},{7,6}} | collective-permute-start | bytes 6291464 | tf_op jit(solution)/shard_map/ppermute | solution.py:616
  138.2 46.2 %collective-permute-start.14 = (bf16[1024,512]{1,0:T(8,128)(2,1)}, bf16[1024,512]{1,0:T(8,128)(2,1)}, u32[]{:S(2)}, u32[]{:S(2)}) collective-permute-start(bf16[1024,512]{1,0:T(8,128)(2,1)} %get-tuple-element.64.refs_1_), channel_id=1, source_target_pairs={{0,1},{1,0},{2,3},{3,2},{4,5},{5,4},{6,7},{7,6}} | collective-permute-start | bytes 3145736 | tf_op jit(solution)/shard_map/ppermute | solution.py:616
  174.1 10.4 %collective-permute-start.15 = (bf16[1024,512]{1,0:T(8,128)(2,1)}, bf16[1024,512]{1,0:T(8,128)(2,1)}, u32[]{:S(2)}, u32[]{:S(2)}) collective-permute-start(bf16[1024,512]{1,0:T(8,128)(2,1)} %get-tuple-element.65.refs_2_), channel_id=1, source_target_pairs={{0,1},{1,0},{2,3},{3,2},{4,5},{5,4},{6,7},{7,6}} | collective-permute-start | bytes 3145736 | tf_op jit(solution)/shard_map/ppermute | solution.py:616
  174.2 34.6 %collective-permute-start.10 = (bf16[1024,1024]{1,0:T(8,128)(2,1)}, bf16[1024,1024]{1,0:T(8,128)(2,1)S(1)}, u32[]{:S(2)}, u32[]{:S(2)}) collective-permute-start(bf16[1024,1024]{1,0:T(8,128)(2,1)} %get-tuple-element.53.q_mine.refs_3_), channel_id=1, source_target_pairs={{0,1},{1,0},{2,3},{3,2},{4,5},{5,4},{6,7},{7,6}} | collective-permute-start | bytes 6291464 | tf_op jit(solution)/shard_map/ppermute | solution.py:616
  174.6 46.3 %collective-permute-start.12 = (bf16[512,1024]{1,0:T(8,128)(2,1)}, bf16[512,1024]{1,0:T(8,128)(2,1)}, u32[]{:S(2)}, u32[]{:S(2)}) collective-permute-start(bf16[512,1024]{1,0:T(8,128)(2,1)} %get-tuple-element.59.refs_4_), channel_id=1, source_target_pairs={{0,1},{1,0},{2,3},{3,2},{4,5},{5,4},{6,7},{7,6}} | collective-permute-start | bytes 3145736 | tf_op jit(solution)/shard_map/ppermute | solution.py:616
  174.7 34.1 %collective-permute-start.11 = (bf16[2048,256]{1,0:T(8,128)(2,1)}, bf16[2048,256]{1,0:T(8,128)(2,1)S(1)}, u32[]{:S(2)}, u32[]{:S(2)}) collective-permute-start(bf16[2048,256]{1,0:T(8,128)(2,1)} %get-tuple-element.54.kv_mine.refs_9_), channel_id=1, source_target_pairs={{0,1},{1,0},{2,3},{3,2},{4,5},{5,4},{6,7},{7,6}} | collective-permute-start | bytes 3145736 | tf_op jit(solution)/shard_map/ppermute | solution.py:616
  184.4 36.5 %collective-permute-start.13 = (bf16[512,1024]{1,0:T(8,128)(2,1)}, bf16[512,1024]{1,0:T(8,128)(2,1)}, u32[]{:S(2)}, u32[]{:S(2)}) collective-permute-start(bf16[512,1024]{1,0:T(8,128)(2,1)} %get-tuple-element.60.refs_5_), channel_id=1, source_target_pairs={{0,1},{1,0},{2,3},{3,2},{4,5},{5,4},{6,7},{7,6}} | collective-permute-start | bytes 3145736 | tf_op jit(solution)/shard_map/ppermute | solution.py:616
  208.8 1.3 copy-start
  208.8 1.7 copy-start.1

commit v6 on v5

--- a/solution.py
+++ b/solution.py
@@ -3,6 +3,7 @@
 
 import jax
 import jax.numpy as jnp
+import numpy as np
 from jax import lax
 from jax.experimental import pallas as pl
 from jax.experimental.pallas import tpu as pltpu
@@ -71,8 +72,8 @@
 
 
 def gather_heads(num, rows):
-    row = jnp.arange(num * rows)
-    return ((row % rows * num + row // rows)[:, None] == row[None, :]).astype(BF16)
+    row = np.arange(num * rows)
+    return jnp.asarray((row % rows * num + row // rows)[:, None] == row[None, :], BF16)
 
 
 def flat_heads(w):
@@ -139,20 +140,54 @@
     )(core, x, dy, wk, wv, gather_heads(2, HD))
 
 
-def attn_kernel(heads, scale, first, final, steps, base, sc, wq_hbm, wo_hbm, *refs):
-    x_hbm, dy_hbm, kv_refs, refs = refs[:2], refs[2:4], refs[4:12], refs[12:]
+def ranks(rank):
+    return rank, rank + 1 - rank % 2 * 2, (rank + 2) % 4, 3 - rank
+
+
+def block_at(kind, rank, i):
+    own, pair, far, far_pair = ranks(rank)
+    if kind == "near":
+        e = jnp.where(i < 2, own, pair)
+        return jnp.where(i % 2 == 0, e, 7 - e)
+    e = jnp.where(i == 0, far, far_pair)
+    return jnp.where(e % 2 == (1 if kind == "a" else 0), e, 7 - e)
+
+
+def slot_at(kind, rank, i):
+    if kind == "near":
+        return (rank + i // 2) % 2 * 2 + i % 2
+    return (rank + i) % 2
+
+
+def attn_kernel(kind, heads, scale, steps, base, sc, wq_hbm, wo_hbm, *refs):
+    x_hbm, dy_hbm, kv_hbm, refs = refs[:2], refs[2:4], refs[4:8], refs[8:]
+    first, final = kind == "near", kind == "b"
     if first:
         o_ref, dq_ref, dkv_ref, xt_ref = refs[:4]
         scratch = refs[4:]
     else:
-        init_ref, o_ref, dq_ref, dkv_ref, xt_ref = refs[:5]
+        init_hbm, o_ref, dq_ref, dkv_ref, xt_ref = refs[:5]
         scratch = refs[5:]
-    ks, vs, kt, vt, dk, dv, qt, dot_t, qst, dost, s_ref, p_ref, ds_ref, ot, dqt, m_ref, l_ref, ref, wq, wo, xs, dys, w_sem, x_sem, dy_sem = scratch
+    ks, vs, kt, vt, dk, dv, qt, dot_t, qst, dost, s_ref, p_ref, ds_ref, ot, dqt, m_ref, l_ref, ref, wq, wo, xs, dys, w_sem, x_sem, dy_sem, g_sem = scratch
     step = pl.program_id(0)
     hd = HD
     c2 = scale * math.log2(math.e)
 
-    core = pl.multiple_of(sc[24] * heads * hd, heads * hd)
+    rank = sc[0]
+    pos = [p for e in ranks(rank) for p in (e, 7 - e)]
+    core = pl.multiple_of(rank % 2 * heads * hd, heads * hd)
+    load_kv = []
+    for n, p in enumerate(pos):
+        src = kv_hbm[n // 2].at[n % 2 * BLK : (n % 2 + 1) * BLK, :]
+        at = pl.ds(pl.multiple_of(p * BLK, BLK), BLK)
+        for v, dst in enumerate((ks, vs)):
+            col = pl.ds(pl.multiple_of((2 * v + rank % 2) * hd, hd), hd)
+            load_kv.append(pltpu.make_async_copy(src.at[:, col], dst.at[at, :], g_sem.at[0]))
+
+    def grads(hbm, out):
+        pairs = [(hbm.at[:, :hd], dk), (hbm.at[:, hd:], dv)]
+        return [pltpu.make_async_copy(*(p[::-1] if out else p), g_sem.at[1]) for p in pairs]
+
     load_wq, load_wo = [], []
     for n in range(4):
         span = slice(n * DUO, (n + 1) * DUO)
@@ -172,12 +207,16 @@
     @pl.when(step == 0)
     def _():
         load_x, load_dy = load_rows(0)
+        for cp in load_kv:
+            cp.start()
         load_x.start()
         for cp in load_wq:
             cp.start()
         load_dy.start()
         for cp in load_wo:
             cp.start()
+        for cp in [] if first else grads(init_hbm, False):
+            cp.start()
 
     for n in range(1, steps):
 
@@ -188,21 +227,15 @@
 
     @pl.when(step == 0)
     def _():
+        if first:
+            dk[...] = jnp.zeros_like(dk)
+            dv[...] = jnp.zeros_like(dv)
+        for cp in load_kv:
+            cp.wait()
         for i in range(8):
-            rows = slice((i % 2) * BLK, (i % 2 + 1) * BLK)
-            at = pl.ds(pl.multiple_of(sc[i] * BLK, BLK), BLK)
-            kk, vv = kv_refs[i // 2][rows, :], kv_refs[4 + i // 2][rows, :]
-            ks[at, :] = kk
-            vs[at, :] = vv
-            kt[:, at] = kk.T
-            vt[:, at] = vv.T
-            if not first:
-                init_rows = slice(i * BLK, (i + 1) * BLK)
-                dk[at, :] = init_ref[init_rows, :hd]
-                dv[at, :] = init_ref[init_rows, hd:]
-            else:
-                dk[at, :] = jnp.zeros((BLK, hd), F32)
-                dv[at, :] = jnp.zeros((BLK, hd), F32)
+            at = slice(i * BLK, (i + 1) * BLK)
+            kt[:, at] = ks[at, :].T
+            vt[:, at] = vs[at, :].T
 
     @pl.when(step == 0)
     def _():
@@ -230,7 +263,7 @@
         dost[h * BLK : (h + 1) * BLK, :] = dh
         dot_t[:, h * BLK : (h + 1) * BLK] = dh.T
 
-    b = sc[8 + step]
+    b = block_at(kind, rank, step)
 
     def scores(j, h):
         at = pl.ds(pl.multiple_of(j * BLK, BLK), BLK)
@@ -306,43 +339,52 @@
         dk[at, :] += dot(ds_ref[...], qst[...])
         return 0
 
+    if not first:
+
+        @pl.when(step == 0)
+        def _():
+            for cp in grads(init_hbm, False):
+                cp.wait()
+
     lax.fori_loop(0, b + 1, grad_block, 0)
 
     for h in range(heads):
         dq_ref[:, h * hd : (h + 1) * hd] = (dqt[:, h * BLK : (h + 1) * BLK] * scale).astype(BF16).T
 
-    @pl.when(step == pl.num_programs(0) - 1)
-    def _():
-        for i in range(8):
-            at = pl.ds(pl.multiple_of(sc[i] * BLK, BLK), BLK)
-            if final:
-                out = pl.ds(pl.multiple_of(sc[16 + i] * BLK, BLK), BLK)
+    @pl.when(step == steps - 1)
+    def _():
+        if not final:
+            for cp in grads(dkv_ref, True):
+                cp.start()
+            for cp in grads(dkv_ref, True):
+                cp.wait()
+        else:
+            for n, (p, e) in enumerate(zip(pos, [e for e in ranks(rank) for _ in "ab"])):
+                at = pl.ds(pl.multiple_of(p * BLK, BLK), BLK)
+                if n < 4:
+                    row = e % 2 * 2 + n % 2
+                else:
+                    row = jnp.where((e + n) % 2 == 1, 4, 6) + e % 2
+                out = pl.ds(pl.multiple_of(row * BLK, BLK), BLK)
                 dkv_ref[out, :hd] = (dk[at, :] * scale).astype(BF16)
                 dkv_ref[out, hd:] = dv[at, :].astype(BF16)
-            else:
-                out = slice(i * BLK, (i + 1) * BLK)
-                dkv_ref[out, :hd] = dk[at, :]
-                dkv_ref[out, hd:] = dv[at, :]
-
-
-def attention(sc, wq, wo, x_pieces, dy_pieces, base, kv_pieces, init, final, scale):
-    first = init is None
+
+
+def attention(kind, rank, wq, wo, x_pieces, dy_pieces, base, kv_pieces, init, scale):
+    final = kind == "b"
     rows, width, model = 2 * (x_pieces[0].shape[0] - base), wq.shape[1] // 2, wq.shape[0]
     hd = HD
     heads = width // hd
     wide = heads * BLK
     seq = SEQ
-    o_spec = pl.BlockSpec((width, BLK), lambda i, s: (0, s[12 + i]))
-    out_spec = pl.BlockSpec((BLK, width), lambda i, s: (s[12 + i], 0))
-    full = lambda shape: pl.BlockSpec(shape, lambda i, s: (0, 0), pipeline_mode=pl.Buffered(1))
-    ins = [wq, wo, *x_pieces, *dy_pieces] + list(kv_pieces) * 2 + ([] if first else [init])
-    in_specs = [pl.BlockSpec(memory_space=pl.ANY)] * 6
-    in_specs += [pl.BlockSpec((2 * BLK, hd), lambda i, s: (0, s[24]))] * 4
-    in_specs += [pl.BlockSpec((2 * BLK, hd), lambda i, s: (0, 2 + s[24]))] * 4
-    if not first:
-        in_specs.append(full(init.shape))
+    slot = functools.partial(slot_at, kind)
+    o_spec = pl.BlockSpec((width, BLK), lambda i, s: (0, slot(s[0], i)))
+    out_spec = pl.BlockSpec((BLK, width), lambda i, s: (slot(s[0], i), 0))
+    xt_spec = pl.BlockSpec((model, BLK), lambda i, s: (0, slot(s[0], i)))
+    dkv_spec = pl.BlockSpec((seq, BLK), lambda i, s: (0, 0)) if final else pl.BlockSpec(memory_space=pl.ANY)
+    ins = [wq, wo, *x_pieces, *dy_pieces, *kv_pieces] + ([] if init is None else [init])
     return pl.pallas_call(
-        functools.partial(attn_kernel, heads, scale, first, final, rows // BLK, base),
+        functools.partial(attn_kernel, kind, heads, scale, rows // BLK, base),
         out_shape=(
             jax.ShapeDtypeStruct((width, rows), BF16),
             jax.ShapeDtypeStruct((rows, width), BF16),
@@ -352,8 +394,8 @@
         grid_spec=pltpu.PrefetchScalarGridSpec(
             num_scalar_prefetch=1,
             grid=(rows // BLK,),
-            in_specs=in_specs,
-            out_specs=(o_spec, out_spec, full((seq, BLK)), pl.BlockSpec((model, BLK), lambda i, s: (0, s[12 + i]))),
+            in_specs=[pl.BlockSpec(memory_space=pl.ANY) for _ in ins],
+            out_specs=(o_spec, out_spec, dkv_spec, xt_spec),
             scratch_shapes=[
                 *[pltpu.VMEM((seq, hd), BF16) for _ in "kv"],
                 *[pltpu.VMEM((hd, seq), BF16) for _ in "kv"],
@@ -369,12 +411,12 @@
                 pltpu.VMEM((model, width), BF16),
                 pltpu.VMEM((width, model), BF16),
                 *[pltpu.VMEM((2, BLK, model), BF16) for _ in "xd"],
-                *[pltpu.SemaphoreType.DMA((2,)) for _ in "wxd"],
+                *[pltpu.SemaphoreType.DMA((2,)) for _ in "wxdg"],
             ],
         ),
         compiler_params=params(1, 63),
         cost_estimate=cost(8e9 * (rows // BLK), 20e6),
-    )(sc, *ins)
+    )(rank, *ins)
 
 
 def y_kernel(sc, o_mine, o_other, w_mine, w_other, out_ref, os):
@@ -599,19 +641,7 @@
         rank = lax.axis_index("cp").astype(jnp.int32)
         c = rank & 1
         core = c.reshape(1)
-        devs = [rank, rank ^ 1, rank ^ 2, rank ^ 3]
-        kv_pos = [p for e in devs for p in (e, 7 - e)]
-        own_slots = [p for e in devs[:2] for p in ((e & 1) * 2, (e & 1) * 2 + 1)]
-        far_slots = []
-        for e in devs[2:]:
-            far_slots += [jnp.where((e & 1) == 1, 4, 6) + (e & 1), jnp.where((e & 1) == 0, 4, 6) + (e & 1)]
-        pos_a = [jnp.where((e & 1) == 0, 7 - e, e) for e in devs[2:]]
-        pos_b = [jnp.where((e & 1) == 0, e, 7 - e) for e in devs[2:]]
-        far = [c, 1 - c]
-        tail = own_slots + far_slots + [c]
-        sc_chip = jnp.stack(kv_pos + kv_pos[:4] + own_slots + tail)
-        sc_a = jnp.stack(kv_pos + pos_a * 2 + far * 2 + tail)
-        sc_b = jnp.stack(kv_pos + pos_b * 2 + far * 2 + tail)
+        rank = rank.reshape(1)
 
         to_core = lambda v: lax.ppermute(v, "cp", core_swap)
         to_chip = lambda v: lax.ppermute(v, "cp", chip_swap)
@@ -632,15 +662,15 @@
         pieces = (kv, kv_p, kv_r, kv_rp)
 
         o_c, dq_c, part, xt_c = attention(
-            sc_chip, wq, wo, (x, x_p), (dy, dy_p), 0, pieces, None, False, scale)
+            "near", rank, wq, wo, (x, x_p), (dy, dy_p), 0, pieces, None, scale)
         r_a, o_c, dq_c = lax.optimization_barrier((r_a, o_c, dq_c))
         r_pa, o_co, dq_co = to_core(r_a), to_core(o_c), to_core(dq_c)
 
-        o_a, dq_a, part, xt_a = attention(sc_a, wq, wo, (r_a, r_pa), (r_a, r_pa), BLK, pieces, part, False, scale)
+        o_a, dq_a, part, xt_a = attention("a", rank, wq, wo, (r_a, r_pa), (r_a, r_pa), BLK, pieces, part, scale)
         r_b, o_a, dq_a = lax.optimization_barrier((r_b, o_a, dq_a))
         r_pb, o_ao, dq_ao = to_core(r_b), to_core(o_a), to_core(dq_a)
 
-        o_b, dq_b, dkv, xt_b = attention(sc_b, wq, wo, (r_b, r_pb), (r_b, r_pb), BLK, pieces, part, True, scale)
+        o_b, dq_b, dkv, xt_b = attention("b", rank, wq, wo, (r_b, r_pb), (r_b, r_pb), BLK, pieces, part, scale)
         o_co, dkv = lax.optimization_barrier((o_co, dkv))
         dkv_o, o_bo, dq_bo = to_core(dkv), to_core(o_b), to_core(dq_b)
         y = out_rows(core, o_c, o_co, wo)

time: 252 us -> 247 us (0.980)
  Pallas kernels: 219 us -> 213 us
  waiting for transfers between devices: 17 us -> 21.5 us
    pallas_call x3, Pallas kernels: 129 us -> 123 us  [attention(): pl.pallas_call(functools.partial(attn_kernel, kind, heads, scale, rows //...]
    ppermute x3, waiting for transfers between devices: 11 us -> 14.1 us  [device_layer(): to_chip = lambda v: lax.ppermute(v, 'cp', chip_swap)]
  transfers between devices with their start and end apart: 16 -> 16, of which waited for: 4 -> 5; matrix products, arithmetic and copies ran while one was open for 1% -> 0% of each run, Pallas kernels for 75% -> 74%
where the time goes in v6:
time: 247 us
  Pallas kernels  213 us (86%)
  waiting for transfers between devices  21.5 us (9%)
  starting transfers between devices  8.51 us (3%)
  local copies, waits for them, and re-layouts  3.17 us (1%)
    pallas_call x3, Pallas kernels, attention(): pl.pallas_call(functools.partial(attn_kernel, kind, heads, scale, rows //...  123 us
    pallas_call x1, Pallas kernels, grad_wq(): pl.pallas_call(dwq_kernel, out_shape=(jax.ShapeDtypeStruct((model, 16, HD...  30.9 us
    pallas_call x1, Pallas kernels, grad_wo(): pl.pallas_call(dwo_kernel, out_shape=jax.ShapeDtypeStruct((2 * half, mode...  24.3 us
    ppermute x3, waiting for transfers between devices, device_layer(): to_chip = lambda v: lax.ppermute(v, 'cp', chip_swap)  14.1 us
    pallas_call x1, Pallas kernels, grad_rows(): pl.pallas_call(dx_kernel, out_shape=jax.ShapeDtypeStruct((rows, model), B...  10.3 us
    pallas_call x1, Pallas kernels, out_rows(): pl.pallas_call(y_kernel, out_shape=jax.ShapeDtypeStruct((rows, model), BF...  9.28 us
    pallas_call x1, Pallas kernels, flat_heads(): pl.pallas_call(heads_kernel, out_shape=jax.ShapeDtypeStruct((model, num *...  7.78 us
    ppermute x13, waiting for transfers between devices, device_layer(): to_core = lambda v: lax.ppermute(v, 'cp', core_swap)  7.45 us
  transfers between devices with their start and end apart: 16, of which 5 were waited for; matrix products, arithmetic and copies ran while one was open for 0% of the time, Pallas kernels for 74%

profile of v6, /device:TPU:0, one launch (start us, length us, event | category | flops | bytes accessed | tf_op | source)
XLA Modules:
  0.0 247.0 jit_solution(5098517910534463859)
XLA Ops:
  0.6 0.9 collective-permute-start.2
  1.5 0.0 collective-permute-start.3
  1.5 7.4 %shard_map.127 = (bf16[512,512]{1,0:T(8,128)(2,1)}, bf16[2048,512]{1,0:T(8,128)(2,1)}, bf16[512,2048]{1,0:T(8,128)(2,1)}, bf16[512,2048]{1,0:T(8,128)(2,1)}) custom-call(s32[1]{0:T(128)} %bitcast.sc, bf16[512,2048]{1,0:T(8,128)(2,1)} %refs_0_.1, bf16[512,2048]{1,0:T(8,128)(2,1)} %refs_6_.1, bf16[4096,128]{1,0:T(8,128)(2,1)} %bitcast.11, ...), custom_call_target="tpu_custom_call" | custom-call | flops 1073741824 | bytes 8000000 | tf_op jit(solution)/shard_map/pallas_call | solution.py:129
  8.9 2.9 %collective-permute-start.1 = (bf16[512,512]{1,0:T(8,128)(2,1)}, bf16[512,512]{1,0:T(8,128)(2,1)S(1)}, u32[]{:S(2)}, u32[]{:S(2)}) collective-permute-start(bf16[512,512]{1,0:T(8,128)(2,1)} %get-tuple-element.37.refs_4_), channel_id=1, source_target_pairs={{0,2},{2,0},{1,3},{3,1},{4,6},{6,4},{5,7},{7,5}} | collective-permute-start | bytes 1572872 | tf_op jit(solution)/shard_map/ppermute | solution.py:647
  11.9 0.0 collective-permute-start.4
  11.9 7.8 %shard_map.128.wq_hbm.wq_mine.wq_other = bf16[2048,2048]{1,0:T(8,128)(2,1)} custom-call(bf16[256,256]{1,0:T(8,128)(2,1)} %constant.11.clone.perm_ref, bf16[2048,16,128]{2,1,0:T(8,128)(2,1)} %w_hbm), custom_call_target="tpu_custom_call" | custom-call | flops 4000000000 | bytes 16777216 | tf_op jit(solution)/shard_map/pallas_call | solution.py:83
  19.7 4.5 %collective-permute-done.1.refs_6_ = bf16[512,512]{1,0:T(8,128)(2,1)S(1)} collective-permute-done((bf16[512,512]{1,0:T(8,128)(2,1)}, bf16[512,512]{1,0:T(8,128)(2,1)S(1)}, u32[]{:S(2)}, u32[]{:S(2)}) %collective-permute-start.1) | collective-permute-done | bytes 524320 | tf_op jit(solution)/shard_map/ppermute | solution.py:647
  24.2 0.0 copy-start.2
  24.2 0.0 collective-permute-start.5
  24.2 1.7 collective-permute-start
  26.0 0.0 collective-permute-done.4.refs_5_
  26.0 0.0 copy-start.3
  26.0 0.2 collective-permute-done.5.refs_7_
  26.1 0.7 copy-done.3
  26.8 0.0 copy-start.4
  26.8 0.0 collective-permute-done.2.refs_1_
  26.8 0.9 copy-done.4
  27.6 0.0 collective-permute-done.3.refs_3_.refs_7_
  27.6 0.0 copy-done.2
  27.6 59.1 %shard_map.129 = (bf16[1024,1024]{1,0:T(8,128)(2,1)}, bf16[1024,1024]{1,0:T(8,128)(2,1)}, f32[2048,256]{1,0:T(8,128)}, bf16[2048,1024]{1,0:T(8,128)(2,1)}) custom-call(s32[1]{0:T(128)} %bitcast.3.sc, bf16[2048,2048]{1,0:T(8,128)(2,1)} %shard_map.128.wq_hbm.wq_mine.wq_other, bf16[2048,2048]{1,0:T(8,128)(2,1)} %bitcast.6, bf16[512,2048]{1,0:T(8,128)(2,1)} %refs_0_.1, ...), custom_call_target="tpu_custom_call" | custom-call | flops 32000000000 | bytes 20000000 | tf_op jit(solution)/shard_map/pallas_call | solution.py:386
  86.8 0.0 collective-permute-done.refs_0_.refs_2_.refs_8_
  86.8 0.2 collective-permute-start.8
  87.0 1.0 collective-permute-start.7
  88.0 3.3 %collective-permute-done.8.refs_1_.refs_3_.refs_9_ = bf16[512,2048]{1,0:T(8,128)(2,1)} collective-permute-done((bf16[512,2048]{1,0:T(8,128)(2,1)}, bf16[512,2048]{1,0:T(8,128)(2,1)}, u32[]{:S(2)}, u32[]{:S(2)}) %collective-permute-start.8) | collective-permute-done | bytes 2097184 | tf_op jit(solution)/shard_map/ppermute | solution.py:646
  91.3 34.3 %shard_map.130 = (bf16[1024,512]{1,0:T(8,128)(2,1)}, bf16[512,1024]{1,0:T(8,128)(2,1)}, f32[2048,256]{1,0:T(8,128)}, bf16[2048,512]{1,0:T(8,128)(2,1)}) custom-call(s32[1]{0:T(128)} %bitcast.3.sc, bf16[2048,2048]{1,0:T(8,128)(2,1)} %shard_map.128.wq_hbm.wq_mine.wq_other, bf16[2048,2048]{1,0:T(8,128)(2,1)} %bitcast.7, ...), custom_call_target="tpu_custom_call" | custom-call | flops 16000000000 | bytes 20000000 | tf_op jit(solution)/shard_map/pallas_call | solution.py:386
  125.6 9.5 %collective-permute-done.7.refs_0_.refs_2_.refs_10_ = bf16[512,2048]{1,0:T(8,128)(2,1)} collective-permute-done((bf16[512,2048]{1,0:T(8,128)(2,1)}, bf16[512,2048]{1,0:T(8,128)(2,1)}, u32[]{:S(2)}, u32[]{:S(2)}) %collective-permute-start.7) | collective-permute-done | bytes 2097184 | tf_op jit(solution)/shard_map/ppermute | solution.py:647
  135.1 0.0 collective-permute-start.9
  135.2 0.5 collective-permute-start.6
  135.7 0.0 collective-permute-start.14
  135.7 4.0 %collective-permute-done.9.refs_1_.refs_3_.refs_11_ = bf16[512,2048]{1,0:T(8,128)(2,1)} collective-permute-done((bf16[512,2048]{1,0:T(8,128)(2,1)}, bf16[512,2048]{1,0:T(8,128)(2,1)}, u32[]{:S(2)}, u32[]{:S(2)}) %collective-permute-start.9) | collective-permute-done | bytes 2097184 | tf_op jit(solution)/shard_map/ppermute | solution.py:646
  139.6 29.4 %shard_map.131 = (bf16[1024,512]{1,0:T(8,128)(2,1)}, bf16[512,1024]{1,0:T(8,128)(2,1)}, bf16[2048,256]{1,0:T(8,128)(2,1)}, bf16[2048,512]{1,0:T(8,128)(2,1)}) custom-call(s32[1]{0:T(128)} %bitcast.3.sc, bf16[2048,2048]{1,0:T(8,128)(2,1)} %shard_map.128.wq_hbm.wq_mine.wq_other, bf16[2048,2048]{1,0:T(8,128)(2,1)} %bitcast.8, ...), custom_call_target="tpu_custom_call" | custom-call | flops 16000000000 | bytes 20000000 | tf_op jit(solution)/shard_map/pallas_call | solution.py:386
  169.1 0.1 collective-permute-start.15
  169.2 0.4 collective-permute-start.10
  169.6 0.1 collective-permute-start.12
  169.7 0.0 collective-permute-done.6.o_other.refs_3_
  169.7 0.4 collective-permute-start.11
  170.1 9.3 %shard_map.132 = bf16[512,2048]{1,0:T(8,128)(2,1)} custom-call(s32[1]{0:T(128)} %bitcast.sc, bf16[1024,1024]{1,0:T(8,128)(2,1)} %get-tuple-element.43.o_mine.refs_0_, bf16[1024,1024]{1,0:T(8,128)(2,1)} %collective-permute-done.6.o_other.refs_3_, bf16[2048,2048]{1,0:T(8,128)(2,1)} %bitcast.9, bf16[2048,2048]{1,0:T(8,128)(2,1)} %bitcast.10), custom_call_target="tpu_custom_call" | custom-call | flops 4294967296 | bytes 12000000 | tf_op jit(solution)/shard_map/pallas_call | solution.py:435
  179.4 0.0 collective-permute-done.14.refs_4_
  179.4 0.1 collective-permute-start.13
  179.5 0.0 collective-permute-done.15.refs_5_
  179.5 24.3 %shard_map.135 = f32[2048,2048]{1,0:T(8,128)} custom-call(s32[1]{0:T(128)} %bitcast.sc, bf16[1024,1024]{1,0:T(8,128)(2,1)} %get-tuple-element.43.o_mine.refs_0_, bf16[1024,512]{1,0:T(8,128)(2,1)} %get-tuple-element.64.refs_1_, bf16[1024,512]{1,0:T(8,128)(2,1)} %get-tuple-element.65.refs_2_, bf16[1024,1024]{1,0:T(8,128)(2,1)} %collective-permute-done.6.o_other.refs_3_, ...), custom_call_target="tpu_custom_call" | custom-call | flops 17179869184 | bytes 40000000 | tf_op jit(solution)/shard_map/pallas_call | solution.py:610
  203.8 0.0 collective-permute-done.10.q_other.refs_6_
  203.8 0.0 copy-start
  203.8 0.0 collective-permute-done.11.kv_other.refs_10_
  203.9 0.0 copy-start.1
  203.9 1.4 copy-done
  205.2 0.3 copy-done.1
  205.5 10.3 %shard_map.133 = bf16[512,2048]{1,0:T(8,128)(2,1)} custom-call(s32[1]{0:T(128)} %bitcast.sc, bf16[1024,1024]{1,0:T(8,128)(2,1)} %get-tuple-element.53.q_mine.refs_3_, bf16[1024,1024]{1,0:T(8,128)(2,1)} %copy-done, bf16[2048,256]{1,0:T(8,128)(2,1)} %get-tuple-element.54.kv_mine.refs_9_, bf16[2048,256]{1,0:T(8,128)(2,1)} %copy-done.1, ...), custom_call_target="tpu_custom_call" | custom-call | flops 5368709120 | bytes 14000000 | tf_op jit(solution)/shard_map/pallas_call | solution.py:472
  215.8 0.0 collective-permute-done.12.refs_7_
  215.8 0.0 collective-permute-done.13.refs_8_
  215.9 30.9 %shard_map.134 = (f32[2048,16,128]{2,1,0:T(8,128)}, f32[2048,2,128]{2,1,0:T(2,128)}, f32[2048,2,128]{2,1,0:T(2,128)}) custom-call(s32[1]{0:T(128)} %bitcast.sc, bf16[2048,1024]{1,0:T(8,128)(2,1)} %get-tuple-element.56.refs_0_, bf16[2048,512]{1,0:T(8,128)(2,1)} %get-tuple-element.57.refs_1_, bf16[2048,512]{1,0:T(8,128)(2,1)} %get-tuple-element.58.refs_2_, ...), custom_call_target="tpu_custom_call" | custom-call | flops 21474836480 | bytes 40000000 | tf_op jit(solution)/shard_map/pallas_call | solution.py:548
Async XLA Ops:
  0.6 26.1 %collective-permute-start.2 = (bf16[512,2048]{1,0:T(8,128)(2,1)}, bf16[512,2048]{1,0:T(8,128)(2,1)}, u32[]{:S(2)}, u32[]{:S(2)}) collective-permute-start(bf16[512,2048]{1,0:T(8,128)(2,1)} %refs_0_.1), channel_id=1, source_target_pairs={{0,1},{1,0},{2,3},{3,2},{4,5},{5,4},{6,7},{7,6}} | collective-permute-start | bytes 6291464 | tf_op jit(solution)/shard_map/ppermute | solution.py:646
  1.5 26.1 %collective-permute-start.3 = (bf16[512,2048]{1,0:T(8,128)(2,1)}, bf16[512,2048]{1,0:T(8,128)(2,1)}, u32[]{:S(2)}, u32[]{:S(2)}) collective-permute-start(bf16[512,2048]{1,0:T(8,128)(2,1)} %refs_6_.1), channel_id=1, source_target_pairs={{0,1},{1,0},{2,3},{3,2},{4,5},{5,4},{6,7},{7,6}} | collective-permute-start | bytes 6291464 | tf_op jit(solution)/shard_map/ppermute | solution.py:646
  8.9 15.3 %collective-permute-start.1 = (bf16[512,512]{1,0:T(8,128)(2,1)}, bf16[512,512]{1,0:T(8,128)(2,1)S(1)}, u32[]{:S(2)}, u32[]{:S(2)}) collective-permute-start(bf16[512,512]{1,0:T(8,128)(2,1)} %get-tuple-element.37.refs_4_), channel_id=1, source_target_pairs={{0,2},{2,0},{1,3},{3,1},{4,6},{6,4},{5,7},{7,5}} | collective-permute-start | bytes 1572872 | tf_op jit(solution)/shard_map/ppermute | solution.py:647
  11.9 14.1 %collective-permute-start.4 = (bf16[512,512]{1,0:T(8,128)(2,1)}, bf16[512,512]{1,0:T(8,128)(2,1)S(1)}, u32[]{:S(2)}, u32[]{:S(2)}) collective-permute-start(bf16[512,512]{1,0:T(8,128)(2,1)} %get-tuple-element.37.refs_4_), channel_id=1, source_target_pairs={{0,1},{1,0},{2,3},{3,2},{4,5},{5,4},{6,7},{7,6}} | collective-permute-start | bytes 1572872 | tf_op jit(solution)/shard_map/ppermute | solution.py:646
  24.2 3.4 %copy-start.2 = (bf16[512,512]{1,0:T(8,128)(2,1)}, bf16[512,512]{1,0:T(8,128)(2,1)S(1)}, u32[]{:S(2)}) copy-start(bf16[512,512]{1,0:T(8,128)(2,1)S(1)} %collective-permute-done.1.refs_6_) | copy-start | bytes 1572868
  24.2 1.9 collective-permute-start.5
  24.2 62.5 %collective-permute-start = (bf16[512,2048]{1,0:T(8,128)(2,1)}, bf16[512,2048]{1,0:T(8,128)(2,1)}, u32[]{:S(2)}, u32[]{:S(2)}) collective-permute-start(bf16[512,2048]{1,0:T(8,128)(2,1)} %get-tuple-element.36), channel_id=1, source_target_pairs={{0,2},{2,0},{1,3},{3,1},{4,6},{6,4},{5,7},{7,5}} | collective-permute-start | bytes 6291464 | tf_op jit(solution)/shard_map/ppermute | solution.py:647
  26.0 0.8 copy-start.3
  26.8 0.9 copy-start.4
  86.8 4.5 %collective-permute-start.8 = (bf16[512,2048]{1,0:T(8,128)(2,1)}, bf16[512,2048]{1,0:T(8,128)(2,1)}, u32[]{:S(2)}, u32[]{:S(2)}) collective-permute-start(bf16[512,2048]{1,0:T(8,128)(2,1)} %collective-permute-done.refs_0_.refs_2_.refs_8_), channel_id=1, source_target_pairs={{0,1},{1,0},{2,3},{3,2},{4,5},{5,4},{6,7},{7,6}} | collective-permute-start | bytes 6291464 | tf_op jit(solution)/shard_map/ppermute | solution.py:646
  87.0 48.1 %collective-permute-start.7 = (bf16[512,2048]{1,0:T(8,128)(2,1)}, bf16[512,2048]{1,0:T(8,128)(2,1)}, u32[]{:S(2)}, u32[]{:S(2)}) collective-permute-start(bf16[512,2048]{1,0:T(8,128)(2,1)} %get-tuple-element.44), channel_id=1, source_target_pairs={{0,2},{2,0},{1,3},{3,1},{4,6},{6,4},{5,7},{7,5}} | collective-permute-start | bytes 6291464 | tf_op jit(solution)/shard_map/ppermute | solution.py:647
  135.1 4.5 %collective-permute-start.9 = (bf16[512,2048]{1,0:T(8,128)(2,1)}, bf16[512,2048]{1,0:T(8,128)(2,1)}, u32[]{:S(2)}, u32[]{:S(2)}) collective-permute-start(bf16[512,2048]{1,0:T(8,128)(2,1)} %collective-permute-done.7.refs_0_.refs_2_.refs_10_), channel_id=1, source_target_pairs={{0,1},{1,0},{2,3},{3,2},{4,5},{5,4},{6,7},{7,6}} | collective-permute-start | bytes 6291464 | tf_op jit(solution)/shard_map/ppermute | solution.py:646
  135.2 34.6 %collective-permute-start.6 = (bf16[1024,1024]{1,0:T(8,128)(2,1)}, bf16[1024,1024]{1,0:T(8,128)(2,1)}, u32[]{:S(2)}, u32[]{:S(2)}) collective-permute-start(bf16[1024,1024]{1,0:T(8,128)(2,1)} %get-tuple-element.43.o_mine.refs_0_), channel_id=1, source_target_pairs={{0,1},{1,0},{2,3},{3,2},{4,5},{5,4},{6,7},{7,6}} | collective-permute-start | bytes 6291464 | tf_op jit(solution)/shard_map/ppermute | solution.py:646
  135.7 43.7 %collective-permute-start.14 = (bf16[1024,512]{1,0:T(8,128)(2,1)}, bf16[1024,512]{1,0:T(8,128)(2,1)}, u32[]{:S(2)}, u32[]{:S(2)}) collective-permute-start(bf16[1024,512]{1,0:T(8,128)(2,1)} %get-tuple-element.64.refs_1_), channel_id=1, source_target_pairs={{0,1},{1,0},{2,3},{3,2},{4,5},{5,4},{6,7},{7,6}} | collective-permute-start | bytes 3145736 | tf_op jit(solution)/shard_map/ppermute | solution.py:646
  169.1 10.5 %collective-permute-start.15 = (bf16[1024,512]{1,0:T(8,128)(2,1)}, bf16[1024,512]{1,0:T(8,128)(2,1)}, u32[]{:S(2)}, u32[]{:S(2)}) collective-permute-start(bf16[1024,512]{1,0:T(8,128)(2,1)} %get-tuple-element.65.refs_2_), channel_id=1, source_target_pairs={{0,1},{1,0},{2,3},{3,2},{4,5},{5,4},{6,7},{7,6}} | collective-permute-start | bytes 3145736 | tf_op jit(solution)/shard_map/ppermute | solution.py:646
  169.2 34.6 %collective-permute-start.10 = (bf16[1024,1024]{1,0:T(8,128)(2,1)}, bf16[1024,1024]{1,0:T(8,128)(2,1)S(1)}, u32[]{:S(2)}, u32[]{:S(2)}) collective-permute-start(bf16[1024,1024]{1,0:T(8,128)(2,1)} %get-tuple-element.53.q_mine.refs_3_), channel_id=1, source_target_pairs={{0,1},{1,0},{2,3},{3,2},{4,5},{5,4},{6,7},{7,6}} | collective-permute-start | bytes 6291464 | tf_op jit(solution)/shard_map/ppermute | solution.py:646
  169.6 46.2 %collective-permute-start.12 = (bf16[512,1024]{1,0:T(8,128)(2,1)}, bf16[512,1024]{1,0:T(8,128)(2,1)}, u32[]{:S(2)}, u32[]{:S(2)}) collective-permute-start(bf16[512,1024]{1,0:T(8,128)(2,1)} %get-tuple-element.59.refs_4_), channel_id=1, source_target_pairs={{0,1},{1,0},{2,3},{3,2},{4,5},{5,4},{6,7},{7,6}} | collective-permute-start | bytes 3145736 | tf_op jit(solution)/shard_map/ppermute | solution.py:646
  169.7 34.1 %collective-permute-start.11 = (bf16[2048,256]{1,0:T(8,128)(2,1)}, bf16[2048,256]{1,0:T(8,128)(2,1)S(1)}, u32[]{:S(2)}, u32[]{:S(2)}) collective-permute-start(bf16[2048,256]{1,0:T(8,128)(2,1)} %get-tuple-element.54.kv_mine.refs_9_), channel_id=1, source_target_pairs={{0,1},{1,0},{2,3},{3,2},{4,5},{5,4},{6,7},{7,6}} | collective-permute-start | bytes 3145736 | tf_op jit(solution)/shard_map/ppermute | solution.py:646
  179.4 36.5 %collective-permute-start.13 = (bf16[512,1024]{1,0:T(8,128)(2,1)}, bf16[512,1024]{1,0:T(8,128)(2,1)}, u32[]{:S(2)}, u32[]{:S(2)}) collective-permute-start(bf16[512,1024]{1,0:T(8,128)(2,1)} %get-tuple-element.60.refs_5_), channel_id=1, source_target_pairs={{0,1},{1,0},{2,3},{3,2},{4,5},{5,4},{6,7},{7,6}} | collective-permute-start | bytes 3145736 | tf_op jit(solution)/shard_map/ppermute | solution.py:646
  203.8 1.4 copy-start
  203.9 1.7 copy-start.1

commit v7 on v6

--- a/solution.py
+++ b/solution.py
@@ -16,6 +16,7 @@
 HALF = 1024
 SEQ = 2048
 TILE_WQ = 512
+LARGE = 2.0**60
 LOW = -3.0e38
 F32 = jnp.float32
 BF16 = jnp.bfloat16
@@ -168,7 +169,7 @@
     else:
         init_hbm, o_ref, dq_ref, dkv_ref, xt_ref = refs[:5]
         scratch = refs[5:]
-    ks, vs, kt, vt, dk, dv, qt, dot_t, qst, dost, s_ref, p_ref, ds_ref, ot, dqt, m_ref, l_ref, ref, wq, wo, xs, dys, w_sem, x_sem, dy_sem, g_sem = scratch
+    ks, vs, kt, vt, dk, dv, qt, dot_t, qst, dost, s_ref, p_ref, ds_ref, ot, dqt, l_ref, ref, wq, wo, xs, dys, w_sem, x_sem, dy_sem, g_sem = scratch
     step = pl.program_id(0)
     hd = HD
     c2 = scale * math.log2(math.e)
@@ -265,63 +266,79 @@
 
     b = block_at(kind, rank, step)
 
-    def scores(j, h):
-        at = pl.ds(pl.multiple_of(j * BLK, BLK), BLK)
+    def sweep(count, block):
+        def pair(j, _):
+            block(pl.multiple_of(j * 2 * BLK, 2 * BLK), 2 * BLK)
+            return 0
+
+        lax.fori_loop(0, count // 2, pair, 0)
+
+        @pl.when(count % 2 == 1)
+        def _():
+            block(pl.multiple_of((count - 1) * BLK, BLK), BLK)
+
+    def scores(start, rows, h):
+        at = pl.ds(start, rows)
         return at, slice(h * BLK, (h + 1) * BLK), dot(ks[at, :], qt[:, h * BLK : (h + 1) * BLK]) * c2
 
     def rows_of(t):
-        return t.reshape(BLK // 8, 8, BLK)
+        return t.reshape(t.shape[0] // 8, 8, BLK)
 
     key = lax.broadcasted_iota(jnp.int32, (BLK, BLK), 0)
     query = lax.broadcasted_iota(jnp.int32, (BLK, BLK), 1)
     for h in range(heads):
-        at, span, t = scores(b, h)
+        at, span, t = scores(pl.multiple_of(b * BLK, BLK), BLK, h)
         t = jnp.where(key <= query, t, LOW)
         s_ref[at, span] = t
-        m8 = jnp.max(rows_of(t), axis=0)
-        base = jnp.max(m8, axis=0, keepdims=True)
+        base = jnp.max(t, axis=0, keepdims=True)
         ref[:, span] = base
-        m_ref[:, span] = m8
         l_ref[:, span] = jnp.sum(jnp.exp2(rows_of(t - base)), axis=0)
 
-    def open_block(j, _):
+    def open_block(start, rows):
         for h in range(heads):
-            at, span, t = scores(j, h)
+            at, span, t = scores(start, rows, h)
             s_ref[at, span] = t
-            m_ref[:, span] = jnp.maximum(m_ref[:, span], jnp.max(rows_of(t), axis=0))
             l_ref[:, span] += jnp.sum(jnp.exp2(rows_of(t - ref[:, span])), axis=0)
-        return 0
-
-    lax.fori_loop(0, b, open_block, 0)
-
-    @pl.when(jnp.max(m_ref[...] - ref[...]) > 60.0)
-    def _():
-        ref[...] = jnp.max(m_ref[...], axis=0, keepdims=True)
-        l_ref[...] = jnp.zeros_like(l_ref)
-
-        def again(j, _):
-            at = pl.ds(pl.multiple_of(j * BLK, BLK), BLK)
+
+    sweep(b, open_block)
+
+    @pl.when(jnp.max(l_ref[...]) > LARGE)
+    def _():
+        def each(start, fn):
             for h in range(heads):
                 span = slice(h * BLK, (h + 1) * BLK)
-                l_ref[:, span] += jnp.sum(jnp.exp2(rows_of(s_ref[at, span] - ref[:, span])), axis=0)
-            return 0
-
-        lax.fori_loop(0, b + 1, again, 0)
+                fn(span, s_ref[pl.ds(start, BLK), span])
+
+        def peak(span, t):
+            ref[:, span] = jnp.maximum(ref[:, span], jnp.max(t, axis=0, keepdims=True))
+
+        def total(span, t):
+            l_ref[:, span] += jnp.sum(jnp.exp2(rows_of(t - ref[:, span])), axis=0)
+
+        def over(fn):
+            def body(j, _):
+                each(pl.multiple_of(j * BLK, BLK), fn)
+                return 0
+
+            lax.fori_loop(0, b + 1, body, 0)
+
+        over(peak)
+        l_ref[...] = jnp.zeros_like(l_ref)
+        over(total)
 
     lse = ref[...] + jnp.log2(jnp.sum(l_ref[...], axis=0, keepdims=True))
 
     ot[...] = jnp.zeros_like(ot)
 
-    def value_block(j, _):
-        at = pl.ds(pl.multiple_of(j * BLK, BLK), BLK)
+    def value_block(start, rows):
+        at = pl.ds(start, rows)
         for h in range(heads):
             span = slice(h * BLK, (h + 1) * BLK)
             p = jnp.exp2(s_ref[at, span] - lse[:, span]).astype(BF16)
             p_ref[at, span] = p
             ot[:, span] += dot(vt[:, at], p)
-        return 0
-
-    lax.fori_loop(0, b + 1, value_block, 0)
+
+    sweep(b + 1, value_block)
 
     o_round = ot[...].astype(BF16)
     delta = jnp.sum(o_round.astype(F32) * dot_t[...].astype(F32), axis=0, keepdims=True)
@@ -406,7 +423,7 @@
                 pltpu.VMEM((seq, wide), BF16),
                 pltpu.VMEM((BLK, wide), BF16),
                 *[pltpu.VMEM((hd, wide), F32) for _ in "od"],
-                *[pltpu.VMEM((8, wide), F32) for _ in "ml"],
+                pltpu.VMEM((8, wide), F32),
                 pltpu.VMEM((1, wide), F32),
                 pltpu.VMEM((model, width), BF16),
                 pltpu.VMEM((width, model), BF16),

time: 247 us -> 242 us (0.980)
  Pallas kernels: 213 us -> 206 us
    pallas_call x3, Pallas kernels: 123 us -> 115 us  [attention(): pl.pallas_call(functools.partial(attn_kernel, kind, heads, scale, rows //...]
  transfers between devices with their start and end apart: 16 -> 16, of which waited for: 5 -> 5; matrix products, arithmetic and copies ran while one was open for 0% -> 0% of each run, Pallas kernels for 74% -> 72%
where the time goes in v7:
time: 242 us
  Pallas kernels  206 us (85%)
  waiting for transfers between devices  23.6 us (10%)
  starting transfers between devices  8.51 us (4%)
  local copies, waits for them, and re-layouts  3.17 us (1%)
    pallas_call x3, Pallas kernels, attention(): pl.pallas_call(functools.partial(attn_kernel, kind, heads, scale, rows //...  115 us
    pallas_call x1, Pallas kernels, grad_wq(): pl.pallas_call(dwq_kernel, out_shape=(jax.ShapeDtypeStruct((model, 16, HD...  30.9 us
    pallas_call x1, Pallas kernels, grad_wo(): pl.pallas_call(dwo_kernel, out_shape=jax.ShapeDtypeStruct((2 * half, mode...  24.3 us
    ppermute x3, waiting for transfers between devices, device_layer(): to_chip = lambda v: lax.ppermute(v, 'cp', chip_swap)  16.2 us
    pallas_call x1, Pallas kernels, grad_rows(): pl.pallas_call(dx_kernel, out_shape=jax.ShapeDtypeStruct((rows, model), B...  10.3 us
    pallas_call x1, Pallas kernels, out_rows(): pl.pallas_call(y_kernel, out_shape=jax.ShapeDtypeStruct((rows, model), BF...  9.28 us
    pallas_call x1, Pallas kernels, flat_heads(): pl.pallas_call(heads_kernel, out_shape=jax.ShapeDtypeStruct((model, num *...  7.78 us
    ppermute x13, waiting for transfers between devices, device_layer(): to_core = lambda v: lax.ppermute(v, 'cp', core_swap)  7.46 us
  transfers between devices with their start and end apart: 16, of which 5 were waited for; matrix products, arithmetic and copies ran while one was open for 0% of the time, Pallas kernels for 72%

profile of v7, /device:TPU:0, one launch (start us, length us, event | category | flops | bytes accessed | tf_op | source)
XLA Modules:
  0.0 241.8 jit_solution(3243606559432919065)
XLA Ops:
  0.6 0.9 collective-permute-start.2
  1.5 0.0 collective-permute-start.3
  1.5 7.4 %shard_map.127 = (bf16[512,512]{1,0:T(8,128)(2,1)}, bf16[2048,512]{1,0:T(8,128)(2,1)}, bf16[512,2048]{1,0:T(8,128)(2,1)}, bf16[512,2048]{1,0:T(8,128)(2,1)}) custom-call(s32[1]{0:T(128)} %bitcast.sc, bf16[512,2048]{1,0:T(8,128)(2,1)} %refs_0_.1, bf16[512,2048]{1,0:T(8,128)(2,1)} %refs_6_.1, bf16[4096,128]{1,0:T(8,128)(2,1)} %bitcast.11, ...), custom_call_target="tpu_custom_call" | custom-call | flops 1073741824 | bytes 8000000 | tf_op jit(solution)/shard_map/pallas_call | solution.py:130
  8.9 2.9 %collective-permute-start.1 = (bf16[512,512]{1,0:T(8,128)(2,1)}, bf16[512,512]{1,0:T(8,128)(2,1)S(1)}, u32[]{:S(2)}, u32[]{:S(2)}) collective-permute-start(bf16[512,512]{1,0:T(8,128)(2,1)} %get-tuple-element.37.refs_4_), channel_id=1, source_target_pairs={{0,2},{2,0},{1,3},{3,1},{4,6},{6,4},{5,7},{7,5}} | collective-permute-start | bytes 1572872 | tf_op jit(solution)/shard_map/ppermute | solution.py:664
  11.9 0.0 collective-permute-start.4
  11.9 7.8 %shard_map.128.wq_hbm.wq_mine.wq_other = bf16[2048,2048]{1,0:T(8,128)(2,1)} custom-call(bf16[256,256]{1,0:T(8,128)(2,1)} %constant.11.clone.perm_ref, bf16[2048,16,128]{2,1,0:T(8,128)(2,1)} %w_hbm), custom_call_target="tpu_custom_call" | custom-call | flops 4000000000 | bytes 16777216 | tf_op jit(solution)/shard_map/pallas_call | solution.py:84
  19.7 4.5 %collective-permute-done.1.refs_6_ = bf16[512,512]{1,0:T(8,128)(2,1)S(1)} collective-permute-done((bf16[512,512]{1,0:T(8,128)(2,1)}, bf16[512,512]{1,0:T(8,128)(2,1)S(1)}, u32[]{:S(2)}, u32[]{:S(2)}) %collective-permute-start.1) | collective-permute-done | bytes 524320 | tf_op jit(solution)/shard_map/ppermute | solution.py:664
  24.2 0.0 copy-start.2
  24.2 0.0 collective-permute-start.5
  24.2 1.7 collective-permute-start
  26.0 0.0 collective-permute-done.4.refs_5_
  26.0 0.0 copy-start.3
  26.0 0.2 collective-permute-done.5.refs_7_
  26.1 0.7 copy-done.3
  26.8 0.0 copy-start.4
  26.8 0.0 collective-permute-done.2.refs_1_
  26.8 0.9 copy-done.4
  27.6 0.0 collective-permute-done.3.refs_3_.refs_7_
  27.6 0.0 copy-done.2
  27.6 55.5 %shard_map.129 = (bf16[1024,1024]{1,0:T(8,128)(2,1)}, bf16[1024,1024]{1,0:T(8,128)(2,1)}, f32[2048,256]{1,0:T(8,128)}, bf16[2048,1024]{1,0:T(8,128)(2,1)}) custom-call(s32[1]{0:T(128)} %bitcast.3.sc, bf16[2048,2048]{1,0:T(8,128)(2,1)} %shard_map.128.wq_hbm.wq_mine.wq_other, bf16[2048,2048]{1,0:T(8,128)(2,1)} %bitcast.6, bf16[512,2048]{1,0:T(8,128)(2,1)} %refs_0_.1, ...), custom_call_target="tpu_custom_call" | custom-call | flops 32000000000 | bytes 20000000 | tf_op jit(solution)/shard_map/pallas_call | solution.py:403
  83.1 0.0 collective-permute-done.refs_0_.refs_2_.refs_8_
  83.1 0.2 collective-permute-start.8
  83.4 1.0 collective-permute-start.7
  84.3 3.3 %collective-permute-done.8.refs_1_.refs_3_.refs_9_ = bf16[512,2048]{1,0:T(8,128)(2,1)} collective-permute-done((bf16[512,2048]{1,0:T(8,128)(2,1)}, bf16[512,2048]{1,0:T(8,128)(2,1)}, u32[]{:S(2)}, u32[]{:S(2)}) %collective-permute-start.8) | collective-permute-done | bytes 2097184 | tf_op jit(solution)/shard_map/ppermute | solution.py:663
  87.6 32.2 %shard_map.130 = (bf16[1024,512]{1,0:T(8,128)(2,1)}, bf16[512,1024]{1,0:T(8,128)(2,1)}, f32[2048,256]{1,0:T(8,128)}, bf16[2048,512]{1,0:T(8,128)(2,1)}) custom-call(s32[1]{0:T(128)} %bitcast.3.sc, bf16[2048,2048]{1,0:T(8,128)(2,1)} %shard_map.128.wq_hbm.wq_mine.wq_other, bf16[2048,2048]{1,0:T(8,128)(2,1)} %bitcast.7, ...), custom_call_target="tpu_custom_call" | custom-call | flops 16000000000 | bytes 20000000 | tf_op jit(solution)/shard_map/pallas_call | solution.py:403
  119.9 11.6 %collective-permute-done.7.refs_0_.refs_2_.refs_10_ = bf16[512,2048]{1,0:T(8,128)(2,1)} collective-permute-done((bf16[512,2048]{1,0:T(8,128)(2,1)}, bf16[512,2048]{1,0:T(8,128)(2,1)}, u32[]{:S(2)}, u32[]{:S(2)}) %collective-permute-start.7) | collective-permute-done | bytes 2097184 | tf_op jit(solution)/shard_map/ppermute | solution.py:664
  131.5 0.0 collective-permute-start.9
  131.5 0.5 collective-permute-start.6
  132.0 0.0 collective-permute-start.14
  132.0 4.0 %collective-permute-done.9.refs_1_.refs_3_.refs_11_ = bf16[512,2048]{1,0:T(8,128)(2,1)} collective-permute-done((bf16[512,2048]{1,0:T(8,128)(2,1)}, bf16[512,2048]{1,0:T(8,128)(2,1)}, u32[]{:S(2)}, u32[]{:S(2)}) %collective-permute-start.9) | collective-permute-done | bytes 2097184 | tf_op jit(solution)/shard_map/ppermute | solution.py:663
  136.0 27.8 %shard_map.131 = (bf16[1024,512]{1,0:T(8,128)(2,1)}, bf16[512,1024]{1,0:T(8,128)(2,1)}, bf16[2048,256]{1,0:T(8,128)(2,1)}, bf16[2048,512]{1,0:T(8,128)(2,1)}) custom-call(s32[1]{0:T(128)} %bitcast.3.sc, bf16[2048,2048]{1,0:T(8,128)(2,1)} %shard_map.128.wq_hbm.wq_mine.wq_other, bf16[2048,2048]{1,0:T(8,128)(2,1)} %bitcast.8, ...), custom_call_target="tpu_custom_call" | custom-call | flops 16000000000 | bytes 20000000 | tf_op jit(solution)/shard_map/pallas_call | solution.py:403
  163.8 0.2 collective-permute-start.15
  164.0 0.4 collective-permute-start.10
  164.4 0.1 collective-permute-start.12
  164.5 0.0 collective-permute-done.6.o_other.refs_3_
  164.5 0.4 collective-permute-start.11
  164.9 9.3 %shard_map.132 = bf16[512,2048]{1,0:T(8,128)(2,1)} custom-call(s32[1]{0:T(128)} %bitcast.sc, bf16[1024,1024]{1,0:T(8,128)(2,1)} %get-tuple-element.43.o_mine.refs_0_, bf16[1024,1024]{1,0:T(8,128)(2,1)} %collective-permute-done.6.o_other.refs_3_, bf16[2048,2048]{1,0:T(8,128)(2,1)} %bitcast.9, bf16[2048,2048]{1,0:T(8,128)(2,1)} %bitcast.10), custom_call_target="tpu_custom_call" | custom-call | flops 4294967296 | bytes 12000000 | tf_op jit(solution)/shard_map/pallas_call | solution.py:452
  174.2 0.0 collective-permute-done.14.refs_4_
  174.2 0.1 collective-permute-start.13
  174.3 0.0 collective-permute-done.15.refs_5_
  174.3 24.3 %shard_map.135 = f32[2048,2048]{1,0:T(8,128)} custom-call(s32[1]{0:T(128)} %bitcast.sc, bf16[1024,1024]{1,0:T(8,128)(2,1)} %get-tuple-element.43.o_mine.refs_0_, bf16[1024,512]{1,0:T(8,128)(2,1)} %get-tuple-element.64.refs_1_, bf16[1024,512]{1,0:T(8,128)(2,1)} %get-tuple-element.65.refs_2_, bf16[1024,1024]{1,0:T(8,128)(2,1)} %collective-permute-done.6.o_other.refs_3_, ...), custom_call_target="tpu_custom_call" | custom-call | flops 17179869184 | bytes 40000000 | tf_op jit(solution)/shard_map/pallas_call | solution.py:627
  198.6 0.0 collective-permute-done.10.q_other.refs_6_
  198.6 0.0 copy-start
  198.6 0.0 collective-permute-done.11.kv_other.refs_10_
  198.6 0.0 copy-start.1
  198.6 1.4 copy-done
  200.0 0.3 copy-done.1
  200.3 10.3 %shard_map.133 = bf16[512,2048]{1,0:T(8,128)(2,1)} custom-call(s32[1]{0:T(128)} %bitcast.sc, bf16[1024,1024]{1,0:T(8,128)(2,1)} %get-tuple-element.53.q_mine.refs_3_, bf16[1024,1024]{1,0:T(8,128)(2,1)} %copy-done, bf16[2048,256]{1,0:T(8,128)(2,1)} %get-tuple-element.54.kv_mine.refs_9_, bf16[2048,256]{1,0:T(8,128)(2,1)} %copy-done.1, ...), custom_call_target="tpu_custom_call" | custom-call | flops 5368709120 | bytes 14000000 | tf_op jit(solution)/shard_map/pallas_call | solution.py:489
  210.6 0.0 collective-permute-done.12.refs_7_
  210.6 0.0 collective-permute-done.13.refs_8_
  210.6 30.9 %shard_map.134 = (f32[2048,16,128]{2,1,0:T(8,128)}, f32[2048,2,128]{2,1,0:T(2,128)}, f32[2048,2,128]{2,1,0:T(2,128)}) custom-call(s32[1]{0:T(128)} %bitcast.sc, bf16[2048,1024]{1,0:T(8,128)(2,1)} %get-tuple-element.56.refs_0_, bf16[2048,512]{1,0:T(8,128)(2,1)} %get-tuple-element.57.refs_1_, bf16[2048,512]{1,0:T(8,128)(2,1)} %get-tuple-element.58.refs_2_, ...), custom_call_target="tpu_custom_call" | custom-call | flops 21474836480 | bytes 40000000 | tf_op jit(solution)/shard_map/pallas_call | solution.py:565
Async XLA Ops:
  0.6 26.1 %collective-permute-start.2 = (bf16[512,2048]{1,0:T(8,128)(2,1)}, bf16[512,2048]{1,0:T(8,128)(2,1)}, u32[]{:S(2)}, u32[]{:S(2)}) collective-permute-start(bf16[512,2048]{1,0:T(8,128)(2,1)} %refs_0_.1), channel_id=1, source_target_pairs={{0,1},{1,0},{2,3},{3,2},{4,5},{5,4},{6,7},{7,6}} | collective-permute-start | bytes 6291464 | tf_op jit(solution)/shard_map/ppermute | solution.py:663
  1.5 26.1 %collective-permute-start.3 = (bf16[512,2048]{1,0:T(8,128)(2,1)}, bf16[512,2048]{1,0:T(8,128)(2,1)}, u32[]{:S(2)}, u32[]{:S(2)}) collective-permute-start(bf16[512,2048]{1,0:T(8,128)(2,1)} %refs_6_.1), channel_id=1, source_target_pairs={{0,1},{1,0},{2,3},{3,2},{4,5},{5,4},{6,7},{7,6}} | collective-permute-start | bytes 6291464 | tf_op jit(solution)/shard_map/ppermute | solution.py:663
  8.9 15.3 %collective-permute-start.1 = (bf16[512,512]{1,0:T(8,128)(2,1)}, bf16[512,512]{1,0:T(8,128)(2,1)S(1)}, u32[]{:S(2)}, u32[]{:S(2)}) collective-permute-start(bf16[512,512]{1,0:T(8,128)(2,1)} %get-tuple-element.37.refs_4_), channel_id=1, source_target_pairs={{0,2},{2,0},{1,3},{3,1},{4,6},{6,4},{5,7},{7,5}} | collective-permute-start | bytes 1572872 | tf_op jit(solution)/shard_map/ppermute | solution.py:664
  11.9 14.1 %collective-permute-start.4 = (bf16[512,512]{1,0:T(8,128)(2,1)}, bf16[512,512]{1,0:T(8,128)(2,1)S(1)}, u32[]{:S(2)}, u32[]{:S(2)}) collective-permute-start(bf16[512,512]{1,0:T(8,128)(2,1)} %get-tuple-element.37.refs_4_), channel_id=1, source_target_pairs={{0,1},{1,0},{2,3},{3,2},{4,5},{5,4},{6,7},{7,6}} | collective-permute-start | bytes 1572872 | tf_op jit(solution)/shard_map/ppermute | solution.py:663
  24.2 3.4 %copy-start.2 = (bf16[512,512]{1,0:T(8,128)(2,1)}, bf16[512,512]{1,0:T(8,128)(2,1)S(1)}, u32[]{:S(2)}) copy-start(bf16[512,512]{1,0:T(8,128)(2,1)S(1)} %collective-permute-done.1.refs_6_) | copy-start | bytes 1572868
  24.2 1.9 collective-permute-start.5
  24.2 58.9 %collective-permute-start = (bf16[512,2048]{1,0:T(8,128)(2,1)}, bf16[512,2048]{1,0:T(8,128)(2,1)}, u32[]{:S(2)}, u32[]{:S(2)}) collective-permute-start(bf16[512,2048]{1,0:T(8,128)(2,1)} %get-tuple-element.36), channel_id=1, source_target_pairs={{0,2},{2,0},{1,3},{3,1},{4,6},{6,4},{5,7},{7,5}} | collective-permute-start | bytes 6291464 | tf_op jit(solution)/shard_map/ppermute | solution.py:664
  26.0 0.8 copy-start.3
  26.8 0.9 copy-start.4
  83.1 4.5 %collective-permute-start.8 = (bf16[512,2048]{1,0:T(8,128)(2,1)}, bf16[512,2048]{1,0:T(8,128)(2,1)}, u32[]{:S(2)}, u32[]{:S(2)}) collective-permute-start(bf16[512,2048]{1,0:T(8,128)(2,1)} %collective-permute-done.refs_0_.refs_2_.refs_8_), channel_id=1, source_target_pairs={{0,1},{1,0},{2,3},{3,2},{4,5},{5,4},{6,7},{7,6}} | collective-permute-start | bytes 6291464 | tf_op jit(solution)/shard_map/ppermute | solution.py:663
  83.4 48.1 %collective-permute-start.7 = (bf16[512,2048]{1,0:T(8,128)(2,1)}, bf16[512,2048]{1,0:T(8,128)(2,1)}, u32[]{:S(2)}, u32[]{:S(2)}) collective-permute-start(bf16[512,2048]{1,0:T(8,128)(2,1)} %get-tuple-element.44), channel_id=1, source_target_pairs={{0,2},{2,0},{1,3},{3,1},{4,6},{6,4},{5,7},{7,5}} | collective-permute-start | bytes 6291464 | tf_op jit(solution)/shard_map/ppermute | solution.py:664
  131.5 4.5 %collective-permute-start.9 = (bf16[512,2048]{1,0:T(8,128)(2,1)}, bf16[512,2048]{1,0:T(8,128)(2,1)}, u32[]{:S(2)}, u32[]{:S(2)}) collective-permute-start(bf16[512,2048]{1,0:T(8,128)(2,1)} %collective-permute-done.7.refs_0_.refs_2_.refs_10_), channel_id=1, source_target_pairs={{0,1},{1,0},{2,3},{3,2},{4,5},{5,4},{6,7},{7,6}} | collective-permute-start | bytes 6291464 | tf_op jit(solution)/shard_map/ppermute | solution.py:663
  131.5 33.0 %collective-permute-start.6 = (bf16[1024,1024]{1,0:T(8,128)(2,1)}, bf16[1024,1024]{1,0:T(8,128)(2,1)}, u32[]{:S(2)}, u32[]{:S(2)}) collective-permute-start(bf16[1024,1024]{1,0:T(8,128)(2,1)} %get-tuple-element.43.o_mine.refs_0_), channel_id=1, source_target_pairs={{0,1},{1,0},{2,3},{3,2},{4,5},{5,4},{6,7},{7,6}} | collective-permute-start | bytes 6291464 | tf_op jit(solution)/shard_map/ppermute | solution.py:663
  132.0 42.2 %collective-permute-start.14 = (bf16[1024,512]{1,0:T(8,128)(2,1)}, bf16[1024,512]{1,0:T(8,128)(2,1)}, u32[]{:S(2)}, u32[]{:S(2)}) collective-permute-start(bf16[1024,512]{1,0:T(8,128)(2,1)} %get-tuple-element.64.refs_1_), channel_id=1, source_target_pairs={{0,1},{1,0},{2,3},{3,2},{4,5},{5,4},{6,7},{7,6}} | collective-permute-start | bytes 3145736 | tf_op jit(solution)/shard_map/ppermute | solution.py:663
  163.8 10.5 %collective-permute-start.15 = (bf16[1024,512]{1,0:T(8,128)(2,1)}, bf16[1024,512]{1,0:T(8,128)(2,1)}, u32[]{:S(2)}, u32[]{:S(2)}) collective-permute-start(bf16[1024,512]{1,0:T(8,128)(2,1)} %get-tuple-element.65.refs_2_), channel_id=1, source_target_pairs={{0,1},{1,0},{2,3},{3,2},{4,5},{5,4},{6,7},{7,6}} | collective-permute-start | bytes 3145736 | tf_op jit(solution)/shard_map/ppermute | solution.py:663
  164.0 34.6 %collective-permute-start.10 = (bf16[1024,1024]{1,0:T(8,128)(2,1)}, bf16[1024,1024]{1,0:T(8,128)(2,1)S(1)}, u32[]{:S(2)}, u32[]{:S(2)}) collective-permute-start(bf16[1024,1024]{1,0:T(8,128)(2,1)} %get-tuple-element.53.q_mine.refs_3_), channel_id=1, source_target_pairs={{0,1},{1,0},{2,3},{3,2},{4,5},{5,4},{6,7},{7,6}} | collective-permute-start | bytes 6291464 | tf_op jit(solution)/shard_map/ppermute | solution.py:663
  164.4 46.3 %collective-permute-start.12 = (bf16[512,1024]{1,0:T(8,128)(2,1)}, bf16[512,1024]{1,0:T(8,128)(2,1)}, u32[]{:S(2)}, u32[]{:S(2)}) collective-permute-start(bf16[512,1024]{1,0:T(8,128)(2,1)} %get-tuple-element.59.refs_4_), channel_id=1, source_target_pairs={{0,1},{1,0},{2,3},{3,2},{4,5},{5,4},{6,7},{7,6}} | collective-permute-start | bytes 3145736 | tf_op jit(solution)/shard_map/ppermute | solution.py:663
  164.5 34.1 %collective-permute-start.11 = (bf16[2048,256]{1,0:T(8,128)(2,1)}, bf16[2048,256]{1,0:T(8,128)(2,1)S(1)}, u32[]{:S(2)}, u32[]{:S(2)}) collective-permute-start(bf16[2048,256]{1,0:T(8,128)(2,1)} %get-tuple-element.54.kv_mine.refs_9_), channel_id=1, source_target_pairs={{0,1},{1,0},{2,3},{3,2},{4,5},{5,4},{6,7},{7,6}} | collective-permute-start | bytes 3145736 | tf_op jit(solution)/shard_map/ppermute | solution.py:663
  174.2 36.5 %collective-permute-start.13 = (bf16[512,1024]{1,0:T(8,128)(2,1)}, bf16[512,1024]{1,0:T(8,128)(2,1)}, u32[]{:S(2)}, u32[]{:S(2)}) collective-permute-start(bf16[512,1024]{1,0:T(8,128)(2,1)} %get-tuple-element.60.refs_5_), channel_id=1, source_target_pairs={{0,1},{1,0},{2,3},{3,2},{4,5},{5,4},{6,7},{7,6}} | collective-permute-start | bytes 3145736 | tf_op jit(solution)/shard_map/ppermute | solution.py:663
  198.6 1.4 copy-start
  198.6 1.7 copy-start.1

commit v8 on v7

--- a/solution.py
+++ b/solution.py
@@ -15,7 +15,8 @@
 DUO = 512
 HALF = 1024
 SEQ = 2048
-TILE_WQ = 512
+WO_STEPS = 8
+DX_STEP = 16
 LARGE = 2.0**60
 LOW = -3.0e38
 F32 = jnp.float32
@@ -97,7 +98,23 @@
     )(gather_heads(num, 16), w)
 
 
-def kv_kernel(sc, x_ref, dy_ref, wk_ref, wv_ref, perm_ref, out_ref, w_ref, rows_a, rows_b):
+def kv_kernel(sc, x_ref, dy_ref, wk_ref, wv_ref, perm_ref, out_ref, w_hbm, rows_a, rows_b, w_ref, sems):
+    step, core = pl.program_id(0), sc[0]
+    save_w = pltpu.make_async_copy(w_ref, w_hbm, sems.at[2])
+
+    def cut(dst, n):
+        return [
+            pltpu.make_async_copy(src, dst.at[at : at + BLK, :], sems.at[n])
+            for src, at in ((x_ref, 0), (dy_ref, BLK))
+        ]
+
+    for n, dst in enumerate((rows_a, rows_b)):
+
+        @pl.when(step == (1 - core if n == 0 else core))
+        def _():
+            for cp in cut(dst, n):
+                cp.start()
+
     @pl.when(pl.program_id(0) == 0)
     def _():
         for g in range(w_ref.shape[0] // HD):
@@ -109,17 +126,16 @@
                     col = (v * 2 + h) * HD
                     w_ref[g * HD : (g + 1) * HD, col : col + HD] = res[h * HD : (h + 1) * HD, v * HD : (v + 1) * HD]
 
+        save_w.start()
+
     out_ref[...] = dot(x_ref[...], w_ref[...]).astype(BF16)
 
-    @pl.when(pl.program_id(0) == 1 - sc[0])
-    def _():
-        rows_a[:BLK, :] = x_ref[...]
-        rows_a[BLK:, :] = dy_ref[...]
-
-    @pl.when(pl.program_id(0) == sc[0])
-    def _():
-        rows_b[:BLK, :] = x_ref[...]
-        rows_b[BLK:, :] = dy_ref[...]
+    @pl.when(step == 1)
+    def _():
+        save_w.wait()
+        for n, dst in enumerate((rows_a, rows_b)):
+            for cp in cut(dst, n):
+                cp.wait()
 
 
 def project_kv(core, x, dy, wk, wv):
@@ -134,7 +150,8 @@
             num_scalar_prefetch=1,
             grid=(rows // BLK,),
             in_specs=[row, row, fixed(wk.shape), fixed(wv.shape), fixed((BLK, BLK))],
-            out_specs=(pl.BlockSpec((BLK, DUO), lambda i, s: (i, 0)), fixed((depth, DUO))) + (fixed((rows, depth)),) * 2,
+            out_specs=(pl.BlockSpec((BLK, DUO), lambda i, s: (i, 0)),) + (pl.BlockSpec(memory_space=pl.ANY),) * 3,
+            scratch_shapes=[pltpu.VMEM((depth, DUO), BF16), pltpu.SemaphoreType.DMA((3,))],
         ),
         compiler_params=params(),
         cost_estimate=cost(2 * rows * depth * DUO, 8e6),
@@ -469,133 +486,26 @@
     )(core, o_mine, o_other, wo, wo)
 
 
-def dx_kernel(sc, q_mine, q_other, kv_mine, kv_other, wq_mine, wq_other, wkv, out_ref, kv):
-    hd = HD
-
-    @pl.when(pl.program_id(0) == 0)
-    def _():
-        for n, src in ((sc[0], kv_mine), (1 - sc[0], kv_other)):
-            kv[:, pl.ds(pl.multiple_of(n * hd, hd), hd)] = src[:, :hd]
-            kv[:, pl.ds(pl.multiple_of((2 + n) * hd, hd), hd)] = src[:, hd:]
-
-    acc = dot_nt(q_mine[...], wq_mine[...]) + dot_nt(q_other[...], wq_other[...])
-    out_ref[...] = (acc + dot_nt(kv[...], wkv[...])).astype(BF16)
-
-
-def grad_rows(core, dq_mine, dq_other, dkv_mine, dkv_other, wq, wkv):
-    rows, half, model, tile = DUO, dq_mine.shape[1], wq.shape[0], DUO
-    mine = lambda i, s: (s[0], 0)
-    near, far = lambda i, s: (i, s[0]), lambda i, s: (i, 1 - s[0])
-    return pl.pallas_call(
-        dx_kernel,
-        out_shape=jax.ShapeDtypeStruct((rows, model), BF16),
-        grid_spec=pltpu.PrefetchScalarGridSpec(
-            num_scalar_prefetch=1,
-            grid=(model // tile,),
-            in_specs=[
-                *[pl.BlockSpec((rows, n), mine) for n in (half, half, BLK, BLK)],
-                *[pl.BlockSpec((tile, half), at) for at in (near, far)],
-                pl.BlockSpec((tile, DUO), lambda i, s: (i, 0)),
-            ],
-            out_specs=pl.BlockSpec((rows, tile), lambda i, s: (0, i)),
-            scratch_shapes=[pltpu.VMEM((rows, DUO), BF16)],
-        ),
-        compiler_params=params(),
-        cost_estimate=cost(4 * rows * half * model * 1.25, 14e6),
-    )(core, dq_mine, dq_other, dkv_mine, dkv_other, wq, wq, wkv)
-
-
 PIECES = ((0, DUO), (1, DUO), (0, BLK), (1, BLK), (0, BLK), (1, BLK))
 STARTS = (0, DUO, HALF, 1280, 1536, 1792)
 
 
-def piece_copies(core, arrays, dst, sem, along):
+def piece_copies(core, arrays, dst, sem):
     copies = []
     for n, ((flip, size), start) in enumerate(zip(PIECES, STARTS)):
         at = pl.ds(pl.multiple_of((1 - core if flip else core) * size, size), size)
-        src = arrays[n // 2]
-        if along:
-            copies.append(pltpu.make_async_copy(src.at[:, at], dst.at[:, start : start + size], sem))
-        else:
-            copies.append(pltpu.make_async_copy(src.at[at, :], dst.at[start : start + size, :], sem))
+        copies.append(pltpu.make_async_copy(arrays[n // 2].at[:, at], dst.at[:, start : start + size], sem))
     return copies
 
 
-def dwq_kernel(sc, *refs):
-    xts, mine, other, kv_in = refs[:3], refs[3:6], refs[6:9], refs[9:11]
-    out_ref, gk_ref, gv_ref, dq, kv, sems = refs[11:]
-    g, i = pl.program_id(0), pl.program_id(1)
-    tile, core, hd = out_ref.shape[0], sc[0], HD
+def tail_kernel(sc, *refs):
+    o_mine, o_other, ys, q_mine, q_other, kv_in = (refs[a:b] for a, b in ((0, 3), (3, 6), (6, 12), (12, 15), (15, 18), (18, 20)))
+    xts, (wq_mine, wq_other, wkv), refs = refs[20:23], refs[23:26], refs[26:]
+    gwo_ref, gwq_ref, gk_ref, gv_ref, dx_ref, o_all, y_all, dq, kv, kv_rows, sems = refs
+    step, core, hd = pl.program_id(0), sc[0], HD
+    tile, wide = gwo_ref.shape
     spans = [slice(0, HALF), slice(HALF, HALF + DUO), slice(HALF + DUO, SEQ)]
-    first = [pltpu.make_async_copy(a, dq.at[0, at, :], sems.at[0]) for a, at in zip(mine, spans)]
-    later = [pltpu.make_async_copy(a, dq.at[1, at, :], sems.at[1]) for a, at in zip(other, spans)]
-    later += [
-        pltpu.make_async_copy(a, kv.at[:, n * BLK : (n + 1) * BLK], sems.at[1]) for n, a in enumerate(kv_in)
-    ]
-
-    def when(gg, ii, copies, start):
-        @pl.when((g == gg) & (i == ii))
-        def _():
-            for cp in copies:
-                cp.start() if start else cp.wait()
-
-    when(0, 0, first, True)
-    when(0, 1, later, True)
-    when(0, 0, first, False)
-    when(1, 0, later, False)
-
-    acc = sum(dot(x[...], dq[g, at, :]) for x, at in zip(xts, spans))
-    flat = out_ref.reshape(tile * 8, hd)
-    for h in range(8):
-        flat[pl.ds(h, tile, stride=8), :] = acc[:, h * hd : (h + 1) * hd]
-
-    @pl.when(g == 1)
-    def _():
-        k_flat, v_flat = gk_ref.reshape(tile * 2, hd), gv_ref.reshape(tile * 2, hd)
-        both = sum(dot(x[...], kv[at, :]) for x, at in zip(xts, spans))
-        for n, head in enumerate((core, 1 - core)):
-            k_flat[pl.ds(head, tile, stride=2), :] = both[:, 2 * n * hd : (2 * n + 1) * hd]
-            v_flat[pl.ds(head, tile, stride=2), :] = both[:, (2 * n + 1) * hd : (2 * n + 2) * hd]
-
-
-def grad_wq(core, xts, mine, other, kvm, kvo):
-    model, half, tile = xts[0].shape[0], mine[0].shape[1], TILE_WQ
-    tiles = model // tile
-    small = pl.BlockSpec((tile, 2, HD), lambda g, i, s: (i * g, 0, 0))
-    return pl.pallas_call(
-        dwq_kernel,
-        out_shape=(
-            jax.ShapeDtypeStruct((model, 16, HD), F32),
-            jax.ShapeDtypeStruct((model, 2, HD), F32),
-            jax.ShapeDtypeStruct((model, 2, HD), F32),
-        ),
-        grid_spec=pltpu.PrefetchScalarGridSpec(
-            num_scalar_prefetch=1,
-            grid=(2, tiles),
-            in_specs=[pl.BlockSpec((tile, x.shape[1]), lambda g, i, s: (i, 0)) for x in xts]
-            + [pl.BlockSpec(memory_space=pl.ANY)] * 8,
-            out_specs=(
-                pl.BlockSpec((tile, 8, HD), lambda g, i, s: (i, (s[0] + g) % 2, 0)),
-                small,
-                small,
-            ),
-            scratch_shapes=[
-                pltpu.VMEM((2, SEQ, half), BF16),
-                pltpu.VMEM((SEQ, DUO), BF16),
-                pltpu.SemaphoreType.DMA((2,)),
-            ],
-        ),
-        compiler_params=params(2),
-        cost_estimate=cost(2 * SEQ * model * (2 * half + DUO), 40e6),
-    )(core, *xts, *mine, *other, kvm, kvo)
-
-
-def dwo_kernel(sc, *refs):
-    mine, other, ys, (out_ref, o_all, y_all, sems) = refs[:3], refs[3:6], refs[6:12], refs[12:]
-    j, g, i = pl.program_id(0), pl.program_id(1), pl.program_id(2)
-    tile, wide = out_ref.shape
-    o_first = piece_copies(sc[0], mine, o_all.at[0], sems.at[0], True)
-    o_later = piece_copies(sc[0], other, o_all.at[1], sems.at[1], True)
+    o_copies = [piece_copies(core, o, o_all.at[n], sems.at[n]) for n, o in enumerate((o_mine, o_other))]
     y_copies = [
         [
             pltpu.make_async_copy(
@@ -605,42 +515,116 @@
         ]
         for n in range(2)
     ]
-
-    def when(jj, gg, ii, copies, start):
-        @pl.when((j == jj) & (g == gg) & (i == ii))
+    q_copies = [
+        [pltpu.make_async_copy(a, dq.at[n, at, :], sems.at[4]) for a, at in zip(part, spans)]
+        for n, part in enumerate((q_mine, q_other))
+    ]
+    kv_copies = [pltpu.make_async_copy(a, kv.at[:, n * BLK : (n + 1) * BLK], sems.at[4]) for n, a in enumerate(kv_in)]
+
+    def start(at, copies):
+        @pl.when(step == at)
         def _():
             for cp in copies:
-                cp.start() if start else cp.wait()
-
-    when(0, 0, 0, y_copies[0] + o_first, True)
-    when(0, 0, 1, o_later, True)
-    when(0, 1, 0, y_copies[1], True)
-    when(0, 0, 0, y_copies[0] + o_first, False)
-    when(0, 1, 0, o_later, False)
-    when(1, 0, 0, y_copies[1], False)
-    out_ref[...] = dot(o_all[g, pl.ds(pl.multiple_of(i * tile, tile), tile), :], y_all[j])
-
-
-def grad_wo(core, ys, mine, other):
-    model, half, tile, wide = ys[0].shape[1], mine[0].shape[0], DUO, HALF
-    steps = half // tile
+                cp.start()
+
+    def wait(at, copies):
+        @pl.when(step == at)
+        def _():
+            for cp in copies:
+                cp.wait()
+
+    rest = q_copies[0] + q_copies[1] + kv_copies
+    start(0, y_copies[0] + o_copies[0])
+    start(1, o_copies[1])
+    start(2, y_copies[1])
+    start(3, rest)
+    wait(0, y_copies[0] + o_copies[0])
+    wait(2, o_copies[1])
+    wait(4, y_copies[1])
+    wait(WO_STEPS, rest)
+
+    @pl.when(step < WO_STEPS)
+    def _():
+        rows = pl.ds(pl.multiple_of(step % 2 * tile, tile), tile)
+        gwo_ref[...] = dot(o_all[step // 2 % 2, rows, :], y_all[step // 4])
+
+    @pl.when((step >= WO_STEPS) & (step < DX_STEP))
+    def _():
+        part = (step - WO_STEPS) // 4
+        acc = sum(dot(x[...], dq[part, at, :]) for x, at in zip(xts, spans))
+        flat = gwq_ref.reshape(tile * 8, hd)
+        for h in range(8):
+            flat[pl.ds(h, tile, stride=8), :] = acc[:, h * hd : (h + 1) * hd]
+
+    @pl.when((step >= DX_STEP - 4) & (step < DX_STEP))
+    def _():
+        k_flat, v_flat = gk_ref.reshape(tile * 2, hd), gv_ref.reshape(tile * 2, hd)
+        both = sum(dot(x[...], kv[at, :]) for x, at in zip(xts, spans))
+        for n, head in enumerate((core, 1 - core)):
+            k_flat[pl.ds(head, tile, stride=2), :] = both[:, 2 * n * hd : (2 * n + 1) * hd]
+            v_flat[pl.ds(head, tile, stride=2), :] = both[:, (2 * n + 1) * hd : (2 * n + 2) * hd]
+
+    own = pl.ds(pl.multiple_of(core * DUO, DUO), DUO)
+
+    @pl.when(step == DX_STEP)
+    def _():
+        for n, head in enumerate((core, 1 - core)):
+            for v in range(2):
+                col = pl.ds(pl.multiple_of((2 * v + head) * hd, hd), hd)
+                kv_rows[:, col] = kv[own, (2 * n + v) * hd : (2 * n + v + 1) * hd]
+
+    @pl.when(step >= DX_STEP)
+    def _():
+        acc = dot_nt(dq[0, own, :], wq_mine[...]) + dot_nt(dq[1, own, :], wq_other[...])
+        dx_ref[...] = (acc + dot_nt(kv_rows[...], wkv[...])).astype(BF16)
+
+
+def tail(core, o_mine, o_other, ys, q_mine, q_other, kvm, kvo, xts, wq, wkv):
+    model, half, tile, wide = ys[0].shape[1], o_mine[0].shape[0], DUO, HALF
+    wo = lambda i: jnp.minimum(i, WO_STEPS - 1)
+    q = lambda i: jnp.clip(i - WO_STEPS, 0, 7)
+    kv = lambda i: jnp.clip(i - DX_STEP + 4, 0, 3)
+    dx = lambda i: jnp.maximum(i - DX_STEP, 0)
+    hbm = [*o_mine, *o_other, *ys, *q_mine, *q_other, kvm, kvo]
+    small = pl.BlockSpec((tile, 2, HD), lambda i, s: (kv(i), 0, 0))
     return pl.pallas_call(
-        dwo_kernel,
-        out_shape=jax.ShapeDtypeStruct((2 * half, model), F32),
+        tail_kernel,
+        out_shape=(
+            jax.ShapeDtypeStruct((2 * half, model), F32),
+            jax.ShapeDtypeStruct((model, 16, HD), F32),
+            jax.ShapeDtypeStruct((model, 2, HD), F32),
+            jax.ShapeDtypeStruct((model, 2, HD), F32),
+            jax.ShapeDtypeStruct((DUO, model), BF16),
+        ),
         grid_spec=pltpu.PrefetchScalarGridSpec(
             num_scalar_prefetch=1,
-            grid=(2, 2, steps),
-            in_specs=[pl.BlockSpec(memory_space=pl.ANY)] * 12,
-            out_specs=pl.BlockSpec((tile, wide), lambda j, g, i, s: ((s[0] + g) % 2 * steps + i, j)),
+            grid=(DX_STEP + 4,),
+            in_specs=[pl.BlockSpec(memory_space=pl.ANY) for _ in hbm]
+            + [pl.BlockSpec((tile, x.shape[1]), lambda i, s: (q(i) % 4, 0)) for x in xts]
+            + [
+                pl.BlockSpec((tile, half), lambda i, s: (dx(i), s[0])),
+                pl.BlockSpec((tile, half), lambda i, s: (dx(i), 1 - s[0])),
+                pl.BlockSpec((tile, DUO), lambda i, s: (dx(i), 0)),
+            ],
+            out_specs=(
+                pl.BlockSpec((tile, wide), lambda i, s: ((s[0] + wo(i) // 2) % 2 * 2 + wo(i) % 2, wo(i) // 4)),
+                pl.BlockSpec((tile, 8, HD), lambda i, s: (q(i) % 4, (s[0] + q(i) // 4) % 2, 0)),
+                small,
+                small,
+                pl.BlockSpec((DUO, tile), lambda i, s: (0, dx(i))),
+            ),
             scratch_shapes=[
                 pltpu.VMEM((2, half, SEQ), BF16),
                 pltpu.VMEM((2, SEQ, wide), BF16),
-                pltpu.SemaphoreType.DMA((4,)),
+                pltpu.VMEM((2, SEQ, half), BF16),
+                pltpu.VMEM((SEQ, DUO), BF16),
+                pltpu.VMEM((DUO, DUO), BF16),
+                pltpu.SemaphoreType.DMA((5,)),
             ],
         ),
-        compiler_params=params(3),
-        cost_estimate=cost(4 * SEQ * model * half, 40e6),
-    )(core, *mine, *other, *ys)
+        compiler_params=params(1, 63),
+        cost_estimate=cost(5e10, 8e7),
+    )(core, *hbm, *xts, wq, wq, wkv)
 
 
 def solution(mesh):
@@ -693,9 +677,10 @@
         y = out_rows(core, o_c, o_co, wo)
 
         ys = (dy, dy_p, r_a, r_pa, r_b, r_pb)
-        gwo = grad_wo(core, ys, (o_c, o_a, o_b), (o_co, o_ao, o_bo))
-        dx = grad_rows(core, dq_c, dq_co, dkv, dkv_o, wq, wkv)
-        gwq, gwk, gwv = grad_wq(core, (xt_c, xt_a, xt_b), (dq_c, dq_a, dq_b), (dq_co, dq_ao, dq_bo), dkv, dkv_o)
+        gwo, gwq, gwk, gwv, dx = tail(
+            core, (o_c, o_a, o_b), (o_co, o_ao, o_bo), ys,
+            (dq_c, dq_a, dq_b), (dq_co, dq_ao, dq_bo), dkv, dkv_o, (xt_c, xt_a, xt_b), wq, wkv,
+        )
         return y, dx, gwq, gwk, gwv, gwo.reshape(num_heads, hd, model)
 
     return jax.shard_map(

time: 242 us -> 235 us (0.971)
  Pallas kernels: 206 us -> 201 us
    pallas_call x3 -> x1, Pallas kernels: 65.6 us -> 63 us  [tail(): pl.pallas_call(tail_kernel, out_shape=(jax.ShapeDtypeStruct((2 * half, mo...]
  transfers between devices with their start and end apart: 16 -> 16, of which waited for: 5 -> 5; matrix products, arithmetic and copies ran while one was open for 0% -> 0% of each run, Pallas kernels for 72% -> 59%
where the time goes in v8:
time: 235 us
  Pallas kernels  201 us (86%)
  waiting for transfers between devices  23 us (10%)
  starting transfers between devices  8.62 us (4%)
    pallas_call x3, Pallas kernels, attention(): pl.pallas_call(functools.partial(attn_kernel, kind, heads, scale, rows //...  115 us
    pallas_call x1, Pallas kernels, tail(): pl.pallas_call(tail_kernel, out_shape=(jax.ShapeDtypeStruct((2 * half, mo...  63 us
    ppermute x3, waiting for transfers between devices, device_layer(): to_chip = lambda v: lax.ppermute(v, 'cp', chip_swap)  16.1 us
    pallas_call x1, Pallas kernels, out_rows(): pl.pallas_call(y_kernel, out_shape=jax.ShapeDtypeStruct((rows, model), BF...  9.28 us
    pallas_call x1, Pallas kernels, flat_heads(): pl.pallas_call(heads_kernel, out_shape=jax.ShapeDtypeStruct((model, num *...  7.87 us
    ppermute x13, waiting for transfers between devices, device_layer(): to_core = lambda v: lax.ppermute(v, 'cp', core_swap)  6.89 us
    ppermute x3, starting transfers between devices, device_layer(): to_chip = lambda v: lax.ppermute(v, 'cp', chip_swap)  5.72 us
    pallas_call x1, Pallas kernels, project_kv(): pl.pallas_call(kv_kernel, out_shape=(jax.ShapeDtypeStruct((rows, DUO), BF...  5.69 us
  transfers between devices with their start and end apart: 16, of which 5 were waited for; matrix products, arithmetic and copies ran while one was open for 0% of the time, Pallas kernels for 59%

profile of v8, /device:TPU:0, one launch (start us, length us, event | category | flops | bytes accessed | tf_op | source)
XLA Modules:
  0.0 235.3 jit_solution(8022668416588728364)
XLA Ops:
  0.6 0.9 collective-permute-start.2
  1.5 0.0 collective-permute-start.3
  1.5 5.7 %shard_map.127 = (bf16[512,512]{1,0:T(8,128)(2,1)}, bf16[2048,512]{1,0:T(8,128)(2,1)}, bf16[512,2048]{1,0:T(8,128)(2,1)}, bf16[512,2048]{1,0:T(8,128)(2,1)}) custom-call(s32[1]{0:T(128)} %bitcast.sc, bf16[512,2048]{1,0:T(8,128)(2,1)} %refs_0_.1, bf16[512,2048]{1,0:T(8,128)(2,1)} %refs_6_.1, bf16[4096,128]{1,0:T(8,128)(2,1)} %bitcast.11, ...), custom_call_target="tpu_custom_call" | custom-call | flops 1073741824 | bytes 8000000 | tf_op jit(solution)/shard_map/pallas_call | solution.py:146
  7.2 3.0 %collective-permute-start.1 = (bf16[512,512]{1,0:T(8,128)(2,1)}, bf16[512,512]{1,0:T(8,128)(2,1)S(1)}, u32[]{:S(2)}, u32[]{:S(2)}) collective-permute-start(bf16[512,512]{1,0:T(8,128)(2,1)} %get-tuple-element.39.refs_4_), channel_id=1, source_target_pairs={{0,2},{2,0},{1,3},{3,1},{4,6},{6,4},{5,7},{7,5}} | collective-permute-start | bytes 1572872 | tf_op jit(solution)/shard_map/ppermute | solution.py:648
  10.2 0.0 collective-permute-start.4
  10.2 7.9 %shard_map.128.wq_hbm.refs_23_.refs_24_ = bf16[2048,2048]{1,0:T(8,128)(2,1)} custom-call(bf16[256,256]{1,0:T(8,128)(2,1)} %constant.11.clone.perm_ref, bf16[2048,16,128]{2,1,0:T(8,128)(2,1)} %w_hbm), custom_call_target="tpu_custom_call" | custom-call | flops 4000000000 | bytes 16777216 | tf_op jit(solution)/shard_map/pallas_call | solution.py:85
  18.1 4.5 %collective-permute-done.1.refs_6_ = bf16[512,512]{1,0:T(8,128)(2,1)S(1)} collective-permute-done((bf16[512,512]{1,0:T(8,128)(2,1)}, bf16[512,512]{1,0:T(8,128)(2,1)S(1)}, u32[]{:S(2)}, u32[]{:S(2)}) %collective-permute-start.1) | collective-permute-done | bytes 524320 | tf_op jit(solution)/shard_map/ppermute | solution.py:648
  22.5 0.0 copy-start
  22.5 0.0 collective-permute-start.5
  22.5 1.7 collective-permute-start
  24.3 0.0 collective-permute-done.4.refs_5_
  24.3 0.0 copy-start.1
  24.3 0.2 collective-permute-done.5.refs_7_
  24.4 0.6 copy-done.1
  25.1 0.0 copy-start.2
  25.1 0.0 collective-permute-done.2.refs_1_
  25.1 0.8 copy-done.2
  25.9 0.0 collective-permute-done.3.refs_3_.refs_7_
  25.9 0.0 copy-done
  25.9 55.5 %shard_map.129 = (bf16[1024,1024]{1,0:T(8,128)(2,1)}, bf16[1024,1024]{1,0:T(8,128)(2,1)}, f32[2048,256]{1,0:T(8,128)}, bf16[2048,1024]{1,0:T(8,128)(2,1)}) custom-call(s32[1]{0:T(128)} %bitcast.3.sc, bf16[2048,2048]{1,0:T(8,128)(2,1)} %shard_map.128.wq_hbm.refs_23_.refs_24_, bf16[2048,2048]{1,0:T(8,128)(2,1)} %bitcast.6, bf16[512,2048]{1,0:T(8,128)(2,1)} %refs_0_.1, ...), custom_call_target="tpu_custom_call" | custom-call | flops 32000000000 | bytes 20000000 | tf_op jit(solution)/shard_map/pallas_call | solution.py:420
  81.4 0.0 collective-permute-done.refs_0_.refs_2_.refs_8_
  81.4 0.3 collective-permute-start.8
  81.7 1.0 collective-permute-start.7
  82.7 3.2 %collective-permute-done.8.refs_1_.refs_3_.refs_9_ = bf16[512,2048]{1,0:T(8,128)(2,1)} collective-permute-done((bf16[512,2048]{1,0:T(8,128)(2,1)}, bf16[512,2048]{1,0:T(8,128)(2,1)}, u32[]{:S(2)}, u32[]{:S(2)}) %collective-permute-start.8) | collective-permute-done | bytes 2097184 | tf_op jit(solution)/shard_map/ppermute | solution.py:647
  86.0 32.2 %shard_map.130 = (bf16[1024,512]{1,0:T(8,128)(2,1)}, bf16[512,1024]{1,0:T(8,128)(2,1)}, f32[2048,256]{1,0:T(8,128)}, bf16[2048,512]{1,0:T(8,128)(2,1)}) custom-call(s32[1]{0:T(128)} %bitcast.3.sc, bf16[2048,2048]{1,0:T(8,128)(2,1)} %shard_map.128.wq_hbm.refs_23_.refs_24_, bf16[2048,2048]{1,0:T(8,128)(2,1)} %bitcast.7, ...), custom_call_target="tpu_custom_call" | custom-call | flops 16000000000 | bytes 20000000 | tf_op jit(solution)/shard_map/pallas_call | solution.py:420
  118.1 11.7 %collective-permute-done.7.refs_0_.refs_2_.refs_10_ = bf16[512,2048]{1,0:T(8,128)(2,1)} collective-permute-done((bf16[512,2048]{1,0:T(8,128)(2,1)}, bf16[512,2048]{1,0:T(8,128)(2,1)}, u32[]{:S(2)}, u32[]{:S(2)}) %collective-permute-start.7) | collective-permute-done | bytes 2097184 | tf_op jit(solution)/shard_map/ppermute | solution.py:648
  129.8 0.0 collective-permute-start.9
  129.8 0.5 collective-permute-start.6
  130.3 0.0 collective-permute-start.12
  130.3 0.5 collective-permute-start.10
  130.8 0.0 collective-permute-start.13
  130.8 3.5 %collective-permute-done.9.refs_1_.refs_3_.refs_11_ = bf16[512,2048]{1,0:T(8,128)(2,1)} collective-permute-done((bf16[512,2048]{1,0:T(8,128)(2,1)}, bf16[512,2048]{1,0:T(8,128)(2,1)}, u32[]{:S(2)}, u32[]{:S(2)}) %collective-permute-start.9) | collective-permute-done | bytes 2097184 | tf_op jit(solution)/shard_map/ppermute | solution.py:647
  134.3 27.8 %shard_map.131 = (bf16[1024,512]{1,0:T(8,128)(2,1)}, bf16[512,1024]{1,0:T(8,128)(2,1)}, bf16[2048,256]{1,0:T(8,128)(2,1)}, bf16[2048,512]{1,0:T(8,128)(2,1)}) custom-call(s32[1]{0:T(128)} %bitcast.3.sc, bf16[2048,2048]{1,0:T(8,128)(2,1)} %shard_map.128.wq_hbm.refs_23_.refs_24_, bf16[2048,2048]{1,0:T(8,128)(2,1)} %bitcast.8, ...), custom_call_target="tpu_custom_call" | custom-call | flops 16000000000 | bytes 20000000 | tf_op jit(solution)/shard_map/pallas_call | solution.py:420
  162.1 0.0 collective-permute-done.6.o_other.refs_3_
  162.1 0.2 collective-permute-start.15
  162.3 0.3 collective-permute-start.11
  162.6 0.0 collective-permute-done.12.refs_15_
  162.7 0.2 collective-permute-start.14
  162.8 9.3 %shard_map.132 = bf16[512,2048]{1,0:T(8,128)(2,1)} custom-call(s32[1]{0:T(128)} %bitcast.sc, bf16[1024,1024]{1,0:T(8,128)(2,1)} %get-tuple-element.45.o_mine.refs_0_, bf16[1024,1024]{1,0:T(8,128)(2,1)} %collective-permute-done.6.o_other.refs_3_, bf16[2048,2048]{1,0:T(8,128)(2,1)} %bitcast.9, bf16[2048,2048]{1,0:T(8,128)(2,1)} %bitcast.10), custom_call_target="tpu_custom_call" | custom-call | flops 4294967296 | bytes 12000000 | tf_op jit(solution)/shard_map/pallas_call | solution.py:469
  172.1 0.0 collective-permute-done.10.refs_4_
  172.1 0.0 collective-permute-done.13.refs_16_
  172.1 0.0 collective-permute-done.15.refs_19_
  172.1 0.0 collective-permute-done.11.refs_5_
  172.1 0.0 collective-permute-done.14.refs_17_
  172.1 63.0 %shard_map.133 = (f32[2048,2048]{1,0:T(8,128)}, f32[2048,16,128]{2,1,0:T(8,128)}, f32[2048,2,128]{2,1,0:T(2,128)}, f32[2048,2,128]{2,1,0:T(2,128)}, bf16[512,2048]{1,0:T(8,128)(2,1)}) custom-call(s32[1]{0:T(128)} %bitcast.sc, bf16[1024,1024]{1,0:T(8,128)(2,1)} %get-tuple-element.45.o_mine.refs_0_, bf16[1024,512]{1,0:T(8,128)(2,1)} %get-tuple-element.55.refs_1_, ...), custom_call_target="tpu_custom_call" | custom-call | flops 49999998976 | bytes 80000000 | tf_op jit(solution)/shard_map/pallas_call | solution.py:590
Async XLA Ops:
  0.6 24.4 %collective-permute-start.2 = (bf16[512,2048]{1,0:T(8,128)(2,1)}, bf16[512,2048]{1,0:T(8,128)(2,1)}, u32[]{:S(2)}, u32[]{:S(2)}) collective-permute-start(bf16[512,2048]{1,0:T(8,128)(2,1)} %refs_0_.1), channel_id=1, source_target_pairs={{0,1},{1,0},{2,3},{3,2},{4,5},{5,4},{6,7},{7,6}} | collective-permute-start | bytes 6291464 | tf_op jit(solution)/shard_map/ppermute | solution.py:647
  1.5 24.4 %collective-permute-start.3 = (bf16[512,2048]{1,0:T(8,128)(2,1)}, bf16[512,2048]{1,0:T(8,128)(2,1)}, u32[]{:S(2)}, u32[]{:S(2)}) collective-permute-start(bf16[512,2048]{1,0:T(8,128)(2,1)} %refs_6_.1), channel_id=1, source_target_pairs={{0,1},{1,0},{2,3},{3,2},{4,5},{5,4},{6,7},{7,6}} | collective-permute-start | bytes 6291464 | tf_op jit(solution)/shard_map/ppermute | solution.py:647
  7.2 15.3 %collective-permute-start.1 = (bf16[512,512]{1,0:T(8,128)(2,1)}, bf16[512,512]{1,0:T(8,128)(2,1)S(1)}, u32[]{:S(2)}, u32[]{:S(2)}) collective-permute-start(bf16[512,512]{1,0:T(8,128)(2,1)} %get-tuple-element.39.refs_4_), channel_id=1, source_target_pairs={{0,2},{2,0},{1,3},{3,1},{4,6},{6,4},{5,7},{7,5}} | collective-permute-start | bytes 1572872 | tf_op jit(solution)/shard_map/ppermute | solution.py:648
  10.2 14.1 %collective-permute-start.4 = (bf16[512,512]{1,0:T(8,128)(2,1)}, bf16[512,512]{1,0:T(8,128)(2,1)S(1)}, u32[]{:S(2)}, u32[]{:S(2)}) collective-permute-start(bf16[512,512]{1,0:T(8,128)(2,1)} %get-tuple-element.39.refs_4_), channel_id=1, source_target_pairs={{0,1},{1,0},{2,3},{3,2},{4,5},{5,4},{6,7},{7,6}} | collective-permute-start | bytes 1572872 | tf_op jit(solution)/shard_map/ppermute | solution.py:647
  22.5 3.4 %copy-start = (bf16[512,512]{1,0:T(8,128)(2,1)}, bf16[512,512]{1,0:T(8,128)(2,1)S(1)}, u32[]{:S(2)}) copy-start(bf16[512,512]{1,0:T(8,128)(2,1)S(1)} %collective-permute-done.1.refs_6_) | copy-start | bytes 1572868
  22.5 1.9 collective-permute-start.5
  22.5 58.9 %collective-permute-start = (bf16[512,2048]{1,0:T(8,128)(2,1)}, bf16[512,2048]{1,0:T(8,128)(2,1)}, u32[]{:S(2)}, u32[]{:S(2)}) collective-permute-start(bf16[512,2048]{1,0:T(8,128)(2,1)} %get-tuple-element.38), channel_id=1, source_target_pairs={{0,2},{2,0},{1,3},{3,1},{4,6},{6,4},{5,7},{7,5}} | collective-permute-start | bytes 6291464 | tf_op jit(solution)/shard_map/ppermute | solution.py:648
  24.3 0.8 copy-start.1
  25.1 0.8 copy-start.2
  81.4 4.5 %collective-permute-start.8 = (bf16[512,2048]{1,0:T(8,128)(2,1)}, bf16[512,2048]{1,0:T(8,128)(2,1)}, u32[]{:S(2)}, u32[]{:S(2)}) collective-permute-start(bf16[512,2048]{1,0:T(8,128)(2,1)} %collective-permute-done.refs_0_.refs_2_.refs_8_), channel_id=1, source_target_pairs={{0,1},{1,0},{2,3},{3,2},{4,5},{5,4},{6,7},{7,6}} | collective-permute-start | bytes 6291464 | tf_op jit(solution)/shard_map/ppermute | solution.py:647
  81.7 48.1 %collective-permute-start.7 = (bf16[512,2048]{1,0:T(8,128)(2,1)}, bf16[512,2048]{1,0:T(8,128)(2,1)}, u32[]{:S(2)}, u32[]{:S(2)}) collective-permute-start(bf16[512,2048]{1,0:T(8,128)(2,1)} %get-tuple-element.46), channel_id=1, source_target_pairs={{0,2},{2,0},{1,3},{3,1},{4,6},{6,4},{5,7},{7,5}} | collective-permute-start | bytes 6291464 | tf_op jit(solution)/shard_map/ppermute | solution.py:648
  129.8 4.5 %collective-permute-start.9 = (bf16[512,2048]{1,0:T(8,128)(2,1)}, bf16[512,2048]{1,0:T(8,128)(2,1)}, u32[]{:S(2)}, u32[]{:S(2)}) collective-permute-start(bf16[512,2048]{1,0:T(8,128)(2,1)} %collective-permute-done.7.refs_0_.refs_2_.refs_10_), channel_id=1, source_target_pairs={{0,1},{1,0},{2,3},{3,2},{4,5},{5,4},{6,7},{7,6}} | collective-permute-start | bytes 6291464 | tf_op jit(solution)/shard_map/ppermute | solution.py:647
  129.8 32.3 %collective-permute-start.6 = (bf16[1024,1024]{1,0:T(8,128)(2,1)}, bf16[1024,1024]{1,0:T(8,128)(2,1)}, u32[]{:S(2)}, u32[]{:S(2)}) collective-permute-start(bf16[1024,1024]{1,0:T(8,128)(2,1)} %get-tuple-element.45.o_mine.refs_0_), channel_id=1, source_target_pairs={{0,1},{1,0},{2,3},{3,2},{4,5},{5,4},{6,7},{7,6}} | collective-permute-start | bytes 6291464 | tf_op jit(solution)/shard_map/ppermute | solution.py:647
  130.3 32.3 %collective-permute-start.12 = (bf16[1024,1024]{1,0:T(8,128)(2,1)}, bf16[1024,1024]{1,0:T(8,128)(2,1)}, u32[]{:S(2)}, u32[]{:S(2)}) collective-permute-start(bf16[1024,1024]{1,0:T(8,128)(2,1)} %get-tuple-element.57.refs_12_), channel_id=1, source_target_pairs={{0,1},{1,0},{2,3},{3,2},{4,5},{5,4},{6,7},{7,6}} | collective-permute-start | bytes 6291464 | tf_op jit(solution)/shard_map/ppermute | solution.py:647
  130.3 41.8 %collective-permute-start.10 = (bf16[1024,512]{1,0:T(8,128)(2,1)}, bf16[1024,512]{1,0:T(8,128)(2,1)}, u32[]{:S(2)}, u32[]{:S(2)}) collective-permute-start(bf16[1024,512]{1,0:T(8,128)(2,1)} %get-tuple-element.55.refs_1_), channel_id=1, source_target_pairs={{0,1},{1,0},{2,3},{3,2},{4,5},{5,4},{6,7},{7,6}} | collective-permute-start | bytes 3145736 | tf_op jit(solution)/shard_map/ppermute | solution.py:647
  130.8 41.3 %collective-permute-start.13 = (bf16[512,1024]{1,0:T(8,128)(2,1)}, bf16[512,1024]{1,0:T(8,128)(2,1)}, u32[]{:S(2)}, u32[]{:S(2)}) collective-permute-start(bf16[512,1024]{1,0:T(8,128)(2,1)} %get-tuple-element.58.refs_13_), channel_id=1, source_target_pairs={{0,1},{1,0},{2,3},{3,2},{4,5},{5,4},{6,7},{7,6}} | collective-permute-start | bytes 3145736 | tf_op jit(solution)/shard_map/ppermute | solution.py:647
  162.1 10.0 %collective-permute-start.15 = (bf16[2048,256]{1,0:T(8,128)(2,1)}, bf16[2048,256]{1,0:T(8,128)(2,1)}, u32[]{:S(2)}, u32[]{:S(2)}) collective-permute-start(bf16[2048,256]{1,0:T(8,128)(2,1)} %get-tuple-element.60.refs_18_), channel_id=1, source_target_pairs={{0,1},{1,0},{2,3},{3,2},{4,5},{5,4},{6,7},{7,6}} | collective-permute-start | bytes 3145736 | tf_op jit(solution)/shard_map/ppermute | solution.py:647
  162.3 9.8 %collective-permute-start.11 = (bf16[1024,512]{1,0:T(8,128)(2,1)}, bf16[1024,512]{1,0:T(8,128)(2,1)}, u32[]{:S(2)}, u32[]{:S(2)}) collective-permute-start(bf16[1024,512]{1,0:T(8,128)(2,1)} %get-tuple-element.56.refs_2_), channel_id=1, source_target_pairs={{0,1},{1,0},{2,3},{3,2},{4,5},{5,4},{6,7},{7,6}} | collective-permute-start | bytes 3145736 | tf_op jit(solution)/shard_map/ppermute | solution.py:647
  162.7 9.5 %collective-permute-start.14 = (bf16[512,1024]{1,0:T(8,128)(2,1)}, bf16[512,1024]{1,0:T(8,128)(2,1)}, u32[]{:S(2)}, u32[]{:S(2)}) collective-permute-start(bf16[512,1024]{1,0:T(8,128)(2,1)} %get-tuple-element.59.refs_14_), channel_id=1, source_target_pairs={{0,1},{1,0},{2,3},{3,2},{4,5},{5,4},{6,7},{7,6}} | collective-permute-start | bytes 3145736 | tf_op jit(solution)/shard_map/ppermute | solution.py:647

commit v9 on v8

--- a/solution.py
+++ b/solution.py
@@ -224,24 +224,12 @@
 
     @pl.when(step == 0)
     def _():
-        load_x, load_dy = load_rows(0)
+        load_x, _ = load_rows(0)
         for cp in load_kv:
             cp.start()
         load_x.start()
         for cp in load_wq:
             cp.start()
-        load_dy.start()
-        for cp in load_wo:
-            cp.start()
-        for cp in [] if first else grads(init_hbm, False):
-            cp.start()
-
-    for n in range(1, steps):
-
-        @pl.when(step == n - 1)
-        def _():
-            for cp in load_rows(n):
-                cp.start()
 
     @pl.when(step == 0)
     def _():
@@ -254,6 +242,8 @@
             at = slice(i * BLK, (i + 1) * BLK)
             kt[:, at] = ks[at, :].T
             vt[:, at] = vs[at, :].T
+        for cp in [load_rows(0)[1], *load_wo, *([] if first else grads(init_hbm, False))]:
+            cp.start()
 
     @pl.when(step == 0)
     def _():
@@ -276,6 +266,14 @@
 
     pltpu.make_async_copy(dy_hbm[0].at[0:BLK, :], dys.at[slot], dy_sem.at[slot]).wait()
     do = dot_nt(dys[slot], wo[...]).astype(BF16)
+
+    for n in range(1, steps):
+
+        @pl.when(step == n - 1)
+        def _():
+            for cp in load_rows(n):
+                cp.start()
+
     for h in range(heads):
         dh = do[:, h * hd : (h + 1) * hd]
         dost[h * BLK : (h + 1) * BLK, :] = dh
@@ -490,11 +488,11 @@
 STARTS = (0, DUO, HALF, 1280, 1536, 1792)
 
 
-def piece_copies(core, arrays, dst, sem):
+def piece_copies(core, arrays, dst, sem, rows):
     copies = []
     for n, ((flip, size), start) in enumerate(zip(PIECES, STARTS)):
         at = pl.ds(pl.multiple_of((1 - core if flip else core) * size, size), size)
-        copies.append(pltpu.make_async_copy(arrays[n // 2].at[:, at], dst.at[:, start : start + size], sem))
+        copies.append(pltpu.make_async_copy(arrays[n // 2].at[rows, at], dst.at[rows, start : start + size], sem))
     return copies
 
 
@@ -505,21 +503,24 @@
     step, core, hd = pl.program_id(0), sc[0], HD
     tile, wide = gwo_ref.shape
     spans = [slice(0, HALF), slice(HALF, HALF + DUO), slice(HALF + DUO, SEQ)]
-    o_copies = [piece_copies(core, o, o_all.at[n], sems.at[n]) for n, o in enumerate((o_mine, o_other))]
+    o_copies = [
+        [piece_copies(core, o, o_all.at[n], sems.at[n, t], slice(t * tile, (t + 1) * tile)) for t in range(2)]
+        for n, o in enumerate((o_mine, o_other))
+    ]
     y_copies = [
         [
             pltpu.make_async_copy(
-                y.at[y.shape[0] - r if r == BLK else 0 :, n * wide : (n + 1) * wide], y_all.at[n, s : s + r, :], sems.at[2 + n]
+                y.at[y.shape[0] - r if r == BLK else 0 :, n * wide : (n + 1) * wide], y_all.at[n, s : s + r, :], sems.at[2, n]
             )
             for y, s, (_, r) in zip(ys, STARTS, PIECES)
         ]
         for n in range(2)
     ]
     q_copies = [
-        [pltpu.make_async_copy(a, dq.at[n, at, :], sems.at[4]) for a, at in zip(part, spans)]
+        [pltpu.make_async_copy(a, dq.at[n, at, :], sems.at[3, 0]) for a, at in zip(part, spans)]
         for n, part in enumerate((q_mine, q_other))
     ]
-    kv_copies = [pltpu.make_async_copy(a, kv.at[:, n * BLK : (n + 1) * BLK], sems.at[4]) for n, a in enumerate(kv_in)]
+    kv_copies = [pltpu.make_async_copy(a, kv.at[:, n * BLK : (n + 1) * BLK], sems.at[3, 0]) for n, a in enumerate(kv_in)]
 
     def start(at, copies):
         @pl.when(step == at)
@@ -534,12 +535,13 @@
                 cp.wait()
 
     rest = q_copies[0] + q_copies[1] + kv_copies
-    start(0, y_copies[0] + o_copies[0])
-    start(1, o_copies[1])
+    start(0, o_copies[0][0] + y_copies[0])
+    wait(0, o_copies[0][0] + y_copies[0])
+    start(0, o_copies[0][1] + o_copies[1][0] + o_copies[1][1])
     start(2, y_copies[1])
     start(3, rest)
-    wait(0, y_copies[0] + o_copies[0])
-    wait(2, o_copies[1])
+    wait(1, o_copies[0][1])
+    wait(2, o_copies[1][0] + o_copies[1][1])
     wait(4, y_copies[1])
     wait(WO_STEPS, rest)
 
@@ -619,7 +621,7 @@
                 pltpu.VMEM((2, SEQ, half), BF16),
                 pltpu.VMEM((SEQ, DUO), BF16),
                 pltpu.VMEM((DUO, DUO), BF16),
-                pltpu.SemaphoreType.DMA((5,)),
+                pltpu.SemaphoreType.DMA((4, 2)),
             ],
         ),
         compiler_params=params(1, 63),

time: 235 us -> 234 us (level)
  no operation moved by 1% of the time
where the time goes in v9:
time: 234 us; the launch traced here: 233 us
  Pallas kernels  200 us (85%)
  waiting for transfers between devices  22.9 us (10%)
  starting transfers between devices  8.58 us (4%)
    pallas_call x3, Pallas kernels, attention(): pl.pallas_call(functools.partial(attn_kernel, kind, heads, scale, rows //...  115 us
    pallas_call x1, Pallas kernels, tail(): pl.pallas_call(tail_kernel, out_shape=(jax.ShapeDtypeStruct((2 * half, mo...  61.8 us
    ppermute x3, waiting for transfers between devices, device_layer(): to_chip = lambda v: lax.ppermute(v, 'cp', chip_swap)  15.9 us
    pallas_call x1, Pallas kernels, out_rows(): pl.pallas_call(y_kernel, out_shape=jax.ShapeDtypeStruct((rows, model), BF...  9.28 us
    pallas_call x1, Pallas kernels, flat_heads(): pl.pallas_call(heads_kernel, out_shape=jax.ShapeDtypeStruct((model, num *...  7.87 us
    ppermute x13, waiting for transfers between devices, device_layer(): to_core = lambda v: lax.ppermute(v, 'cp', core_swap)  6.91 us
    ppermute x3, starting transfers between devices, device_layer(): to_chip = lambda v: lax.ppermute(v, 'cp', chip_swap)  5.7 us
    pallas_call x1, Pallas kernels, project_kv(): pl.pallas_call(kv_kernel, out_shape=(jax.ShapeDtypeStruct((rows, DUO), BF...  5.69 us
  transfers between devices with their start and end apart: 16, of which 5 were waited for; matrix products, arithmetic and copies ran while one was open for 0% of the time, Pallas kernels for 59%

profile of v9, /device:TPU:0, one launch (start us, length us, event | category | flops | bytes accessed | tf_op | source)
XLA Modules:
  0.0 233.4 jit_solution(15863160928286240303)
XLA Ops:
  0.6 0.9 collective-permute-start.2
  1.5 0.0 collective-permute-start.3
  1.5 5.7 %shard_map.127 = (bf16[512,512]{1,0:T(8,128)(2,1)}, bf16[2048,512]{1,0:T(8,128)(2,1)}, bf16[512,2048]{1,0:T(8,128)(2,1)}, bf16[512,2048]{1,0:T(8,128)(2,1)}) custom-call(s32[1]{0:T(128)} %bitcast.sc, bf16[512,2048]{1,0:T(8,128)(2,1)} %refs_0_.1, bf16[512,2048]{1,0:T(8,128)(2,1)} %refs_6_.1, bf16[4096,128]{1,0:T(8,128)(2,1)} %bitcast.11, ...), custom_call_target="tpu_custom_call" | custom-call | flops 1073741824 | bytes 8000000 | tf_op jit(solution)/shard_map/pallas_call | solution.py:146
  7.2 3.0 %collective-permute-start.1 = (bf16[512,512]{1,0:T(8,128)(2,1)}, bf16[512,512]{1,0:T(8,128)(2,1)S(1)}, u32[]{:S(2)}, u32[]{:S(2)}) collective-permute-start(bf16[512,512]{1,0:T(8,128)(2,1)} %get-tuple-element.39.refs_4_), channel_id=1, source_target_pairs={{0,2},{2,0},{1,3},{3,1},{4,6},{6,4},{5,7},{7,5}} | collective-permute-start | bytes 1572872 | tf_op jit(solution)/shard_map/ppermute | solution.py:650
  10.2 0.0 collective-permute-start.4
  10.2 7.9 %shard_map.128.wq_hbm.refs_23_.refs_24_ = bf16[2048,2048]{1,0:T(8,128)(2,1)} custom-call(bf16[256,256]{1,0:T(8,128)(2,1)} %constant.11.clone.perm_ref, bf16[2048,16,128]{2,1,0:T(8,128)(2,1)} %w_hbm), custom_call_target="tpu_custom_call" | custom-call | flops 4000000000 | bytes 16777216 | tf_op jit(solution)/shard_map/pallas_call | solution.py:85
  18.1 4.5 %collective-permute-done.1.refs_6_ = bf16[512,512]{1,0:T(8,128)(2,1)S(1)} collective-permute-done((bf16[512,512]{1,0:T(8,128)(2,1)}, bf16[512,512]{1,0:T(8,128)(2,1)S(1)}, u32[]{:S(2)}, u32[]{:S(2)}) %collective-permute-start.1) | collective-permute-done | bytes 524320 | tf_op jit(solution)/shard_map/ppermute | solution.py:650
  22.5 0.0 copy-start
  22.5 0.0 collective-permute-start.5
  22.5 1.7 collective-permute-start
  24.3 0.0 collective-permute-done.4.refs_5_
  24.3 0.0 copy-start.1
  24.3 0.2 collective-permute-done.5.refs_7_
  24.4 0.6 copy-done.1
  25.1 0.0 copy-start.2
  25.1 0.0 collective-permute-done.2.refs_1_
  25.1 0.8 copy-done.2
  25.9 0.0 collective-permute-done.3.refs_3_.refs_7_
  25.9 0.0 copy-done
  25.9 54.6 %shard_map.129 = (bf16[1024,1024]{1,0:T(8,128)(2,1)}, bf16[1024,1024]{1,0:T(8,128)(2,1)}, f32[2048,256]{1,0:T(8,128)}, bf16[2048,1024]{1,0:T(8,128)(2,1)}) custom-call(s32[1]{0:T(128)} %bitcast.3.sc, bf16[2048,2048]{1,0:T(8,128)(2,1)} %shard_map.128.wq_hbm.refs_23_.refs_24_, bf16[2048,2048]{1,0:T(8,128)(2,1)} %bitcast.6, bf16[512,2048]{1,0:T(8,128)(2,1)} %refs_0_.1, ...), custom_call_target="tpu_custom_call" | custom-call | flops 32000000000 | bytes 20000000 | tf_op jit(solution)/shard_map/pallas_call | solution.py:418
  80.5 0.0 collective-permute-done.refs_0_.refs_2_.refs_8_
  80.5 0.3 collective-permute-start.8
  80.8 1.0 collective-permute-start.7
  81.8 3.2 %collective-permute-done.8.refs_1_.refs_3_.refs_9_ = bf16[512,2048]{1,0:T(8,128)(2,1)} collective-permute-done((bf16[512,2048]{1,0:T(8,128)(2,1)}, bf16[512,2048]{1,0:T(8,128)(2,1)}, u32[]{:S(2)}, u32[]{:S(2)}) %collective-permute-start.8) | collective-permute-done | bytes 2097184 | tf_op jit(solution)/shard_map/ppermute | solution.py:649
  85.0 32.4 %shard_map.130 = (bf16[1024,512]{1,0:T(8,128)(2,1)}, bf16[512,1024]{1,0:T(8,128)(2,1)}, f32[2048,256]{1,0:T(8,128)}, bf16[2048,512]{1,0:T(8,128)(2,1)}) custom-call(s32[1]{0:T(128)} %bitcast.3.sc, bf16[2048,2048]{1,0:T(8,128)(2,1)} %shard_map.128.wq_hbm.refs_23_.refs_24_, bf16[2048,2048]{1,0:T(8,128)(2,1)} %bitcast.7, ...), custom_call_target="tpu_custom_call" | custom-call | flops 16000000000 | bytes 20000000 | tf_op jit(solution)/shard_map/pallas_call | solution.py:418
  117.4 11.5 %collective-permute-done.7.refs_0_.refs_2_.refs_10_ = bf16[512,2048]{1,0:T(8,128)(2,1)} collective-permute-done((bf16[512,2048]{1,0:T(8,128)(2,1)}, bf16[512,2048]{1,0:T(8,128)(2,1)}, u32[]{:S(2)}, u32[]{:S(2)}) %collective-permute-start.7) | collective-permute-done | bytes 2097184 | tf_op jit(solution)/shard_map/ppermute | solution.py:650
  128.9 0.0 collective-permute-start.9
  128.9 0.5 collective-permute-start.6
  129.4 0.0 collective-permute-start.12
  129.4 0.5 collective-permute-start.10
  129.9 0.0 collective-permute-start.13
  129.9 3.5 %collective-permute-done.9.refs_1_.refs_3_.refs_11_ = bf16[512,2048]{1,0:T(8,128)(2,1)} collective-permute-done((bf16[512,2048]{1,0:T(8,128)(2,1)}, bf16[512,2048]{1,0:T(8,128)(2,1)}, u32[]{:S(2)}, u32[]{:S(2)}) %collective-permute-start.9) | collective-permute-done | bytes 2097184 | tf_op jit(solution)/shard_map/ppermute | solution.py:649
  133.4 28.0 %shard_map.131 = (bf16[1024,512]{1,0:T(8,128)(2,1)}, bf16[512,1024]{1,0:T(8,128)(2,1)}, bf16[2048,256]{1,0:T(8,128)(2,1)}, bf16[2048,512]{1,0:T(8,128)(2,1)}) custom-call(s32[1]{0:T(128)} %bitcast.3.sc, bf16[2048,2048]{1,0:T(8,128)(2,1)} %shard_map.128.wq_hbm.refs_23_.refs_24_, bf16[2048,2048]{1,0:T(8,128)(2,1)} %bitcast.8, ...), custom_call_target="tpu_custom_call" | custom-call | flops 16000000000 | bytes 20000000 | tf_op jit(solution)/shard_map/pallas_call | solution.py:418
  161.4 0.0 collective-permute-done.6.o_other.refs_3_
  161.4 0.2 collective-permute-start.15
  161.6 0.4 collective-permute-start.11
  162.0 0.0 collective-permute-done.12.refs_15_
  162.0 0.1 collective-permute-start.14
  162.1 9.3 %shard_map.132 = bf16[512,2048]{1,0:T(8,128)(2,1)} custom-call(s32[1]{0:T(128)} %bitcast.sc, bf16[1024,1024]{1,0:T(8,128)(2,1)} %get-tuple-element.45.o_mine.refs_0_, bf16[1024,1024]{1,0:T(8,128)(2,1)} %collective-permute-done.6.o_other.refs_3_, bf16[2048,2048]{1,0:T(8,128)(2,1)} %bitcast.9, bf16[2048,2048]{1,0:T(8,128)(2,1)} %bitcast.10), custom_call_target="tpu_custom_call" | custom-call | flops 4294967296 | bytes 12000000 | tf_op jit(solution)/shard_map/pallas_call | solution.py:467
  171.4 0.0 collective-permute-done.10.refs_4_
  171.4 0.0 collective-permute-done.13.refs_16_
  171.4 0.0 collective-permute-done.15.refs_19_
  171.4 0.0 collective-permute-done.11.refs_5_
  171.4 0.0 collective-permute-done.14.refs_17_
  171.4 61.8 %shard_map.133 = (f32[2048,2048]{1,0:T(8,128)}, f32[2048,16,128]{2,1,0:T(8,128)}, f32[2048,2,128]{2,1,0:T(2,128)}, f32[2048,2,128]{2,1,0:T(2,128)}, bf16[512,2048]{1,0:T(8,128)(2,1)}) custom-call(s32[1]{0:T(128)} %bitcast.sc, bf16[1024,1024]{1,0:T(8,128)(2,1)} %get-tuple-element.45.o_mine.refs_0_, bf16[1024,512]{1,0:T(8,128)(2,1)} %get-tuple-element.55.refs_1_, ...), custom_call_target="tpu_custom_call" | custom-call | flops 49999998976 | bytes 80000000 | tf_op jit(solution)/shard_map/pallas_call | solution.py:592
Async XLA Ops:
  0.6 24.4 %collective-permute-start.2 = (bf16[512,2048]{1,0:T(8,128)(2,1)}, bf16[512,2048]{1,0:T(8,128)(2,1)}, u32[]{:S(2)}, u32[]{:S(2)}) collective-permute-start(bf16[512,2048]{1,0:T(8,128)(2,1)} %refs_0_.1), channel_id=1, source_target_pairs={{0,1},{1,0},{2,3},{3,2},{4,5},{5,4},{6,7},{7,6}} | collective-permute-start | bytes 6291464 | tf_op jit(solution)/shard_map/ppermute | solution.py:649
  1.5 24.4 %collective-permute-start.3 = (bf16[512,2048]{1,0:T(8,128)(2,1)}, bf16[512,2048]{1,0:T(8,128)(2,1)}, u32[]{:S(2)}, u32[]{:S(2)}) collective-permute-start(bf16[512,2048]{1,0:T(8,128)(2,1)} %refs_6_.1), channel_id=1, source_target_pairs={{0,1},{1,0},{2,3},{3,2},{4,5},{5,4},{6,7},{7,6}} | collective-permute-start | bytes 6291464 | tf_op jit(solution)/shard_map/ppermute | solution.py:649
  7.2 15.3 %collective-permute-start.1 = (bf16[512,512]{1,0:T(8,128)(2,1)}, bf16[512,512]{1,0:T(8,128)(2,1)S(1)}, u32[]{:S(2)}, u32[]{:S(2)}) collective-permute-start(bf16[512,512]{1,0:T(8,128)(2,1)} %get-tuple-element.39.refs_4_), channel_id=1, source_target_pairs={{0,2},{2,0},{1,3},{3,1},{4,6},{6,4},{5,7},{7,5}} | collective-permute-start | bytes 1572872 | tf_op jit(solution)/shard_map/ppermute | solution.py:650
  10.2 14.1 %collective-permute-start.4 = (bf16[512,512]{1,0:T(8,128)(2,1)}, bf16[512,512]{1,0:T(8,128)(2,1)S(1)}, u32[]{:S(2)}, u32[]{:S(2)}) collective-permute-start(bf16[512,512]{1,0:T(8,128)(2,1)} %get-tuple-element.39.refs_4_), channel_id=1, source_target_pairs={{0,1},{1,0},{2,3},{3,2},{4,5},{5,4},{6,7},{7,6}} | collective-permute-start | bytes 1572872 | tf_op jit(solution)/shard_map/ppermute | solution.py:649
  22.5 3.4 %copy-start = (bf16[512,512]{1,0:T(8,128)(2,1)}, bf16[512,512]{1,0:T(8,128)(2,1)S(1)}, u32[]{:S(2)}) copy-start(bf16[512,512]{1,0:T(8,128)(2,1)S(1)} %collective-permute-done.1.refs_6_) | copy-start | bytes 1572868
  22.5 1.9 collective-permute-start.5
  22.5 58.0 %collective-permute-start = (bf16[512,2048]{1,0:T(8,128)(2,1)}, bf16[512,2048]{1,0:T(8,128)(2,1)}, u32[]{:S(2)}, u32[]{:S(2)}) collective-permute-start(bf16[512,2048]{1,0:T(8,128)(2,1)} %get-tuple-element.38), channel_id=1, source_target_pairs={{0,2},{2,0},{1,3},{3,1},{4,6},{6,4},{5,7},{7,5}} | collective-permute-start | bytes 6291464 | tf_op jit(solution)/shard_map/ppermute | solution.py:650
  24.3 0.8 copy-start.1
  25.1 0.8 copy-start.2
  80.5 4.5 %collective-permute-start.8 = (bf16[512,2048]{1,0:T(8,128)(2,1)}, bf16[512,2048]{1,0:T(8,128)(2,1)}, u32[]{:S(2)}, u32[]{:S(2)}) collective-permute-start(bf16[512,2048]{1,0:T(8,128)(2,1)} %collective-permute-done.refs_0_.refs_2_.refs_8_), channel_id=1, source_target_pairs={{0,1},{1,0},{2,3},{3,2},{4,5},{5,4},{6,7},{7,6}} | collective-permute-start | bytes 6291464 | tf_op jit(solution)/shard_map/ppermute | solution.py:649
  80.8 48.1 %collective-permute-start.7 = (bf16[512,2048]{1,0:T(8,128)(2,1)}, bf16[512,2048]{1,0:T(8,128)(2,1)}, u32[]{:S(2)}, u32[]{:S(2)}) collective-permute-start(bf16[512,2048]{1,0:T(8,128)(2,1)} %get-tuple-element.46), channel_id=1, source_target_pairs={{0,2},{2,0},{1,3},{3,1},{4,6},{6,4},{5,7},{7,5}} | collective-permute-start | bytes 6291464 | tf_op jit(solution)/shard_map/ppermute | solution.py:650
  128.9 4.5 %collective-permute-start.9 = (bf16[512,2048]{1,0:T(8,128)(2,1)}, bf16[512,2048]{1,0:T(8,128)(2,1)}, u32[]{:S(2)}, u32[]{:S(2)}) collective-permute-start(bf16[512,2048]{1,0:T(8,128)(2,1)} %collective-permute-done.7.refs_0_.refs_2_.refs_10_), channel_id=1, source_target_pairs={{0,1},{1,0},{2,3},{3,2},{4,5},{5,4},{6,7},{7,6}} | collective-permute-start | bytes 6291464 | tf_op jit(solution)/shard_map/ppermute | solution.py:649
  128.9 32.5 %collective-permute-start.6 = (bf16[1024,1024]{1,0:T(8,128)(2,1)}, bf16[1024,1024]{1,0:T(8,128)(2,1)}, u32[]{:S(2)}, u32[]{:S(2)}) collective-permute-start(bf16[1024,1024]{1,0:T(8,128)(2,1)} %get-tuple-element.45.o_mine.refs_0_), channel_id=1, source_target_pairs={{0,1},{1,0},{2,3},{3,2},{4,5},{5,4},{6,7},{7,6}} | collective-permute-start | bytes 6291464 | tf_op jit(solution)/shard_map/ppermute | solution.py:649
  129.4 32.5 %collective-permute-start.12 = (bf16[1024,1024]{1,0:T(8,128)(2,1)}, bf16[1024,1024]{1,0:T(8,128)(2,1)}, u32[]{:S(2)}, u32[]{:S(2)}) collective-permute-start(bf16[1024,1024]{1,0:T(8,128)(2,1)} %get-tuple-element.57.refs_12_), channel_id=1, source_target_pairs={{0,1},{1,0},{2,3},{3,2},{4,5},{5,4},{6,7},{7,6}} | collective-permute-start | bytes 6291464 | tf_op jit(solution)/shard_map/ppermute | solution.py:649
  129.4 42.0 %collective-permute-start.10 = (bf16[1024,512]{1,0:T(8,128)(2,1)}, bf16[1024,512]{1,0:T(8,128)(2,1)}, u32[]{:S(2)}, u32[]{:S(2)}) collective-permute-start(bf16[1024,512]{1,0:T(8,128)(2,1)} %get-tuple-element.55.refs_1_), channel_id=1, source_target_pairs={{0,1},{1,0},{2,3},{3,2},{4,5},{5,4},{6,7},{7,6}} | collective-permute-start | bytes 3145736 | tf_op jit(solution)/shard_map/ppermute | solution.py:649
  129.9 41.5 %collective-permute-start.13 = (bf16[512,1024]{1,0:T(8,128)(2,1)}, bf16[512,1024]{1,0:T(8,128)(2,1)}, u32[]{:S(2)}, u32[]{:S(2)}) collective-permute-start(bf16[512,1024]{1,0:T(8,128)(2,1)} %get-tuple-element.58.refs_13_), channel_id=1, source_target_pairs={{0,1},{1,0},{2,3},{3,2},{4,5},{5,4},{6,7},{7,6}} | collective-permute-start | bytes 3145736 | tf_op jit(solution)/shard_map/ppermute | solution.py:649
  161.4 10.0 %collective-permute-start.15 = (bf16[2048,256]{1,0:T(8,128)(2,1)}, bf16[2048,256]{1,0:T(8,128)(2,1)}, u32[]{:S(2)}, u32[]{:S(2)}) collective-permute-start(bf16[2048,256]{1,0:T(8,128)(2,1)} %get-tuple-element.60.refs_18_), channel_id=1, source_target_pairs={{0,1},{1,0},{2,3},{3,2},{4,5},{5,4},{6,7},{7,6}} | collective-permute-start | bytes 3145736 | tf_op jit(solution)/shard_map/ppermute | solution.py:649
  161.6 9.8 %collective-permute-start.11 = (bf16[1024,512]{1,0:T(8,128)(2,1)}, bf16[1024,512]{1,0:T(8,128)(2,1)}, u32[]{:S(2)}, u32[]{:S(2)}) collective-permute-start(bf16[1024,512]{1,0:T(8,128)(2,1)} %get-tuple-element.56.refs_2_), channel_id=1, source_target_pairs={{0,1},{1,0},{2,3},{3,2},{4,5},{5,4},{6,7},{7,6}} | collective-permute-start | bytes 3145736 | tf_op jit(solution)/shard_map/ppermute | solution.py:649
  162.0 9.5 %collective-permute-start.14 = (bf16[512,1024]{1,0:T(8,128)(2,1)}, bf16[512,1024]{1,0:T(8,128)(2,1)}, u32[]{:S(2)}, u32[]{:S(2)}) collective-permute-start(bf16[512,1024]{1,0:T(8,128)(2,1)} %get-tuple-element.59.refs_14_), channel_id=1, source_target_pairs={{0,1},{1,0},{2,3},{3,2},{4,5},{5,4},{6,7},{7,6}} | collective-permute-start | bytes 3145736 | tf_op jit(solution)/shard_map/ppermute | solution.py:649

commit v10 on v9

--- a/solution.py
+++ b/solution.py
@@ -361,15 +361,13 @@
         o_ref[h * hd : (h + 1) * hd, :] = o_round[:, h * BLK : (h + 1) * BLK]
     dqt[...] = jnp.zeros_like(dqt)
 
-    def grad_block(j, _):
-        at = pl.ds(pl.multiple_of(j * BLK, BLK), BLK)
+    def grad_block(start, rows):
+        at = pl.ds(start, rows)
         dp = dot(vs[at, :], dot_t[...])
         dv[at, :] += dot(p_ref[at, :], dost[...])
-        ds = (p_ref[at, :].astype(F32) * (dp - delta)).astype(BF16)
-        ds_ref[...] = ds
-        dqt[...] += dot(kt[:, at], ds_ref[...])
-        dk[at, :] += dot(ds_ref[...], qst[...])
-        return 0
+        ds_ref[:rows, :] = (p_ref[at, :].astype(F32) * (dp - delta)).astype(BF16)
+        dqt[...] += dot(kt[:, at], ds_ref[:rows, :])
+        dk[at, :] += dot(ds_ref[:rows, :], qst[...])
 
     if not first:
 
@@ -378,7 +376,15 @@
             for cp in grads(init_hbm, False):
                 cp.wait()
 
-    lax.fori_loop(0, b + 1, grad_block, 0)
+    if first:
+        sweep(b + 1, grad_block)
+    else:
+
+        def one_block(j, _):
+            grad_block(pl.multiple_of(j * BLK, BLK), BLK)
+            return 0
+
+        lax.fori_loop(0, b + 1, one_block, 0)
 
     for h in range(heads):
         dq_ref[:, h * hd : (h + 1) * hd] = (dqt[:, h * BLK : (h + 1) * BLK] * scale).astype(BF16).T
@@ -436,7 +442,7 @@
                 *[pltpu.VMEM((wide, hd), BF16) for _ in "qd"],
                 pltpu.VMEM((seq, wide), F32),
                 pltpu.VMEM((seq, wide), BF16),
-                pltpu.VMEM((BLK, wide), BF16),
+                pltpu.VMEM((2 * BLK, wide), BF16),
                 *[pltpu.VMEM((hd, wide), F32) for _ in "od"],
                 pltpu.VMEM((8, wide), F32),
                 pltpu.VMEM((1, wide), F32),

time: 234 us -> 232 us (level)
  no operation moved by 1% of the time
where the time goes in v10:
time: 232 us
  Pallas kernels  198 us (85%)
  waiting for transfers between devices  22.8 us (10%)
  starting transfers between devices  8.6 us (4%)
    pallas_call x3, Pallas kernels, attention(): pl.pallas_call(functools.partial(attn_kernel, kind, heads, scale, rows //...  114 us
    pallas_call x1, Pallas kernels, tail(): pl.pallas_call(tail_kernel, out_shape=(jax.ShapeDtypeStruct((2 * half, mo...  61.8 us
    ppermute x3, waiting for transfers between devices, device_layer(): to_chip = lambda v: lax.ppermute(v, 'cp', chip_swap)  15.9 us
    pallas_call x1, Pallas kernels, out_rows(): pl.pallas_call(y_kernel, out_shape=jax.ShapeDtypeStruct((rows, model), BF...  9.28 us
    pallas_call x1, Pallas kernels, flat_heads(): pl.pallas_call(heads_kernel, out_shape=jax.ShapeDtypeStruct((model, num *...  7.87 us
    ppermute x13, waiting for transfers between devices, device_layer(): to_core = lambda v: lax.ppermute(v, 'cp', core_swap)  6.89 us
    ppermute x3, starting transfers between devices, device_layer(): to_chip = lambda v: lax.ppermute(v, 'cp', chip_swap)  5.72 us
    pallas_call x1, Pallas kernels, project_kv(): pl.pallas_call(kv_kernel, out_shape=(jax.ShapeDtypeStruct((rows, DUO), BF...  5.69 us
  transfers between devices with their start and end apart: 16, of which 5 were waited for; matrix products, arithmetic and copies ran while one was open for 0% of the time, Pallas kernels for 59%

profile of v10, /device:TPU:0, one launch (start us, length us, event | category | flops | bytes accessed | tf_op | source)
XLA Modules:
  0.0 232.2 jit_solution(13342441745447374994)
XLA Ops:
  0.6 0.9 collective-permute-start.2
  1.5 0.0 collective-permute-start.3
  1.5 5.7 %shard_map.127 = (bf16[512,512]{1,0:T(8,128)(2,1)}, bf16[2048,512]{1,0:T(8,128)(2,1)}, bf16[512,2048]{1,0:T(8,128)(2,1)}, bf16[512,2048]{1,0:T(8,128)(2,1)}) custom-call(s32[1]{0:T(128)} %bitcast.sc, bf16[512,2048]{1,0:T(8,128)(2,1)} %refs_0_.1, bf16[512,2048]{1,0:T(8,128)(2,1)} %refs_6_.1, bf16[4096,128]{1,0:T(8,128)(2,1)} %bitcast.11, ...), custom_call_target="tpu_custom_call" | custom-call | flops 1073741824 | bytes 8000000 | tf_op jit(solution)/shard_map/pallas_call | solution.py:146
  7.2 3.0 %collective-permute-start.1 = (bf16[512,512]{1,0:T(8,128)(2,1)}, bf16[512,512]{1,0:T(8,128)(2,1)S(1)}, u32[]{:S(2)}, u32[]{:S(2)}) collective-permute-start(bf16[512,512]{1,0:T(8,128)(2,1)} %get-tuple-element.39.refs_4_), channel_id=1, source_target_pairs={{0,2},{2,0},{1,3},{3,1},{4,6},{6,4},{5,7},{7,5}} | collective-permute-start | bytes 1572872 | tf_op jit(solution)/shard_map/ppermute | solution.py:656
  10.2 0.0 collective-permute-start.4
  10.2 7.9 %shard_map.128.wq_hbm.refs_23_.refs_24_ = bf16[2048,2048]{1,0:T(8,128)(2,1)} custom-call(bf16[256,256]{1,0:T(8,128)(2,1)} %constant.11.clone.perm_ref, bf16[2048,16,128]{2,1,0:T(8,128)(2,1)} %w_hbm), custom_call_target="tpu_custom_call" | custom-call | flops 4000000000 | bytes 16777216 | tf_op jit(solution)/shard_map/pallas_call | solution.py:85
  18.1 4.5 %collective-permute-done.1.refs_6_ = bf16[512,512]{1,0:T(8,128)(2,1)S(1)} collective-permute-done((bf16[512,512]{1,0:T(8,128)(2,1)}, bf16[512,512]{1,0:T(8,128)(2,1)S(1)}, u32[]{:S(2)}, u32[]{:S(2)}) %collective-permute-start.1) | collective-permute-done | bytes 524320 | tf_op jit(solution)/shard_map/ppermute | solution.py:656
  22.5 0.0 copy-start
  22.5 0.0 collective-permute-start.5
  22.5 1.7 collective-permute-start
  24.3 0.0 collective-permute-done.4.refs_5_
  24.3 0.0 copy-start.1
  24.3 0.2 collective-permute-done.5.refs_7_
  24.4 0.6 copy-done.1
  25.1 0.0 copy-start.2
  25.1 0.0 collective-permute-done.2.refs_1_
  25.1 0.8 copy-done.2
  25.9 0.0 collective-permute-done.3.refs_3_.refs_7_
  25.9 0.0 copy-done
  25.9 53.4 %shard_map.129 = (bf16[1024,1024]{1,0:T(8,128)(2,1)}, bf16[1024,1024]{1,0:T(8,128)(2,1)}, f32[2048,256]{1,0:T(8,128)}, bf16[2048,1024]{1,0:T(8,128)(2,1)}) custom-call(s32[1]{0:T(128)} %bitcast.3.sc, bf16[2048,2048]{1,0:T(8,128)(2,1)} %shard_map.128.wq_hbm.refs_23_.refs_24_, bf16[2048,2048]{1,0:T(8,128)(2,1)} %bitcast.6, bf16[512,2048]{1,0:T(8,128)(2,1)} %refs_0_.1, ...), custom_call_target="tpu_custom_call" | custom-call | flops 32000000000 | bytes 20000000 | tf_op jit(solution)/shard_map/pallas_call | solution.py:424
  79.3 0.0 collective-permute-done.refs_0_.refs_2_.refs_8_
  79.3 0.3 collective-permute-start.8
  79.6 1.0 collective-permute-start.7
  80.6 3.2 %collective-permute-done.8.refs_1_.refs_3_.refs_9_ = bf16[512,2048]{1,0:T(8,128)(2,1)} collective-permute-done((bf16[512,2048]{1,0:T(8,128)(2,1)}, bf16[512,2048]{1,0:T(8,128)(2,1)}, u32[]{:S(2)}, u32[]{:S(2)}) %collective-permute-start.8) | collective-permute-done | bytes 2097184 | tf_op jit(solution)/shard_map/ppermute | solution.py:655
  83.8 32.4 %shard_map.130 = (bf16[1024,512]{1,0:T(8,128)(2,1)}, bf16[512,1024]{1,0:T(8,128)(2,1)}, f32[2048,256]{1,0:T(8,128)}, bf16[2048,512]{1,0:T(8,128)(2,1)}) custom-call(s32[1]{0:T(128)} %bitcast.3.sc, bf16[2048,2048]{1,0:T(8,128)(2,1)} %shard_map.128.wq_hbm.refs_23_.refs_24_, bf16[2048,2048]{1,0:T(8,128)(2,1)} %bitcast.7, ...), custom_call_target="tpu_custom_call" | custom-call | flops 16000000000 | bytes 20000000 | tf_op jit(solution)/shard_map/pallas_call | solution.py:424
  116.2 11.5 %collective-permute-done.7.refs_0_.refs_2_.refs_10_ = bf16[512,2048]{1,0:T(8,128)(2,1)} collective-permute-done((bf16[512,2048]{1,0:T(8,128)(2,1)}, bf16[512,2048]{1,0:T(8,128)(2,1)}, u32[]{:S(2)}, u32[]{:S(2)}) %collective-permute-start.7) | collective-permute-done | bytes 2097184 | tf_op jit(solution)/shard_map/ppermute | solution.py:656
  127.7 0.0 collective-permute-start.9
  127.7 0.5 collective-permute-start.6
  128.2 0.0 collective-permute-start.12
  128.2 0.5 collective-permute-start.10
  128.7 0.0 collective-permute-start.13
  128.7 3.5 %collective-permute-done.9.refs_1_.refs_3_.refs_11_ = bf16[512,2048]{1,0:T(8,128)(2,1)} collective-permute-done((bf16[512,2048]{1,0:T(8,128)(2,1)}, bf16[512,2048]{1,0:T(8,128)(2,1)}, u32[]{:S(2)}, u32[]{:S(2)}) %collective-permute-start.9) | collective-permute-done | bytes 2097184 | tf_op jit(solution)/shard_map/ppermute | solution.py:655
  132.2 28.0 %shard_map.131 = (bf16[1024,512]{1,0:T(8,128)(2,1)}, bf16[512,1024]{1,0:T(8,128)(2,1)}, bf16[2048,256]{1,0:T(8,128)(2,1)}, bf16[2048,512]{1,0:T(8,128)(2,1)}) custom-call(s32[1]{0:T(128)} %bitcast.3.sc, bf16[2048,2048]{1,0:T(8,128)(2,1)} %shard_map.128.wq_hbm.refs_23_.refs_24_, bf16[2048,2048]{1,0:T(8,128)(2,1)} %bitcast.8, ...), custom_call_target="tpu_custom_call" | custom-call | flops 16000000000 | bytes 20000000 | tf_op jit(solution)/shard_map/pallas_call | solution.py:424
  160.1 0.0 collective-permute-done.6.o_other.refs_3_
  160.2 0.2 collective-permute-start.15
  160.3 0.4 collective-permute-start.11
  160.7 0.0 collective-permute-done.12.refs_15_
  160.7 0.2 collective-permute-start.14
  160.8 9.3 %shard_map.132 = bf16[512,2048]{1,0:T(8,128)(2,1)} custom-call(s32[1]{0:T(128)} %bitcast.sc, bf16[1024,1024]{1,0:T(8,128)(2,1)} %get-tuple-element.45.o_mine.refs_0_, bf16[1024,1024]{1,0:T(8,128)(2,1)} %collective-permute-done.6.o_other.refs_3_, bf16[2048,2048]{1,0:T(8,128)(2,1)} %bitcast.9, bf16[2048,2048]{1,0:T(8,128)(2,1)} %bitcast.10), custom_call_target="tpu_custom_call" | custom-call | flops 4294967296 | bytes 12000000 | tf_op jit(solution)/shard_map/pallas_call | solution.py:473
  170.1 0.0 collective-permute-done.10.refs_4_
  170.1 0.0 collective-permute-done.13.refs_16_
  170.1 0.0 collective-permute-done.15.refs_19_
  170.1 0.0 collective-permute-done.11.refs_5_
  170.2 0.0 collective-permute-done.14.refs_17_
  170.2 61.8 %shard_map.133 = (f32[2048,2048]{1,0:T(8,128)}, f32[2048,16,128]{2,1,0:T(8,128)}, f32[2048,2,128]{2,1,0:T(2,128)}, f32[2048,2,128]{2,1,0:T(2,128)}, bf16[512,2048]{1,0:T(8,128)(2,1)}) custom-call(s32[1]{0:T(128)} %bitcast.sc, bf16[1024,1024]{1,0:T(8,128)(2,1)} %get-tuple-element.45.o_mine.refs_0_, bf16[1024,512]{1,0:T(8,128)(2,1)} %get-tuple-element.55.refs_1_, ...), custom_call_target="tpu_custom_call" | custom-call | flops 49999998976 | bytes 80000000 | tf_op jit(solution)/shard_map/pallas_call | solution.py:598
Async XLA Ops:
  0.6 24.4 %collective-permute-start.2 = (bf16[512,2048]{1,0:T(8,128)(2,1)}, bf16[512,2048]{1,0:T(8,128)(2,1)}, u32[]{:S(2)}, u32[]{:S(2)}) collective-permute-start(bf16[512,2048]{1,0:T(8,128)(2,1)} %refs_0_.1), channel_id=1, source_target_pairs={{0,1},{1,0},{2,3},{3,2},{4,5},{5,4},{6,7},{7,6}} | collective-permute-start | bytes 6291464 | tf_op jit(solution)/shard_map/ppermute | solution.py:655
  1.5 24.4 %collective-permute-start.3 = (bf16[512,2048]{1,0:T(8,128)(2,1)}, bf16[512,2048]{1,0:T(8,128)(2,1)}, u32[]{:S(2)}, u32[]{:S(2)}) collective-permute-start(bf16[512,2048]{1,0:T(8,128)(2,1)} %refs_6_.1), channel_id=1, source_target_pairs={{0,1},{1,0},{2,3},{3,2},{4,5},{5,4},{6,7},{7,6}} | collective-permute-start | bytes 6291464 | tf_op jit(solution)/shard_map/ppermute | solution.py:655
  7.2 15.3 %collective-permute-start.1 = (bf16[512,512]{1,0:T(8,128)(2,1)}, bf16[512,512]{1,0:T(8,128)(2,1)S(1)}, u32[]{:S(2)}, u32[]{:S(2)}) collective-permute-start(bf16[512,512]{1,0:T(8,128)(2,1)} %get-tuple-element.39.refs_4_), channel_id=1, source_target_pairs={{0,2},{2,0},{1,3},{3,1},{4,6},{6,4},{5,7},{7,5}} | collective-permute-start | bytes 1572872 | tf_op jit(solution)/shard_map/ppermute | solution.py:656
  10.2 14.1 %collective-permute-start.4 = (bf16[512,512]{1,0:T(8,128)(2,1)}, bf16[512,512]{1,0:T(8,128)(2,1)S(1)}, u32[]{:S(2)}, u32[]{:S(2)}) collective-permute-start(bf16[512,512]{1,0:T(8,128)(2,1)} %get-tuple-element.39.refs_4_), channel_id=1, source_target_pairs={{0,1},{1,0},{2,3},{3,2},{4,5},{5,4},{6,7},{7,6}} | collective-permute-start | bytes 1572872 | tf_op jit(solution)/shard_map/ppermute | solution.py:655
  22.5 3.4 %copy-start = (bf16[512,512]{1,0:T(8,128)(2,1)}, bf16[512,512]{1,0:T(8,128)(2,1)S(1)}, u32[]{:S(2)}) copy-start(bf16[512,512]{1,0:T(8,128)(2,1)S(1)} %collective-permute-done.1.refs_6_) | copy-start | bytes 1572868
  22.5 1.9 collective-permute-start.5
  22.5 56.7 %collective-permute-start = (bf16[512,2048]{1,0:T(8,128)(2,1)}, bf16[512,2048]{1,0:T(8,128)(2,1)}, u32[]{:S(2)}, u32[]{:S(2)}) collective-permute-start(bf16[512,2048]{1,0:T(8,128)(2,1)} %get-tuple-element.38), channel_id=1, source_target_pairs={{0,2},{2,0},{1,3},{3,1},{4,6},{6,4},{5,7},{7,5}} | collective-permute-start | bytes 6291464 | tf_op jit(solution)/shard_map/ppermute | solution.py:656
  24.3 0.8 copy-start.1
  25.1 0.8 copy-start.2
  79.3 4.5 %collective-permute-start.8 = (bf16[512,2048]{1,0:T(8,128)(2,1)}, bf16[512,2048]{1,0:T(8,128)(2,1)}, u32[]{:S(2)}, u32[]{:S(2)}) collective-permute-start(bf16[512,2048]{1,0:T(8,128)(2,1)} %collective-permute-done.refs_0_.refs_2_.refs_8_), channel_id=1, source_target_pairs={{0,1},{1,0},{2,3},{3,2},{4,5},{5,4},{6,7},{7,6}} | collective-permute-start | bytes 6291464 | tf_op jit(solution)/shard_map/ppermute | solution.py:655
  79.6 48.1 %collective-permute-start.7 = (bf16[512,2048]{1,0:T(8,128)(2,1)}, bf16[512,2048]{1,0:T(8,128)(2,1)}, u32[]{:S(2)}, u32[]{:S(2)}) collective-permute-start(bf16[512,2048]{1,0:T(8,128)(2,1)} %get-tuple-element.46), channel_id=1, source_target_pairs={{0,2},{2,0},{1,3},{3,1},{4,6},{6,4},{5,7},{7,5}} | collective-permute-start | bytes 6291464 | tf_op jit(solution)/shard_map/ppermute | solution.py:656
  127.7 4.5 %collective-permute-start.9 = (bf16[512,2048]{1,0:T(8,128)(2,1)}, bf16[512,2048]{1,0:T(8,128)(2,1)}, u32[]{:S(2)}, u32[]{:S(2)}) collective-permute-start(bf16[512,2048]{1,0:T(8,128)(2,1)} %collective-permute-done.7.refs_0_.refs_2_.refs_10_), channel_id=1, source_target_pairs={{0,1},{1,0},{2,3},{3,2},{4,5},{5,4},{6,7},{7,6}} | collective-permute-start | bytes 6291464 | tf_op jit(solution)/shard_map/ppermute | solution.py:655
  127.7 32.5 %collective-permute-start.6 = (bf16[1024,1024]{1,0:T(8,128)(2,1)}, bf16[1024,1024]{1,0:T(8,128)(2,1)}, u32[]{:S(2)}, u32[]{:S(2)}) collective-permute-start(bf16[1024,1024]{1,0:T(8,128)(2,1)} %get-tuple-element.45.o_mine.refs_0_), channel_id=1, source_target_pairs={{0,1},{1,0},{2,3},{3,2},{4,5},{5,4},{6,7},{7,6}} | collective-permute-start | bytes 6291464 | tf_op jit(solution)/shard_map/ppermute | solution.py:655
  128.2 32.5 %collective-permute-start.12 = (bf16[1024,1024]{1,0:T(8,128)(2,1)}, bf16[1024,1024]{1,0:T(8,128)(2,1)}, u32[]{:S(2)}, u32[]{:S(2)}) collective-permute-start(bf16[1024,1024]{1,0:T(8,128)(2,1)} %get-tuple-element.57.refs_12_), channel_id=1, source_target_pairs={{0,1},{1,0},{2,3},{3,2},{4,5},{5,4},{6,7},{7,6}} | collective-permute-start | bytes 6291464 | tf_op jit(solution)/shard_map/ppermute | solution.py:655
  128.2 42.0 %collective-permute-start.10 = (bf16[1024,512]{1,0:T(8,128)(2,1)}, bf16[1024,512]{1,0:T(8,128)(2,1)}, u32[]{:S(2)}, u32[]{:S(2)}) collective-permute-start(bf16[1024,512]{1,0:T(8,128)(2,1)} %get-tuple-element.55.refs_1_), channel_id=1, source_target_pairs={{0,1},{1,0},{2,3},{3,2},{4,5},{5,4},{6,7},{7,6}} | collective-permute-start | bytes 3145736 | tf_op jit(solution)/shard_map/ppermute | solution.py:655
  128.7 41.5 %collective-permute-start.13 = (bf16[512,1024]{1,0:T(8,128)(2,1)}, bf16[512,1024]{1,0:T(8,128)(2,1)}, u32[]{:S(2)}, u32[]{:S(2)}) collective-permute-start(bf16[512,1024]{1,0:T(8,128)(2,1)} %get-tuple-element.58.refs_13_), channel_id=1, source_target_pairs={{0,1},{1,0},{2,3},{3,2},{4,5},{5,4},{6,7},{7,6}} | collective-permute-start | bytes 3145736 | tf_op jit(solution)/shard_map/ppermute | solution.py:655
  160.2 10.0 %collective-permute-start.15 = (bf16[2048,256]{1,0:T(8,128)(2,1)}, bf16[2048,256]{1,0:T(8,128)(2,1)}, u32[]{:S(2)}, u32[]{:S(2)}) collective-permute-start(bf16[2048,256]{1,0:T(8,128)(2,1)} %get-tuple-element.60.refs_18_), channel_id=1, source_target_pairs={{0,1},{1,0},{2,3},{3,2},{4,5},{5,4},{6,7},{7,6}} | collective-permute-start | bytes 3145736 | tf_op jit(solution)/shard_map/ppermute | solution.py:655
  160.3 9.8 %collective-permute-start.11 = (bf16[1024,512]{1,0:T(8,128)(2,1)}, bf16[1024,512]{1,0:T(8,128)(2,1)}, u32[]{:S(2)}, u32[]{:S(2)}) collective-permute-start(bf16[1024,512]{1,0:T(8,128)(2,1)} %get-tuple-element.56.refs_2_), channel_id=1, source_target_pairs={{0,1},{1,0},{2,3},{3,2},{4,5},{5,4},{6,7},{7,6}} | collective-permute-start | bytes 3145736 | tf_op jit(solution)/shard_map/ppermute | solution.py:655
  160.7 9.5 %collective-permute-start.14 = (bf16[512,1024]{1,0:T(8,128)(2,1)}, bf16[512,1024]{1,0:T(8,128)(2,1)}, u32[]{:S(2)}, u32[]{:S(2)}) collective-permute-start(bf16[512,1024]{1,0:T(8,128)(2,1)} %get-tuple-element.59.refs_14_), channel_id=1, source_target_pairs={{0,1},{1,0},{2,3},{3,2},{4,5},{5,4},{6,7},{7,6}} | collective-permute-start | bytes 3145736 | tf_op jit(solution)/shard_map/ppermute | solution.py:655
